TPU v7x, 32 devices: a whole 2x2x4 slice. The times are simulated.
32 devices in a mesh: groups: 2 (over x), mp: 8 (over z, y), psg: 2 (over core).
Axes of the slice: x: 2, y: 2, z: 4, core: 2. Of those that a mesh axis runs over, the one named last changes fastest.
Arguments:
- tokens: bfloat16 [512, 1024], P(('groups', 'mp', 'psg')), parts along dimension 0, may hold values from -6 to 6
- enc_gain: float32 [1024], replicated, may hold values from 0.25 to 1.75
- w_in: bfloat16 [1024, 32768], P(None, 'mp'), may hold values from -0.1875 to 0.1875
- w_out: bfloat16 [32768, 1024], P('mp'), may hold values from -0.046875 to 0.046875
- final_gain: float32 [1024], replicated, may hold values from 0.25 to 1.75
- w_keyval: bfloat16 [1024, 2, 16384], P(None, None, 'mp'), may hold values from -0.1875 to 0.1875
- answer_states: bfloat16 [256, 1024], P('groups'), parts along dimension 0, may hold values from -6 to 6
- dec_gain: float32 [1024], replicated, may hold values from 0.25 to 1.75
- w_query: bfloat16 [1024, 16384], P(None, 'mp')
- w_attn_out: bfloat16 [16384, 1024], P('mp'), may hold values from -0.046875 to 0.046875
- passage_lengths: int32 [32], P('groups'), parts along dimension 0, may hold values from 1 to 16
- passage_owner: int32 [32], P('groups'), parts along dimension 0, may hold values from 0 to 3, as said below
- answer_lengths: int32 [8], P('groups'), parts along dimension 0, may hold values from 1 to 64, 128 in all
Outputs:
- encoded: bfloat16 [512, 1024], P(('groups', 'mp', 'psg')), parts along dimension 0
- answer: bfloat16 [256, 1024], P(('groups', 'mp')), parts along dimension 0
There are 2 independent parts, one for each index of `groups`. A program takes and returns all parts, laid end to end along the dimension named above; an argument that names none is the same for every part. Nothing has to cross between parts.
Inputs may be any that keep to these rules, and one draw needn't show every extreme that they name: `passage_owner`: every one of the 4 questions owns at least one passage.
All inputs are finite; a program needn't handle non-finite values.
Results may differ from a plain program's by a relative error of at most 0.028.
Values may be sent and summed in bfloat16 or wider, within the bound.
No kernel may reach another device: no remote copies, remote signals or barrier semaphores. Data moves between devices by JAX's collectives and lax.ppermute only.
A program may use at most 128 MiB of HBM per device.

v0:
```python
import jax
import jax.numpy as jnp
from jax import lax
from jax.sharding import PartitionSpec as P

DH = 128
P_SLOT = 16


eps = 1e-06


def merged(x, axis, combine):
    everything = jax.tree.map(lambda part: lax.all_gather(part, axis), x)
    initial = jax.tree.map(lambda part: part[0], everything)

    def step(k, so_far):
        return combine(so_far, jax.tree.map(lambda part: part[k], everything))

    return lax.fori_loop(1, lax.axis_size(axis), step, initial)


def norm_rows(states, gain):
    wide = states.astype(jnp.float32)
    factor = lax.rsqrt(jnp.mean(wide * wide, axis=-1, keepdims=True) + eps)
    return wide * factor * gain


def key_mask(token_index, passage_lengths, passage_owner, answer_lengths, answer_count):
    passage = token_index // P_SLOT
    place = token_index % P_SLOT
    count = passage_lengths.shape[0]
    match = passage[:, None] == jnp.arange(count, dtype=jnp.int32)[None, :]
    token_length = jnp.sum(jnp.where(match, passage_lengths[None, :], 0), axis=1)
    token_owner = jnp.sum(jnp.where(match, passage_owner[None, :], 0), axis=1)
    ends = jnp.cumsum(answer_lengths)
    answer_index = jnp.arange(answer_count, dtype=jnp.int32)
    question = jnp.sum((answer_index[:, None] >= ends[None, :]).astype(jnp.int32), axis=1)
    return (place < token_length)[None, :] & (token_owner[None, :] == question[:, None])


def attend_local(query, keys, values, allowed):
    scores = jnp.einsum("qhd,khd->hqk", query, keys, preferred_element_type=jnp.float32) * DH ** (
        -0.5
    )
    scores = jnp.where(allowed[None], scores, -1e30)
    top = jnp.max(scores, axis=2)
    weights = jnp.where(allowed[None], jnp.exp(scores - top[..., None]), 0.0)
    total = jnp.sum(weights, axis=2)
    summed = jnp.einsum(
        "hqk,khd->hqd", weights.astype(jnp.bfloat16), values, preferred_element_type=jnp.float32
    )
    return (top, total, summed)


def combine(left_part, right_part):
    left_top, left_total, left_sum = left_part
    right_top, right_total, right_sum = right_part
    new_top = jnp.maximum(left_top, right_top)
    left_factor = jnp.exp(left_top - new_top)
    right_factor = jnp.exp(right_top - new_top)
    new_total = left_total * left_factor + right_total * right_factor
    new_sum = left_sum * left_factor[..., None] + right_sum * right_factor[..., None]
    return (new_top, new_total, new_sum)


def per_device(
    tokens,
    enc_gain,
    w_in,
    w_out,
    final_gain,
    w_keyval,
    answer_states,
    dec_gain,
    w_query,
    w_attn_out,
    passage_lengths,
    passage_owner,
    answer_lengths,
):
    row_count = tokens.shape[0]
    model_width = tokens.shape[1]
    answer_count = answer_states.shape[0]
    mp_count = lax.axis_size("mp")
    psg_count = lax.axis_size("psg")
    mp_index = lax.axis_index("mp")
    psg_index = lax.axis_index("psg")
    head_local = w_query.shape[1] // DH
    inner_local = head_local * DH
    joined_weight = w_keyval.reshape(model_width, 2 * inner_local)
    normed = norm_rows(lax.all_gather(tokens, "mp", axis=0, tiled=True), enc_gain).astype(
        jnp.bfloat16
    )
    hidden = jnp.maximum(jnp.dot(normed, w_in, preferred_element_type=jnp.float32), 0.0).astype(
        jnp.bfloat16
    )
    partial_sums = jnp.dot(hidden, w_out, preferred_element_type=jnp.float32)
    own_rows = tokens.astype(jnp.float32)
    summed_rows = lax.psum_scatter(partial_sums, "mp", scatter_dimension=0, tiled=True)
    encoded = (own_rows + summed_rows).astype(jnp.bfloat16)
    memory = norm_rows(encoded, final_gain).astype(jnp.bfloat16)
    joined = jnp.dot(
        lax.all_gather(memory, "mp", axis=0, tiled=True),
        joined_weight,
        preferred_element_type=jnp.float32,
    ).astype(jnp.bfloat16)
    key_rows = joined.shape[0]
    keys = joined[:, :inner_local].reshape(key_rows, head_local, DH)
    values = joined[:, inner_local:].reshape(key_rows, head_local, DH)
    normed_answer = norm_rows(answer_states, dec_gain).astype(jnp.bfloat16)
    query = jnp.dot(normed_answer, w_query, preferred_element_type=jnp.float32).astype(jnp.bfloat16)
    query = query.reshape(answer_count, head_local, DH)
    local_index = jnp.arange(key_rows, dtype=jnp.int32)
    block = local_index // row_count
    token_index = (block * psg_count + psg_index) * row_count + local_index % row_count
    allowed = key_mask(token_index, passage_lengths, passage_owner, answer_lengths, answer_count)
    partial_attention = attend_local(query, keys, values, allowed)
    top, total, summed = merged(partial_attention, "psg", combine)
    context = (summed / total[..., None]).astype(jnp.bfloat16)
    context = context.transpose(1, 0, 2).reshape(answer_count, inner_local)
    out_count = answer_count // mp_count
    block = context
    result = lax.psum_scatter(
        jnp.dot(block, w_attn_out, preferred_element_type=jnp.float32),
        "mp",
        scatter_dimension=0,
        tiled=True,
    )
    own_answer = lax.dynamic_slice_in_dim(answer_states, mp_index * out_count, out_count, 0).astype(
        jnp.float32
    )
    return (encoded, (own_answer + result).astype(jnp.bfloat16))


def solution(mesh):
    placed = (
        P(("groups", "mp", "psg"), None),
        P(),
        P(None, "mp"),
        P("mp", None),
        P(),
        P(None, None, "mp"),
        P("groups", None),
        P(),
        P(None, "mp"),
        P("mp", None),
        P("groups"),
        P("groups"),
        P("groups"),
    )
    return jax.shard_map(
        per_device,
        mesh=mesh,
        in_specs=placed,
        out_specs=(P(("groups", "mp", "psg"), None), P(("groups", "mp"), None)),
        check_vma=False,
    )
```

profile of v0, /device:TPU:0, one launch (start us, length us, event | category | flops | bytes accessed | tf_op | source)
XLA Modules:
  0.0 240.3 jit_solution(5375088046361659702)
XLA Ops:
  7.2 0.0 reduce-scatter.3.cloned.1.call-start
  7.2 32.8 %all_gather.24 = bf16[128,1024]{1,0:T(8,128)(2,1)S(1)} all-gather(bf16[16,1024]{1,0:T(8,128)(2,1)} %param.13), channel_id=1, replica_groups=mesh['groups'=2,'mp'=8,'psg'=2] {'mp'}, dimensions={0}, use_global_device_ids=true | all-gather | bytes 294912 | tf_op jit(solution)/shard_map/all_gather | solution.py:92
  40.0 0.1 fusion.6
  40.1 0.0 copy-start.1
  40.1 0.0 copy-start.8
  40.1 0.0 copy-start.6
  40.2 0.0 copy-start.7
  40.2 9.1 %fusion.5 = f32[128,1024]{1,0:T(8,128)} fusion(bf16[4096,1024]{1,0:T(8,128)(2,1)} %param.16, bf16[1024,4096]{1,0:T(8,128)(2,1)} %param.15, bf16[128,1024]{1,0:T(8,128)(2,1)S(1)} %all_gather.24, f32[1024]{0:T(1024)} %param.14, f32[128]{0:T(128)S(1)} %add_rsqrt_fusion.2), kind=kOutput, calls=%fused_computation.11 | convolution fusion | flops 2149056512 | bytes 17568256 | tf_op jit(solution)/shard_map/dot_general | solution.py:98
  49.2 0.0 reduce-scatter.3.cloned.1.call-update
  49.3 0.0 all-gather.5.cloned.1.call-start
  49.3 0.0 copy-done.1
  49.3 0.1 fusion.9
  49.5 0.0 copy-done.8
  49.5 0.2 reduce-window.8
  49.7 0.0 copy-done.6
  49.7 0.0 copy-done.7
  49.7 0.1 select_reduce_fusion.1
  49.8 0.1 convert_reduce_fusion
  49.8 0.0 copy-start
  49.8 0.0 copy-start.5
  49.8 0.0 copy-start.2
  49.9 0.0 copy-start.4
  49.9 12.2 %copy.42 = bf16[128,8,2,2048]{3,1,2,0:T(8,128)(2,1)} copy(bf16[128,8,2,2048]{3,2,1,0:T(2,128)(2,1)} %bitcast.34) | data formatting | bytes 16777216
  62.1 0.1 compare_and_fusion
  62.2 0.0 copy-done
  62.2 0.0 copy-done.5
  62.2 0.8 fusion.2
  63.0 50.1 %reduce-scatter.3.cloned.1.call-done = f32[16,1024]{1,0:T(8,128)} async-done(((f32[128,1024]{1,0:T(8,128)}), f32[16,1024]{1,0:T(8,128)}) %reduce-scatter.3.cloned.1.call-update) | async-done | bytes 65552 | tf_op jit(solution)/shard_map/reduce_scatter | solution.py:100
  113.1 0.0 copy-done.2
  113.1 1.0 fusion.32
  114.1 0.0 copy-start.3
  114.1 0.0 copy-done.4
  114.1 0.1 fusion.34
  114.2 31.0 %all_gather.25 = bf16[128,1024]{1,0:T(8,128)(2,1)S(1)} all-gather(bf16[16,1024]{1,0:T(8,128)(2,1)S(1)} %fusion.34), channel_id=1, replica_groups=mesh['groups'=2,'mp'=8,'psg'=2] {'mp'}, dimensions={0}, use_global_device_ids=true | all-gather | bytes 294912 | tf_op jit(solution)/shard_map/all_gather | solution.py:104
  145.2 4.6 %convolution_convert_fusion = bf16[128,4096]{1,0:T(8,128)(2,1)S(1)} fusion(bf16[128,1024]{1,0:T(8,128)(2,1)S(1)} %all_gather.25, bf16[1024,4096]{1,0:T(8,128)(2,1)} %bitcast.33), kind=kOutput, calls=%fused_computation.2 | convolution fusion | flops 1074266112 | bytes 9699328 | tf_op jit(solution)/shard_map/dot_general | solution.py:103
  149.8 0.1 slice_bitcast_fusion
  149.9 0.5 fusion.48
  150.5 0.0 copy-done.3
  150.5 1.4 fusion.12
  151.9 0.0 all-gather.5.cloned.1.call-update
  151.9 0.0 reduce-scatter.5.cloned.1.call-start
  151.9 1.8 all-gather.1
  153.8 0.2 fusion.3
  154.0 1.8 all-gather.2
  155.8 5.8 %all-gather.5.cloned.1.call-done = f32[32,128,128]{2,1,0:T(8,128)} async-done(((f32[16,128,128]{2,1,0:T(8,128)}), f32[32,128,128]{2,1,0:T(8,128)}) %all-gather.5.cloned.1.call-update) | async-done | bytes 2097168 | tf_op jit(solution)/shard_map/all_gather | solution.py:14
  161.5 1.7 fusion.47
  163.2 0.3 copy.38
  163.6 0.3 copy.37
  163.9 0.2 divide_convert_fusion
  164.1 3.7 %fusion.49 = f32[128,1024]{1,0:T(8,128)} fusion(bf16[128,2048]{0,1:T(8,128)(2,1)S(1)} %bitcast.35, bf16[2048,1024]{1,0:T(8,128)(2,1)} %param.22), kind=kOutput, calls=%fused_computation.80 | convolution fusion | flops 536870912 | bytes 5242880 | tf_op jit(solution)/shard_map/dot_general | solution.py:125
  167.9 0.0 reduce-scatter.5.cloned.1.call-update
  167.9 64.4 %reduce-scatter.5.cloned.1.call-done = f32[16,1024]{1,0:T(8,128)} async-done(((f32[128,1024]{1,0:T(8,128)}), f32[16,1024]{1,0:T(8,128)}) %reduce-scatter.5.cloned.1.call-update) | async-done | bytes 65552 | tf_op jit(solution)/shard_map/reduce_scatter | solution.py:124
  232.3 1.5 add_convert_fusion
  (6 shorter events, 0.1 us)
Async XLA Ops:
  7.2 105.9 %reduce-scatter.3.cloned.1.call-start = ((), (), s32[]{:S(2)}) async-start(), calls=%async_computation.2 | async-start | bytes 589824 | tf_op jit(solution)/shard_map/reduce_scatter | solution.py:100
  40.1 9.2 %copy-start.1 = (bf16[128,1024]{1,0:T(8,128)(2,1)S(1)}, bf16[128,1024]{1,0:T(8,128)(2,1)}, u32[]{:S(2)}) copy-start(bf16[128,1024]{1,0:T(8,128)(2,1)} %param.19) | copy-start | bytes 786436
  40.1 9.4 %copy-start.8 = (s32[4]{0:T(128)S(1)}, s32[4]{0:T(128)}, u32[]{:S(2)}) copy-start(s32[4]{0:T(128)} %param.25) | copy-start | bytes 52
  40.1 9.5 %copy-start.6 = (s32[16]{0:T(128)S(1)}, s32[16]{0:T(128)}, u32[]{:S(2)}) copy-start(s32[16]{0:T(128)} %param.23) | copy-start | bytes 196
  40.2 9.5 %copy-start.7 = (s32[16]{0:T(128)S(1)}, s32[16]{0:T(128)}, u32[]{:S(2)}) copy-start(s32[16]{0:T(128)} %param.24) | copy-start | bytes 196
  49.3 112.3 %all-gather.5.cloned.1.call-start = ((), (), s32[]{:S(2)}) async-start(), calls=%async_computation.4 | async-start | bytes 3145728 | tf_op jit(solution)/shard_map/all_gather | solution.py:14
  49.8 12.4 %copy-start = (bf16[1024,2048]{1,0:T(8,128)(2,1)S(1)}, bf16[1024,2048]{1,0:T(8,128)(2,1)}, u32[]{:S(2)}) copy-start(bf16[1024,2048]{1,0:T(8,128)(2,1)} %param.21) | copy-start | bytes 12582916
  49.8 12.4 %copy-start.5 = (f32[1024]{0:T(1024)S(1)}, f32[1024]{0:T(1024)}, u32[]{:S(2)}) copy-start(f32[1024]{0:T(1024)} %param.20) | copy-start | bytes 12292
  49.8 63.3 %copy-start.2 = (bf16[16,1024]{1,0:T(8,128)(2,1)S(1)}, bf16[16,1024]{1,0:T(8,128)(2,1)}, u32[]{:S(2)}) copy-start(bf16[16,1024]{1,0:T(8,128)(2,1)} %param.13) | copy-start | bytes 98308
  49.9 64.2 %copy-start.4 = (f32[1024]{0:T(1024)S(1)}, f32[1024]{0:T(1024)}, u32[]{:S(2)}) copy-start(f32[1024]{0:T(1024)} %param.17) | copy-start | bytes 12292
  114.1 36.4 %copy-start.3 = (bf16[16,1024]{1,0:T(8,128)(2,1)}, bf16[16,1024]{1,0:T(8,128)(2,1)S(1)}, u32[]{:S(2)}) copy-start(bf16[16,1024]{1,0:T(8,128)(2,1)S(1)} %get-tuple-element.32) | copy-start | bytes 98308
  151.9 80.4 %reduce-scatter.5.cloned.1.call-start = ((), (), s32[]{:S(2)}) async-start(), calls=%async_computation.3 | async-start | bytes 589824 | tf_op jit(solution)/shard_map/reduce_scatter | solution.py:124
Sparse Core Ops, SparseCore 0:
  49.4 63.6 reduce-scatter.2
  152.0 9.4 all-gather.4
  168.0 64.2 reduce-scatter.4
where the time goes:
time: 241 us; the launch traced here: 240 us
  waiting for transfers between devices  120 us (50%)
  blocking collectives  67.4 us (28%)
  matrix products  20.2 us (8%)
  local copies, waits for them, and re-layouts  14.7 us (6%)
  between operations  13.9 us (6%)
  other arithmetic  3.72 us (2%)
    reduce_scatter x1, waiting for transfers between devices, per_device(): lax.psum_scatter(jnp.dot(block, w_attn_out, preferred_element_type=jnp.fl...  64.4 us
    reduce_scatter x1, waiting for transfers between devices, per_device(): lax.psum_scatter(partial_sums, 'mp', scatter_dimension=0, tiled=True)  50.1 us
    all_gather x1, blocking collectives, per_device(): lax.all_gather(tokens, 'mp', axis=0, tiled=True)  32.8 us
    all_gather x1, blocking collectives, per_device(): lax.all_gather(memory, 'mp', axis=0, tiled=True)  31 us
    unnamed x22, local copies, waits for them, and re-layouts  13 us
    dot_general x1, matrix products, per_device(): partial_sums = jnp.dot(hidden, w_out, preferred_element_type=jnp.float32)  9.08 us
    all_gather x1, waiting for transfers between devices, merged(): everything = jax.tree.map(lambda part: lax.all_gather(part, axis), x)  5.75 us
  transfers between devices with their start and end apart: 3, of which 3 were waited for; matrix products, arithmetic and copies ran while one was open for 6% of the time, Pallas kernels for 0%

commit v1 on v0

v1 whole, which is shorter than its diff:
```python
import jax
import jax.numpy as jnp
from jax import lax
from jax.sharding import PartitionSpec as P

DH = 128
P_SLOT = 16


eps = 1e-06


def norm_rows(states, gain):
    wide = states.astype(jnp.float32)
    factor = lax.rsqrt(jnp.mean(wide * wide, axis=-1, keepdims=True) + eps)
    return wide * factor * gain


def key_mask(token_index, passage_lengths, passage_owner, answer_lengths, answer_count):
    passage = token_index // P_SLOT
    place = token_index % P_SLOT
    count = passage_lengths.shape[0]
    match = passage[:, None] == jnp.arange(count, dtype=jnp.int32)[None, :]
    token_length = jnp.sum(jnp.where(match, passage_lengths[None, :], 0), axis=1)
    token_owner = jnp.sum(jnp.where(match, passage_owner[None, :], 0), axis=1)
    number = answer_lengths.shape[0]
    order = jnp.arange(number, dtype=jnp.int32)
    ends = jnp.sum(jnp.where(order[:, None] <= order[None, :], answer_lengths[:, None], 0), axis=0)
    answer_index = jnp.arange(answer_count, dtype=jnp.int32)
    question = jnp.sum((answer_index[:, None] >= ends[None, :]).astype(jnp.int32), axis=1)
    return (place < token_length)[None, :] & (token_owner[None, :] == question[:, None])


def gather_mp(x, count):
    return lax.all_to_all(jnp.broadcast_to(x[None], (count,) + x.shape), "mp", 0, 0)


def swap_psg(x):
    return lax.ppermute(x, "psg", [(0, 1), (1, 0)])


def per_device(
    tokens,
    enc_gain,
    w_in,
    w_out,
    final_gain,
    w_keyval,
    answer_states,
    dec_gain,
    w_query,
    w_attn_out,
    passage_lengths,
    passage_owner,
    answer_lengths,
):
    row_count = tokens.shape[0]
    width = tokens.shape[1]
    answer_count = answer_states.shape[0]
    mp = lax.axis_size("mp")
    psg = lax.axis_size("psg")
    mp_index = lax.axis_index("mp")
    psg_index = lax.axis_index("psg")
    heads = w_query.shape[1] // DH // psg
    inner = heads * DH

    everyone = gather_mp(tokens, mp).reshape(mp * row_count, width)
    normed = norm_rows(everyone, enc_gain).astype(jnp.bfloat16)
    hidden = jnp.maximum(jnp.dot(normed, w_in, preferred_element_type=jnp.float32), 0.0).astype(
        jnp.bfloat16
    )
    partial_sums = jnp.dot(hidden, w_out, preferred_element_type=jnp.float32).astype(jnp.bfloat16)
    parts = lax.all_to_all(partial_sums.reshape(mp, row_count, width), "mp", 0, 0)
    summed_rows = jnp.sum(parts.astype(jnp.float32), axis=0)
    encoded = (tokens.astype(jnp.float32) + summed_rows).astype(jnp.bfloat16)
    memory = norm_rows(encoded, final_gain).astype(jnp.bfloat16)
    mine = gather_mp(memory, mp).reshape(mp * row_count, width)
    theirs = swap_psg(mine)
    both = jnp.concatenate([mine, theirs], axis=0)
    key_rows = both.shape[0]

    start = psg_index * inner
    w_kv = lax.dynamic_slice_in_dim(w_keyval, start, inner, 2)
    w_q = lax.dynamic_slice_in_dim(w_query, start, inner, 1)
    w_o = lax.dynamic_slice_in_dim(w_attn_out, start, inner, 0)
    keys = jnp.dot(both, w_kv[:, 0], preferred_element_type=jnp.float32).astype(jnp.bfloat16)
    values = jnp.dot(both, w_kv[:, 1], preferred_element_type=jnp.float32).astype(jnp.bfloat16)
    keys = keys.reshape(key_rows, heads, DH)
    values = values.reshape(key_rows, heads, DH)
    normed_answer = norm_rows(answer_states, dec_gain).astype(jnp.bfloat16)
    query = jnp.dot(normed_answer, w_q, preferred_element_type=jnp.float32).astype(jnp.bfloat16)
    query = query.reshape(answer_count, heads, DH)

    local = jnp.arange(key_rows, dtype=jnp.int32)
    half = local // (mp * row_count)
    block = (local % (mp * row_count)) // row_count
    core = jnp.where(half == 0, psg_index, 1 - psg_index)
    token_index = (block * psg + core) * row_count + local % row_count
    allowed = key_mask(token_index, passage_lengths, passage_owner, answer_lengths, answer_count)
    scores = jnp.einsum("qhd,khd->hqk", query, keys, preferred_element_type=jnp.float32) * DH ** (
        -0.5
    )
    scores = jnp.where(allowed[None], scores, -1e30)
    top = jnp.max(scores, axis=2, keepdims=True)
    weights = jnp.where(allowed[None], jnp.exp(scores - top), 0.0)
    total = jnp.sum(weights, axis=2, keepdims=True)
    summed = jnp.einsum(
        "hqk,khd->hqd", weights.astype(jnp.bfloat16), values, preferred_element_type=jnp.float32
    )
    context = (summed / total).astype(jnp.bfloat16)
    context = context.transpose(1, 0, 2).reshape(answer_count, inner)
    partial_answer = jnp.dot(context, w_o, preferred_element_type=jnp.float32)

    out_count = answer_count // mp
    small = out_count // psg
    halves = partial_answer.reshape(mp, psg, small, width)
    keep = lax.dynamic_index_in_dim(halves, psg_index, 1, False)
    give = lax.dynamic_index_in_dim(halves, 1 - psg_index, 1, False)
    chip_sum = (keep + swap_psg(give)).astype(jnp.bfloat16)
    answer_parts = lax.all_to_all(chip_sum, "mp", 0, 0)
    own_start = mp_index * out_count + psg_index * small
    own_answer = lax.dynamic_slice_in_dim(answer_states, own_start, small, 0).astype(jnp.float32)
    piece = (own_answer + jnp.sum(answer_parts.astype(jnp.float32), axis=0)).astype(jnp.bfloat16)
    other = swap_psg(piece)
    first = jnp.where(psg_index == 0, piece, other)
    second = jnp.where(psg_index == 0, other, piece)
    return (encoded, jnp.concatenate([first, second], axis=0))


def solution(mesh):
    placed = (
        P(("groups", "mp", "psg"), None),
        P(),
        P(None, "mp"),
        P("mp", None),
        P(),
        P(None, None, "mp"),
        P("groups", None),
        P(),
        P(None, "mp"),
        P("mp", None),
        P("groups"),
        P("groups"),
        P("groups"),
    )
    return jax.shard_map(
        per_device,
        mesh=mesh,
        in_specs=placed,
        out_specs=(P(("groups", "mp", "psg"), None), P(("groups", "mp"), None)),
        check_vma=False,
    )
```

time: 241 us -> 87.3 us (0.36)
  waiting for transfers between devices: 120 us -> 24.7 us
  blocking collectives: 67.4 us -> 0 us
  starting transfers between devices: 0.12 us -> 20.8 us
  between operations: 13.9 us -> 0.85 us
    reduce_scatter x2 -> x0, waiting for transfers between devices: 114 us -> none  [the longest x1 64.4 us: per_device(): lax.psum_scatter(jnp.dot(block, w_attn_out, preferred_element_type=jnp.fl...]
    all_gather x4 -> x0, blocking collectives: 67.4 us -> none  [the longest x1 32.8 us: per_device(): lax.all_gather(tokens, 'mp', axis=0, tiled=True)]
    all_to_all x0 -> x4, waiting for transfers between devices: none -> 20.7 us  [the longest x1 7.34 us: per_device(): answer_parts = lax.all_to_all(chip_sum, 'mp', 0, 0)]
    all_to_all x0 -> x4, starting transfers between devices: none -> 20.5 us  [the longest x2 10.9 us: gather_mp(): lax.all_to_all(jnp.broadcast_to(x[None], (count,) + x.shape), 'mp', 0, 0)]
    unnamed x22 -> x12, local copies, waits for them, and re-layouts: 13 us -> 0.04 us
    slice x1, local copies, waits for them, and re-layouts: 1.68 us -> 12.2 us  [per_device(): w_kv[:, 0]]
    all_gather x1 -> x0, waiting for transfers between devices: 5.75 us -> none  [merged(): everything = jax.tree.map(lambda part: lax.all_gather(part, axis), x)]
    ppermute x0 -> x3, waiting for transfers between devices: none -> 3.91 us  [swap_psg(): return lax.ppermute(x, 'psg', [(0, 1), (1, 0)])]
  transfers between devices with their start and end apart: 3 -> 7, of which waited for: 3 -> 6; matrix products, arithmetic and copies ran while one was open for 6% -> 19% of each run, Pallas kernels for 0% -> 0%
where the time goes in v1:
time: 87.3 us; the launch traced here: 86.5 us
  waiting for transfers between devices  24.7 us (28%)
  starting transfers between devices  20.8 us (24%)
  matrix products  20.6 us (24%)
  local copies, waits for them, and re-layouts  14.9 us (17%)
  other arithmetic  4.69 us (5%)
    slice x1, local copies, waits for them, and re-layouts, per_device(): w_kv[:, 0]  12.2 us
    all_to_all x2, starting transfers between devices, gather_mp(): lax.all_to_all(jnp.broadcast_to(x[None], (count,) + x.shape), 'mp', 0, 0)  10.9 us
    dot_general x1, matrix products, per_device(): jnp.dot(hidden, w_out, preferred_element_type=jnp.float32)  8.86 us
    all_to_all x1, waiting for transfers between devices, per_device(): answer_parts = lax.all_to_all(chip_sum, 'mp', 0, 0)  7.34 us
    all_to_all x2, waiting for transfers between devices, gather_mp(): lax.all_to_all(jnp.broadcast_to(x[None], (count,) + x.shape), 'mp', 0, 0)  7.05 us
    all_to_all x1, waiting for transfers between devices, per_device(): lax.all_to_all(partial_sums.reshape(mp, row_count, width), 'mp', 0, 0)  6.35 us
    all_to_all x1, starting transfers between devices, per_device(): answer_parts = lax.all_to_all(chip_sum, 'mp', 0, 0)  6 us
    ppermute x3, waiting for transfers between devices, swap_psg(): return lax.ppermute(x, 'psg', [(0, 1), (1, 0)])  3.91 us
  transfers between devices with their start and end apart: 7, of which 6 were waited for; matrix products, arithmetic and copies ran while one was open for 19% of the time, Pallas kernels for 0%

profile of v1, /device:TPU:0, one launch (start us, length us, event | category | flops | bytes accessed | tf_op | source)
XLA Modules:
  0.0 86.5 jit_solution(3858813904209944091)
XLA Ops:
  0.6 1.5 %broadcast_in_dim.90 = bf16[8,16,1024]{2,1,0:T(8,128)(2,1)} broadcast(bf16[16,1024]{1,0:T(8,128)(2,1)} %param.13), dimensions={1,2} | broadcast | bytes 294912 | tf_op jit(solution)/shard_map/broadcast_in_dim | solution.py:35
  2.1 7.3 %all-to-all-start = ((bf16[8,16,1024]{2,1,0:T(8,128)(2,1)}), bf16[8,16,1024]{2,1,0:T(8,128)(2,1)S(1)}, u32[]{:S(2)}, u32[]{:S(2)}) async-start(bf16[8,16,1024]{2,1,0:T(8,128)(2,1)} %broadcast_in_dim.90), calls=%async_computation | async-start | bytes 524288 | tf_op jit(solution)/shard_map/all_to_all | solution.py:35
  9.4 0.8 select_reduce_fusion.1
  10.2 1.1 %fusion.25 = f32[128]{0:T(128)S(1)} fusion(bf16[128,1024]{1,0:T(8,128)(2,1)} %param.19), kind=kLoop, calls=%fused_computation.29 | loop fusion | flops 393088 | bytes 262656 | tf_op jit(solution)/shard_map/reduce_sum | solution.py:15
  11.3 7.0 %all-to-all-done = bf16[8,16,1024]{2,1,0:T(8,128)(2,1)S(1)} async-done(((bf16[8,16,1024]{2,1,0:T(8,128)(2,1)}), bf16[8,16,1024]{2,1,0:T(8,128)(2,1)S(1)}, u32[]{:S(2)}, u32[]{:S(2)}) %all-to-all-start) | async-done | bytes 262176 | tf_op jit(solution)/shard_map/all_to_all | solution.py:35
  18.3 0.1 multiply_reduce_fusion
  18.5 0.1 rsqrt.28
  18.6 0.8 fusion.33
  19.4 0.0 copy-start.5
  19.4 0.0 copy-start
  19.4 0.0 copy-start.3
  19.4 0.0 copy-start.1
  19.4 0.0 copy-start.4
  19.4 8.9 %convolution_convert_fusion = bf16[128,1024]{1,0:T(8,128)(2,1)} fusion(bf16[4096,1024]{1,0:T(8,128)(2,1)} %param.16, bf16[128,1024]{1,0:T(8,128)(2,1)S(1)} %fusion.33, bf16[1024,4096]{1,0:T(8,128)(2,1)} %param.15), kind=kOutput, calls=%fused_computation.25 | convolution fusion | flops 2148663296 | bytes 17301504 | tf_op jit(solution)/shard_map/dot_general | solution.py:72
  28.3 3.6 %all-to-all-start.1 = ((bf16[8,16,1024]{2,1,0:T(8,128)(2,1)}), bf16[8,16,1024]{2,1,0:T(8,128)(2,1)S(1)}, u32[]{:S(2)}, u32[]{:S(2)}) async-start(bf16[8,16,1024]{2,1,0:T(8,128)(2,1)} %bitcast.1), calls=%async_computation.1 | async-start | bytes 524288 | tf_op jit(solution)/shard_map/all_to_all | solution.py:73
  31.9 0.0 copy-done.5
  31.9 0.1 select_reduce_fusion.2
  32.0 0.0 copy-done
  32.0 0.0 copy-done.3
  32.0 2.1 %fusion.22 = bf16[16,8,8,128]{3,2,1,0:T(8,128)(2,1)S(1)} fusion(bf16[1024,2048]{1,0:T(8,128)(2,1)} %param.21, s32[]{:T(128)S(6)} %select_n.135, bf16[128,1024]{1,0:T(8,128)(2,1)S(1)} %copy-done, f32[1024]{0:T(1024)S(1)} %copy-done.3, f32[128]{0:T(128)S(1)} %add_rsqrt_fusion.2), kind=kOutput, calls=%fused_computation.26 | convolution fusion | flops 269090816 | bytes 2626052 | tf_op jit(solution)/shard_map/dot_general | solution.py:91
  34.1 6.4 %all-to-all-done.1 = bf16[8,16,1024]{2,1,0:T(8,128)(2,1)S(1)} async-done(((bf16[8,16,1024]{2,1,0:T(8,128)(2,1)}), bf16[8,16,1024]{2,1,0:T(8,128)(2,1)S(1)}, u32[]{:S(2)}, u32[]{:S(2)}) %all-to-all-start.1) | async-done | bytes 262176 | tf_op jit(solution)/shard_map/all_to_all | solution.py:73
  40.5 0.0 copy-done.1
  40.5 0.1 fusion.41
  40.6 0.0 copy-start.2
  40.7 0.0 copy-done.4
  40.7 0.1 fusion.43
  40.7 0.7 broadcast_in_dim.99
  41.5 3.6 %all-to-all-start.2 = ((bf16[8,16,1024]{2,1,0:T(8,128)(2,1)}), bf16[8,16,1024]{2,1,0:T(8,128)(2,1)S(1)}, u32[]{:S(2)}, u32[]{:S(2)}) async-start(bf16[8,16,1024]{2,1,0:T(8,128)(2,1)} %broadcast_in_dim.99), calls=%async_computation.2 | async-start | bytes 524288 | tf_op jit(solution)/shard_map/all_to_all | solution.py:35
  45.1 12.2 %constant_dynamic-slice_fusion = (bf16[1024,1,1024]{2,1,0:T(2,128)(2,1)}, bf16[1024,1,1024]{2,1,0:T(2,128)(2,1)}) fusion(bf16[1024,2,2048]{2,1,0:T(2,128)(2,1)} %param.18, s32[]{:T(128)S(6)} %select_n.135, s32[]{:T(128)S(6)} %add.148), kind=kLoop, calls=%fused_computation.77 | loop fusion | bytes 8388616 | tf_op jit(solution)/shard_map/slice | solution.py:86
  57.3 0.0 copy-done.2
  57.3 0.0 all-to-all-done.2
  57.3 0.1 collective-permute-start
  57.4 0.1 convert_reduce_fusion.2
  57.5 0.1 compare_and_fusion
  57.6 1.3 %collective-permute-done = bf16[128,1024]{1,0:T(8,128)(2,1)S(1)} collective-permute-done((bf16[128,1024]{1,0:T(8,128)(2,1)S(1)}, bf16[128,1024]{1,0:T(8,128)(2,1)S(1)}, u32[]{:S(2)}, u32[]{:S(2)}) %collective-permute-start) | collective-permute-done | bytes 262176 | tf_op jit(solution)/shard_map/ppermute | solution.py:39
  58.9 3.1 %fusion.16 = bf16[32,8,8,128]{3,2,1,0:T(8,128)(2,1)S(1)} fusion(bf16[1024,1,1024]{2,1,0:T(2,128)(2,1)} %get-tuple-element.6, bf16[128,1024]{1,0:T(8,128)(2,1)S(1)} %collective-permute-done, bf16[128,1024]{1,0:T(8,128)(2,1)S(1)} %bitcast.69), kind=kOutput, calls=%fused_computation.20 | convolution fusion | flops 538181632 | bytes 3145728 | tf_op jit(solution)/shard_map/dot_general | solution.py:86
  62.0 0.6 fusion.60
  62.7 0.3 fusion.12
  63.0 3.1 %fusion.15 = bf16[32,8,8,128]{3,2,1,0:T(8,128)(2,1)S(1)} fusion(bf16[1024,1,1024]{2,1,0:T(2,128)(2,1)} %get-tuple-element.7, bf16[128,1024]{1,0:T(8,128)(2,1)S(1)} %collective-permute-done, bf16[128,1024]{1,0:T(8,128)(2,1)S(1)} %bitcast.70), kind=kOutput, calls=%fused_computation.19 | convolution fusion | flops 538181632 | bytes 3145728 | tf_op jit(solution)/shard_map/dot_general | solution.py:87
  66.1 0.4 fusion.18
  66.5 0.2 copy.27
  66.7 0.1 dot_general.36
  66.8 2.0 %fusion.4 = f32[8,2,8,1024]{3,2,1,0:T(8,128)S(1)} fusion(bf16[8,2,8,1024]{3,2,1,0:T(8,128)(2,1)S(1)} %dot_general.36, bf16[2048,1024]{1,0:T(8,128)(2,1)} %param.22, s32[]{:T(128)S(6)} %select_n.135), kind=kOutput, calls=%fused_computation.7 | convolution fusion | flops 268435456 | bytes 2883588 | tf_op jit(solution)/shard_map/dot_general | solution.py:112
  68.9 0.2 collective-permute-start.1
  69.1 1.4 %collective-permute-done.1 = f32[8,8,1024]{2,1,0:T(8,128)S(1)} collective-permute-done((f32[8,8,1024]{2,1,0:T(8,128)S(1)}, f32[8,8,1024]{2,1,0:T(8,128)S(1)}, u32[]{:S(2)}, u32[]{:S(2)}) %collective-permute-start.1) | collective-permute-done | bytes 262176 | tf_op jit(solution)/shard_map/ppermute | solution.py:39
  70.5 0.7 fusion.38
  71.2 6.0 %all-to-all-start.3 = ((bf16[8,8,1024]{2,1,0:T(8,128)(2,1)}), bf16[8,8,1024]{2,1,0:T(8,128)(2,1)S(1)}, u32[]{:S(2)}, u32[]{:S(2)}) async-start(bf16[8,8,1024]{2,1,0:T(8,128)(2,1)} %fusion.38), calls=%async_computation.3 | async-start | bytes 262144 | tf_op jit(solution)/shard_map/all_to_all | solution.py:120
  77.2 7.3 %all-to-all-done.3 = bf16[8,8,1024]{2,1,0:T(8,128)(2,1)S(1)} async-done(((bf16[8,8,1024]{2,1,0:T(8,128)(2,1)}), bf16[8,8,1024]{2,1,0:T(8,128)(2,1)S(1)}, u32[]{:S(2)}, u32[]{:S(2)}) %all-to-all-start.3) | async-done | bytes 131104 | tf_op jit(solution)/shard_map/all_to_all | solution.py:120
  84.6 0.1 collective-permute-start.2
  84.7 1.2 %collective-permute-done.2 = bf16[8,1024]{1,0:T(8,128)(2,1)S(1)} collective-permute-done((bf16[8,1024]{1,0:T(8,128)(2,1)S(1)}, bf16[8,1024]{1,0:T(8,128)(2,1)S(1)}, u32[]{:S(2)}, u32[]{:S(2)}) %collective-permute-start.2) | collective-permute-done | bytes 16416 | tf_op jit(solution)/shard_map/ppermute | solution.py:39
  85.8 0.6 pad_maximum_fusion.3
  (10 shorter events, 0.2 us)
Async XLA Ops:
  2.1 16.2 %all-to-all-start = ((bf16[8,16,1024]{2,1,0:T(8,128)(2,1)}), bf16[8,16,1024]{2,1,0:T(8,128)(2,1)S(1)}, u32[]{:S(2)}, u32[]{:S(2)}) async-start(bf16[8,16,1024]{2,1,0:T(8,128)(2,1)} %broadcast_in_dim.90), calls=%async_computation | async-start | bytes 524288 | tf_op jit(solution)/shard_map/all_to_all | solution.py:35
  19.4 12.5 %copy-start.5 = (s32[4]{0:T(128)S(1)}, s32[4]{0:T(128)}, u32[]{:S(2)}) copy-start(s32[4]{0:T(128)} %param.25) | copy-start | bytes 52
  19.4 12.6 %copy-start = (bf16[128,1024]{1,0:T(8,128)(2,1)S(1)}, bf16[128,1024]{1,0:T(8,128)(2,1)}, u32[]{:S(2)}) copy-start(bf16[128,1024]{1,0:T(8,128)(2,1)} %param.19) | copy-start | bytes 786436
  19.4 12.6 %copy-start.3 = (f32[1024]{0:T(1024)S(1)}, f32[1024]{0:T(1024)}, u32[]{:S(2)}) copy-start(f32[1024]{0:T(1024)} %param.20) | copy-start | bytes 12292
  19.4 21.1 %copy-start.1 = (bf16[16,1024]{1,0:T(8,128)(2,1)S(1)}, bf16[16,1024]{1,0:T(8,128)(2,1)}, u32[]{:S(2)}) copy-start(bf16[16,1024]{1,0:T(8,128)(2,1)} %param.13) | copy-start | bytes 98308
  19.4 21.2 %copy-start.4 = (f32[1024]{0:T(1024)S(1)}, f32[1024]{0:T(1024)}, u32[]{:S(2)}) copy-start(f32[1024]{0:T(1024)} %param.17) | copy-start | bytes 12292
  28.3 12.2 %all-to-all-start.1 = ((bf16[8,16,1024]{2,1,0:T(8,128)(2,1)}), bf16[8,16,1024]{2,1,0:T(8,128)(2,1)S(1)}, u32[]{:S(2)}, u32[]{:S(2)}) async-start(bf16[8,16,1024]{2,1,0:T(8,128)(2,1)} %bitcast.1), calls=%async_computation.1 | async-start | bytes 524288 | tf_op jit(solution)/shard_map/all_to_all | solution.py:73
  40.6 16.7 %copy-start.2 = (bf16[16,1024]{1,0:T(8,128)(2,1)}, bf16[16,1024]{1,0:T(8,128)(2,1)S(1)}, u32[]{:S(2)}) copy-start(bf16[16,1024]{1,0:T(8,128)(2,1)S(1)} %get-tuple-element.5) | copy-start | bytes 98308
  41.5 15.8 %all-to-all-start.2 = ((bf16[8,16,1024]{2,1,0:T(8,128)(2,1)}), bf16[8,16,1024]{2,1,0:T(8,128)(2,1)S(1)}, u32[]{:S(2)}, u32[]{:S(2)}) async-start(bf16[8,16,1024]{2,1,0:T(8,128)(2,1)} %broadcast_in_dim.99), calls=%async_computation.2 | async-start | bytes 524288 | tf_op jit(solution)/shard_map/all_to_all | solution.py:35
  57.3 1.6 %collective-permute-start = (bf16[128,1024]{1,0:T(8,128)(2,1)S(1)}, bf16[128,1024]{1,0:T(8,128)(2,1)S(1)}, u32[]{:S(2)}, u32[]{:S(2)}) collective-permute-start(bf16[128,1024]{1,0:T(8,128)(2,1)S(1)} %bitcast.68), channel_id=1, source_target_pairs={{0,1},{1,0},{2,3},{3,2},{4,5},{5,4},{6,7},{7,6},{8,9},{9,8},{10,11... | collective-permute-start | bytes 786440 | tf_op jit(solution)/shard_map/ppermute | solution.py:39
  68.9 1.6 %collective-permute-start.1 = (f32[8,8,1024]{2,1,0:T(8,128)S(1)}, f32[8,8,1024]{2,1,0:T(8,128)S(1)}, u32[]{:S(2)}, u32[]{:S(2)}) collective-permute-start(f32[8,8,1024]{2,1,0:T(8,128)S(1)} %dynamic-slice_bitcast_fusion), channel_id=1, source_target_pairs={{0,1},{1,0},{2,3},{3,2},{4,5},{5,4},{6,7},{7,6},{8,9},{9,8},{10,11... | collective-permute-start | bytes 786440 | tf_op jit(solution)/shard_map/ppermute | solution.py:39
  71.2 13.3 %all-to-all-start.3 = ((bf16[8,8,1024]{2,1,0:T(8,128)(2,1)}), bf16[8,8,1024]{2,1,0:T(8,128)(2,1)S(1)}, u32[]{:S(2)}, u32[]{:S(2)}) async-start(bf16[8,8,1024]{2,1,0:T(8,128)(2,1)} %fusion.38), calls=%async_computation.3 | async-start | bytes 262144 | tf_op jit(solution)/shard_map/all_to_all | solution.py:120
  84.6 1.2 %collective-permute-start.2 = (bf16[8,1024]{1,0:T(8,128)(2,1)S(1)}, bf16[8,1024]{1,0:T(8,128)(2,1)S(1)}, u32[]{:S(2)}, u32[]{:S(2)}) collective-permute-start(bf16[8,1024]{1,0:T(8,128)(2,1)S(1)} %add_convert_fusion.1), channel_id=1, source_target_pairs={{0,1},{1,0},{2,3},{3,2},{4,5},{5,4},{6,7},{7,6},{8,9},{9,8},{10,11... | collective-permute-start | bytes 49160 | tf_op jit(solution)/shard_map/ppermute | solution.py:39

commit v2 on v1

--- a/solution.py
+++ b/solution.py
@@ -1,6 +1,8 @@
 import jax
 import jax.numpy as jnp
 from jax import lax
+from jax.experimental import pallas as pl
+from jax.experimental.pallas import tpu as pltpu
 from jax.sharding import PartitionSpec as P
 
 DH = 128
@@ -37,6 +39,238 @@
 
 def swap_psg(x):
     return lax.ppermute(x, "psg", [(0, 1), (1, 0)])
+
+
+BF16 = jnp.bfloat16
+F32 = jnp.float32
+SMEM_SPEC = pl.BlockSpec(memory_space=pltpu.SMEM)
+VMEM_SPEC = pl.BlockSpec(memory_space=pltpu.VMEM)
+HBM_SPEC = pl.BlockSpec(memory_space=pltpu.HBM)
+
+
+def limit(mib):
+    return pltpu.CompilerParams(vmem_limit_bytes=mib << 20)
+
+
+def prepare_kernel(half, states, gain, w_query, w_keyval, query, wkv, scr_q, scr_kv, sems):
+    width = states.shape[1]
+    inner = query.shape[1]
+    strips = inner // 128
+    start = pl.multiple_of(half[0] * inner, 128)
+    q_copy = pltpu.make_async_copy(w_query.at[:, pl.ds(start, inner)], scr_q, sems.at[strips])
+    copies = [
+        pltpu.make_async_copy(
+            w_keyval.at[:, :, pl.ds(pl.multiple_of(start + s * 128, 128), 128)],
+            scr_kv.at[s],
+            sems.at[s],
+        )
+        for s in range(strips)
+    ]
+    q_copy.start()
+    for copy in copies:
+        copy.start()
+    normed = norm_rows(states[...], gain[...]).astype(BF16)
+    q_copy.wait()
+    for c in range(inner // 256):
+        columns = pl.ds(c * 256, 256)
+        query[:, columns] = jnp.dot(
+            normed, scr_q[:, columns], preferred_element_type=F32
+        ).astype(BF16)
+    row = lax.broadcasted_iota(jnp.int32, (256, 256), 0)
+    column = lax.broadcasted_iota(jnp.int32, (256, 256), 1)
+    source = jnp.where(row < 128, 2 * row, 2 * (row - 128) + 1)
+    pick = jnp.where(column == source, 1.0, 0.0).astype(BF16)
+    for s in range(0, strips, 2):
+        copies[s].wait()
+        copies[s + 1].wait()
+        for b in range(width // 128):
+            rows = pl.ds(b * 128, 128)
+            mixed = jnp.concatenate(
+                [scr_kv[s, rows].reshape(256, 128), scr_kv[s + 1, rows].reshape(256, 128)], axis=1
+            )
+            apart = jnp.dot(pick, mixed, preferred_element_type=F32).astype(BF16)
+            wkv[0, rows, pl.ds(s * 128, 256)] = apart[:128]
+            wkv[1, rows, pl.ds(s * 128, 256)] = apart[128:]
+
+
+def prepare(half, states, gain, w_query, w_keyval, inner):
+    count, width = states.shape
+    strips = inner // 128
+    return pl.pallas_call(
+        prepare_kernel,
+        out_shape=(
+            jax.ShapeDtypeStruct((count, inner), BF16),
+            jax.ShapeDtypeStruct((2, width, inner), BF16),
+        ),
+        in_specs=[SMEM_SPEC, VMEM_SPEC, VMEM_SPEC, HBM_SPEC, HBM_SPEC],
+        out_specs=(VMEM_SPEC, VMEM_SPEC),
+        scratch_shapes=[
+            pltpu.VMEM((width, inner), BF16),
+            pltpu.VMEM((strips, width, 2, 128), BF16),
+            pltpu.SemaphoreType.DMA((strips + 1,)),
+        ],
+        compiler_params=limit(52),
+        cost_estimate=pl.CostEstimate(
+            flops=2 * count * width * inner + 4 * width * 256 * inner,
+            bytes_accessed=10 * width * inner,
+            transcendentals=0,
+        ),
+        name="prepare",
+    )(half, states, gain.reshape(1, width), w_query, w_keyval)
+
+
+def feed_kernel(everyone, gain, w_in, w_out, out, scr_in, scr_out, acc, sems):
+    chunks, _, size = scr_in.shape
+    copies = []
+    for c in range(chunks):
+        copies.append(
+            (
+                pltpu.make_async_copy(w_in.at[:, pl.ds(c * size, size)], scr_in.at[c], sems.at[0, c]),
+                pltpu.make_async_copy(w_out.at[pl.ds(c * size, size)], scr_out.at[c], sems.at[1, c]),
+            )
+        )
+    for first, second in copies:
+        first.start()
+        second.start()
+    normed = norm_rows(everyone[...], gain[...]).astype(BF16)
+    for c in range(chunks):
+        copies[c][0].wait()
+        hidden = jnp.maximum(
+            jnp.dot(normed, scr_in[c], preferred_element_type=F32), 0.0
+        ).astype(BF16)
+        copies[c][1].wait()
+        part = jnp.dot(hidden, scr_out[c], preferred_element_type=F32)
+        if c > 0:
+            part = part + acc[...]
+        if c < chunks - 1:
+            acc[...] = part
+        else:
+            out[...] = part.astype(BF16)
+
+
+def feed(everyone, gain, w_in, w_out):
+    rows, width = everyone.shape
+    units = w_in.shape[1]
+    size = min(512, units)
+    chunks = units // size
+    return pl.pallas_call(
+        feed_kernel,
+        out_shape=jax.ShapeDtypeStruct((rows, width), BF16),
+        in_specs=[VMEM_SPEC, VMEM_SPEC, HBM_SPEC, HBM_SPEC],
+        out_specs=VMEM_SPEC,
+        scratch_shapes=[
+            pltpu.VMEM((chunks, width, size), BF16),
+            pltpu.VMEM((chunks, size, width), BF16),
+            pltpu.VMEM((rows, width), F32),
+            pltpu.SemaphoreType.DMA((2, chunks)),
+        ],
+        compiler_params=limit(52),
+        cost_estimate=pl.CostEstimate(
+            flops=4 * rows * width * units, bytes_accessed=4 * width * units, transcendentals=0
+        ),
+        name="feed",
+    )(everyone, gain.reshape(1, width), w_in, w_out)
+
+
+def settle_kernel(parts, tokens, gain, encoded, spread):
+    total = tokens[...].astype(F32)
+    for k in range(parts.shape[0]):
+        total = total + parts[k].astype(F32)
+    rounded = total.astype(BF16)
+    encoded[...] = rounded
+    memory = norm_rows(rounded, gain[...]).astype(BF16)
+    for k in range(spread.shape[0]):
+        spread[k] = memory
+
+
+def settle(parts, tokens, gain):
+    count, rows, width = parts.shape
+    return pl.pallas_call(
+        settle_kernel,
+        out_shape=(
+            jax.ShapeDtypeStruct((rows, width), BF16),
+            jax.ShapeDtypeStruct((count, rows, width), BF16),
+        ),
+        in_specs=[VMEM_SPEC] * 3,
+        out_specs=(VMEM_SPEC, VMEM_SPEC),
+        compiler_params=limit(8),
+        name="settle",
+    )(parts, tokens, gain.reshape(1, width))
+
+
+def attend_kernel(half, mine, theirs, query, allowed, wkv, w_out, out, scr_k, scr_v, scr_o, context, sems):
+    chunks, _, size = scr_k.shape
+    inner = chunks * size
+    width = out.shape[1]
+    start = pl.multiple_of(half[0] * inner, 128)
+    copies = []
+    for c in range(chunks):
+        columns = pl.ds(c * size, size)
+        copies.append(
+            (
+                pltpu.make_async_copy(wkv.at[0, :, columns], scr_k.at[c], sems.at[0, c]),
+                pltpu.make_async_copy(wkv.at[1, :, columns], scr_v.at[c], sems.at[1, c]),
+            )
+        )
+    o_copy = pltpu.make_async_copy(w_out.at[pl.ds(start, inner)], scr_o, sems.at[2, 0])
+    for first, second in copies:
+        first.start()
+        second.start()
+    o_copy.start()
+    live = allowed[...] > 0
+    both = jnp.concatenate([mine[...], theirs[...]], axis=0)
+    for c in range(chunks):
+        copies[c][0].wait()
+        keys = jnp.dot(both, scr_k[c], preferred_element_type=F32).astype(BF16)
+        copies[c][1].wait()
+        values = jnp.dot(both, scr_v[c], preferred_element_type=F32).astype(BF16)
+        for h in range(size // DH):
+            lanes = slice(h * DH, (h + 1) * DH)
+            columns = pl.ds(c * size + h * DH, DH)
+            scores = lax.dot_general(
+                query[:, columns],
+                keys[:, lanes],
+                (((1,), (1,)), ((), ())),
+                preferred_element_type=F32,
+            ) * DH ** (-0.5)
+            scores = jnp.where(live, scores, -1e30)
+            top = jnp.max(scores, axis=1, keepdims=True)
+            weights = jnp.where(live, jnp.exp(scores - top), 0.0)
+            total = jnp.sum(weights, axis=1, keepdims=True)
+            summed = jnp.dot(weights.astype(BF16), values[:, lanes], preferred_element_type=F32)
+            context[:, columns] = (summed / total).astype(BF16)
+    o_copy.wait()
+    for c in range(width // 256):
+        columns = pl.ds(c * 256, 256)
+        out[:, columns] = jnp.dot(context[...], scr_o[:, columns], preferred_element_type=F32)
+
+
+def attend(half, mine, theirs, query, allowed, wkv, w_attn_out):
+    rows, width = mine.shape
+    count, inner = query.shape
+    size = min(256, inner)
+    chunks = inner // size
+    keys = 2 * rows
+    return pl.pallas_call(
+        attend_kernel,
+        out_shape=jax.ShapeDtypeStruct((count, width), F32),
+        in_specs=[SMEM_SPEC] + [VMEM_SPEC] * 4 + [HBM_SPEC] * 2,
+        out_specs=VMEM_SPEC,
+        scratch_shapes=[
+            pltpu.VMEM((chunks, width, size), BF16),
+            pltpu.VMEM((chunks, width, size), BF16),
+            pltpu.VMEM((inner, width), BF16),
+            pltpu.VMEM((count, inner), BF16),
+            pltpu.SemaphoreType.DMA((3, chunks)),
+        ],
+        compiler_params=limit(52),
+        cost_estimate=pl.CostEstimate(
+            flops=4 * keys * width * inner + 4 * count * keys * inner + 2 * count * inner * width,
+            bytes_accessed=6 * width * inner,
+            transcendentals=count * keys * inner // DH,
+        ),
+        name="attend",
+    )(half, mine, theirs, query, allowed, wkv, w_attn_out)
 
 
 def per_device(
@@ -64,52 +298,25 @@
     heads = w_query.shape[1] // DH // psg
     inner = heads * DH
 
+    half = jnp.reshape(psg_index, (1,)).astype(jnp.int32)
     everyone = gather_mp(tokens, mp).reshape(mp * row_count, width)
-    normed = norm_rows(everyone, enc_gain).astype(jnp.bfloat16)
-    hidden = jnp.maximum(jnp.dot(normed, w_in, preferred_element_type=jnp.float32), 0.0).astype(
-        jnp.bfloat16
-    )
-    partial_sums = jnp.dot(hidden, w_out, preferred_element_type=jnp.float32).astype(jnp.bfloat16)
+    query, wkv = prepare(half, answer_states, dec_gain, w_query, w_keyval, inner)
+    partial_sums = feed(everyone, enc_gain, w_in, w_out)
     parts = lax.all_to_all(partial_sums.reshape(mp, row_count, width), "mp", 0, 0)
-    summed_rows = jnp.sum(parts.astype(jnp.float32), axis=0)
-    encoded = (tokens.astype(jnp.float32) + summed_rows).astype(jnp.bfloat16)
-    memory = norm_rows(encoded, final_gain).astype(jnp.bfloat16)
-    mine = gather_mp(memory, mp).reshape(mp * row_count, width)
+    encoded, spread = settle(parts, tokens, final_gain)
+    mine = lax.all_to_all(spread, "mp", 0, 0).reshape(mp * row_count, width)
     theirs = swap_psg(mine)
-    both = jnp.concatenate([mine, theirs], axis=0)
-    key_rows = both.shape[0]
-
-    start = psg_index * inner
-    w_kv = lax.dynamic_slice_in_dim(w_keyval, start, inner, 2)
-    w_q = lax.dynamic_slice_in_dim(w_query, start, inner, 1)
-    w_o = lax.dynamic_slice_in_dim(w_attn_out, start, inner, 0)
-    keys = jnp.dot(both, w_kv[:, 0], preferred_element_type=jnp.float32).astype(jnp.bfloat16)
-    values = jnp.dot(both, w_kv[:, 1], preferred_element_type=jnp.float32).astype(jnp.bfloat16)
-    keys = keys.reshape(key_rows, heads, DH)
-    values = values.reshape(key_rows, heads, DH)
-    normed_answer = norm_rows(answer_states, dec_gain).astype(jnp.bfloat16)
-    query = jnp.dot(normed_answer, w_q, preferred_element_type=jnp.float32).astype(jnp.bfloat16)
-    query = query.reshape(answer_count, heads, DH)
+    key_rows = 2 * mp * row_count
 
     local = jnp.arange(key_rows, dtype=jnp.int32)
-    half = local // (mp * row_count)
+    far = local // (mp * row_count)
     block = (local % (mp * row_count)) // row_count
-    core = jnp.where(half == 0, psg_index, 1 - psg_index)
+    core = jnp.where(far == 0, psg_index, 1 - psg_index)
     token_index = (block * psg + core) * row_count + local % row_count
     allowed = key_mask(token_index, passage_lengths, passage_owner, answer_lengths, answer_count)
-    scores = jnp.einsum("qhd,khd->hqk", query, keys, preferred_element_type=jnp.float32) * DH ** (
-        -0.5
+    partial_answer = attend(
+        half, mine, theirs, query, allowed.astype(jnp.int32), wkv, w_attn_out
     )
-    scores = jnp.where(allowed[None], scores, -1e30)
-    top = jnp.max(scores, axis=2, keepdims=True)
-    weights = jnp.where(allowed[None], jnp.exp(scores - top), 0.0)
-    total = jnp.sum(weights, axis=2, keepdims=True)
-    summed = jnp.einsum(
-        "hqk,khd->hqd", weights.astype(jnp.bfloat16), values, preferred_element_type=jnp.float32
-    )
-    context = (summed / total).astype(jnp.bfloat16)
-    context = context.transpose(1, 0, 2).reshape(answer_count, inner)
-    partial_answer = jnp.dot(context, w_o, preferred_element_type=jnp.float32)
 
     out_count = answer_count // mp
     small = out_count // psg

time: 87.3 us -> 74.7 us (0.86)
  Pallas kernels: 0 us -> 20.9 us
  matrix products: 20.6 us -> 0 us
  blocking collectives: 0 us -> 16 us
  local copies, waits for them, and re-layouts: 14.9 us -> 1.52 us
  starting transfers between devices: 20.8 us -> 12.3 us
  waiting for transfers between devices: 24.7 us -> 21 us
  other arithmetic: 4.69 us -> 1.72 us
    pallas_call x0 -> x4, Pallas kernels: none -> 20.9 us  [the longest x1 7.15 us: prepare(): pl.pallas_call(prepare_kernel, out_shape=(jax.ShapeDtypeStruct((count, in...]
    dot_general x7 -> x0, matrix products: 20 us -> none  [the longest x1 8.86 us: per_device(): jnp.dot(hidden, w_out, preferred_element_type=jnp.float32)]
    all_to_all x0 -> x1, blocking collectives: none -> 16 us  [gather_mp(): lax.all_to_all(jnp.broadcast_to(x[None], (count,) + x.shape), 'mp', 0, 0)]
    slice x1 -> x0, local copies, waits for them, and re-layouts: 12.2 us -> none  [per_device(): w_kv[:, 0]]
    all_to_all x2 -> x1, starting transfers between devices: 10.9 us -> 3.59 us  [per_device(): mine = lax.all_to_all(spread, 'mp', 0, 0).reshape(mp * row_count, width)]
    all_to_all x2 -> x1, waiting for transfers between devices: 7.05 us -> 1.25 us  [per_device(): mine = lax.all_to_all(spread, 'mp', 0, 0).reshape(mp * row_count, width)]
    all_to_all x1, waiting for transfers between devices: 6.35 us -> 8.44 us  [per_device(): lax.all_to_all(partial_sums.reshape(mp, row_count, width), 'mp', 0, 0)]
    broadcast_in_dim x2 -> x1, local copies, waits for them, and re-layouts: 2.21 us -> 0.78 us  [gather_mp(): jnp.broadcast_to(x[None], (count,) + x.shape)]
  transfers between devices with their start and end apart: 7 -> 6, of which waited for: 6 -> 6; matrix products, arithmetic and copies ran while one was open for 19% -> 1% of each run, Pallas kernels for 0% -> 10%
where the time goes in v2:
time: 74.7 us; the launch traced here: 74.1 us
  waiting for transfers between devices  21 us (28%)
  Pallas kernels  20.9 us (28%)
  blocking collectives  16 us (21%)
  starting transfers between devices  12.3 us (16%)
  other arithmetic  1.72 us (2%)
  local copies, waits for them, and re-layouts  1.52 us (2%)
  between operations  0.76 us (1%)
    all_to_all x1, blocking collectives, gather_mp(): lax.all_to_all(jnp.broadcast_to(x[None], (count,) + x.shape), 'mp', 0, 0)  16 us
    all_to_all x1, waiting for transfers between devices, per_device(): lax.all_to_all(partial_sums.reshape(mp, row_count, width), 'mp', 0, 0)  8.44 us
    all_to_all x1, waiting for transfers between devices, per_device(): answer_parts = lax.all_to_all(chip_sum, 'mp', 0, 0)  7.34 us
    pallas_call x1, Pallas kernels, prepare(): pl.pallas_call(prepare_kernel, out_shape=(jax.ShapeDtypeStruct((count, in...  7.15 us
    pallas_call x1, Pallas kernels, feed(): pl.pallas_call(feed_kernel, out_shape=jax.ShapeDtypeStruct((rows, width),...  7.13 us
    pallas_call x1, Pallas kernels, attend(): pl.pallas_call(attend_kernel, out_shape=jax.ShapeDtypeStruct((count, widt...  5.74 us
    all_to_all x1, starting transfers between devices, per_device(): answer_parts = lax.all_to_all(chip_sum, 'mp', 0, 0)  4.8 us
    ppermute x3, waiting for transfers between devices, swap_psg(): return lax.ppermute(x, 'psg', [(0, 1), (1, 0)])  3.92 us
  transfers between devices with their start and end apart: 6, of which 6 were waited for; matrix products, arithmetic and copies ran while one was open for 1% of the time, Pallas kernels for 10%

profile of v2, /device:TPU:0, one launch (start us, length us, event | category | flops | bytes accessed | tf_op | source)
XLA Modules:
  0.0 74.1 jit_solution(10146559209590234403)
XLA Ops:
  0.6 0.8 %broadcast_in_dim.56 = bf16[8,16,1024]{2,1,0:T(8,128)(2,1)S(1)} broadcast(bf16[16,1024]{1,0:T(8,128)(2,1)} %tokens.1), dimensions={1,2} | broadcast | bytes 294912 | tf_op jit(solution)/shard_map/broadcast_in_dim | solution.py:37
  1.4 16.0 %all_to_all.20 = bf16[8,16,1024]{2,1,0:T(8,128)(2,1)S(1)} all-to-all(bf16[8,16,1024]{2,1,0:T(8,128)(2,1)S(1)} %broadcast_in_dim.56), channel_id=1, replica_groups=mesh['groups'=2,'mp'=8,'psg'=2] {'mp'}, dimensions={0} | all-to-all | bytes 524288 | tf_op jit(solution)/shard_map/all_to_all | solution.py:37
  17.4 0.0 copy-start.2
  17.4 0.7 copy-done.2
  18.1 0.0 copy-start.5
  18.1 0.0 copy-start.6
  18.1 0.0 copy-start.1
  18.1 0.0 copy-start.3
  18.1 0.0 copy-start.7
  18.1 0.0 copy-start
  18.2 0.0 copy-start.4
  18.2 7.1 %feed.1 = bf16[128,1024]{1,0:T(8,128)(2,1)} custom-call(bf16[128,1024]{1,0:T(8,128)(2,1)S(1)} %bitcast.16, f32[1,1024]{1,0:T(1,128)S(1)} %bitcast.19, bf16[1024,4096]{1,0:T(8,128)(2,1)} %w_in.1, bf16[4096,1024]{1,0:T(8,128)(2,1)} %w_out.2), custom_call_target="tpu_custom_call" | custom-call | flops 2147483648 | bytes 16777216 | tf_op jit(solution)/shard_map/feed/pallas_call | solution.py:156
  25.3 3.6 %all-to-all-start.1 = ((bf16[8,16,1024]{2,1,0:T(8,128)(2,1)}), bf16[8,16,1024]{2,1,0:T(8,128)(2,1)S(1)}, u32[]{:S(2)}, u32[]{:S(2)}) async-start(bf16[8,16,1024]{2,1,0:T(8,128)(2,1)} %bitcast.2), calls=%async_computation.1 | async-start | bytes 524288 | tf_op jit(solution)/shard_map/all_to_all | solution.py:305
  28.9 0.0 copy-done.5
  28.9 0.0 copy-done.6
  29.0 0.1 select_reduce_fusion.1
  29.0 8.4 %all-to-all-done.1.parts = bf16[8,16,1024]{2,1,0:T(8,128)(2,1)S(1)} async-done(((bf16[8,16,1024]{2,1,0:T(8,128)(2,1)}), bf16[8,16,1024]{2,1,0:T(8,128)(2,1)S(1)}, u32[]{:S(2)}, u32[]{:S(2)}) %all-to-all-start.1) | async-done | bytes 262176 | tf_op jit(solution)/shard_map/all_to_all | solution.py:305
  37.5 0.0 copy-done.1
  37.5 0.0 copy-done.3
  37.5 0.9 %settle.1 = (bf16[16,1024]{1,0:T(8,128)(2,1)}, bf16[8,16,1024]{2,1,0:T(8,128)(2,1)}) custom-call(bf16[8,16,1024]{2,1,0:T(8,128)(2,1)S(1)} %all-to-all-done.1.parts, bf16[16,1024]{1,0:T(8,128)(2,1)S(1)} %copy-done.1, f32[1,1024]{1,0:T(1,128)S(1)} %bitcast.20), custom_call_target="tpu_custom_call" | custom-call | tf_op jit(solution)/shard_map/settle/pallas_call | solution.py:188
  38.3 3.6 %all-to-all-start.2 = ((bf16[8,16,1024]{2,1,0:T(8,128)(2,1)}), bf16[8,16,1024]{2,1,0:T(8,128)(2,1)S(1)}, u32[]{:S(2)}, u32[]{:S(2)}) async-start(bf16[8,16,1024]{2,1,0:T(8,128)(2,1)} %get-tuple-element.7), calls=%async_computation.2 | async-start | bytes 524288 | tf_op jit(solution)/shard_map/all_to_all | solution.py:307
  41.9 0.0 copy-done.7
  41.9 0.1 select_reduce_fusion.2
  42.0 0.0 copy-done
  42.0 0.0 copy-done.4
  42.0 7.1 %prepare.1 = (bf16[128,1024]{1,0:T(8,128)(2,1)S(1)}, bf16[2,1024,1024]{2,1,0:T(8,128)(2,1)}) custom-call(s32[1]{0:T(128)} %bitcast.4.half, bf16[128,1024]{1,0:T(8,128)(2,1)S(1)} %copy-done, f32[1,1024]{1,0:T(1,128)S(1)} %bitcast.21, bf16[1024,2048]{1,0:T(8,128)(2,1)} %w_query.1, bf16[1024,2,2048]{2,1,0:T(2,128)(2,1)} %w_keyval.1), custom_call_target="tpu_custom_call" | custom-call | flops 1342177280 | bytes 10485760 | tf_op jit(solution)/shard_map/prepare/pallas_call | solution.py:99
  49.2 1.3 %all-to-all-done.2 = bf16[8,16,1024]{2,1,0:T(8,128)(2,1)S(1)} async-done(((bf16[8,16,1024]{2,1,0:T(8,128)(2,1)}), bf16[8,16,1024]{2,1,0:T(8,128)(2,1)S(1)}, u32[]{:S(2)}, u32[]{:S(2)}) %all-to-all-start.2) | async-done | bytes 262176 | tf_op jit(solution)/shard_map/all_to_all | solution.py:307
  50.5 0.0 collective-permute-start
  50.5 0.1 convert_reduce_fusion.1
  50.6 0.1 and_convert_fusion.allowed
  50.6 1.4 %collective-permute-done.theirs = bf16[128,1024]{1,0:T(8,128)(2,1)S(1)} collective-permute-done((bf16[128,1024]{1,0:T(8,128)(2,1)S(1)}, bf16[128,1024]{1,0:T(8,128)(2,1)S(1)}, u32[]{:S(2)}, u32[]{:S(2)}) %collective-permute-start) | collective-permute-done | bytes 262176 | tf_op jit(solution)/shard_map/ppermute | solution.py:41
  52.0 5.7 %attend.1 = f32[128,1024]{1,0:T(8,128)S(1)} custom-call(s32[1]{0:T(128)} %bitcast.4.half, bf16[128,1024]{1,0:T(8,128)(2,1)S(1)} %bitcast.18, bf16[128,1024]{1,0:T(8,128)(2,1)S(1)} %collective-permute-done.theirs, bf16[128,1024]{1,0:T(8,128)(2,1)S(1)} %get-tuple-element.8.query, s32[128,256]{1,0:T(8,128)S(1)} %and_convert_fusion.allowed, ...), custom_call_target="tpu_custom_call" | custom-call | flops 1476395008 | bytes 6291456 | tf_op jit(solution)/shard_map/attend/pallas_call | solution.py:254
  57.8 0.2 collective-permute-start.1
  58.0 1.4 %collective-permute-done.1 = f32[8,8,1024]{2,1,0:T(8,128)S(1)} collective-permute-done((f32[8,8,1024]{2,1,0:T(8,128)S(1)}, f32[8,8,1024]{2,1,0:T(8,128)S(1)}, u32[]{:S(2)}, u32[]{:S(2)}) %collective-permute-start.1) | collective-permute-done | bytes 262176 | tf_op jit(solution)/shard_map/ppermute | solution.py:41
  59.4 0.7 fusion
  60.1 4.8 %all-to-all-start.3 = ((bf16[8,8,1024]{2,1,0:T(8,128)(2,1)}), bf16[8,8,1024]{2,1,0:T(8,128)(2,1)S(1)}, u32[]{:S(2)}, u32[]{:S(2)}) async-start(bf16[8,8,1024]{2,1,0:T(8,128)(2,1)} %fusion), calls=%async_computation.3 | async-start | bytes 262144 | tf_op jit(solution)/shard_map/all_to_all | solution.py:327
  64.9 7.3 %all-to-all-done.3 = bf16[8,8,1024]{2,1,0:T(8,128)(2,1)S(1)} async-done(((bf16[8,8,1024]{2,1,0:T(8,128)(2,1)}), bf16[8,8,1024]{2,1,0:T(8,128)(2,1)S(1)}, u32[]{:S(2)}, u32[]{:S(2)}) %all-to-all-start.3) | async-done | bytes 131104 | tf_op jit(solution)/shard_map/all_to_all | solution.py:327
  72.3 0.1 collective-permute-start.2
  72.3 1.2 %collective-permute-done.2 = bf16[8,1024]{1,0:T(8,128)(2,1)S(1)} collective-permute-done((bf16[8,1024]{1,0:T(8,128)(2,1)S(1)}, bf16[8,1024]{1,0:T(8,128)(2,1)S(1)}, u32[]{:S(2)}, u32[]{:S(2)}) %collective-permute-start.2) | collective-permute-done | bytes 16416 | tf_op jit(solution)/shard_map/ppermute | solution.py:41
  73.5 0.6 pad_maximum_fusion
  (6 shorter events, 0.1 us)
Async XLA Ops:
  17.4 0.7 copy-start.2
  18.1 10.8 %copy-start.5 = (s32[16]{0:T(128)S(1)}, s32[16]{0:T(128)}, u32[]{:S(2)}) copy-start(s32[16]{0:T(128)} %param.23) | copy-start | bytes 196
  18.1 10.8 %copy-start.6 = (s32[16]{0:T(128)S(1)}, s32[16]{0:T(128)}, u32[]{:S(2)}) copy-start(s32[16]{0:T(128)} %param.24) | copy-start | bytes 196
  18.1 19.4 %copy-start.1 = (bf16[16,1024]{1,0:T(8,128)(2,1)S(1)}, bf16[16,1024]{1,0:T(8,128)(2,1)}, u32[]{:S(2)}) copy-start(bf16[16,1024]{1,0:T(8,128)(2,1)} %tokens.1) | copy-start | bytes 98308
  18.1 19.4 %copy-start.3 = (f32[1024]{0:T(1024)S(1)}, f32[1024]{0:T(1024)}, u32[]{:S(2)}) copy-start(f32[1024]{0:T(1024)} %param.17) | copy-start | bytes 12292
  18.1 23.8 %copy-start.7 = (s32[4]{0:T(128)S(1)}, s32[4]{0:T(128)}, u32[]{:S(2)}) copy-start(s32[4]{0:T(128)} %param.25) | copy-start | bytes 52
  18.1 23.9 %copy-start = (bf16[128,1024]{1,0:T(8,128)(2,1)S(1)}, bf16[128,1024]{1,0:T(8,128)(2,1)}, u32[]{:S(2)}) copy-start(bf16[128,1024]{1,0:T(8,128)(2,1)} %states.1) | copy-start | bytes 786436
  18.2 23.9 %copy-start.4 = (f32[1024]{0:T(1024)S(1)}, f32[1024]{0:T(1024)}, u32[]{:S(2)}) copy-start(f32[1024]{0:T(1024)} %param.20) | copy-start | bytes 12292
  25.3 12.2 %all-to-all-start.1 = ((bf16[8,16,1024]{2,1,0:T(8,128)(2,1)}), bf16[8,16,1024]{2,1,0:T(8,128)(2,1)S(1)}, u32[]{:S(2)}, u32[]{:S(2)}) async-start(bf16[8,16,1024]{2,1,0:T(8,128)(2,1)} %bitcast.2), calls=%async_computation.1 | async-start | bytes 524288 | tf_op jit(solution)/shard_map/all_to_all | solution.py:305
  38.3 12.1 %all-to-all-start.2 = ((bf16[8,16,1024]{2,1,0:T(8,128)(2,1)}), bf16[8,16,1024]{2,1,0:T(8,128)(2,1)S(1)}, u32[]{:S(2)}, u32[]{:S(2)}) async-start(bf16[8,16,1024]{2,1,0:T(8,128)(2,1)} %get-tuple-element.7), calls=%async_computation.2 | async-start | bytes 524288 | tf_op jit(solution)/shard_map/all_to_all | solution.py:307
  50.5 1.5 %collective-permute-start = (bf16[128,1024]{1,0:T(8,128)(2,1)S(1)}, bf16[128,1024]{1,0:T(8,128)(2,1)S(1)}, u32[]{:S(2)}, u32[]{:S(2)}) collective-permute-start(bf16[128,1024]{1,0:T(8,128)(2,1)S(1)} %bitcast.17), channel_id=1, source_target_pairs={{0,1},{1,0},{2,3},{3,2},{4,5},{5,4},{6,7},{7,6},{8,9},{9,8},{10,11... | collective-permute-start | bytes 786440 | tf_op jit(solution)/shard_map/ppermute | solution.py:41
  57.8 1.6 %collective-permute-start.1 = (f32[8,8,1024]{2,1,0:T(8,128)S(1)}, f32[8,8,1024]{2,1,0:T(8,128)S(1)}, u32[]{:S(2)}, u32[]{:S(2)}) collective-permute-start(f32[8,8,1024]{2,1,0:T(8,128)S(1)} %dynamic-slice_bitcast_fusion), channel_id=1, source_target_pairs={{0,1},{1,0},{2,3},{3,2},{4,5},{5,4},{6,7},{7,6},{8,9},{9,8},{10,11... | collective-permute-start | bytes 786440 | tf_op jit(solution)/shard_map/ppermute | solution.py:41
  60.1 12.1 %all-to-all-start.3 = ((bf16[8,8,1024]{2,1,0:T(8,128)(2,1)}), bf16[8,8,1024]{2,1,0:T(8,128)(2,1)S(1)}, u32[]{:S(2)}, u32[]{:S(2)}) async-start(bf16[8,8,1024]{2,1,0:T(8,128)(2,1)} %fusion), calls=%async_computation.3 | async-start | bytes 262144 | tf_op jit(solution)/shard_map/all_to_all | solution.py:327
  72.3 1.2 %collective-permute-start.2 = (bf16[8,1024]{1,0:T(8,128)(2,1)S(1)}, bf16[8,1024]{1,0:T(8,128)(2,1)S(1)}, u32[]{:S(2)}, u32[]{:S(2)}) collective-permute-start(bf16[8,1024]{1,0:T(8,128)(2,1)S(1)} %add_convert_fusion), channel_id=1, source_target_pairs={{0,1},{1,0},{2,3},{3,2},{4,5},{5,4},{6,7},{7,6},{8,9},{9,8},{10,11... | collective-permute-start | bytes 49160 | tf_op jit(solution)/shard_map/ppermute | solution.py:41

commit v3 on v2

--- a/solution.py
+++ b/solution.py
@@ -1,3 +1,5 @@
+import functools
+
 import jax
 import jax.numpy as jnp
 from jax import lax
@@ -119,57 +121,83 @@
     )(half, states, gain.reshape(1, width), w_query, w_keyval)
 
 
-def feed_kernel(everyone, gain, w_in, w_out, out, scr_in, scr_out, acc, sems):
-    chunks, _, size = scr_in.shape
+def stage_kernel(after, whole, out, sems, *, axis, start):
+    del after
+    size = out.shape[axis]
+    number = sems.shape[0]
+    step = size // number
     copies = []
-    for c in range(chunks):
-        copies.append(
-            (
-                pltpu.make_async_copy(w_in.at[:, pl.ds(c * size, size)], scr_in.at[c], sems.at[0, c]),
-                pltpu.make_async_copy(w_out.at[pl.ds(c * size, size)], scr_out.at[c], sems.at[1, c]),
-            )
-        )
-    for first, second in copies:
-        first.start()
-        second.start()
-    normed = norm_rows(everyone[...], gain[...]).astype(BF16)
-    for c in range(chunks):
-        copies[c][0].wait()
-        hidden = jnp.maximum(
-            jnp.dot(normed, scr_in[c], preferred_element_type=F32), 0.0
-        ).astype(BF16)
-        copies[c][1].wait()
-        part = jnp.dot(hidden, scr_out[c], preferred_element_type=F32)
-        if c > 0:
-            part = part + acc[...]
-        if c < chunks - 1:
-            acc[...] = part
+    for k in range(number):
+        if axis == 0:
+            source = whole.at[pl.ds(start + k * step, step)]
+            target = out.at[pl.ds(k * step, step)]
         else:
-            out[...] = part.astype(BF16)
-
-
-def feed(everyone, gain, w_in, w_out):
-    rows, width = everyone.shape
-    units = w_in.shape[1]
+            source = whole.at[:, pl.ds(start + k * step, step)]
+            target = out.at[:, pl.ds(k * step, step)]
+        copies.append(pltpu.make_async_copy(source, target, sems.at[k]))
+    for copy in copies:
+        copy.start()
+    for copy in copies:
+        copy.wait()
+
+
+def stage(after, whole, axis, part, parts):
+    shape = list(whole.shape)
+    shape[axis] //= parts
+    return pl.pallas_call(
+        functools.partial(stage_kernel, axis=axis, start=part * shape[axis]),
+        out_shape=jax.ShapeDtypeStruct(tuple(shape), BF16),
+        in_specs=[SMEM_SPEC if after.size == 1 else HBM_SPEC, HBM_SPEC],
+        out_specs=VMEM_SPEC,
+        scratch_shapes=[pltpu.SemaphoreType.DMA((4,))],
+        compiler_params=limit(44),
+        cost_estimate=pl.CostEstimate(
+            flops=1 << 30, bytes_accessed=4 * shape[0] * shape[1], transcendentals=0
+        ),
+        name="stage",
+    )(after, whole)
+
+
+def feed_kernel(index, mine, theirs, gain, *refs, patterns):
+    *weights, out, normed, acc = refs
+    half = len(weights) // 2
+    pairs, rows, width = mine.shape
+    units = weights[0].shape[1]
     size = min(512, units)
-    chunks = units // size
+    weight = gain[...]
+    for k in range(2 * pairs):
+        place = pl.multiple_of((index[0] ^ patterns[k]) * rows, rows)
+        states = mine[k] if k < pairs else theirs[k - pairs]
+        normed[pl.ds(place, rows)] = norm_rows(states, weight).astype(BF16)
+    first = True
+    for w_in, w_out in zip(weights[:half], weights[half:]):
+        for c in range(units // size):
+            columns = pl.ds(c * size, size)
+            hidden = jnp.maximum(
+                jnp.dot(normed[...], w_in[:, columns], preferred_element_type=F32), 0.0
+            ).astype(BF16)
+            part = jnp.dot(hidden, w_out[columns], preferred_element_type=F32)
+            acc[...] = part if first else part + acc[...]
+            first = False
+    out[...] = acc[...].astype(BF16)
+
+
+def feed(index, mine, theirs, gain, weights, patterns):
+    pairs, rows, width = mine.shape
+    count = 2 * pairs * rows
+    units = weights[0].shape[1] * len(weights) // 2
     return pl.pallas_call(
-        feed_kernel,
-        out_shape=jax.ShapeDtypeStruct((rows, width), BF16),
-        in_specs=[VMEM_SPEC, VMEM_SPEC, HBM_SPEC, HBM_SPEC],
+        functools.partial(feed_kernel, patterns=patterns),
+        out_shape=jax.ShapeDtypeStruct((count, width), BF16),
+        in_specs=[SMEM_SPEC] + [VMEM_SPEC] * (3 + len(weights)),
         out_specs=VMEM_SPEC,
-        scratch_shapes=[
-            pltpu.VMEM((chunks, width, size), BF16),
-            pltpu.VMEM((chunks, size, width), BF16),
-            pltpu.VMEM((rows, width), F32),
-            pltpu.SemaphoreType.DMA((2, chunks)),
-        ],
-        compiler_params=limit(52),
+        scratch_shapes=[pltpu.VMEM((count, width), BF16), pltpu.VMEM((count, width), F32)],
+        compiler_params=limit(24),
         cost_estimate=pl.CostEstimate(
-            flops=4 * rows * width * units, bytes_accessed=4 * width * units, transcendentals=0
+            flops=4 * count * width * units, bytes_accessed=4 * width * units, transcendentals=0
         ),
         name="feed",
-    )(everyone, gain.reshape(1, width), w_in, w_out)
+    )(index, mine, theirs, gain.reshape(1, width), *weights)
 
 
 def settle_kernel(parts, tokens, gain, encoded, spread):
@@ -299,9 +327,27 @@
     inner = heads * DH
 
     half = jnp.reshape(psg_index, (1,)).astype(jnp.int32)
-    everyone = gather_mp(tokens, mp).reshape(mp * row_count, width)
+    index = jnp.reshape(mp_index, (1,)).astype(jnp.int32)
+    patterns = [0]
+    held = tokens[None]
+    weights = []
+    step = mp // 2
+    while step > 0:
+        got = lax.ppermute(held, "mp", [(j, j ^ step) for j in range(mp)])
+        after = index if step == mp // 2 else held
+        if step == mp // 2:
+            weights.append(stage(after, w_in, 1, 0, 2))
+        elif step == mp // 4:
+            weights.append(stage(after, w_in, 1, 1, 2))
+        elif step == 1:
+            weights.append(stage(after, w_out, 0, 0, 2))
+            weights.append(stage(after, w_out, 0, 1, 2))
+        patterns = patterns + [p ^ step for p in patterns]
+        if step > 1:
+            held = jnp.concatenate([held, got], axis=0)
+        step //= 2
     query, wkv = prepare(half, answer_states, dec_gain, w_query, w_keyval, inner)
-    partial_sums = feed(everyone, enc_gain, w_in, w_out)
+    partial_sums = feed(index, held, got, enc_gain, weights, patterns)
     parts = lax.all_to_all(partial_sums.reshape(mp, row_count, width), "mp", 0, 0)
     encoded, spread = settle(parts, tokens, final_gain)
     mine = lax.all_to_all(spread, "mp", 0, 0).reshape(mp * row_count, width)

time: 74.7 us -> 72 us (0.964)
  blocking collectives: 16 us -> 0 us
  starting transfers between devices: 12.3 us -> 21.3 us
  Pallas kernels: 20.9 us -> 26.7 us
  local copies, waits for them, and re-layouts: 1.52 us -> 0.07 us
    all_to_all x1 -> x0, blocking collectives: 16 us -> none  [gather_mp(): lax.all_to_all(jnp.broadcast_to(x[None], (count,) + x.shape), 'mp', 0, 0)]
    ppermute x0 -> x3, starting transfers between devices: none -> 7.54 us  [per_device(): got = lax.ppermute(held, 'mp', [(j, j ^ step) for j in range(mp)])]
    pallas_call x1 -> x5, Pallas kernels: 7.13 us -> 13 us  [the longest x4 8.88 us: stage(): pl.pallas_call(functools.partial(stage_kernel, axis=axis, start=part * sh...]
    all_to_all x1, starting transfers between devices: 3.6 us -> 4.89 us  [per_device(): lax.all_to_all(partial_sums.reshape(mp, row_count, width), 'mp', 0, 0)]
    broadcast_in_dim x1 -> x0, local copies, waits for them, and re-layouts: 0.78 us -> none  [gather_mp(): jnp.broadcast_to(x[None], (count,) + x.shape)]
  transfers between devices with their start and end apart: 6 -> 9, of which waited for: 6 -> 8; matrix products, arithmetic and copies ran while one was open for 1% -> 1% of each run, Pallas kernels for 10% -> 22%
where the time goes in v3:
time: 72 us; the launch traced here: 71.5 us
  Pallas kernels  26.7 us (37%)
  starting transfers between devices  21.3 us (30%)
  waiting for transfers between devices  20.9 us (29%)
  other arithmetic  1.74 us (2%)
  between operations  0.84 us (1%)
    pallas_call x4, Pallas kernels, stage(): pl.pallas_call(functools.partial(stage_kernel, axis=axis, start=part * sh...  8.88 us
    all_to_all x1, waiting for transfers between devices, per_device(): lax.all_to_all(partial_sums.reshape(mp, row_count, width), 'mp', 0, 0)  8.1 us
    ppermute x3, starting transfers between devices, per_device(): got = lax.ppermute(held, 'mp', [(j, j ^ step) for j in range(mp)])  7.54 us
    all_to_all x1, waiting for transfers between devices, per_device(): answer_parts = lax.all_to_all(chip_sum, 'mp', 0, 0)  7.34 us
    pallas_call x1, Pallas kernels, prepare(): pl.pallas_call(prepare_kernel, out_shape=(jax.ShapeDtypeStruct((count, in...  7.14 us
    pallas_call x1, Pallas kernels, attend(): pl.pallas_call(attend_kernel, out_shape=jax.ShapeDtypeStruct((count, widt...  5.74 us
    all_to_all x1, starting transfers between devices, per_device(): answer_parts = lax.all_to_all(chip_sum, 'mp', 0, 0)  5.13 us
    all_to_all x1, starting transfers between devices, per_device(): lax.all_to_all(partial_sums.reshape(mp, row_count, width), 'mp', 0, 0)  4.89 us
  transfers between devices with their start and end apart: 9, of which 8 were waited for; matrix products, arithmetic and copies ran while one was open for 1% of the time, Pallas kernels for 22%

profile of v3, /device:TPU:0, one launch (start us, length us, event | category | flops | bytes accessed | tf_op | source)
XLA Modules:
  0.0 71.5 jit_solution(4130209620655407748)
XLA Ops:
  0.6 4.1 %collective-permute-start = (bf16[1,16,1024]{2,1,0:T(8,128)(2,1)}, bf16[1,16,1024]{2,1,0:T(8,128)(2,1)S(1)}, u32[]{:S(2)}, u32[]{:S(2)}) collective-permute-start(bf16[1,16,1024]{2,1,0:T(8,128)(2,1)} %bitcast.19), channel_id=1, source_target_pairs={{0,8},{2,10},{4,12},{6,14},{8,0},{10,2},{12,4},{14,6},{1,9},{3,11}... | collective-permute-start | bytes 98312 | tf_op jit(solution)/shard_map/ppermute | solution.py:336
  4.8 0.0 copy-start.1
  4.8 2.2 %stage.4.refs_0_ = bf16[1024,2048]{1,0:T(8,128)(2,1)S(1)} custom-call(s32[1]{0:T(128)} %bitcast.after.index, bf16[1024,4096]{1,0:T(8,128)(2,1)} %whole.5), custom_call_target="tpu_custom_call" | custom-call | flops 1073741824 | bytes 8388608 | tf_op jit(solution)/shard_map/stage/pallas_call | solution.py:147
  7.0 0.2 collective-permute-done
  7.2 0.0 copy-done.1
  7.2 1.6 %collective-permute-start.1 = (bf16[2,16,1024]{2,1,0:T(8,128)(2,1)S(1)}, bf16[2,16,1024]{2,1,0:T(8,128)(2,1)S(1)}, u32[]{:S(2)}, u32[]{:S(2)}) collective-permute-start(bf16[2,16,1024]{2,1,0:T(8,128)(2,1)S(1)} %pad_maximum_fusion.1.after), channel_id=1, source_target_pairs={{0,4},{2,6},{4,0},{6,2},{8,12},{10,14},{12,8},{14,10},{1,5},{3,7},... | collective-permute-start | bytes 196616 | tf_op jit(solution)/shard_map/ppermute | solution.py:336
  8.8 2.2 %stage.5.refs_1_ = bf16[1024,2048]{1,0:T(8,128)(2,1)S(1)} custom-call(bf16[2,16,1024]{2,1,0:T(8,128)(2,1)S(1)} %pad_maximum_fusion.1.after, bf16[1024,4096]{1,0:T(8,128)(2,1)} %whole.5), custom_call_target="tpu_custom_call" | custom-call | flops 1073741824 | bytes 8388608 | tf_op jit(solution)/shard_map/stage/pallas_call | solution.py:147
  11.1 0.5 collective-permute-done.1
  11.6 1.8 %collective-permute-start.2 = (bf16[4,16,1024]{2,1,0:T(8,128)(2,1)S(1)}, bf16[4,16,1024]{2,1,0:T(8,128)(2,1)S(1)}, u32[]{:S(2)}, u32[]{:S(2)}) collective-permute-start(bf16[4,16,1024]{2,1,0:T(8,128)(2,1)S(1)} %pad_maximum_fusion.after.mine), channel_id=1, source_target_pairs={{0,2},{2,0},{4,6},{6,4},{8,10},{10,8},{12,14},{14,12},{1,3},{3,1},... | collective-permute-start | bytes 393224 | tf_op jit(solution)/shard_map/ppermute | solution.py:336
  13.4 2.2 %stage.6.refs_2_ = bf16[2048,1024]{1,0:T(8,128)(2,1)S(1)} custom-call(bf16[4,16,1024]{2,1,0:T(8,128)(2,1)S(1)} %pad_maximum_fusion.after.mine, bf16[4096,1024]{1,0:T(8,128)(2,1)} %whole.7), custom_call_target="tpu_custom_call" | custom-call | flops 1073741824 | bytes 8388608 | tf_op jit(solution)/shard_map/stage/pallas_call | solution.py:147
  15.6 0.0 copy-start.4
  15.6 2.2 %stage.7.refs_3_ = bf16[2048,1024]{1,0:T(8,128)(2,1)S(1)} custom-call(bf16[4,16,1024]{2,1,0:T(8,128)(2,1)S(1)} %pad_maximum_fusion.after.mine, bf16[4096,1024]{1,0:T(8,128)(2,1)} %whole.7), custom_call_target="tpu_custom_call" | custom-call | flops 1073741824 | bytes 8388608 | tf_op jit(solution)/shard_map/stage/pallas_call | solution.py:147
  17.8 0.0 collective-permute-done.2.theirs
  17.8 0.0 copy-done.4
  17.8 0.0 copy-start.5
  17.8 0.0 copy-start.6
  17.9 0.0 copy-start.2
  17.9 0.0 copy-start.7
  17.9 0.0 copy-start
  17.9 0.0 copy-start.3
  17.9 4.1 %feed.1 = bf16[128,1024]{1,0:T(8,128)(2,1)} custom-call(s32[1]{0:T(128)} %bitcast.after.index, bf16[4,16,1024]{2,1,0:T(8,128)(2,1)S(1)} %pad_maximum_fusion.after.mine, bf16[4,16,1024]{2,1,0:T(8,128)(2,1)S(1)} %collective-permute-done.2.theirs, f32[1,1024]{1,0:T(1,128)S(1)} %bitcast.24, bf16[1024,2048]{1,0:T(8,128)(2,1)S(1)} %stage.4.refs_0_, ...), custom_call_target="tpu_custom_call" | custom-call | flops 2147483648 | bytes 16777216 | tf_op jit(solution)/shard_map/feed/pallas_call | solution.py:189
  22.0 4.9 %all-to-all-start = ((bf16[8,16,1024]{2,1,0:T(8,128)(2,1)}), bf16[8,16,1024]{2,1,0:T(8,128)(2,1)S(1)}, u32[]{:S(2)}, u32[]{:S(2)}) async-start(bf16[8,16,1024]{2,1,0:T(8,128)(2,1)} %bitcast.3), calls=%async_computation | async-start | bytes 524288 | tf_op jit(solution)/shard_map/all_to_all | solution.py:351
  26.9 0.0 copy-done.5
  26.9 0.0 copy-done.6
  26.9 0.1 select_reduce_fusion.1
  27.0 8.1 %all-to-all-done.parts = bf16[8,16,1024]{2,1,0:T(8,128)(2,1)S(1)} async-done(((bf16[8,16,1024]{2,1,0:T(8,128)(2,1)}), bf16[8,16,1024]{2,1,0:T(8,128)(2,1)S(1)}, u32[]{:S(2)}, u32[]{:S(2)}) %all-to-all-start) | async-done | bytes 262176 | tf_op jit(solution)/shard_map/all_to_all | solution.py:351
  35.1 0.0 copy-done.2
  35.1 0.9 %settle.1 = (bf16[16,1024]{1,0:T(8,128)(2,1)}, bf16[8,16,1024]{2,1,0:T(8,128)(2,1)}) custom-call(bf16[8,16,1024]{2,1,0:T(8,128)(2,1)S(1)} %all-to-all-done.parts, bf16[16,1024]{1,0:T(8,128)(2,1)S(1)} %copy-done.1, f32[1,1024]{1,0:T(1,128)S(1)} %bitcast.22), custom_call_target="tpu_custom_call" | custom-call | tf_op jit(solution)/shard_map/settle/pallas_call | solution.py:216
  35.9 3.4 %all-to-all-start.1 = ((bf16[8,16,1024]{2,1,0:T(8,128)(2,1)}), bf16[8,16,1024]{2,1,0:T(8,128)(2,1)S(1)}, u32[]{:S(2)}, u32[]{:S(2)}) async-start(bf16[8,16,1024]{2,1,0:T(8,128)(2,1)} %get-tuple-element.7), calls=%async_computation.1 | async-start | bytes 524288 | tf_op jit(solution)/shard_map/all_to_all | solution.py:353
  39.4 0.0 copy-done.7
  39.4 0.1 select_reduce_fusion.2
  39.5 0.0 copy-done
  39.5 0.0 copy-done.3
  39.5 7.1 %prepare.1 = (bf16[128,1024]{1,0:T(8,128)(2,1)S(1)}, bf16[2,1024,1024]{2,1,0:T(8,128)(2,1)}) custom-call(s32[1]{0:T(128)} %bitcast.5.half, bf16[128,1024]{1,0:T(8,128)(2,1)S(1)} %copy-done, f32[1,1024]{1,0:T(1,128)S(1)} %bitcast.23, bf16[1024,2048]{1,0:T(8,128)(2,1)} %w_query.1, bf16[1024,2,2048]{2,1,0:T(2,128)(2,1)} %w_keyval.1), custom_call_target="tpu_custom_call" | custom-call | flops 1342177280 | bytes 10485760 | tf_op jit(solution)/shard_map/prepare/pallas_call | solution.py:101
  46.6 0.9 %all-to-all-done.1 = bf16[8,16,1024]{2,1,0:T(8,128)(2,1)S(1)} async-done(((bf16[8,16,1024]{2,1,0:T(8,128)(2,1)}), bf16[8,16,1024]{2,1,0:T(8,128)(2,1)S(1)}, u32[]{:S(2)}, u32[]{:S(2)}) %all-to-all-start.1) | async-done | bytes 262176 | tf_op jit(solution)/shard_map/all_to_all | solution.py:353
  47.5 0.0 collective-permute-start.3
  47.5 0.1 convert_reduce_fusion.1
  47.6 0.1 and_convert_fusion.allowed
  47.7 1.4 %collective-permute-done.3.theirs = bf16[128,1024]{1,0:T(8,128)(2,1)S(1)} collective-permute-done((bf16[128,1024]{1,0:T(8,128)(2,1)S(1)}, bf16[128,1024]{1,0:T(8,128)(2,1)S(1)}, u32[]{:S(2)}, u32[]{:S(2)}) %collective-permute-start.3) | collective-permute-done | bytes 262176 | tf_op jit(solution)/shard_map/ppermute | solution.py:43
  49.1 5.7 %attend.1 = f32[128,1024]{1,0:T(8,128)S(1)} custom-call(s32[1]{0:T(128)} %bitcast.5.half, bf16[128,1024]{1,0:T(8,128)(2,1)S(1)} %bitcast.18, bf16[128,1024]{1,0:T(8,128)(2,1)S(1)} %collective-permute-done.3.theirs, bf16[128,1024]{1,0:T(8,128)(2,1)S(1)} %get-tuple-element.8.query, s32[128,256]{1,0:T(8,128)S(1)} %and_convert_fusion.allowed, ...), custom_call_target="tpu_custom_call" | custom-call | flops 1476395008 | bytes 6291456 | tf_op jit(solution)/shard_map/attend/pallas_call | solution.py:282
  54.8 0.2 collective-permute-start.4
  55.0 1.4 %collective-permute-done.4 = f32[8,8,1024]{2,1,0:T(8,128)S(1)} collective-permute-done((f32[8,8,1024]{2,1,0:T(8,128)S(1)}, f32[8,8,1024]{2,1,0:T(8,128)S(1)}, u32[]{:S(2)}, u32[]{:S(2)}) %collective-permute-start.4) | collective-permute-done | bytes 262176 | tf_op jit(solution)/shard_map/ppermute | solution.py:43
  56.4 0.7 fusion
  57.1 5.1 %all-to-all-start.2 = ((bf16[8,8,1024]{2,1,0:T(8,128)(2,1)}), bf16[8,8,1024]{2,1,0:T(8,128)(2,1)S(1)}, u32[]{:S(2)}, u32[]{:S(2)}) async-start(bf16[8,8,1024]{2,1,0:T(8,128)(2,1)} %fusion), calls=%async_computation.2 | async-start | bytes 262144 | tf_op jit(solution)/shard_map/all_to_all | solution.py:373
  62.2 7.3 %all-to-all-done.2 = bf16[8,8,1024]{2,1,0:T(8,128)(2,1)S(1)} async-done(((bf16[8,8,1024]{2,1,0:T(8,128)(2,1)}), bf16[8,8,1024]{2,1,0:T(8,128)(2,1)S(1)}, u32[]{:S(2)}, u32[]{:S(2)}) %all-to-all-start.2) | async-done | bytes 131104 | tf_op jit(solution)/shard_map/all_to_all | solution.py:373
  69.6 0.1 collective-permute-start.5
  69.7 1.2 %collective-permute-done.5 = bf16[8,1024]{1,0:T(8,128)(2,1)S(1)} collective-permute-done((bf16[8,1024]{1,0:T(8,128)(2,1)S(1)}, bf16[8,1024]{1,0:T(8,128)(2,1)S(1)}, u32[]{:S(2)}, u32[]{:S(2)}) %collective-permute-start.5) | collective-permute-done | bytes 16416 | tf_op jit(solution)/shard_map/ppermute | solution.py:43
  70.9 0.6 pad_maximum_fusion.2
  (8 shorter events, 0.1 us)
Async XLA Ops:
  0.6 6.6 %collective-permute-start = (bf16[1,16,1024]{2,1,0:T(8,128)(2,1)}, bf16[1,16,1024]{2,1,0:T(8,128)(2,1)S(1)}, u32[]{:S(2)}, u32[]{:S(2)}) collective-permute-start(bf16[1,16,1024]{2,1,0:T(8,128)(2,1)} %bitcast.19), channel_id=1, source_target_pairs={{0,8},{2,10},{4,12},{6,14},{8,0},{10,2},{12,4},{14,6},{1,9},{3,11}... | collective-permute-start | bytes 98312 | tf_op jit(solution)/shard_map/ppermute | solution.py:336
  4.8 2.5 %copy-start.1 = (bf16[16,1024]{1,0:T(8,128)(2,1)S(1)}, bf16[16,1024]{1,0:T(8,128)(2,1)}, u32[]{:S(2)}) copy-start(bf16[16,1024]{1,0:T(8,128)(2,1)} %tokens.1) | copy-start | bytes 98308
  7.2 4.3 %collective-permute-start.1 = (bf16[2,16,1024]{2,1,0:T(8,128)(2,1)S(1)}, bf16[2,16,1024]{2,1,0:T(8,128)(2,1)S(1)}, u32[]{:S(2)}, u32[]{:S(2)}) collective-permute-start(bf16[2,16,1024]{2,1,0:T(8,128)(2,1)S(1)} %pad_maximum_fusion.1.after), channel_id=1, source_target_pairs={{0,4},{2,6},{4,0},{6,2},{8,12},{10,14},{12,8},{14,10},{1,5},{3,7},... | collective-permute-start | bytes 196616 | tf_op jit(solution)/shard_map/ppermute | solution.py:336
  11.6 6.2 %collective-permute-start.2 = (bf16[4,16,1024]{2,1,0:T(8,128)(2,1)S(1)}, bf16[4,16,1024]{2,1,0:T(8,128)(2,1)S(1)}, u32[]{:S(2)}, u32[]{:S(2)}) collective-permute-start(bf16[4,16,1024]{2,1,0:T(8,128)(2,1)S(1)} %pad_maximum_fusion.after.mine), channel_id=1, source_target_pairs={{0,2},{2,0},{4,6},{6,4},{8,10},{10,8},{12,14},{14,12},{1,3},{3,1},... | collective-permute-start | bytes 393224 | tf_op jit(solution)/shard_map/ppermute | solution.py:336
  15.6 2.2 %copy-start.4 = (f32[1024]{0:T(1024)S(1)}, f32[1024]{0:T(1024)}, u32[]{:S(2)}) copy-start(f32[1024]{0:T(1024)} %param.14) | copy-start | bytes 12292
  17.8 9.1 %copy-start.5 = (s32[16]{0:T(128)S(1)}, s32[16]{0:T(128)}, u32[]{:S(2)}) copy-start(s32[16]{0:T(128)} %param.23) | copy-start | bytes 196
  17.8 9.1 %copy-start.6 = (s32[16]{0:T(128)S(1)}, s32[16]{0:T(128)}, u32[]{:S(2)}) copy-start(s32[16]{0:T(128)} %param.24) | copy-start | bytes 196
  17.9 17.2 %copy-start.2 = (f32[1024]{0:T(1024)S(1)}, f32[1024]{0:T(1024)}, u32[]{:S(2)}) copy-start(f32[1024]{0:T(1024)} %param.17) | copy-start | bytes 12292
  17.9 21.5 %copy-start.7 = (s32[4]{0:T(128)S(1)}, s32[4]{0:T(128)}, u32[]{:S(2)}) copy-start(s32[4]{0:T(128)} %param.25) | copy-start | bytes 52
  17.9 21.6 %copy-start = (bf16[128,1024]{1,0:T(8,128)(2,1)S(1)}, bf16[128,1024]{1,0:T(8,128)(2,1)}, u32[]{:S(2)}) copy-start(bf16[128,1024]{1,0:T(8,128)(2,1)} %states.1) | copy-start | bytes 786436
  17.9 21.6 %copy-start.3 = (f32[1024]{0:T(1024)S(1)}, f32[1024]{0:T(1024)}, u32[]{:S(2)}) copy-start(f32[1024]{0:T(1024)} %param.20) | copy-start | bytes 12292
  22.0 13.1 %all-to-all-start = ((bf16[8,16,1024]{2,1,0:T(8,128)(2,1)}), bf16[8,16,1024]{2,1,0:T(8,128)(2,1)S(1)}, u32[]{:S(2)}, u32[]{:S(2)}) async-start(bf16[8,16,1024]{2,1,0:T(8,128)(2,1)} %bitcast.3), calls=%async_computation | async-start | bytes 524288 | tf_op jit(solution)/shard_map/all_to_all | solution.py:351
  35.9 11.6 %all-to-all-start.1 = ((bf16[8,16,1024]{2,1,0:T(8,128)(2,1)}), bf16[8,16,1024]{2,1,0:T(8,128)(2,1)S(1)}, u32[]{:S(2)}, u32[]{:S(2)}) async-start(bf16[8,16,1024]{2,1,0:T(8,128)(2,1)} %get-tuple-element.7), calls=%async_computation.1 | async-start | bytes 524288 | tf_op jit(solution)/shard_map/all_to_all | solution.py:353
  47.5 1.5 %collective-permute-start.3 = (bf16[128,1024]{1,0:T(8,128)(2,1)S(1)}, bf16[128,1024]{1,0:T(8,128)(2,1)S(1)}, u32[]{:S(2)}, u32[]{:S(2)}) collective-permute-start(bf16[128,1024]{1,0:T(8,128)(2,1)S(1)} %bitcast.17), channel_id=1, source_target_pairs={{0,1},{1,0},{2,3},{3,2},{4,5},{5,4},{6,7},{7,6},{8,9},{9,8},{10,11... | collective-permute-start | bytes 786440 | tf_op jit(solution)/shard_map/ppermute | solution.py:43
  54.8 1.6 %collective-permute-start.4 = (f32[8,8,1024]{2,1,0:T(8,128)S(1)}, f32[8,8,1024]{2,1,0:T(8,128)S(1)}, u32[]{:S(2)}, u32[]{:S(2)}) collective-permute-start(f32[8,8,1024]{2,1,0:T(8,128)S(1)} %dynamic-slice_bitcast_fusion), channel_id=1, source_target_pairs={{0,1},{1,0},{2,3},{3,2},{4,5},{5,4},{6,7},{7,6},{8,9},{9,8},{10,11... | collective-permute-start | bytes 786440 | tf_op jit(solution)/shard_map/ppermute | solution.py:43
  57.1 12.5 %all-to-all-start.2 = ((bf16[8,8,1024]{2,1,0:T(8,128)(2,1)}), bf16[8,8,1024]{2,1,0:T(8,128)(2,1)S(1)}, u32[]{:S(2)}, u32[]{:S(2)}) async-start(bf16[8,8,1024]{2,1,0:T(8,128)(2,1)} %fusion), calls=%async_computation.2 | async-start | bytes 262144 | tf_op jit(solution)/shard_map/all_to_all | solution.py:373
  69.6 1.2 %collective-permute-start.5 = (bf16[8,1024]{1,0:T(8,128)(2,1)S(1)}, bf16[8,1024]{1,0:T(8,128)(2,1)S(1)}, u32[]{:S(2)}, u32[]{:S(2)}) collective-permute-start(bf16[8,1024]{1,0:T(8,128)(2,1)S(1)} %add_convert_fusion), channel_id=1, source_target_pairs={{0,1},{1,0},{2,3},{3,2},{4,5},{5,4},{6,7},{7,6},{8,9},{9,8},{10,11... | collective-permute-start | bytes 49160 | tf_op jit(solution)/shard_map/ppermute | solution.py:43

commit v4 on v3

--- a/solution.py
+++ b/solution.py
@@ -54,7 +54,7 @@
     return pltpu.CompilerParams(vmem_limit_bytes=mib << 20)
 
 
-def prepare_kernel(half, states, gain, w_query, w_keyval, query, wkv, scr_q, scr_kv, sems):
+def prepare_kernel(half, states, gain, w_query, w_keyval, query, w_key, wkv, scr_q, scr_kv, sems):
     width = states.shape[1]
     inner = query.shape[1]
     strips = inner // 128
@@ -91,6 +91,7 @@
                 [scr_kv[s, rows].reshape(256, 128), scr_kv[s + 1, rows].reshape(256, 128)], axis=1
             )
             apart = jnp.dot(pick, mixed, preferred_element_type=F32).astype(BF16)
+            w_key[rows, pl.ds(s * 128, 256)] = apart[:128]
             wkv[0, rows, pl.ds(s * 128, 256)] = apart[:128]
             wkv[1, rows, pl.ds(s * 128, 256)] = apart[128:]
 
@@ -102,16 +103,17 @@
         prepare_kernel,
         out_shape=(
             jax.ShapeDtypeStruct((count, inner), BF16),
+            jax.ShapeDtypeStruct((width, inner), BF16),
             jax.ShapeDtypeStruct((2, width, inner), BF16),
         ),
         in_specs=[SMEM_SPEC, VMEM_SPEC, VMEM_SPEC, HBM_SPEC, HBM_SPEC],
-        out_specs=(VMEM_SPEC, VMEM_SPEC),
+        out_specs=(VMEM_SPEC,) * 3,
         scratch_shapes=[
             pltpu.VMEM((width, inner), BF16),
             pltpu.VMEM((strips, width, 2, 128), BF16),
             pltpu.SemaphoreType.DMA((strips + 1,)),
         ],
-        compiler_params=limit(52),
+        compiler_params=limit(51),
         cost_estimate=pl.CostEstimate(
             flops=2 * count * width * inner + 4 * width * 256 * inner,
             bytes_accessed=10 * width * inner,
@@ -141,7 +143,7 @@
         copy.wait()
 
 
-def stage(after, whole, axis, part, parts):
+def stage(after, whole, axis, part, parts, room=44):
     shape = list(whole.shape)
     shape[axis] //= parts
     return pl.pallas_call(
@@ -150,7 +152,7 @@
         in_specs=[SMEM_SPEC if after.size == 1 else HBM_SPEC, HBM_SPEC],
         out_specs=VMEM_SPEC,
         scratch_shapes=[pltpu.SemaphoreType.DMA((4,))],
-        compiler_params=limit(44),
+        compiler_params=limit(room),
         cost_estimate=pl.CostEstimate(
             flops=1 << 30, bytes_accessed=4 * shape[0] * shape[1], transcendentals=0
         ),
@@ -159,27 +161,30 @@
 
 
 def feed_kernel(index, mine, theirs, gain, *refs, patterns):
-    *weights, out, normed, acc = refs
+    *weights, out, normed, hidden = refs
     half = len(weights) // 2
     pairs, rows, width = mine.shape
     units = weights[0].shape[1]
-    size = min(512, units)
+    size = min(256, units)
     weight = gain[...]
     for k in range(2 * pairs):
         place = pl.multiple_of((index[0] ^ patterns[k]) * rows, rows)
         states = mine[k] if k < pairs else theirs[k - pairs]
         normed[pl.ds(place, rows)] = norm_rows(states, weight).astype(BF16)
-    first = True
-    for w_in, w_out in zip(weights[:half], weights[half:]):
+    for part in range(half):
         for c in range(units // size):
             columns = pl.ds(c * size, size)
-            hidden = jnp.maximum(
-                jnp.dot(normed[...], w_in[:, columns], preferred_element_type=F32), 0.0
+            hidden[part, :, columns] = jnp.maximum(
+                jnp.dot(normed[...], weights[part][:, columns], preferred_element_type=F32), 0.0
             ).astype(BF16)
-            part = jnp.dot(hidden, w_out[columns], preferred_element_type=F32)
-            acc[...] = part if first else part + acc[...]
-            first = False
-    out[...] = acc[...].astype(BF16)
+    for c in range(width // 256):
+        columns = pl.ds(c * 256, 256)
+        total = jnp.dot(hidden[0], weights[half][:, columns], preferred_element_type=F32)
+        for part in range(1, half):
+            total = total + jnp.dot(
+                hidden[part], weights[half + part][:, columns], preferred_element_type=F32
+            )
+        out[:, columns] = total.astype(BF16)
 
 
 def feed(index, mine, theirs, gain, weights, patterns):
@@ -191,7 +196,10 @@
         out_shape=jax.ShapeDtypeStruct((count, width), BF16),
         in_specs=[SMEM_SPEC] + [VMEM_SPEC] * (3 + len(weights)),
         out_specs=VMEM_SPEC,
-        scratch_shapes=[pltpu.VMEM((count, width), BF16), pltpu.VMEM((count, width), F32)],
+        scratch_shapes=[
+            pltpu.VMEM((count, width), BF16),
+            pltpu.VMEM((len(weights) // 2, count, weights[0].shape[1]), BF16),
+        ],
         compiler_params=limit(24),
         cost_estimate=pl.CostEstimate(
             flops=4 * count * width * units, bytes_accessed=4 * width * units, transcendentals=0
@@ -200,7 +208,8 @@
     )(index, mine, theirs, gain.reshape(1, width), *weights)
 
 
-def settle_kernel(parts, tokens, gain, encoded, spread):
+def settle_kernel(parts, tokens, gain, after, encoded, spread):
+    del after
     total = tokens[...].astype(F32)
     for k in range(parts.shape[0]):
         total = total + parts[k].astype(F32)
@@ -211,7 +220,7 @@
         spread[k] = memory
 
 
-def settle(parts, tokens, gain):
+def settle(parts, tokens, gain, after):
     count, rows, width = parts.shape
     return pl.pallas_call(
         settle_kernel,
@@ -219,86 +228,118 @@
             jax.ShapeDtypeStruct((rows, width), BF16),
             jax.ShapeDtypeStruct((count, rows, width), BF16),
         ),
-        in_specs=[VMEM_SPEC] * 3,
+        in_specs=[VMEM_SPEC] * 3 + [HBM_SPEC],
         out_specs=(VMEM_SPEC, VMEM_SPEC),
         compiler_params=limit(8),
         name="settle",
-    )(parts, tokens, gain.reshape(1, width))
-
-
-def attend_kernel(half, mine, theirs, query, allowed, wkv, w_out, out, scr_k, scr_v, scr_o, context, sems):
-    chunks, _, size = scr_k.shape
-    inner = chunks * size
-    width = out.shape[1]
+    )(parts, tokens, gain.reshape(1, width), after)
+
+
+def project_kernel(half, mine, w_key, wkv, w_out, keys, values, w_value, w_last, sems):
+    inner = keys.shape[1]
+    size = min(256, inner)
     start = pl.multiple_of(half[0] * inner, 128)
-    copies = []
+    chunks = inner // size
+    copies = [
+        pltpu.make_async_copy(
+            wkv.at[1, :, pl.ds(c * size, size)], w_value.at[:, pl.ds(c * size, size)], sems.at[c]
+        )
+        for c in range(chunks)
+    ]
+    last = pltpu.make_async_copy(w_out.at[pl.ds(start, inner)], w_last, sems.at[chunks])
+    for copy in copies:
+        copy.start()
+    last.start()
     for c in range(chunks):
         columns = pl.ds(c * size, size)
-        copies.append(
-            (
-                pltpu.make_async_copy(wkv.at[0, :, columns], scr_k.at[c], sems.at[0, c]),
-                pltpu.make_async_copy(wkv.at[1, :, columns], scr_v.at[c], sems.at[1, c]),
-            )
-        )
-    o_copy = pltpu.make_async_copy(w_out.at[pl.ds(start, inner)], scr_o, sems.at[2, 0])
-    for first, second in copies:
-        first.start()
-        second.start()
-    o_copy.start()
-    live = allowed[...] > 0
-    both = jnp.concatenate([mine[...], theirs[...]], axis=0)
+        keys[:, columns] = jnp.dot(
+            mine[...], w_key[:, columns], preferred_element_type=F32
+        ).astype(BF16)
     for c in range(chunks):
-        copies[c][0].wait()
-        keys = jnp.dot(both, scr_k[c], preferred_element_type=F32).astype(BF16)
-        copies[c][1].wait()
-        values = jnp.dot(both, scr_v[c], preferred_element_type=F32).astype(BF16)
+        columns = pl.ds(c * size, size)
+        copies[c].wait()
+        values[:, columns] = jnp.dot(
+            mine[...], w_value[:, columns], preferred_element_type=F32
+        ).astype(BF16)
+    last.wait()
+
+
+def project(half, mine, w_key, wkv, w_attn_out):
+    rows, width = mine.shape
+    inner = w_key.shape[1]
+    return pl.pallas_call(
+        project_kernel,
+        out_shape=(
+            jax.ShapeDtypeStruct((rows, inner), BF16),
+            jax.ShapeDtypeStruct((rows, inner), BF16),
+            jax.ShapeDtypeStruct((width, inner), BF16),
+            jax.ShapeDtypeStruct((inner, width), BF16),
+        ),
+        in_specs=[SMEM_SPEC, VMEM_SPEC, VMEM_SPEC, HBM_SPEC, HBM_SPEC],
+        out_specs=(VMEM_SPEC,) * 4,
+        scratch_shapes=[pltpu.SemaphoreType.DMA((inner // min(256, inner) + 1,))],
+        compiler_params=limit(45),
+        cost_estimate=pl.CostEstimate(
+            flops=4 * rows * width * inner, bytes_accessed=6 * width * inner, transcendentals=0
+        ),
+        name="project",
+    )(half, mine, w_key, wkv, w_attn_out)
+
+
+def attend_kernel(near_keys, near_values, theirs, query, allowed, w_key, w_value, w_last, out, context):
+    rows, inner = near_keys.shape
+    width = out.shape[1]
+    size = min(256, inner)
+    near = allowed[:, :rows] > 0
+    far = allowed[:, rows:] > 0
+    for c in range(inner // size):
+        columns = pl.ds(c * size, size)
+        far_keys = jnp.dot(theirs[...], w_key[:, columns], preferred_element_type=F32).astype(BF16)
+        far_values = jnp.dot(
+            theirs[...], w_value[:, columns], preferred_element_type=F32
+        ).astype(BF16)
+        keys = jnp.concatenate([near_keys[:, columns], far_keys], axis=0)
+        values = jnp.concatenate([near_values[:, columns], far_values], axis=0)
         for h in range(size // DH):
             lanes = slice(h * DH, (h + 1) * DH)
-            columns = pl.ds(c * size + h * DH, DH)
+            place = pl.ds(c * size + h * DH, DH)
             scores = lax.dot_general(
-                query[:, columns],
+                query[:, place],
                 keys[:, lanes],
                 (((1,), (1,)), ((), ())),
                 preferred_element_type=F32,
             ) * DH ** (-0.5)
-            scores = jnp.where(live, scores, -1e30)
-            top = jnp.max(scores, axis=1, keepdims=True)
-            weights = jnp.where(live, jnp.exp(scores - top), 0.0)
-            total = jnp.sum(weights, axis=1, keepdims=True)
-            summed = jnp.dot(weights.astype(BF16), values[:, lanes], preferred_element_type=F32)
-            context[:, columns] = (summed / total).astype(BF16)
-    o_copy.wait()
+            near_scores = jnp.where(near, scores[:, :rows], -1e30)
+            far_scores = jnp.where(far, scores[:, rows:], -1e30)
+            top = jnp.max(jnp.maximum(near_scores, far_scores), axis=1, keepdims=True)
+            near_weights = jnp.where(near, jnp.exp(near_scores - top), 0.0)
+            far_weights = jnp.where(far, jnp.exp(far_scores - top), 0.0)
+            total = jnp.sum(near_weights + far_weights, axis=1, keepdims=True)
+            weights = jnp.concatenate([near_weights, far_weights], axis=1).astype(BF16)
+            summed = jnp.dot(weights, values[:, lanes], preferred_element_type=F32)
+            context[:, place] = (summed * (1.0 / total)).astype(BF16)
     for c in range(width // 256):
         columns = pl.ds(c * 256, 256)
-        out[:, columns] = jnp.dot(context[...], scr_o[:, columns], preferred_element_type=F32)
-
-
-def attend(half, mine, theirs, query, allowed, wkv, w_attn_out):
-    rows, width = mine.shape
+        out[:, columns] = jnp.dot(context[...], w_last[:, columns], preferred_element_type=F32)
+
+
+def attend(near_keys, near_values, theirs, query, allowed, w_key, w_value, w_last):
+    rows, width = theirs.shape
     count, inner = query.shape
-    size = min(256, inner)
-    chunks = inner // size
-    keys = 2 * rows
     return pl.pallas_call(
         attend_kernel,
         out_shape=jax.ShapeDtypeStruct((count, width), F32),
-        in_specs=[SMEM_SPEC] + [VMEM_SPEC] * 4 + [HBM_SPEC] * 2,
+        in_specs=[VMEM_SPEC] * 8,
         out_specs=VMEM_SPEC,
-        scratch_shapes=[
-            pltpu.VMEM((chunks, width, size), BF16),
-            pltpu.VMEM((chunks, width, size), BF16),
-            pltpu.VMEM((inner, width), BF16),
-            pltpu.VMEM((count, inner), BF16),
-            pltpu.SemaphoreType.DMA((3, chunks)),
-        ],
-        compiler_params=limit(52),
+        scratch_shapes=[pltpu.VMEM((count, inner), BF16)],
+        compiler_params=limit(24),
         cost_estimate=pl.CostEstimate(
-            flops=4 * keys * width * inner + 4 * count * keys * inner + 2 * count * inner * width,
+            flops=4 * rows * width * inner + 8 * count * rows * inner + 2 * count * inner * width,
             bytes_accessed=6 * width * inner,
-            transcendentals=count * keys * inner // DH,
+            transcendentals=2 * count * rows * inner // DH,
         ),
         name="attend",
-    )(half, mine, theirs, query, allowed, wkv, w_attn_out)
+    )(near_keys, near_values, theirs, query, allowed, w_key, w_value, w_last)
 
 
 def per_device(
@@ -346,10 +387,10 @@
         if step > 1:
             held = jnp.concatenate([held, got], axis=0)
         step //= 2
-    query, wkv = prepare(half, answer_states, dec_gain, w_query, w_keyval, inner)
+    query, w_key, wkv = prepare(half, answer_states, dec_gain, w_query, w_keyval, inner)
     partial_sums = feed(index, held, got, enc_gain, weights, patterns)
     parts = lax.all_to_all(partial_sums.reshape(mp, row_count, width), "mp", 0, 0)
-    encoded, spread = settle(parts, tokens, final_gain)
+    encoded, spread = settle(parts, tokens, final_gain, query)
     mine = lax.all_to_all(spread, "mp", 0, 0).reshape(mp * row_count, width)
     theirs = swap_psg(mine)
     key_rows = 2 * mp * row_count
@@ -360,8 +401,9 @@
     core = jnp.where(far == 0, psg_index, 1 - psg_index)
     token_index = (block * psg + core) * row_count + local % row_count
     allowed = key_mask(token_index, passage_lengths, passage_owner, answer_lengths, answer_count)
+    near_keys, near_values, w_value, w_last = project(half, mine, w_key, wkv, w_attn_out)
     partial_answer = attend(
-        half, mine, theirs, query, allowed.astype(jnp.int32), wkv, w_attn_out
+        near_keys, near_values, theirs, query, allowed.astype(jnp.int32), w_key, w_value, w_last
     )
 
     out_count = answer_count // mp

time: 72 us -> 69.1 us (0.960)
  Pallas kernels: 26.7 us -> 24.8 us
  waiting for transfers between devices: 20.9 us -> 19.6 us
    all_to_all x1, waiting for transfers between devices: 8.1 us -> 0.86 us  [per_device(): lax.all_to_all(partial_sums.reshape(mp, row_count, width), 'mp', 0, 0)]
    all_to_all x1, waiting for transfers between devices: 0.89 us -> 8 us  [per_device(): mine = lax.all_to_all(spread, 'mp', 0, 0).reshape(mp * row_count, width)]
    pallas_call x1, Pallas kernels: 5.74 us -> 2.05 us  [attend(): pl.pallas_call(attend_kernel, out_shape=jax.ShapeDtypeStruct((count, widt...]
    pallas_call x0 -> x1, Pallas kernels: none -> 2.62 us  [project(): pl.pallas_call(project_kernel, out_shape=(jax.ShapeDtypeStruct((rows, inn...]
    all_to_all x1, starting transfers between devices: 5.13 us -> 3.37 us  [per_device(): answer_parts = lax.all_to_all(chip_sum, 'mp', 0, 0)]
    all_to_all x1, starting transfers between devices: 3.41 us -> 5.16 us  [per_device(): mine = lax.all_to_all(spread, 'mp', 0, 0).reshape(mp * row_count, width)]
    ppermute x3, waiting for transfers between devices: 3.92 us -> 2.33 us  [swap_psg(): return lax.ppermute(x, 'psg', [(0, 1), (1, 0)])]
    pallas_call x1, Pallas kernels: 4.07 us -> 3.17 us  [feed(): pl.pallas_call(functools.partial(feed_kernel, patterns=patterns), out_sha...]
  transfers between devices with their start and end apart: 9 -> 9, of which waited for: 8 -> 7; matrix products, arithmetic and copies ran while one was open for 1% -> 1% of each run, Pallas kernels for 22% -> 27%
where the time goes in v4:
time: 69.1 us; the launch traced here: 68.7 us
  Pallas kernels  24.8 us (36%)
  starting transfers between devices  21.6 us (31%)
  waiting for transfers between devices  19.6 us (28%)
  other arithmetic  1.74 us (3%)
  between operations  0.85 us (1%)
    pallas_call x4, Pallas kernels, stage(): pl.pallas_call(functools.partial(stage_kernel, axis=axis, start=part * sh...  8.88 us
    all_to_all x1, waiting for transfers between devices, per_device(): mine = lax.all_to_all(spread, 'mp', 0, 0).reshape(mp * row_count, width)  8 us
    all_to_all x1, waiting for transfers between devices, per_device(): answer_parts = lax.all_to_all(chip_sum, 'mp', 0, 0)  7.73 us
    ppermute x3, starting transfers between devices, per_device(): got = lax.ppermute(held, 'mp', [(j, j ^ step) for j in range(mp)])  7.54 us
    pallas_call x1, Pallas kernels, prepare(): pl.pallas_call(prepare_kernel, out_shape=(jax.ShapeDtypeStruct((count, in...  7.22 us
    all_to_all x1, starting transfers between devices, per_device(): mine = lax.all_to_all(spread, 'mp', 0, 0).reshape(mp * row_count, width)  5.16 us
    all_to_all x1, starting transfers between devices, per_device(): lax.all_to_all(partial_sums.reshape(mp, row_count, width), 'mp', 0, 0)  4.88 us
    all_to_all x1, starting transfers between devices, per_device(): answer_parts = lax.all_to_all(chip_sum, 'mp', 0, 0)  3.37 us
  transfers between devices with their start and end apart: 9, of which 7 were waited for; matrix products, arithmetic and copies ran while one was open for 1% of the time, Pallas kernels for 27%

profile of v4, /device:TPU:0, one launch (start us, length us, event | category | flops | bytes accessed | tf_op | source)
XLA Modules:
  0.0 68.7 jit_solution(11180614413457173147)
XLA Ops:
  0.6 4.1 %collective-permute-start = (bf16[1,16,1024]{2,1,0:T(8,128)(2,1)}, bf16[1,16,1024]{2,1,0:T(8,128)(2,1)S(1)}, u32[]{:S(2)}, u32[]{:S(2)}) collective-permute-start(bf16[1,16,1024]{2,1,0:T(8,128)(2,1)} %bitcast.19), channel_id=1, source_target_pairs={{0,8},{2,10},{4,12},{6,14},{8,0},{10,2},{12,4},{14,6},{1,9},{3,11}... | collective-permute-start | bytes 98312 | tf_op jit(solution)/shard_map/ppermute | solution.py:377
  4.8 0.0 copy-start.1
  4.8 2.2 %stage.4.refs_0_ = bf16[1024,2048]{1,0:T(8,128)(2,1)S(1)} custom-call(s32[1]{0:T(128)} %bitcast.after.index, bf16[1024,4096]{1,0:T(8,128)(2,1)} %whole.5), custom_call_target="tpu_custom_call" | custom-call | flops 1073741824 | bytes 8388608 | tf_op jit(solution)/shard_map/stage/pallas_call | solution.py:149
  7.0 0.2 collective-permute-done
  7.2 0.0 copy-done.1
  7.2 1.6 %collective-permute-start.1 = (bf16[2,16,1024]{2,1,0:T(8,128)(2,1)S(1)}, bf16[2,16,1024]{2,1,0:T(8,128)(2,1)S(1)}, u32[]{:S(2)}, u32[]{:S(2)}) collective-permute-start(bf16[2,16,1024]{2,1,0:T(8,128)(2,1)S(1)} %pad_maximum_fusion.1.after), channel_id=1, source_target_pairs={{0,4},{2,6},{4,0},{6,2},{8,12},{10,14},{12,8},{14,10},{1,5},{3,7},... | collective-permute-start | bytes 196616 | tf_op jit(solution)/shard_map/ppermute | solution.py:377
  8.8 2.2 %stage.5.refs_1_ = bf16[1024,2048]{1,0:T(8,128)(2,1)S(1)} custom-call(bf16[2,16,1024]{2,1,0:T(8,128)(2,1)S(1)} %pad_maximum_fusion.1.after, bf16[1024,4096]{1,0:T(8,128)(2,1)} %whole.5), custom_call_target="tpu_custom_call" | custom-call | flops 1073741824 | bytes 8388608 | tf_op jit(solution)/shard_map/stage/pallas_call | solution.py:149
  11.1 0.5 collective-permute-done.1
  11.6 1.8 %collective-permute-start.2 = (bf16[4,16,1024]{2,1,0:T(8,128)(2,1)S(1)}, bf16[4,16,1024]{2,1,0:T(8,128)(2,1)S(1)}, u32[]{:S(2)}, u32[]{:S(2)}) collective-permute-start(bf16[4,16,1024]{2,1,0:T(8,128)(2,1)S(1)} %pad_maximum_fusion.after.mine), channel_id=1, source_target_pairs={{0,2},{2,0},{4,6},{6,4},{8,10},{10,8},{12,14},{14,12},{1,3},{3,1},... | collective-permute-start | bytes 393224 | tf_op jit(solution)/shard_map/ppermute | solution.py:377
  13.4 2.2 %stage.6.refs_2_ = bf16[2048,1024]{1,0:T(8,128)(2,1)S(1)} custom-call(bf16[4,16,1024]{2,1,0:T(8,128)(2,1)S(1)} %pad_maximum_fusion.after.mine, bf16[4096,1024]{1,0:T(8,128)(2,1)} %whole.7), custom_call_target="tpu_custom_call" | custom-call | flops 1073741824 | bytes 8388608 | tf_op jit(solution)/shard_map/stage/pallas_call | solution.py:149
  15.6 0.0 copy-start.4
  15.6 2.2 %stage.7.refs_3_ = bf16[2048,1024]{1,0:T(8,128)(2,1)S(1)} custom-call(bf16[4,16,1024]{2,1,0:T(8,128)(2,1)S(1)} %pad_maximum_fusion.after.mine, bf16[4096,1024]{1,0:T(8,128)(2,1)} %whole.7), custom_call_target="tpu_custom_call" | custom-call | flops 1073741824 | bytes 8388608 | tf_op jit(solution)/shard_map/stage/pallas_call | solution.py:149
  17.8 0.0 collective-permute-done.2.theirs
  17.8 0.0 copy-done.4
  17.8 0.0 copy-start.7
  17.8 0.0 copy-start
  17.9 0.0 copy-start.2
  17.9 3.2 %feed.1 = bf16[128,1024]{1,0:T(8,128)(2,1)} custom-call(s32[1]{0:T(128)} %bitcast.after.index, bf16[4,16,1024]{2,1,0:T(8,128)(2,1)S(1)} %pad_maximum_fusion.after.mine, bf16[4,16,1024]{2,1,0:T(8,128)(2,1)S(1)} %collective-permute-done.2.theirs, f32[1,1024]{1,0:T(1,128)S(1)} %bitcast.24, bf16[1024,2048]{1,0:T(8,128)(2,1)S(1)} %stage.4.refs_0_, ...), custom_call_target="tpu_custom_call" | custom-call | flops 2147483648 | bytes 16777216 | tf_op jit(solution)/shard_map/feed/pallas_call | solution.py:194
  21.0 4.9 %all-to-all-start = ((bf16[8,16,1024]{2,1,0:T(8,128)(2,1)}), bf16[8,16,1024]{2,1,0:T(8,128)(2,1)S(1)}, u32[]{:S(2)}, u32[]{:S(2)}) async-start(bf16[8,16,1024]{2,1,0:T(8,128)(2,1)} %bitcast.3), calls=%async_computation | async-start | bytes 524288 | tf_op jit(solution)/shard_map/all_to_all | solution.py:392
  25.9 0.0 copy-done.7
  25.9 0.1 select_reduce_fusion.2
  26.0 0.0 copy-done
  26.0 0.0 copy-done.2
  26.0 0.0 copy-start.3
  26.0 0.0 copy-start.5
  26.1 0.0 copy-start.6
  26.1 7.2 %prepare.1 = (bf16[128,1024]{1,0:T(8,128)(2,1)S(1)}, bf16[1024,1024]{1,0:T(8,128)(2,1)S(1)}, bf16[2,1024,1024]{2,1,0:T(8,128)(2,1)}) custom-call(s32[1]{0:T(128)} %bitcast.5.half, bf16[128,1024]{1,0:T(8,128)(2,1)S(1)} %copy-done, f32[1,1024]{1,0:T(1,128)S(1)} %bitcast.22, bf16[1024,2048]{1,0:T(8,128)(2,1)} %w_query.1, bf16[1024,2,2048]{2,1,0:T(2,128)(2,1)} %w_keyval.1), custom_call_target="tpu_custom_call" | custom-call | flops 1342177280 | bytes 10485760 | tf_op jit(solution)/shard_map/prepare/pallas_call | solution.py:102
  33.3 0.9 %all-to-all-done.parts = bf16[8,16,1024]{2,1,0:T(8,128)(2,1)S(1)} async-done(((bf16[8,16,1024]{2,1,0:T(8,128)(2,1)}), bf16[8,16,1024]{2,1,0:T(8,128)(2,1)S(1)}, u32[]{:S(2)}, u32[]{:S(2)}) %all-to-all-start) | async-done | bytes 262176 | tf_op jit(solution)/shard_map/all_to_all | solution.py:392
  34.2 0.0 copy-done.3
  34.2 0.9 %settle.1 = (bf16[16,1024]{1,0:T(8,128)(2,1)}, bf16[8,16,1024]{2,1,0:T(8,128)(2,1)}) custom-call(bf16[8,16,1024]{2,1,0:T(8,128)(2,1)S(1)} %all-to-all-done.parts, bf16[16,1024]{1,0:T(8,128)(2,1)S(1)} %copy-done.1, f32[1,1024]{1,0:T(1,128)S(1)} %bitcast.23, bf16[128,1024]{1,0:T(8,128)(2,1)S(1)} %get-tuple-element.11.after.query), custom_call_target="tpu_custom_call" | custom-call | tf_op jit(solution)/shard_map/settle/pallas_call | solution.py:225
  35.0 5.2 %all-to-all-start.1 = ((bf16[8,16,1024]{2,1,0:T(8,128)(2,1)}), bf16[8,16,1024]{2,1,0:T(8,128)(2,1)S(1)}, u32[]{:S(2)}, u32[]{:S(2)}) async-start(bf16[8,16,1024]{2,1,0:T(8,128)(2,1)} %get-tuple-element.13), calls=%async_computation.1 | async-start | bytes 524288 | tf_op jit(solution)/shard_map/all_to_all | solution.py:394
  40.2 0.1 convert_reduce_fusion.1
  40.3 0.0 copy-done.5
  40.3 0.0 copy-done.6
  40.3 0.1 select_reduce_fusion.1
  40.4 8.0 %all-to-all-done.1 = bf16[8,16,1024]{2,1,0:T(8,128)(2,1)S(1)} async-done(((bf16[8,16,1024]{2,1,0:T(8,128)(2,1)}), bf16[8,16,1024]{2,1,0:T(8,128)(2,1)S(1)}, u32[]{:S(2)}, u32[]{:S(2)}) %all-to-all-start.1) | async-done | bytes 262176 | tf_op jit(solution)/shard_map/all_to_all | solution.py:394
  48.4 0.0 collective-permute-start.3
  48.4 0.1 and_convert_fusion.allowed
  48.5 2.6 %project.1 = (bf16[128,1024]{1,0:T(8,128)(2,1)S(1)}, bf16[128,1024]{1,0:T(8,128)(2,1)S(1)}, bf16[1024,1024]{1,0:T(8,128)(2,1)S(1)}, bf16[1024,1024]{1,0:T(8,128)(2,1)S(1)}) custom-call(s32[1]{0:T(128)} %bitcast.5.half, bf16[128,1024]{1,0:T(8,128)(2,1)S(1)} %bitcast.18, bf16[1024,1024]{1,0:T(8,128)(2,1)S(1)} %get-tuple-element.14.w_key, ...), custom_call_target="tpu_custom_call" | custom-call | flops 536870912 | bytes 6291456 | tf_op jit(solution)/shard_map/project/pallas_call | solution.py:270
  51.1 0.0 collective-permute-done.3.theirs
  51.1 2.0 %attend.1 = f32[128,1024]{1,0:T(8,128)S(1)} custom-call(bf16[128,1024]{1,0:T(8,128)(2,1)S(1)} %get-tuple-element.16.near_keys, bf16[128,1024]{1,0:T(8,128)(2,1)S(1)} %get-tuple-element.17.near_values, bf16[128,1024]{1,0:T(8,128)(2,1)S(1)} %collective-permute-done.3.theirs, bf16[128,1024]{1,0:T(8,128)(2,1)S(1)} %get-tuple-element.11.after.query, ...), custom_call_target="tpu_custom_call" | custom-call | flops 939524096 | bytes 6291456 | tf_op jit(solution)/shard_map/attend/pallas_call | solution.py:329
  53.2 0.6 collective-permute-start.4
  53.8 1.2 %collective-permute-done.4 = f32[8,8,1024]{2,1,0:T(8,128)S(1)} collective-permute-done((f32[8,8,1024]{2,1,0:T(8,128)S(1)}, f32[8,8,1024]{2,1,0:T(8,128)S(1)}, u32[]{:S(2)}, u32[]{:S(2)}) %collective-permute-start.4) | collective-permute-done | bytes 262176 | tf_op jit(solution)/shard_map/ppermute | solution.py:43
  54.9 0.7 fusion
  55.6 3.4 %all-to-all-start.2 = ((bf16[8,8,1024]{2,1,0:T(8,128)(2,1)}), bf16[8,8,1024]{2,1,0:T(8,128)(2,1)S(1)}, u32[]{:S(2)}, u32[]{:S(2)}) async-start(bf16[8,8,1024]{2,1,0:T(8,128)(2,1)} %fusion), calls=%async_computation.2 | async-start | bytes 262144 | tf_op jit(solution)/shard_map/all_to_all | solution.py:415
  59.0 7.7 %all-to-all-done.2 = bf16[8,8,1024]{2,1,0:T(8,128)(2,1)S(1)} async-done(((bf16[8,8,1024]{2,1,0:T(8,128)(2,1)}), bf16[8,8,1024]{2,1,0:T(8,128)(2,1)S(1)}, u32[]{:S(2)}, u32[]{:S(2)}) %all-to-all-start.2) | async-done | bytes 131104 | tf_op jit(solution)/shard_map/all_to_all | solution.py:415
  66.8 0.1 collective-permute-start.5
  66.9 1.2 %collective-permute-done.5 = bf16[8,1024]{1,0:T(8,128)(2,1)S(1)} collective-permute-done((bf16[8,1024]{1,0:T(8,128)(2,1)S(1)}, bf16[8,1024]{1,0:T(8,128)(2,1)S(1)}, u32[]{:S(2)}, u32[]{:S(2)}) %collective-permute-start.5) | collective-permute-done | bytes 16416 | tf_op jit(solution)/shard_map/ppermute | solution.py:43
  68.0 0.6 pad_maximum_fusion.2
  (8 shorter events, 0.1 us)
Async XLA Ops:
  0.6 6.6 %collective-permute-start = (bf16[1,16,1024]{2,1,0:T(8,128)(2,1)}, bf16[1,16,1024]{2,1,0:T(8,128)(2,1)S(1)}, u32[]{:S(2)}, u32[]{:S(2)}) collective-permute-start(bf16[1,16,1024]{2,1,0:T(8,128)(2,1)} %bitcast.19), channel_id=1, source_target_pairs={{0,8},{2,10},{4,12},{6,14},{8,0},{10,2},{12,4},{14,6},{1,9},{3,11}... | collective-permute-start | bytes 98312 | tf_op jit(solution)/shard_map/ppermute | solution.py:377
  4.8 2.5 %copy-start.1 = (bf16[16,1024]{1,0:T(8,128)(2,1)S(1)}, bf16[16,1024]{1,0:T(8,128)(2,1)}, u32[]{:S(2)}) copy-start(bf16[16,1024]{1,0:T(8,128)(2,1)} %tokens.1) | copy-start | bytes 98308
  7.2 4.3 %collective-permute-start.1 = (bf16[2,16,1024]{2,1,0:T(8,128)(2,1)S(1)}, bf16[2,16,1024]{2,1,0:T(8,128)(2,1)S(1)}, u32[]{:S(2)}, u32[]{:S(2)}) collective-permute-start(bf16[2,16,1024]{2,1,0:T(8,128)(2,1)S(1)} %pad_maximum_fusion.1.after), channel_id=1, source_target_pairs={{0,4},{2,6},{4,0},{6,2},{8,12},{10,14},{12,8},{14,10},{1,5},{3,7},... | collective-permute-start | bytes 196616 | tf_op jit(solution)/shard_map/ppermute | solution.py:377
  11.6 6.2 %collective-permute-start.2 = (bf16[4,16,1024]{2,1,0:T(8,128)(2,1)S(1)}, bf16[4,16,1024]{2,1,0:T(8,128)(2,1)S(1)}, u32[]{:S(2)}, u32[]{:S(2)}) collective-permute-start(bf16[4,16,1024]{2,1,0:T(8,128)(2,1)S(1)} %pad_maximum_fusion.after.mine), channel_id=1, source_target_pairs={{0,2},{2,0},{4,6},{6,4},{8,10},{10,8},{12,14},{14,12},{1,3},{3,1},... | collective-permute-start | bytes 393224 | tf_op jit(solution)/shard_map/ppermute | solution.py:377
  15.6 2.2 %copy-start.4 = (f32[1024]{0:T(1024)S(1)}, f32[1024]{0:T(1024)}, u32[]{:S(2)}) copy-start(f32[1024]{0:T(1024)} %param.14) | copy-start | bytes 12292
  17.8 8.1 %copy-start.7 = (s32[4]{0:T(128)S(1)}, s32[4]{0:T(128)}, u32[]{:S(2)}) copy-start(s32[4]{0:T(128)} %param.25) | copy-start | bytes 52
  17.8 8.2 %copy-start = (bf16[128,1024]{1,0:T(8,128)(2,1)S(1)}, bf16[128,1024]{1,0:T(8,128)(2,1)}, u32[]{:S(2)}) copy-start(bf16[128,1024]{1,0:T(8,128)(2,1)} %states.1) | copy-start | bytes 786436
  17.9 8.2 %copy-start.2 = (f32[1024]{0:T(1024)S(1)}, f32[1024]{0:T(1024)}, u32[]{:S(2)}) copy-start(f32[1024]{0:T(1024)} %param.20) | copy-start | bytes 12292
  21.0 13.1 %all-to-all-start = ((bf16[8,16,1024]{2,1,0:T(8,128)(2,1)}), bf16[8,16,1024]{2,1,0:T(8,128)(2,1)S(1)}, u32[]{:S(2)}, u32[]{:S(2)}) async-start(bf16[8,16,1024]{2,1,0:T(8,128)(2,1)} %bitcast.3), calls=%async_computation | async-start | bytes 524288 | tf_op jit(solution)/shard_map/all_to_all | solution.py:392
  26.0 8.1 %copy-start.3 = (f32[1024]{0:T(1024)S(1)}, f32[1024]{0:T(1024)}, u32[]{:S(2)}) copy-start(f32[1024]{0:T(1024)} %param.17) | copy-start | bytes 12292
  26.0 14.2 %copy-start.5 = (s32[16]{0:T(128)S(1)}, s32[16]{0:T(128)}, u32[]{:S(2)}) copy-start(s32[16]{0:T(128)} %param.23) | copy-start | bytes 196
  26.1 14.2 %copy-start.6 = (s32[16]{0:T(128)S(1)}, s32[16]{0:T(128)}, u32[]{:S(2)}) copy-start(s32[16]{0:T(128)} %param.24) | copy-start | bytes 196
  35.0 13.4 %all-to-all-start.1 = ((bf16[8,16,1024]{2,1,0:T(8,128)(2,1)}), bf16[8,16,1024]{2,1,0:T(8,128)(2,1)S(1)}, u32[]{:S(2)}, u32[]{:S(2)}) async-start(bf16[8,16,1024]{2,1,0:T(8,128)(2,1)} %get-tuple-element.13), calls=%async_computation.1 | async-start | bytes 524288 | tf_op jit(solution)/shard_map/all_to_all | solution.py:394
  48.4 2.7 %collective-permute-start.3 = (bf16[128,1024]{1,0:T(8,128)(2,1)S(1)}, bf16[128,1024]{1,0:T(8,128)(2,1)S(1)}, u32[]{:S(2)}, u32[]{:S(2)}) collective-permute-start(bf16[128,1024]{1,0:T(8,128)(2,1)S(1)} %bitcast.17), channel_id=1, source_target_pairs={{0,1},{1,0},{2,3},{3,2},{4,5},{5,4},{6,7},{7,6},{8,9},{9,8},{10,11... | collective-permute-start | bytes 786440 | tf_op jit(solution)/shard_map/ppermute | solution.py:43
  53.2 1.7 %collective-permute-start.4 = (f32[8,8,1024]{2,1,0:T(8,128)S(1)}, f32[8,8,1024]{2,1,0:T(8,128)S(1)}, u32[]{:S(2)}, u32[]{:S(2)}) collective-permute-start(f32[8,8,1024]{2,1,0:T(8,128)S(1)} %dynamic-slice_bitcast_fusion), channel_id=1, source_target_pairs={{0,1},{1,0},{2,3},{3,2},{4,5},{5,4},{6,7},{7,6},{8,9},{9,8},{10,11... | collective-permute-start | bytes 786440 | tf_op jit(solution)/shard_map/ppermute | solution.py:43
  55.6 11.1 %all-to-all-start.2 = ((bf16[8,8,1024]{2,1,0:T(8,128)(2,1)}), bf16[8,8,1024]{2,1,0:T(8,128)(2,1)S(1)}, u32[]{:S(2)}, u32[]{:S(2)}) async-start(bf16[8,8,1024]{2,1,0:T(8,128)(2,1)} %fusion), calls=%async_computation.2 | async-start | bytes 262144 | tf_op jit(solution)/shard_map/all_to_all | solution.py:415
  66.8 1.2 %collective-permute-start.5 = (bf16[8,1024]{1,0:T(8,128)(2,1)S(1)}, bf16[8,1024]{1,0:T(8,128)(2,1)S(1)}, u32[]{:S(2)}, u32[]{:S(2)}) collective-permute-start(bf16[8,1024]{1,0:T(8,128)(2,1)S(1)} %add_convert_fusion), channel_id=1, source_target_pairs={{0,1},{1,0},{2,3},{3,2},{4,5},{5,4},{6,7},{7,6},{8,9},{9,8},{10,11... | collective-permute-start | bytes 49160 | tf_op jit(solution)/shard_map/ppermute | solution.py:43

commit v5 on v4

v5 whole, which is shorter than its diff:
```python
import functools

import jax
import jax.numpy as jnp
from jax import lax
from jax.experimental import pallas as pl
from jax.experimental.pallas import tpu as pltpu
from jax.sharding import PartitionSpec as P


DH = 128
P_SLOT = 16


eps = 1e-06


def norm_rows(states, gain):
    wide = states.astype(jnp.float32)
    factor = lax.rsqrt(jnp.mean(wide * wide, axis=-1, keepdims=True) + eps)
    return wide * factor * gain


def key_mask(token_index, passage_lengths, passage_owner, answer_lengths, answer_count):
    passage = token_index // P_SLOT
    place = token_index % P_SLOT
    count = passage_lengths.shape[0]
    match = passage[:, None] == jnp.arange(count, dtype=jnp.int32)[None, :]
    token_length = jnp.sum(jnp.where(match, passage_lengths[None, :], 0), axis=1)
    token_owner = jnp.sum(jnp.where(match, passage_owner[None, :], 0), axis=1)
    number = answer_lengths.shape[0]
    order = jnp.arange(number, dtype=jnp.int32)
    ends = jnp.sum(jnp.where(order[:, None] <= order[None, :], answer_lengths[:, None], 0), axis=0)
    answer_index = jnp.arange(answer_count, dtype=jnp.int32)
    question = jnp.sum((answer_index[:, None] >= ends[None, :]).astype(jnp.int32), axis=1)
    return (place < token_length)[None, :] & (token_owner[None, :] == question[:, None])


def swap_psg(x):
    return lax.ppermute(x, "psg", [(0, 1), (1, 0)])


BF16 = jnp.bfloat16
F32 = jnp.float32
SMEM_SPEC = pl.BlockSpec(memory_space=pltpu.SMEM)
VMEM_SPEC = pl.BlockSpec(memory_space=pltpu.VMEM)
HBM_SPEC = pl.BlockSpec(memory_space=pltpu.HBM)


def limit(mib):
    return pltpu.CompilerParams(vmem_limit_bytes=mib << 20)


def ask_kernel(half, states, gain, w_query, query, scr, sems):
    inner = query.shape[1]
    size = scr.shape[2]
    start = pl.multiple_of(half[0] * inner, 128)
    copies = [
        pltpu.make_async_copy(
            w_query.at[:, pl.ds(pl.multiple_of(start + c * size, 128), size)],
            scr.at[c],
            sems.at[c],
        )
        for c in range(inner // size)
    ]
    for copy in copies:
        copy.start()
    normed = norm_rows(states[...], gain[...]).astype(BF16)
    for c in range(inner // size):
        copies[c].wait()
        query[:, pl.ds(c * size, size)] = jnp.dot(
            normed, scr[c], preferred_element_type=F32
        ).astype(BF16)


def ask(half, states, gain, w_query, inner):
    count, width = states.shape
    size = min(256, inner)
    return pl.pallas_call(
        ask_kernel,
        out_shape=jax.ShapeDtypeStruct((count, inner), BF16),
        in_specs=[SMEM_SPEC, VMEM_SPEC, VMEM_SPEC, HBM_SPEC],
        out_specs=VMEM_SPEC,
        scratch_shapes=[
            pltpu.VMEM((inner // size, width, size), BF16),
            pltpu.SemaphoreType.DMA((inner // size,)),
        ],
        compiler_params=limit(52),
        cost_estimate=pl.CostEstimate(
            flops=1 << 30, bytes_accessed=2 * width * inner, transcendentals=0
        ),
        name="ask",
    )(half, states, gain.reshape(1, width), w_query)


def prepare_kernel(half, w_keyval, first_key, last_key, w_value, scr, sems):
    inner = w_value.shape[1]
    blocks = scr.shape[0]
    start = pl.multiple_of(half[0] * inner, 128)
    copies = [
        pltpu.make_async_copy(
            w_keyval.at[pl.ds(b * 128, 128), :, pl.ds(start, inner)], scr.at[b], sems.at[b]
        )
        for b in range(blocks)
    ]
    for copy in copies:
        copy.start()
    row = lax.broadcasted_iota(jnp.int32, (256, 256), 0)
    column = lax.broadcasted_iota(jnp.int32, (256, 256), 1)
    source = jnp.where(row < 128, 2 * row, 2 * (row - 128) + 1)
    pick = jnp.where(column == source, 1.0, 0.0).astype(BF16)
    for b in range(blocks):
        rows = pl.ds(b * 128, 128)
        copies[b].wait()
        for s in range(0, inner, 128):
            mixed = scr[b, :, :, pl.ds(s, 128)].reshape(256, 128)
            apart = jnp.dot(pick, mixed, preferred_element_type=F32).astype(BF16)
            if s < inner // 2:
                first_key[rows, pl.ds(s, 128)] = apart[:128]
            else:
                last_key[rows, pl.ds(s - inner // 2, 128)] = apart[:128]
            w_value[rows, pl.ds(s, 128)] = apart[128:]


def prepare(half, w_keyval, inner):
    width = w_keyval.shape[0]
    return pl.pallas_call(
        prepare_kernel,
        out_shape=(
            jax.ShapeDtypeStruct((width, inner // 2), BF16),
            jax.ShapeDtypeStruct((width, inner // 2), BF16),
            jax.ShapeDtypeStruct((width, inner), BF16),
        ),
        in_specs=[SMEM_SPEC, HBM_SPEC],
        out_specs=(VMEM_SPEC,) * 3,
        scratch_shapes=[
            pltpu.VMEM((width // 128, 128, 2, inner), BF16),
            pltpu.SemaphoreType.DMA((width // 128,)),
        ],
        compiler_params=limit(51),
        cost_estimate=pl.CostEstimate(
            flops=4 * width * 256 * inner, bytes_accessed=8 * width * inner, transcendentals=0
        ),
        name="prepare",
    )(half, w_keyval)


def stage_kernel(after, whole, out, sems, *, axis, start):
    del after
    size = out.shape[axis]
    number = sems.shape[0]
    step = size // number
    copies = []
    for k in range(number):
        if axis == 0:
            source = whole.at[pl.ds(start + k * step, step)]
            target = out.at[pl.ds(k * step, step)]
        else:
            source = whole.at[:, pl.ds(start + k * step, step)]
            target = out.at[:, pl.ds(k * step, step)]
        copies.append(pltpu.make_async_copy(source, target, sems.at[k]))
    for copy in copies:
        copy.start()
    for copy in copies:
        copy.wait()


def stage(after, whole, axis, part, parts):
    shape = list(whole.shape)
    shape[axis] //= parts
    return pl.pallas_call(
        functools.partial(stage_kernel, axis=axis, start=part * shape[axis]),
        out_shape=jax.ShapeDtypeStruct(tuple(shape), BF16),
        in_specs=[SMEM_SPEC, HBM_SPEC],
        out_specs=VMEM_SPEC,
        scratch_shapes=[pltpu.SemaphoreType.DMA((4,))],
        compiler_params=limit(44),
        cost_estimate=pl.CostEstimate(
            flops=1 << 30, bytes_accessed=4 * shape[0] * shape[1], transcendentals=0
        ),
        name="stage",
    )(after, whole)


def feed_kernel(index, mine, theirs, gain, first_in, last_in, first_out, w_out, out, normed, hidden, last_out, sems, *, patterns):
    pairs, rows, width = mine.shape
    units = first_in.shape[1]
    number = sems.shape[0]
    step = width // number
    copies = [
        pltpu.make_async_copy(
            w_out.at[pl.ds(units, units), pl.ds(k * step, step)],
            last_out.at[:, pl.ds(k * step, step)],
            sems.at[k],
        )
        for k in range(number)
    ]
    for copy in copies:
        copy.start()
    size = min(256, units)
    weight = gain[...]
    for k in range(2 * pairs):
        place = pl.multiple_of((index[0] ^ patterns[k]) * rows, rows)
        states = mine[k] if k < pairs else theirs[k - pairs]
        normed[pl.ds(place, rows)] = norm_rows(states, weight).astype(BF16)
    for part, w_in in enumerate((first_in, last_in)):
        for c in range(units // size):
            columns = pl.ds(c * size, size)
            hidden[part, :, columns] = jnp.maximum(
                jnp.dot(normed[...], w_in[:, columns], preferred_element_type=F32), 0.0
            ).astype(BF16)
    for c in range(number):
        columns = pl.ds(c * step, step)
        total = jnp.dot(hidden[0], first_out[:, columns], preferred_element_type=F32)
        copies[c].wait()
        total = total + jnp.dot(hidden[1], last_out[:, columns], preferred_element_type=F32)
        out[:, columns] = total.astype(BF16)


def feed(index, mine, theirs, gain, first_in, last_in, first_out, w_out, patterns):
    pairs, rows, width = mine.shape
    count = 2 * pairs * rows
    units = first_in.shape[1]
    return pl.pallas_call(
        functools.partial(feed_kernel, patterns=patterns),
        out_shape=jax.ShapeDtypeStruct((count, width), BF16),
        in_specs=[SMEM_SPEC] + [VMEM_SPEC] * 6 + [HBM_SPEC],
        out_specs=VMEM_SPEC,
        scratch_shapes=[
            pltpu.VMEM((count, width), BF16),
            pltpu.VMEM((2, count, units), BF16),
            pltpu.VMEM((units, width), BF16),
            pltpu.SemaphoreType.DMA((width // 256,)),
        ],
        compiler_params=limit(37),
        cost_estimate=pl.CostEstimate(
            flops=8 * count * width * units, bytes_accessed=8 * width * units, transcendentals=0
        ),
        name="feed",
    )(index, mine, theirs, gain.reshape(1, width), first_in, last_in, first_out, w_out)


def settle_kernel(parts, tokens, gain, encoded, spread):
    total = tokens[...].astype(F32)
    for k in range(parts.shape[0]):
        total = total + parts[k].astype(F32)
    rounded = total.astype(BF16)
    encoded[...] = rounded
    memory = norm_rows(rounded, gain[...]).astype(BF16)
    for k in range(spread.shape[0]):
        spread[k] = memory


def settle(parts, tokens, gain):
    count, rows, width = parts.shape
    return pl.pallas_call(
        settle_kernel,
        out_shape=(
            jax.ShapeDtypeStruct((rows, width), BF16),
            jax.ShapeDtypeStruct((count, rows, width), BF16),
        ),
        in_specs=[VMEM_SPEC] * 3,
        out_specs=(VMEM_SPEC, VMEM_SPEC),
        compiler_params=limit(8),
        name="settle",
    )(parts, tokens, gain.reshape(1, width))


def project_kernel(half, mine, first_key, last_key, value, w_out, keys, values, first_value, last_value, w_last, sems):
    inner = keys.shape[1]
    part = inner // 2
    start = pl.multiple_of(half[0] * inner, 128)
    copies = [
        pltpu.make_async_copy(value.at[:, pl.ds(0, part)], first_value, sems.at[0]),
        pltpu.make_async_copy(value.at[:, pl.ds(part, part)], last_value, sems.at[1]),
    ]
    last = pltpu.make_async_copy(w_out.at[pl.ds(start, inner)], w_last, sems.at[2])
    for copy in copies:
        copy.start()
    last.start()
    size = min(256, part)
    for k, w_key in enumerate((first_key, last_key)):
        for c in range(part // size):
            keys[:, pl.ds(k * part + c * size, size)] = jnp.dot(
                mine[...], w_key[:, pl.ds(c * size, size)], preferred_element_type=F32
            ).astype(BF16)
    for k, w_value in enumerate((first_value, last_value)):
        copies[k].wait()
        for c in range(part // size):
            values[:, pl.ds(k * part + c * size, size)] = jnp.dot(
                mine[...], w_value[:, pl.ds(c * size, size)], preferred_element_type=F32
            ).astype(BF16)
    last.wait()


def project(half, mine, first_key, last_key, value, w_attn_out):
    rows, width = mine.shape
    inner = value.shape[1]
    return pl.pallas_call(
        project_kernel,
        out_shape=(
            jax.ShapeDtypeStruct((rows, inner), BF16),
            jax.ShapeDtypeStruct((rows, inner), BF16),
            jax.ShapeDtypeStruct((width, inner // 2), BF16),
            jax.ShapeDtypeStruct((width, inner // 2), BF16),
            jax.ShapeDtypeStruct((inner, width), BF16),
        ),
        in_specs=[SMEM_SPEC] + [VMEM_SPEC] * 3 + [HBM_SPEC, HBM_SPEC],
        out_specs=(VMEM_SPEC,) * 5,
        scratch_shapes=[pltpu.SemaphoreType.DMA((3,))],
        compiler_params=limit(46),
        cost_estimate=pl.CostEstimate(
            flops=4 * rows * width * inner, bytes_accessed=6 * width * inner, transcendentals=0
        ),
        name="project",
    )(half, mine, first_key, last_key, value, w_attn_out)


def attend_kernel(near_keys, near_values, theirs, query, allowed, first_key, last_key, first_value, last_value, w_last, out, context):
    rows, inner = near_keys.shape
    width = out.shape[1]
    part = inner // 2
    size = min(256, part)
    near = allowed[:, :rows] > 0
    far = allowed[:, rows:] > 0
    for c in range(inner // size):
        columns = pl.ds(c * size, size)
        w_key = first_key if c * size < part else last_key
        w_value = first_value if c * size < part else last_value
        local = pl.ds(c * size % part, size)
        far_keys = jnp.dot(theirs[...], w_key[:, local], preferred_element_type=F32).astype(BF16)
        far_values = jnp.dot(
            theirs[...], w_value[:, local], preferred_element_type=F32
        ).astype(BF16)
        keys = jnp.concatenate([near_keys[:, columns], far_keys], axis=0)
        values = jnp.concatenate([near_values[:, columns], far_values], axis=0)
        for h in range(size // DH):
            lanes = slice(h * DH, (h + 1) * DH)
            place = pl.ds(c * size + h * DH, DH)
            scores = lax.dot_general(
                query[:, place],
                keys[:, lanes],
                (((1,), (1,)), ((), ())),
                preferred_element_type=F32,
            ) * DH ** (-0.5)
            near_scores = jnp.where(near, scores[:, :rows], -1e30)
            far_scores = jnp.where(far, scores[:, rows:], -1e30)
            top = jnp.max(jnp.maximum(near_scores, far_scores), axis=1, keepdims=True)
            near_weights = jnp.where(near, jnp.exp(near_scores - top), 0.0)
            far_weights = jnp.where(far, jnp.exp(far_scores - top), 0.0)
            total = jnp.sum(near_weights + far_weights, axis=1, keepdims=True)
            weights = jnp.concatenate([near_weights, far_weights], axis=1).astype(BF16)
            summed = jnp.dot(weights, values[:, lanes], preferred_element_type=F32)
            context[:, place] = (summed * (1.0 / total)).astype(BF16)
    for c in range(width // 256):
        columns = pl.ds(c * 256, 256)
        out[:, columns] = jnp.dot(context[...], w_last[:, columns], preferred_element_type=F32)


def attend(near_keys, near_values, theirs, query, allowed, weights, w_last):
    rows, width = theirs.shape
    count, inner = query.shape
    return pl.pallas_call(
        attend_kernel,
        out_shape=jax.ShapeDtypeStruct((count, width), F32),
        in_specs=[VMEM_SPEC] * 10,
        out_specs=VMEM_SPEC,
        scratch_shapes=[pltpu.VMEM((count, inner), BF16)],
        compiler_params=limit(24),
        cost_estimate=pl.CostEstimate(
            flops=4 * rows * width * inner + 8 * count * rows * inner + 2 * count * inner * width,
            bytes_accessed=6 * width * inner,
            transcendentals=2 * count * rows * inner // DH,
        ),
        name="attend",
    )(near_keys, near_values, theirs, query, allowed, *weights, w_last)


def per_device(
    tokens,
    enc_gain,
    w_in,
    w_out,
    final_gain,
    w_keyval,
    answer_states,
    dec_gain,
    w_query,
    w_attn_out,
    passage_lengths,
    passage_owner,
    answer_lengths,
):
    row_count = tokens.shape[0]
    width = tokens.shape[1]
    answer_count = answer_states.shape[0]
    mp = lax.axis_size("mp")
    psg = lax.axis_size("psg")
    mp_index = lax.axis_index("mp")
    psg_index = lax.axis_index("psg")
    heads = w_query.shape[1] // DH // psg
    inner = heads * DH

    half = jnp.reshape(psg_index, (1,)).astype(jnp.int32)
    index = jnp.reshape(mp_index, (1,)).astype(jnp.int32)
    patterns = [0]
    held = tokens[None]
    step = mp // 2
    while step > 0:
        got = lax.ppermute(held, "mp", [(j, j ^ step) for j in range(mp)])
        patterns = patterns + [p ^ step for p in patterns]
        if step > 1:
            held = jnp.concatenate([held, got], axis=0)
        step //= 2
    first_in = stage(index, w_in, 1, 0, 2)
    last_in = stage(index, w_in, 1, 1, 2)
    first_out = stage(index, w_out, 0, 0, 2)
    query = ask(half, answer_states, dec_gain, w_query, inner)
    first_key, last_key, value = prepare(half, w_keyval, inner)
    partial_sums = feed(index, held, got, enc_gain, first_in, last_in, first_out, w_out, patterns)
    parts = lax.all_to_all(partial_sums.reshape(mp, row_count, width), "mp", 0, 0)
    encoded, spread = settle(parts, tokens, final_gain)
    mine = lax.all_to_all(spread, "mp", 0, 0)
    mine = mine.reshape(mp * row_count, width)
    theirs = swap_psg(mine)
    key_rows = 2 * mp * row_count

    local = jnp.arange(key_rows, dtype=jnp.int32)
    far = local // (mp * row_count)
    block = (local % (mp * row_count)) // row_count
    core = jnp.where(far == 0, psg_index, 1 - psg_index)
    token_index = (block * psg + core) * row_count + local % row_count
    allowed = key_mask(token_index, passage_lengths, passage_owner, answer_lengths, answer_count)
    near_keys, near_values, first_value, last_value, w_last = project(
        half, mine, first_key, last_key, value, w_attn_out
    )
    partial_answer = attend(
        near_keys,
        near_values,
        theirs,
        query,
        allowed.astype(jnp.int32),
        (first_key, last_key, first_value, last_value),
        w_last,
    )

    out_count = answer_count // mp
    small = out_count // psg
    halves = partial_answer.reshape(mp, psg, small, width)
    keep = lax.dynamic_index_in_dim(halves, psg_index, 1, False)
    give = lax.dynamic_index_in_dim(halves, 1 - psg_index, 1, False)
    chip_sum = (keep + swap_psg(give)).astype(jnp.bfloat16)
    answer_parts = lax.all_to_all(chip_sum, "mp", 0, 0)
    own_start = mp_index * out_count + psg_index * small
    own_answer = lax.dynamic_slice_in_dim(answer_states, own_start, small, 0).astype(jnp.float32)
    piece = (own_answer + jnp.sum(answer_parts.astype(jnp.float32), axis=0)).astype(jnp.bfloat16)
    other = swap_psg(piece)
    first = jnp.where(psg_index == 0, piece, other)
    second = jnp.where(psg_index == 0, other, piece)
    return (encoded, jnp.concatenate([first, second], axis=0))


def solution(mesh):
    placed = (
        P(("groups", "mp", "psg"), None),
        P(),
        P(None, "mp"),
        P("mp", None),
        P(),
        P(None, None, "mp"),
        P("groups", None),
        P(),
        P(None, "mp"),
        P("mp", None),
        P("groups"),
        P("groups"),
        P("groups"),
    )
    return jax.shard_map(
        per_device,
        mesh=mesh,
        in_specs=placed,
        out_specs=(P(("groups", "mp", "psg"), None), P(("groups", "mp"), None)),
        check_vma=False,
    )
```

time: 69.1 us -> 71.6 us (1.036)
  Pallas kernels: 24.8 us -> 26.5 us
  other arithmetic: 1.74 us -> 2.5 us
    pallas_call x1, Pallas kernels: 3.17 us -> 5.83 us  [feed(): pl.pallas_call(functools.partial(feed_kernel, patterns=patterns), out_sha...]
    ppermute x3, waiting for transfers between devices: 0.68 us -> 2.92 us  [per_device(): got = lax.ppermute(held, 'mp', [(j, j ^ step) for j in range(mp)])]
    all_to_all x1, waiting for transfers between devices: 8 us -> 5.77 us  [per_device(): mine = lax.all_to_all(spread, 'mp', 0, 0)]
    pallas_call x4 -> x3, Pallas kernels: 8.88 us -> 6.68 us  [stage(): pl.pallas_call(functools.partial(stage_kernel, axis=axis, start=part * sh...]
    pallas_call x1 -> x2, Pallas kernels: 7.22 us -> 8.81 us  [the longest x1 6.58 us: prepare(): pl.pallas_call(prepare_kernel, out_shape=(jax.ShapeDtypeStruct((width, in...]
    concatenate x2, other arithmetic: 0.02 us -> 0.78 us  [per_device(): held = jnp.concatenate([held, got], axis=0)]
  transfers between devices with their start and end apart: 9 -> 9, of which waited for: 7 -> 7; matrix products, arithmetic and copies ran while one was open for 1% -> 1% of each run, Pallas kernels for 27% -> 25%
where the time goes in v5:
time: 71.6 us; the launch traced here: 71.1 us
  Pallas kernels  26.5 us (37%)
  starting transfers between devices  20.9 us (29%)
  waiting for transfers between devices  20.2 us (28%)
  other arithmetic  2.5 us (3%)
  between operations  0.86 us (1%)
    all_to_all x1, waiting for transfers between devices, per_device(): answer_parts = lax.all_to_all(chip_sum, 'mp', 0, 0)  7.73 us
    ppermute x3, starting transfers between devices, per_device(): got = lax.ppermute(held, 'mp', [(j, j ^ step) for j in range(mp)])  7.47 us
    pallas_call x3, Pallas kernels, stage(): pl.pallas_call(functools.partial(stage_kernel, axis=axis, start=part * sh...  6.68 us
    pallas_call x1, Pallas kernels, prepare(): pl.pallas_call(prepare_kernel, out_shape=(jax.ShapeDtypeStruct((width, in...  6.58 us
    pallas_call x1, Pallas kernels, feed(): pl.pallas_call(functools.partial(feed_kernel, patterns=patterns), out_sha...  5.83 us
    all_to_all x1, waiting for transfers between devices, per_device(): mine = lax.all_to_all(spread, 'mp', 0, 0)  5.77 us
    all_to_all x1, starting transfers between devices, per_device(): lax.all_to_all(partial_sums.reshape(mp, row_count, width), 'mp', 0, 0)  4.9 us
    all_to_all x1, starting transfers between devices, per_device(): mine = lax.all_to_all(spread, 'mp', 0, 0)  4.54 us
  transfers between devices with their start and end apart: 9, of which 7 were waited for; matrix products, arithmetic and copies ran while one was open for 1% of the time, Pallas kernels for 25%

profile of v5, /device:TPU:0, one launch (start us, length us, event | category | flops | bytes accessed | tf_op | source)
XLA Modules:
  0.0 71.1 jit_solution(4246384530840624354)
XLA Ops:
  0.6 4.1 %collective-permute-start = (bf16[1,16,1024]{2,1,0:T(8,128)(2,1)}, bf16[1,16,1024]{2,1,0:T(8,128)(2,1)S(1)}, u32[]{:S(2)}, u32[]{:S(2)}) collective-permute-start(bf16[1,16,1024]{2,1,0:T(8,128)(2,1)} %bitcast.19), channel_id=1, source_target_pairs={{0,8},{2,10},{4,12},{6,14},{8,0},{10,2},{12,4},{14,6},{1,9},{3,11}... | collective-permute-start | bytes 98312 | tf_op jit(solution)/shard_map/ppermute | solution.py:410
  4.8 2.5 %collective-permute-done = bf16[1,16,1024]{2,1,0:T(8,128)(2,1)S(1)} collective-permute-done((bf16[1,16,1024]{2,1,0:T(8,128)(2,1)}, bf16[1,16,1024]{2,1,0:T(8,128)(2,1)S(1)}, u32[]{:S(2)}, u32[]{:S(2)}) %collective-permute-start) | collective-permute-done | bytes 32800 | tf_op jit(solution)/shard_map/ppermute | solution.py:410
  7.2 0.8 %pad_maximum_fusion.1 = bf16[2,16,1024]{2,1,0:T(8,128)(2,1)S(1)} fusion(bf16[1,16,1024]{2,1,0:T(8,128)(2,1)S(1)} %collective-permute-done, bf16[1,16,1024]{2,1,0:T(8,128)(2,1)} %bitcast.20), kind=kLoop, calls=%fused_computation.6 | loop fusion | flops 32768 | bytes 131072 | tf_op jit(solution)/shard_map/concatenate | solution.py:413
  8.0 1.6 %collective-permute-start.1 = (bf16[2,16,1024]{2,1,0:T(8,128)(2,1)S(1)}, bf16[2,16,1024]{2,1,0:T(8,128)(2,1)S(1)}, u32[]{:S(2)}, u32[]{:S(2)}) collective-permute-start(bf16[2,16,1024]{2,1,0:T(8,128)(2,1)S(1)} %pad_maximum_fusion.1), channel_id=1, source_target_pairs={{0,4},{2,6},{4,0},{6,2},{8,12},{10,14},{12,8},{14,10},{1,5},{3,7},... | collective-permute-start | bytes 196616 | tf_op jit(solution)/shard_map/ppermute | solution.py:410
  9.5 0.0 copy-start.1
  9.5 2.2 %stage.3.first_in = bf16[1024,2048]{1,0:T(8,128)(2,1)S(1)} custom-call(s32[1]{0:T(128)} %bitcast.after.index, bf16[1024,4096]{1,0:T(8,128)(2,1)} %whole.4), custom_call_target="tpu_custom_call" | custom-call | flops 1073741824 | bytes 8388608 | tf_op jit(solution)/shard_map/stage/pallas_call | solution.py:171
  11.8 0.5 collective-permute-done.1
  12.2 0.0 copy-done.1
  12.3 1.8 %collective-permute-start.2 = (bf16[4,16,1024]{2,1,0:T(8,128)(2,1)S(1)}, bf16[4,16,1024]{2,1,0:T(8,128)(2,1)S(1)}, u32[]{:S(2)}, u32[]{:S(2)}) collective-permute-start(bf16[4,16,1024]{2,1,0:T(8,128)(2,1)S(1)} %pad_maximum_fusion.mine), channel_id=1, source_target_pairs={{0,2},{2,0},{4,6},{6,4},{8,10},{10,8},{12,14},{14,12},{1,3},{3,1},... | collective-permute-start | bytes 393224 | tf_op jit(solution)/shard_map/ppermute | solution.py:410
  14.1 2.2 %stage.4.last_in = bf16[1024,2048]{1,0:T(8,128)(2,1)S(1)} custom-call(s32[1]{0:T(128)} %bitcast.after.index, bf16[1024,4096]{1,0:T(8,128)(2,1)} %whole.4), custom_call_target="tpu_custom_call" | custom-call | flops 1073741824 | bytes 8388608 | tf_op jit(solution)/shard_map/stage/pallas_call | solution.py:171
  16.3 0.0 copy-start.2
  16.3 2.2 %stage.5.first_out = bf16[2048,1024]{1,0:T(8,128)(2,1)S(1)} custom-call(s32[1]{0:T(128)} %bitcast.after.index, bf16[4096,1024]{1,0:T(8,128)(2,1)} %w_out.2), custom_call_target="tpu_custom_call" | custom-call | flops 1073741824 | bytes 8388608 | tf_op jit(solution)/shard_map/stage/pallas_call | solution.py:171
  18.5 0.0 collective-permute-done.2.theirs
  18.5 0.0 copy-done.2
  18.6 5.8 %feed.1 = bf16[128,1024]{1,0:T(8,128)(2,1)} custom-call(s32[1]{0:T(128)} %bitcast.after.index, bf16[4,16,1024]{2,1,0:T(8,128)(2,1)S(1)} %pad_maximum_fusion.mine, bf16[4,16,1024]{2,1,0:T(8,128)(2,1)S(1)} %collective-permute-done.2.theirs, f32[1,1024]{1,0:T(1,128)S(1)} %bitcast.22, bf16[1024,2048]{1,0:T(8,128)(2,1)S(1)} %stage.3.first_in, ...), custom_call_target="tpu_custom_call" | custom-call | flops 2147483648 | bytes 16777216 | tf_op jit(solution)/shard_map/feed/pallas_call | solution.py:224
  24.4 4.9 %all-to-all-start = ((bf16[8,16,1024]{2,1,0:T(8,128)(2,1)}), bf16[8,16,1024]{2,1,0:T(8,128)(2,1)S(1)}, u32[]{:S(2)}, u32[]{:S(2)}) async-start(bf16[8,16,1024]{2,1,0:T(8,128)(2,1)} %bitcast.3), calls=%async_computation | async-start | bytes 524288 | tf_op jit(solution)/shard_map/all_to_all | solution.py:421
  29.3 0.0 copy-start.7
  29.3 0.0 copy-start.3
  29.3 0.0 copy-start
  29.3 0.0 copy-start.4
  29.3 6.6 %prepare.1 = (bf16[1024,512]{1,0:T(8,128)(2,1)S(1)}, bf16[1024,512]{1,0:T(8,128)(2,1)S(1)}, bf16[1024,1024]{1,0:T(8,128)(2,1)}) custom-call(s32[1]{0:T(128)} %bitcast.5.half, bf16[1024,2,2048]{2,1,0:T(2,128)(2,1)} %w_keyval.1), custom_call_target="tpu_custom_call" | custom-call | flops 1073741824 | bytes 8388608 | tf_op jit(solution)/shard_map/prepare/pallas_call | solution.py:127
  35.9 0.0 copy-start.5
  35.9 0.0 copy-start.6
  36.0 0.0 copy-done.7
  36.0 0.1 select_reduce_fusion.2
  36.1 1.4 %all-to-all-done.parts = bf16[8,16,1024]{2,1,0:T(8,128)(2,1)S(1)} async-done(((bf16[8,16,1024]{2,1,0:T(8,128)(2,1)}), bf16[8,16,1024]{2,1,0:T(8,128)(2,1)S(1)}, u32[]{:S(2)}, u32[]{:S(2)}) %all-to-all-start) | async-done | bytes 262176 | tf_op jit(solution)/shard_map/all_to_all | solution.py:421
  37.5 0.0 copy-done.3
  37.5 0.9 %settle.1 = (bf16[16,1024]{1,0:T(8,128)(2,1)}, bf16[8,16,1024]{2,1,0:T(8,128)(2,1)}) custom-call(bf16[8,16,1024]{2,1,0:T(8,128)(2,1)S(1)} %all-to-all-done.parts, bf16[16,1024]{1,0:T(8,128)(2,1)S(1)} %copy-done.1, f32[1,1024]{1,0:T(1,128)S(1)} %bitcast.23), custom_call_target="tpu_custom_call" | custom-call | tf_op jit(solution)/shard_map/settle/pallas_call | solution.py:256
  38.4 4.5 %all-to-all-start.1 = ((bf16[8,16,1024]{2,1,0:T(8,128)(2,1)}), bf16[8,16,1024]{2,1,0:T(8,128)(2,1)S(1)}, u32[]{:S(2)}, u32[]{:S(2)}) async-start(bf16[8,16,1024]{2,1,0:T(8,128)(2,1)} %get-tuple-element.13), calls=%async_computation.1 | async-start | bytes 524288 | tf_op jit(solution)/shard_map/all_to_all | solution.py:423
  42.9 0.0 copy-done
  42.9 0.0 copy-done.4
  42.9 2.2 %ask.1.query = bf16[128,1024]{1,0:T(8,128)(2,1)S(1)} custom-call(s32[1]{0:T(128)} %bitcast.5.half, bf16[128,1024]{1,0:T(8,128)(2,1)S(1)} %copy-done, f32[1,1024]{1,0:T(1,128)S(1)} %bitcast.24, bf16[1024,2048]{1,0:T(8,128)(2,1)} %w_query.1), custom_call_target="tpu_custom_call" | custom-call | flops 1073741824 | bytes 2097152 | tf_op jit(solution)/shard_map/ask/pallas_call | solution.py:79
  45.2 0.1 convert_reduce_fusion.1
  45.2 0.0 copy-done.5
  45.2 0.0 copy-done.6
  45.2 0.1 select_reduce_fusion.1
  45.4 5.8 %all-to-all-done.1 = bf16[8,16,1024]{2,1,0:T(8,128)(2,1)S(1)} async-done(((bf16[8,16,1024]{2,1,0:T(8,128)(2,1)}), bf16[8,16,1024]{2,1,0:T(8,128)(2,1)S(1)}, u32[]{:S(2)}, u32[]{:S(2)}) %all-to-all-start.1) | async-done | bytes 262176 | tf_op jit(solution)/shard_map/all_to_all | solution.py:423
  51.1 0.0 collective-permute-start.3
  51.1 0.1 and_convert_fusion.allowed
  51.2 2.3 %project.1 = (bf16[128,1024]{1,0:T(8,128)(2,1)S(1)}, bf16[128,1024]{1,0:T(8,128)(2,1)S(1)}, bf16[1024,512]{1,0:T(8,128)(2,1)S(1)}, bf16[1024,512]{1,0:T(8,128)(2,1)S(1)}, bf16[1024,1024]{1,0:T(8,128)(2,1)S(1)}) custom-call(s32[1]{0:T(128)} %bitcast.5.half, bf16[128,1024]{1,0:T(8,128)(2,1)S(1)} %bitcast.18, ...), custom_call_target="tpu_custom_call" | custom-call | flops 536870912 | bytes 6291456 | tf_op jit(solution)/shard_map/project/pallas_call | solution.py:299
  53.5 0.0 collective-permute-done.3.theirs
  53.5 2.1 %attend.1 = f32[128,1024]{1,0:T(8,128)S(1)} custom-call(bf16[128,1024]{1,0:T(8,128)(2,1)S(1)} %get-tuple-element.17.near_keys, bf16[128,1024]{1,0:T(8,128)(2,1)S(1)} %get-tuple-element.18.near_values, bf16[128,1024]{1,0:T(8,128)(2,1)S(1)} %collective-permute-done.3.theirs, bf16[128,1024]{1,0:T(8,128)(2,1)S(1)} %ask.1.query, ...), custom_call_target="tpu_custom_call" | custom-call | flops 939524096 | bytes 6291456 | tf_op jit(solution)/shard_map/attend/pallas_call | solution.py:363
  55.6 0.6 collective-permute-start.4
  56.2 1.2 %collective-permute-done.4 = f32[8,8,1024]{2,1,0:T(8,128)S(1)} collective-permute-done((f32[8,8,1024]{2,1,0:T(8,128)S(1)}, f32[8,8,1024]{2,1,0:T(8,128)S(1)}, u32[]{:S(2)}, u32[]{:S(2)}) %collective-permute-start.4) | collective-permute-done | bytes 262176 | tf_op jit(solution)/shard_map/ppermute | solution.py:40
  57.4 0.7 fusion
  58.0 3.4 %all-to-all-start.2 = ((bf16[8,8,1024]{2,1,0:T(8,128)(2,1)}), bf16[8,8,1024]{2,1,0:T(8,128)(2,1)S(1)}, u32[]{:S(2)}, u32[]{:S(2)}) async-start(bf16[8,8,1024]{2,1,0:T(8,128)(2,1)} %fusion), calls=%async_computation.2 | async-start | bytes 262144 | tf_op jit(solution)/shard_map/all_to_all | solution.py:453
  61.4 7.7 %all-to-all-done.2 = bf16[8,8,1024]{2,1,0:T(8,128)(2,1)S(1)} async-done(((bf16[8,8,1024]{2,1,0:T(8,128)(2,1)}), bf16[8,8,1024]{2,1,0:T(8,128)(2,1)S(1)}, u32[]{:S(2)}, u32[]{:S(2)}) %all-to-all-start.2) | async-done | bytes 131104 | tf_op jit(solution)/shard_map/all_to_all | solution.py:453
  69.2 0.1 collective-permute-start.5
  69.3 1.2 %collective-permute-done.5 = bf16[8,1024]{1,0:T(8,128)(2,1)S(1)} collective-permute-done((bf16[8,1024]{1,0:T(8,128)(2,1)S(1)}, bf16[8,1024]{1,0:T(8,128)(2,1)S(1)}, u32[]{:S(2)}, u32[]{:S(2)}) %collective-permute-start.5) | collective-permute-done | bytes 16416 | tf_op jit(solution)/shard_map/ppermute | solution.py:40
  70.5 0.6 pad_maximum_fusion.2
  (7 shorter events, 0.1 us)
Async XLA Ops:
  0.6 6.6 %collective-permute-start = (bf16[1,16,1024]{2,1,0:T(8,128)(2,1)}, bf16[1,16,1024]{2,1,0:T(8,128)(2,1)S(1)}, u32[]{:S(2)}, u32[]{:S(2)}) collective-permute-start(bf16[1,16,1024]{2,1,0:T(8,128)(2,1)} %bitcast.19), channel_id=1, source_target_pairs={{0,8},{2,10},{4,12},{6,14},{8,0},{10,2},{12,4},{14,6},{1,9},{3,11}... | collective-permute-start | bytes 98312 | tf_op jit(solution)/shard_map/ppermute | solution.py:410
  8.0 4.3 %collective-permute-start.1 = (bf16[2,16,1024]{2,1,0:T(8,128)(2,1)S(1)}, bf16[2,16,1024]{2,1,0:T(8,128)(2,1)S(1)}, u32[]{:S(2)}, u32[]{:S(2)}) collective-permute-start(bf16[2,16,1024]{2,1,0:T(8,128)(2,1)S(1)} %pad_maximum_fusion.1), channel_id=1, source_target_pairs={{0,4},{2,6},{4,0},{6,2},{8,12},{10,14},{12,8},{14,10},{1,5},{3,7},... | collective-permute-start | bytes 196616 | tf_op jit(solution)/shard_map/ppermute | solution.py:410
  9.5 2.7 %copy-start.1 = (bf16[16,1024]{1,0:T(8,128)(2,1)S(1)}, bf16[16,1024]{1,0:T(8,128)(2,1)}, u32[]{:S(2)}) copy-start(bf16[16,1024]{1,0:T(8,128)(2,1)} %tokens.1) | copy-start | bytes 98308
  12.3 6.3 %collective-permute-start.2 = (bf16[4,16,1024]{2,1,0:T(8,128)(2,1)S(1)}, bf16[4,16,1024]{2,1,0:T(8,128)(2,1)S(1)}, u32[]{:S(2)}, u32[]{:S(2)}) collective-permute-start(bf16[4,16,1024]{2,1,0:T(8,128)(2,1)S(1)} %pad_maximum_fusion.mine), channel_id=1, source_target_pairs={{0,2},{2,0},{4,6},{6,4},{8,10},{10,8},{12,14},{14,12},{1,3},{3,1},... | collective-permute-start | bytes 393224 | tf_op jit(solution)/shard_map/ppermute | solution.py:410
  16.3 2.2 %copy-start.2 = (f32[1024]{0:T(1024)S(1)}, f32[1024]{0:T(1024)}, u32[]{:S(2)}) copy-start(f32[1024]{0:T(1024)} %param.14) | copy-start | bytes 12292
  24.4 13.1 %all-to-all-start = ((bf16[8,16,1024]{2,1,0:T(8,128)(2,1)}), bf16[8,16,1024]{2,1,0:T(8,128)(2,1)S(1)}, u32[]{:S(2)}, u32[]{:S(2)}) async-start(bf16[8,16,1024]{2,1,0:T(8,128)(2,1)} %bitcast.3), calls=%async_computation | async-start | bytes 524288 | tf_op jit(solution)/shard_map/all_to_all | solution.py:421
  29.3 6.7 %copy-start.7 = (s32[4]{0:T(128)S(1)}, s32[4]{0:T(128)}, u32[]{:S(2)}) copy-start(s32[4]{0:T(128)} %param.25) | copy-start | bytes 52
  29.3 8.2 %copy-start.3 = (f32[1024]{0:T(1024)S(1)}, f32[1024]{0:T(1024)}, u32[]{:S(2)}) copy-start(f32[1024]{0:T(1024)} %param.17) | copy-start | bytes 12292
  29.3 13.6 %copy-start = (bf16[128,1024]{1,0:T(8,128)(2,1)S(1)}, bf16[128,1024]{1,0:T(8,128)(2,1)}, u32[]{:S(2)}) copy-start(bf16[128,1024]{1,0:T(8,128)(2,1)} %states.1) | copy-start | bytes 786436
  29.3 13.6 %copy-start.4 = (f32[1024]{0:T(1024)S(1)}, f32[1024]{0:T(1024)}, u32[]{:S(2)}) copy-start(f32[1024]{0:T(1024)} %param.20) | copy-start | bytes 12292
  35.9 9.3 %copy-start.5 = (s32[16]{0:T(128)S(1)}, s32[16]{0:T(128)}, u32[]{:S(2)}) copy-start(s32[16]{0:T(128)} %param.23) | copy-start | bytes 196
  35.9 9.3 %copy-start.6 = (s32[16]{0:T(128)S(1)}, s32[16]{0:T(128)}, u32[]{:S(2)}) copy-start(s32[16]{0:T(128)} %param.24) | copy-start | bytes 196
  38.4 12.8 %all-to-all-start.1 = ((bf16[8,16,1024]{2,1,0:T(8,128)(2,1)}), bf16[8,16,1024]{2,1,0:T(8,128)(2,1)S(1)}, u32[]{:S(2)}, u32[]{:S(2)}) async-start(bf16[8,16,1024]{2,1,0:T(8,128)(2,1)} %get-tuple-element.13), calls=%async_computation.1 | async-start | bytes 524288 | tf_op jit(solution)/shard_map/all_to_all | solution.py:423
  51.1 2.4 %collective-permute-start.3 = (bf16[128,1024]{1,0:T(8,128)(2,1)S(1)}, bf16[128,1024]{1,0:T(8,128)(2,1)S(1)}, u32[]{:S(2)}, u32[]{:S(2)}) collective-permute-start(bf16[128,1024]{1,0:T(8,128)(2,1)S(1)} %bitcast.17), channel_id=1, source_target_pairs={{0,1},{1,0},{2,3},{3,2},{4,5},{5,4},{6,7},{7,6},{8,9},{9,8},{10,11... | collective-permute-start | bytes 786440 | tf_op jit(solution)/shard_map/ppermute | solution.py:40
  55.6 1.7 %collective-permute-start.4 = (f32[8,8,1024]{2,1,0:T(8,128)S(1)}, f32[8,8,1024]{2,1,0:T(8,128)S(1)}, u32[]{:S(2)}, u32[]{:S(2)}) collective-permute-start(f32[8,8,1024]{2,1,0:T(8,128)S(1)} %dynamic-slice_bitcast_fusion), channel_id=1, source_target_pairs={{0,1},{1,0},{2,3},{3,2},{4,5},{5,4},{6,7},{7,6},{8,9},{9,8},{10,11... | collective-permute-start | bytes 786440 | tf_op jit(solution)/shard_map/ppermute | solution.py:40
  58.0 11.1 %all-to-all-start.2 = ((bf16[8,8,1024]{2,1,0:T(8,128)(2,1)}), bf16[8,8,1024]{2,1,0:T(8,128)(2,1)S(1)}, u32[]{:S(2)}, u32[]{:S(2)}) async-start(bf16[8,8,1024]{2,1,0:T(8,128)(2,1)} %fusion), calls=%async_computation.2 | async-start | bytes 262144 | tf_op jit(solution)/shard_map/all_to_all | solution.py:453
  69.2 1.2 %collective-permute-start.5 = (bf16[8,1024]{1,0:T(8,128)(2,1)S(1)}, bf16[8,1024]{1,0:T(8,128)(2,1)S(1)}, u32[]{:S(2)}, u32[]{:S(2)}) collective-permute-start(bf16[8,1024]{1,0:T(8,128)(2,1)S(1)} %add_convert_fusion), channel_id=1, source_target_pairs={{0,1},{1,0},{2,3},{3,2},{4,5},{5,4},{6,7},{7,6},{8,9},{9,8},{10,11... | collective-permute-start | bytes 49160 | tf_op jit(solution)/shard_map/ppermute | solution.py:40

commit v6 on v5

--- a/solution.py
+++ b/solution.py
@@ -145,99 +145,91 @@
     )(half, w_keyval)
 
 
-def stage_kernel(after, whole, out, sems, *, axis, start):
+def stage_kernel(after, whole, first, last, sems, *, axis):
     del after
-    size = out.shape[axis]
-    number = sems.shape[0]
+    size = first.shape[axis]
+    number = sems.shape[0] // 2
     step = size // number
     copies = []
-    for k in range(number):
-        if axis == 0:
-            source = whole.at[pl.ds(start + k * step, step)]
-            target = out.at[pl.ds(k * step, step)]
-        else:
-            source = whole.at[:, pl.ds(start + k * step, step)]
-            target = out.at[:, pl.ds(k * step, step)]
-        copies.append(pltpu.make_async_copy(source, target, sems.at[k]))
+    for half, out in enumerate((first, last)):
+        for k in range(number):
+            if axis == 0:
+                source = whole.at[pl.ds(half * size + k * step, step)]
+                target = out.at[pl.ds(k * step, step)]
+            else:
+                source = whole.at[:, pl.ds(half * size + k * step, step)]
+                target = out.at[:, pl.ds(k * step, step)]
+            copies.append(pltpu.make_async_copy(source, target, sems.at[half * number + k]))
     for copy in copies:
         copy.start()
     for copy in copies:
         copy.wait()
 
 
-def stage(after, whole, axis, part, parts):
+def stage(after, whole, axis):
     shape = list(whole.shape)
-    shape[axis] //= parts
-    return pl.pallas_call(
-        functools.partial(stage_kernel, axis=axis, start=part * shape[axis]),
-        out_shape=jax.ShapeDtypeStruct(tuple(shape), BF16),
+    shape[axis] //= 2
+    part = jax.ShapeDtypeStruct(tuple(shape), BF16)
+    return pl.pallas_call(
+        functools.partial(stage_kernel, axis=axis),
+        out_shape=(part, part),
         in_specs=[SMEM_SPEC, HBM_SPEC],
-        out_specs=VMEM_SPEC,
-        scratch_shapes=[pltpu.SemaphoreType.DMA((4,))],
-        compiler_params=limit(44),
-        cost_estimate=pl.CostEstimate(
-            flops=1 << 30, bytes_accessed=4 * shape[0] * shape[1], transcendentals=0
+        out_specs=(VMEM_SPEC, VMEM_SPEC),
+        scratch_shapes=[pltpu.SemaphoreType.DMA((8,))],
+        compiler_params=limit(42),
+        cost_estimate=pl.CostEstimate(
+            flops=1 << 30, bytes_accessed=8 * shape[0] * shape[1], transcendentals=0
         ),
         name="stage",
     )(after, whole)
 
 
-def feed_kernel(index, mine, theirs, gain, first_in, last_in, first_out, w_out, out, normed, hidden, last_out, sems, *, patterns):
+def feed_kernel(index, mine, theirs, gain, *refs, patterns):
+    *weights, out, normed, hidden = refs
+    half = len(weights) // 2
     pairs, rows, width = mine.shape
-    units = first_in.shape[1]
-    number = sems.shape[0]
-    step = width // number
-    copies = [
-        pltpu.make_async_copy(
-            w_out.at[pl.ds(units, units), pl.ds(k * step, step)],
-            last_out.at[:, pl.ds(k * step, step)],
-            sems.at[k],
-        )
-        for k in range(number)
-    ]
-    for copy in copies:
-        copy.start()
+    units = weights[0].shape[1]
     size = min(256, units)
     weight = gain[...]
     for k in range(2 * pairs):
         place = pl.multiple_of((index[0] ^ patterns[k]) * rows, rows)
         states = mine[k] if k < pairs else theirs[k - pairs]
         normed[pl.ds(place, rows)] = norm_rows(states, weight).astype(BF16)
-    for part, w_in in enumerate((first_in, last_in)):
+    for part in range(half):
         for c in range(units // size):
             columns = pl.ds(c * size, size)
             hidden[part, :, columns] = jnp.maximum(
-                jnp.dot(normed[...], w_in[:, columns], preferred_element_type=F32), 0.0
+                jnp.dot(normed[...], weights[part][:, columns], preferred_element_type=F32), 0.0
             ).astype(BF16)
-    for c in range(number):
-        columns = pl.ds(c * step, step)
-        total = jnp.dot(hidden[0], first_out[:, columns], preferred_element_type=F32)
-        copies[c].wait()
-        total = total + jnp.dot(hidden[1], last_out[:, columns], preferred_element_type=F32)
+    for c in range(width // 256):
+        columns = pl.ds(c * 256, 256)
+        total = jnp.dot(hidden[0], weights[half][:, columns], preferred_element_type=F32)
+        for part in range(1, half):
+            total = total + jnp.dot(
+                hidden[part], weights[half + part][:, columns], preferred_element_type=F32
+            )
         out[:, columns] = total.astype(BF16)
 
 
-def feed(index, mine, theirs, gain, first_in, last_in, first_out, w_out, patterns):
+def feed(index, mine, theirs, gain, weights, patterns):
     pairs, rows, width = mine.shape
     count = 2 * pairs * rows
-    units = first_in.shape[1]
+    units = weights[0].shape[1] * len(weights) // 2
     return pl.pallas_call(
         functools.partial(feed_kernel, patterns=patterns),
         out_shape=jax.ShapeDtypeStruct((count, width), BF16),
-        in_specs=[SMEM_SPEC] + [VMEM_SPEC] * 6 + [HBM_SPEC],
+        in_specs=[SMEM_SPEC] + [VMEM_SPEC] * (3 + len(weights)),
         out_specs=VMEM_SPEC,
         scratch_shapes=[
             pltpu.VMEM((count, width), BF16),
-            pltpu.VMEM((2, count, units), BF16),
-            pltpu.VMEM((units, width), BF16),
-            pltpu.SemaphoreType.DMA((width // 256,)),
+            pltpu.VMEM((len(weights) // 2, count, weights[0].shape[1]), BF16),
         ],
-        compiler_params=limit(37),
-        cost_estimate=pl.CostEstimate(
-            flops=8 * count * width * units, bytes_accessed=8 * width * units, transcendentals=0
+        compiler_params=limit(24),
+        cost_estimate=pl.CostEstimate(
+            flops=4 * count * width * units, bytes_accessed=4 * width * units, transcendentals=0
         ),
         name="feed",
-    )(index, mine, theirs, gain.reshape(1, width), first_in, last_in, first_out, w_out)
+    )(index, mine, theirs, gain.reshape(1, width), *weights)
 
 
 def settle_kernel(parts, tokens, gain, encoded, spread):
@@ -403,21 +395,27 @@
 
     half = jnp.reshape(psg_index, (1,)).astype(jnp.int32)
     index = jnp.reshape(mp_index, (1,)).astype(jnp.int32)
+    quarter = mp // 4
     patterns = [0]
-    held = tokens[None]
-    step = mp // 2
+    blocks = [tokens[None]]
+    for k in (3, 2, 1):
+        blocks.append(lax.ppermute(tokens[None], "mp", [(j, j ^ (k * quarter)) for j in range(mp)]))
+        patterns.append(k * quarter)
+    held = jnp.concatenate(blocks, axis=0)
+    step = quarter // 2
     while step > 0:
         got = lax.ppermute(held, "mp", [(j, j ^ step) for j in range(mp)])
         patterns = patterns + [p ^ step for p in patterns]
         if step > 1:
             held = jnp.concatenate([held, got], axis=0)
         step //= 2
-    first_in = stage(index, w_in, 1, 0, 2)
-    last_in = stage(index, w_in, 1, 1, 2)
-    first_out = stage(index, w_out, 0, 0, 2)
+    first_in, last_in = stage(index, w_in, 1)
+    first_out, last_out = stage(index, w_out, 0)
     query = ask(half, answer_states, dec_gain, w_query, inner)
     first_key, last_key, value = prepare(half, w_keyval, inner)
-    partial_sums = feed(index, held, got, enc_gain, first_in, last_in, first_out, w_out, patterns)
+    partial_sums = feed(
+        index, held, got, enc_gain, [first_in, last_in, first_out, last_out], patterns
+    )
     parts = lax.all_to_all(partial_sums.reshape(mp, row_count, width), "mp", 0, 0)
     encoded, spread = settle(parts, tokens, final_gain)
     mine = lax.all_to_all(spread, "mp", 0, 0)

time: 71.6 us -> 69.1 us (0.965)
  Pallas kernels: 26.5 us -> 24.2 us
  starting transfers between devices: 20.9 us -> 19.3 us
  waiting for transfers between devices: 20.2 us -> 21.6 us
    ppermute x3 -> x1, starting transfers between devices: 7.47 us -> 1.58 us  [per_device(): got = lax.ppermute(held, 'mp', [(j, j ^ step) for j in range(mp)])]
    ppermute x0 -> x3, starting transfers between devices: none -> 5.79 us  [per_device(): lax.ppermute(tokens[None], 'mp', [(j, j ^ k * quarter) for j in range(mp)])]
    ppermute x0 -> x3, waiting for transfers between devices: none -> 4.38 us  [per_device(): lax.ppermute(tokens[None], 'mp', [(j, j ^ k * quarter) for j in range(mp)])]
    ppermute x3 -> x1, waiting for transfers between devices: 2.92 us -> 0.01 us  [per_device(): got = lax.ppermute(held, 'mp', [(j, j ^ step) for j in range(mp)])]
    pallas_call x1, Pallas kernels: 5.83 us -> 3.23 us  [feed(): pl.pallas_call(functools.partial(feed_kernel, patterns=patterns), out_sha...]
    all_to_all x1, starting transfers between devices: 4.9 us -> 3.41 us  [per_device(): lax.all_to_all(partial_sums.reshape(mp, row_count, width), 'mp', 0, 0)]
    pallas_call x3 -> x2, Pallas kernels: 6.68 us -> 7.01 us  [stage(): pl.pallas_call(functools.partial(stage_kernel, axis=axis), out_shape=(par...]
  transfers between devices with their start and end apart: 9 -> 10, of which waited for: 7 -> 7; matrix products, arithmetic and copies ran while one was open for 1% -> 1% of each run, Pallas kernels for 25% -> 26%
where the time goes in v6:
time: 69.1 us; the launch traced here: 68.6 us
  Pallas kernels  24.2 us (35%)
  waiting for transfers between devices  21.6 us (31%)
  starting transfers between devices  19.3 us (28%)
  other arithmetic  2.5 us (4%)
  between operations  0.87 us (1%)
    all_to_all x1, waiting for transfers between devices, per_device(): answer_parts = lax.all_to_all(chip_sum, 'mp', 0, 0)  7.73 us
    pallas_call x2, Pallas kernels, stage(): pl.pallas_call(functools.partial(stage_kernel, axis=axis), out_shape=(par...  7.01 us
    pallas_call x1, Pallas kernels, prepare(): pl.pallas_call(prepare_kernel, out_shape=(jax.ShapeDtypeStruct((width, in...  6.57 us
    ppermute x3, starting transfers between devices, per_device(): lax.ppermute(tokens[None], 'mp', [(j, j ^ k * quarter) for j in range(mp)])  5.79 us
    all_to_all x1, waiting for transfers between devices, per_device(): mine = lax.all_to_all(spread, 'mp', 0, 0)  5.77 us
    all_to_all x1, starting transfers between devices, per_device(): mine = lax.all_to_all(spread, 'mp', 0, 0)  4.55 us
    ppermute x3, waiting for transfers between devices, per_device(): lax.ppermute(tokens[None], 'mp', [(j, j ^ k * quarter) for j in range(mp)])  4.38 us
    all_to_all x1, starting transfers between devices, per_device(): lax.all_to_all(partial_sums.reshape(mp, row_count, width), 'mp', 0, 0)  3.41 us
  transfers between devices with their start and end apart: 10, of which 7 were waited for; matrix products, arithmetic and copies ran while one was open for 1% of the time, Pallas kernels for 26%

profile of v6, /device:TPU:0, one launch (start us, length us, event | category | flops | bytes accessed | tf_op | source)
XLA Modules:
  0.0 68.6 jit_solution(14483248501940280675)
XLA Ops:
  0.6 5.1 %collective-permute-start = (bf16[1,16,1024]{2,1,0:T(8,128)(2,1)}, bf16[1,16,1024]{2,1,0:T(8,128)(2,1)S(1)}, u32[]{:S(2)}, u32[]{:S(2)}) collective-permute-start(bf16[1,16,1024]{2,1,0:T(8,128)(2,1)} %bitcast.19), channel_id=1, source_target_pairs={{0,12},{2,14},{4,8},{6,10},{8,4},{10,6},{12,0},{14,2},{1,13},{3,15... | collective-permute-start | bytes 98312 | tf_op jit(solution)/shard_map/ppermute | solution.py:402
  5.8 0.0 collective-permute-start.1
  5.8 0.6 collective-permute-start.2
  6.4 1.5 %collective-permute-done = bf16[1,16,1024]{2,1,0:T(8,128)(2,1)S(1)} collective-permute-done((bf16[1,16,1024]{2,1,0:T(8,128)(2,1)}, bf16[1,16,1024]{2,1,0:T(8,128)(2,1)S(1)}, u32[]{:S(2)}, u32[]{:S(2)}) %collective-permute-start) | collective-permute-done | bytes 32800 | tf_op jit(solution)/shard_map/ppermute | solution.py:402
  7.9 2.9 %collective-permute-done.1 = bf16[1,16,1024]{2,1,0:T(8,128)(2,1)S(1)} collective-permute-done((bf16[1,16,1024]{2,1,0:T(8,128)(2,1)}, bf16[1,16,1024]{2,1,0:T(8,128)(2,1)S(1)}, u32[]{:S(2)}, u32[]{:S(2)}) %collective-permute-start.1) | collective-permute-done | bytes 32800 | tf_op jit(solution)/shard_map/ppermute | solution.py:402
  10.8 0.0 collective-permute-done.2
  10.8 0.8 %pad_maximum_fusion.mine = bf16[4,16,1024]{2,1,0:T(8,128)(2,1)S(1)} fusion(bf16[1,16,1024]{2,1,0:T(8,128)(2,1)S(1)} %collective-permute-done.2, bf16[1,16,1024]{2,1,0:T(8,128)(2,1)S(1)} %collective-permute-done.1, bf16[1,16,1024]{2,1,0:T(8,128)(2,1)S(1)} %collective-permute-done, bf16[1,16,1024]{2,1,0:T(8,128)(2,1)} %bitcast.22), kind=kLoop, calls=%fused_computation.4 | loop fusion | flops 196608 | bytes 262144 | tf_op jit(solution)/shard_map/concatenate | solution.py:404
  11.6 1.6 %collective-permute-start.3 = (bf16[4,16,1024]{2,1,0:T(8,128)(2,1)S(1)}, bf16[4,16,1024]{2,1,0:T(8,128)(2,1)S(1)}, u32[]{:S(2)}, u32[]{:S(2)}) collective-permute-start(bf16[4,16,1024]{2,1,0:T(8,128)(2,1)S(1)} %pad_maximum_fusion.mine), channel_id=1, source_target_pairs={{0,2},{2,0},{4,6},{6,4},{8,10},{10,8},{12,14},{14,12},{1,3},{3,1},... | collective-permute-start | bytes 393224 | tf_op jit(solution)/shard_map/ppermute | solution.py:407
  13.2 3.5 %stage.2 = (bf16[1024,2048]{1,0:T(8,128)(2,1)S(1)}, bf16[1024,2048]{1,0:T(8,128)(2,1)S(1)}) custom-call(s32[1]{0:T(128)} %bitcast.after.index, bf16[1024,4096]{1,0:T(8,128)(2,1)} %whole.2), custom_call_target="tpu_custom_call" | custom-call | flops 1073741824 | bytes 16777216 | tf_op jit(solution)/shard_map/stage/pallas_call | solution.py:173
  16.7 0.0 copy-start.4
  16.7 3.5 %stage.3 = (bf16[2048,1024]{1,0:T(8,128)(2,1)S(1)}, bf16[2048,1024]{1,0:T(8,128)(2,1)S(1)}) custom-call(s32[1]{0:T(128)} %bitcast.after.index, bf16[4096,1024]{1,0:T(8,128)(2,1)} %whole.3), custom_call_target="tpu_custom_call" | custom-call | flops 1073741824 | bytes 16777216 | tf_op jit(solution)/shard_map/stage/pallas_call | solution.py:173
  20.2 0.0 collective-permute-done.3.theirs
  20.2 0.0 copy-done.4
  20.2 3.2 %feed.1 = bf16[128,1024]{1,0:T(8,128)(2,1)} custom-call(s32[1]{0:T(128)} %bitcast.after.index, bf16[4,16,1024]{2,1,0:T(8,128)(2,1)S(1)} %pad_maximum_fusion.mine, bf16[4,16,1024]{2,1,0:T(8,128)(2,1)S(1)} %collective-permute-done.3.theirs, f32[1,1024]{1,0:T(1,128)S(1)} %bitcast.25, bf16[1024,2048]{1,0:T(8,128)(2,1)S(1)} %get-tuple-element.16.refs_0_, ...), custom_call_target="tpu_custom_call" | custom-call | flops 2147483648 | bytes 16777216 | tf_op jit(solution)/shard_map/feed/pallas_call | solution.py:218
  23.4 3.4 %all-to-all-start = ((bf16[8,16,1024]{2,1,0:T(8,128)(2,1)}), bf16[8,16,1024]{2,1,0:T(8,128)(2,1)S(1)}, u32[]{:S(2)}, u32[]{:S(2)}) async-start(bf16[8,16,1024]{2,1,0:T(8,128)(2,1)} %bitcast.3), calls=%async_computation | async-start | bytes 524288 | tf_op jit(solution)/shard_map/all_to_all | solution.py:419
  26.9 0.0 copy-start.7
  26.9 0.0 copy-start.1
  26.9 0.0 copy-start.2
  26.9 0.0 copy-start
  26.9 0.0 copy-start.3
  26.9 6.6 %prepare.1 = (bf16[1024,512]{1,0:T(8,128)(2,1)S(1)}, bf16[1024,512]{1,0:T(8,128)(2,1)S(1)}, bf16[1024,1024]{1,0:T(8,128)(2,1)}) custom-call(s32[1]{0:T(128)} %bitcast.5.half, bf16[1024,2,2048]{2,1,0:T(2,128)(2,1)} %w_keyval.1), custom_call_target="tpu_custom_call" | custom-call | flops 1073741824 | bytes 8388608 | tf_op jit(solution)/shard_map/prepare/pallas_call | solution.py:127
  33.5 0.0 copy-start.5
  33.5 0.0 copy-start.6
  33.6 0.0 copy-done.7
  33.6 0.1 select_reduce_fusion.2
  33.7 1.4 %all-to-all-done.parts = bf16[8,16,1024]{2,1,0:T(8,128)(2,1)S(1)} async-done(((bf16[8,16,1024]{2,1,0:T(8,128)(2,1)}), bf16[8,16,1024]{2,1,0:T(8,128)(2,1)S(1)}, u32[]{:S(2)}, u32[]{:S(2)}) %all-to-all-start) | async-done | bytes 262176 | tf_op jit(solution)/shard_map/all_to_all | solution.py:419
  35.0 0.0 copy-done.1
  35.0 0.0 copy-done.2
  35.0 0.8 %settle.1 = (bf16[16,1024]{1,0:T(8,128)(2,1)}, bf16[8,16,1024]{2,1,0:T(8,128)(2,1)}) custom-call(bf16[8,16,1024]{2,1,0:T(8,128)(2,1)S(1)} %all-to-all-done.parts, bf16[16,1024]{1,0:T(8,128)(2,1)S(1)} %copy-done.1, f32[1,1024]{1,0:T(1,128)S(1)} %bitcast.23), custom_call_target="tpu_custom_call" | custom-call | tf_op jit(solution)/shard_map/settle/pallas_call | solution.py:248
  35.9 4.6 %all-to-all-start.1 = ((bf16[8,16,1024]{2,1,0:T(8,128)(2,1)}), bf16[8,16,1024]{2,1,0:T(8,128)(2,1)S(1)}, u32[]{:S(2)}, u32[]{:S(2)}) async-start(bf16[8,16,1024]{2,1,0:T(8,128)(2,1)} %get-tuple-element.21), calls=%async_computation.1 | async-start | bytes 524288 | tf_op jit(solution)/shard_map/all_to_all | solution.py:421
  40.4 0.0 copy-done
  40.4 0.0 copy-done.3
  40.4 2.2 %ask.1.query = bf16[128,1024]{1,0:T(8,128)(2,1)S(1)} custom-call(s32[1]{0:T(128)} %bitcast.5.half, bf16[128,1024]{1,0:T(8,128)(2,1)S(1)} %copy-done, f32[1,1024]{1,0:T(1,128)S(1)} %bitcast.24, bf16[1024,2048]{1,0:T(8,128)(2,1)} %w_query.1), custom_call_target="tpu_custom_call" | custom-call | flops 1073741824 | bytes 2097152 | tf_op jit(solution)/shard_map/ask/pallas_call | solution.py:79
  42.7 0.1 convert_reduce_fusion.1
  42.8 0.0 copy-done.5
  42.8 0.0 copy-done.6
  42.8 0.1 select_reduce_fusion.1
  42.9 5.8 %all-to-all-done.1 = bf16[8,16,1024]{2,1,0:T(8,128)(2,1)S(1)} async-done(((bf16[8,16,1024]{2,1,0:T(8,128)(2,1)}), bf16[8,16,1024]{2,1,0:T(8,128)(2,1)S(1)}, u32[]{:S(2)}, u32[]{:S(2)}) %all-to-all-start.1) | async-done | bytes 262176 | tf_op jit(solution)/shard_map/all_to_all | solution.py:421
  48.7 0.0 collective-permute-start.4
  48.7 0.1 and_convert_fusion.allowed
  48.7 2.3 %project.1 = (bf16[128,1024]{1,0:T(8,128)(2,1)S(1)}, bf16[128,1024]{1,0:T(8,128)(2,1)S(1)}, bf16[1024,512]{1,0:T(8,128)(2,1)S(1)}, bf16[1024,512]{1,0:T(8,128)(2,1)S(1)}, bf16[1024,1024]{1,0:T(8,128)(2,1)S(1)}) custom-call(s32[1]{0:T(128)} %bitcast.5.half, bf16[128,1024]{1,0:T(8,128)(2,1)S(1)} %bitcast.18, ...), custom_call_target="tpu_custom_call" | custom-call | flops 536870912 | bytes 6291456 | tf_op jit(solution)/shard_map/project/pallas_call | solution.py:291
  51.0 0.0 collective-permute-done.4.theirs
  51.0 2.1 %attend.1 = f32[128,1024]{1,0:T(8,128)S(1)} custom-call(bf16[128,1024]{1,0:T(8,128)(2,1)S(1)} %get-tuple-element.25.near_keys, bf16[128,1024]{1,0:T(8,128)(2,1)S(1)} %get-tuple-element.26.near_values, bf16[128,1024]{1,0:T(8,128)(2,1)S(1)} %collective-permute-done.4.theirs, bf16[128,1024]{1,0:T(8,128)(2,1)S(1)} %ask.1.query, ...), custom_call_target="tpu_custom_call" | custom-call | flops 939524096 | bytes 6291456 | tf_op jit(solution)/shard_map/attend/pallas_call | solution.py:355
  53.2 0.6 collective-permute-start.5
  53.7 1.2 %collective-permute-done.5 = f32[8,8,1024]{2,1,0:T(8,128)S(1)} collective-permute-done((f32[8,8,1024]{2,1,0:T(8,128)S(1)}, f32[8,8,1024]{2,1,0:T(8,128)S(1)}, u32[]{:S(2)}, u32[]{:S(2)}) %collective-permute-start.5) | collective-permute-done | bytes 262176 | tf_op jit(solution)/shard_map/ppermute | solution.py:40
  54.9 0.7 fusion
  55.6 3.4 %all-to-all-start.2 = ((bf16[8,8,1024]{2,1,0:T(8,128)(2,1)}), bf16[8,8,1024]{2,1,0:T(8,128)(2,1)S(1)}, u32[]{:S(2)}, u32[]{:S(2)}) async-start(bf16[8,8,1024]{2,1,0:T(8,128)(2,1)} %fusion), calls=%async_computation.2 | async-start | bytes 262144 | tf_op jit(solution)/shard_map/all_to_all | solution.py:451
  59.0 7.7 %all-to-all-done.2 = bf16[8,8,1024]{2,1,0:T(8,128)(2,1)S(1)} async-done(((bf16[8,8,1024]{2,1,0:T(8,128)(2,1)}), bf16[8,8,1024]{2,1,0:T(8,128)(2,1)S(1)}, u32[]{:S(2)}, u32[]{:S(2)}) %all-to-all-start.2) | async-done | bytes 131104 | tf_op jit(solution)/shard_map/all_to_all | solution.py:451
  66.7 0.1 collective-permute-start.6
  66.8 1.2 %collective-permute-done.6 = bf16[8,1024]{1,0:T(8,128)(2,1)S(1)} collective-permute-done((bf16[8,1024]{1,0:T(8,128)(2,1)S(1)}, bf16[8,1024]{1,0:T(8,128)(2,1)S(1)}, u32[]{:S(2)}, u32[]{:S(2)}) %collective-permute-start.6) | collective-permute-done | bytes 16416 | tf_op jit(solution)/shard_map/ppermute | solution.py:40
  68.0 0.6 pad_maximum_fusion.1
  (6 shorter events, 0.1 us)
Async XLA Ops:
  0.6 7.2 %collective-permute-start = (bf16[1,16,1024]{2,1,0:T(8,128)(2,1)}, bf16[1,16,1024]{2,1,0:T(8,128)(2,1)S(1)}, u32[]{:S(2)}, u32[]{:S(2)}) collective-permute-start(bf16[1,16,1024]{2,1,0:T(8,128)(2,1)} %bitcast.19), channel_id=1, source_target_pairs={{0,12},{2,14},{4,8},{6,10},{8,4},{10,6},{12,0},{14,2},{1,13},{3,15... | collective-permute-start | bytes 98312 | tf_op jit(solution)/shard_map/ppermute | solution.py:402
  5.8 5.0 %collective-permute-start.1 = (bf16[1,16,1024]{2,1,0:T(8,128)(2,1)}, bf16[1,16,1024]{2,1,0:T(8,128)(2,1)S(1)}, u32[]{:S(2)}, u32[]{:S(2)}) collective-permute-start(bf16[1,16,1024]{2,1,0:T(8,128)(2,1)} %bitcast.20), channel_id=1, source_target_pairs={{0,8},{2,10},{4,12},{6,14},{8,0},{10,2},{12,4},{14,6},{1,9},{3,11}... | collective-permute-start | bytes 98312 | tf_op jit(solution)/shard_map/ppermute | solution.py:402
  5.8 5.0 %collective-permute-start.2 = (bf16[1,16,1024]{2,1,0:T(8,128)(2,1)}, bf16[1,16,1024]{2,1,0:T(8,128)(2,1)S(1)}, u32[]{:S(2)}, u32[]{:S(2)}) collective-permute-start(bf16[1,16,1024]{2,1,0:T(8,128)(2,1)} %bitcast.21), channel_id=1, source_target_pairs={{0,4},{2,6},{4,0},{6,2},{8,12},{10,14},{12,8},{14,10},{1,5},{3,7},... | collective-permute-start | bytes 98312 | tf_op jit(solution)/shard_map/ppermute | solution.py:402
  11.6 8.6 %collective-permute-start.3 = (bf16[4,16,1024]{2,1,0:T(8,128)(2,1)S(1)}, bf16[4,16,1024]{2,1,0:T(8,128)(2,1)S(1)}, u32[]{:S(2)}, u32[]{:S(2)}) collective-permute-start(bf16[4,16,1024]{2,1,0:T(8,128)(2,1)S(1)} %pad_maximum_fusion.mine), channel_id=1, source_target_pairs={{0,2},{2,0},{4,6},{6,4},{8,10},{10,8},{12,14},{14,12},{1,3},{3,1},... | collective-permute-start | bytes 393224 | tf_op jit(solution)/shard_map/ppermute | solution.py:407
  16.7 3.5 %copy-start.4 = (f32[1024]{0:T(1024)S(1)}, f32[1024]{0:T(1024)}, u32[]{:S(2)}) copy-start(f32[1024]{0:T(1024)} %param.14) | copy-start | bytes 12292
  23.4 11.6 %all-to-all-start = ((bf16[8,16,1024]{2,1,0:T(8,128)(2,1)}), bf16[8,16,1024]{2,1,0:T(8,128)(2,1)S(1)}, u32[]{:S(2)}, u32[]{:S(2)}) async-start(bf16[8,16,1024]{2,1,0:T(8,128)(2,1)} %bitcast.3), calls=%async_computation | async-start | bytes 524288 | tf_op jit(solution)/shard_map/all_to_all | solution.py:419
  26.9 6.7 %copy-start.7 = (s32[4]{0:T(128)S(1)}, s32[4]{0:T(128)}, u32[]{:S(2)}) copy-start(s32[4]{0:T(128)} %param.25) | copy-start | bytes 52
  26.9 8.1 %copy-start.1 = (bf16[16,1024]{1,0:T(8,128)(2,1)S(1)}, bf16[16,1024]{1,0:T(8,128)(2,1)}, u32[]{:S(2)}) copy-start(bf16[16,1024]{1,0:T(8,128)(2,1)} %tokens.1) | copy-start | bytes 98308
  26.9 8.1 %copy-start.2 = (f32[1024]{0:T(1024)S(1)}, f32[1024]{0:T(1024)}, u32[]{:S(2)}) copy-start(f32[1024]{0:T(1024)} %param.17) | copy-start | bytes 12292
  26.9 13.5 %copy-start = (bf16[128,1024]{1,0:T(8,128)(2,1)S(1)}, bf16[128,1024]{1,0:T(8,128)(2,1)}, u32[]{:S(2)}) copy-start(bf16[128,1024]{1,0:T(8,128)(2,1)} %states.1) | copy-start | bytes 786436
  26.9 13.5 %copy-start.3 = (f32[1024]{0:T(1024)S(1)}, f32[1024]{0:T(1024)}, u32[]{:S(2)}) copy-start(f32[1024]{0:T(1024)} %param.20) | copy-start | bytes 12292
  33.5 9.3 %copy-start.5 = (s32[16]{0:T(128)S(1)}, s32[16]{0:T(128)}, u32[]{:S(2)}) copy-start(s32[16]{0:T(128)} %param.23) | copy-start | bytes 196
  33.5 9.2 %copy-start.6 = (s32[16]{0:T(128)S(1)}, s32[16]{0:T(128)}, u32[]{:S(2)}) copy-start(s32[16]{0:T(128)} %param.24) | copy-start | bytes 196
  35.9 12.8 %all-to-all-start.1 = ((bf16[8,16,1024]{2,1,0:T(8,128)(2,1)}), bf16[8,16,1024]{2,1,0:T(8,128)(2,1)S(1)}, u32[]{:S(2)}, u32[]{:S(2)}) async-start(bf16[8,16,1024]{2,1,0:T(8,128)(2,1)} %get-tuple-element.21), calls=%async_computation.1 | async-start | bytes 524288 | tf_op jit(solution)/shard_map/all_to_all | solution.py:421
  48.7 2.4 %collective-permute-start.4 = (bf16[128,1024]{1,0:T(8,128)(2,1)S(1)}, bf16[128,1024]{1,0:T(8,128)(2,1)S(1)}, u32[]{:S(2)}, u32[]{:S(2)}) collective-permute-start(bf16[128,1024]{1,0:T(8,128)(2,1)S(1)} %bitcast.17), channel_id=1, source_target_pairs={{0,1},{1,0},{2,3},{3,2},{4,5},{5,4},{6,7},{7,6},{8,9},{9,8},{10,11... | collective-permute-start | bytes 786440 | tf_op jit(solution)/shard_map/ppermute | solution.py:40
  53.2 1.7 %collective-permute-start.5 = (f32[8,8,1024]{2,1,0:T(8,128)S(1)}, f32[8,8,1024]{2,1,0:T(8,128)S(1)}, u32[]{:S(2)}, u32[]{:S(2)}) collective-permute-start(f32[8,8,1024]{2,1,0:T(8,128)S(1)} %dynamic-slice_bitcast_fusion), channel_id=1, source_target_pairs={{0,1},{1,0},{2,3},{3,2},{4,5},{5,4},{6,7},{7,6},{8,9},{9,8},{10,11... | collective-permute-start | bytes 786440 | tf_op jit(solution)/shard_map/ppermute | solution.py:40
  55.6 11.1 %all-to-all-start.2 = ((bf16[8,8,1024]{2,1,0:T(8,128)(2,1)}), bf16[8,8,1024]{2,1,0:T(8,128)(2,1)S(1)}, u32[]{:S(2)}, u32[]{:S(2)}) async-start(bf16[8,8,1024]{2,1,0:T(8,128)(2,1)} %fusion), calls=%async_computation.2 | async-start | bytes 262144 | tf_op jit(solution)/shard_map/all_to_all | solution.py:451
  66.7 1.2 %collective-permute-start.6 = (bf16[8,1024]{1,0:T(8,128)(2,1)S(1)}, bf16[8,1024]{1,0:T(8,128)(2,1)S(1)}, u32[]{:S(2)}, u32[]{:S(2)}) collective-permute-start(bf16[8,1024]{1,0:T(8,128)(2,1)S(1)} %add_convert_fusion), channel_id=1, source_target_pairs={{0,1},{1,0},{2,3},{3,2},{4,5},{5,4},{6,7},{7,6},{8,9},{9,8},{10,11... | collective-permute-start | bytes 49160 | tf_op jit(solution)/shard_map/ppermute | solution.py:40

commit v7 on v6

--- a/solution.py
+++ b/solution.py
@@ -21,7 +21,7 @@
     return wide * factor * gain
 
 
-def key_mask(token_index, passage_lengths, passage_owner, answer_lengths, answer_count):
+def key_mask(token_index, answer_index, passage_lengths, passage_owner, answer_lengths):
     passage = token_index // P_SLOT
     place = token_index % P_SLOT
     count = passage_lengths.shape[0]
@@ -31,9 +31,26 @@
     number = answer_lengths.shape[0]
     order = jnp.arange(number, dtype=jnp.int32)
     ends = jnp.sum(jnp.where(order[:, None] <= order[None, :], answer_lengths[:, None], 0), axis=0)
-    answer_index = jnp.arange(answer_count, dtype=jnp.int32)
     question = jnp.sum((answer_index[:, None] >= ends[None, :]).astype(jnp.int32), axis=1)
     return (place < token_length)[None, :] & (token_owner[None, :] == question[:, None])
+
+
+def spread_out(x, mp):
+    quarter = mp // 4
+    patterns = [0]
+    blocks = [x[None]]
+    for k in (3, 2, 1):
+        blocks.append(lax.ppermute(x[None], "mp", [(j, j ^ (k * quarter)) for j in range(mp)]))
+        patterns.append(k * quarter)
+    held = jnp.concatenate(blocks, axis=0)
+    step = quarter // 2
+    while step > 0:
+        got = lax.ppermute(held, "mp", [(j, j ^ step) for j in range(mp)])
+        patterns = patterns + [p ^ step for p in patterns]
+        if step > 1:
+            held = jnp.concatenate([held, got], axis=0)
+        step //= 2
+    return held, got, patterns
 
 
 def swap_psg(x):
@@ -51,9 +68,11 @@
     return pltpu.CompilerParams(vmem_limit_bytes=mib << 20)
 
 
-def ask_kernel(half, states, gain, w_query, query, scr, sems):
+def ask_kernel(half, states, gain, w_query, value, query, first_value, last_value, scr, sems, *, mp):
     inner = query.shape[1]
+    part = first_value.shape[1]
     size = scr.shape[2]
+    chunks = inner // size
     start = pl.multiple_of(half[0] * inner, 128)
     copies = [
         pltpu.make_async_copy(
@@ -61,36 +80,55 @@
             scr.at[c],
             sems.at[c],
         )
-        for c in range(inner // size)
+        for c in range(chunks)
     ]
-    for copy in copies:
+    others = [
+        pltpu.make_async_copy(value.at[:, pl.ds(0, part)], first_value, sems.at[chunks]),
+        pltpu.make_async_copy(value.at[:, pl.ds(part, part)], last_value, sems.at[chunks + 1]),
+    ]
+    for copy in copies + others:
         copy.start()
     normed = norm_rows(states[...], gain[...]).astype(BF16)
-    for c in range(inner // size):
+    count = states.shape[0]
+    small = count // mp // 2
+    row = lax.broadcasted_iota(jnp.int32, (count, count), 0)
+    column = lax.broadcasted_iota(jnp.int32, (count, count), 1)
+    side = half[0] ^ lax.div(row, mp * small)
+    source = lax.rem(lax.div(row, small), mp) * (2 * small) + side * small + lax.rem(row, small)
+    pick = jnp.where(column == source, 1.0, 0.0).astype(BF16)
+    normed = jnp.dot(pick, normed, preferred_element_type=F32).astype(BF16)
+    for c in range(chunks):
         copies[c].wait()
         query[:, pl.ds(c * size, size)] = jnp.dot(
             normed, scr[c], preferred_element_type=F32
         ).astype(BF16)
-
-
-def ask(half, states, gain, w_query, inner):
+    for copy in others:
+        copy.wait()
+
+
+def ask(half, states, gain, w_query, value, mp):
     count, width = states.shape
+    inner = value.shape[1]
     size = min(256, inner)
     return pl.pallas_call(
-        ask_kernel,
-        out_shape=jax.ShapeDtypeStruct((count, inner), BF16),
-        in_specs=[SMEM_SPEC, VMEM_SPEC, VMEM_SPEC, HBM_SPEC],
-        out_specs=VMEM_SPEC,
+        functools.partial(ask_kernel, mp=mp),
+        out_shape=(
+            jax.ShapeDtypeStruct((count, inner), BF16),
+            jax.ShapeDtypeStruct((width, inner // 2), BF16),
+            jax.ShapeDtypeStruct((width, inner // 2), BF16),
+        ),
+        in_specs=[SMEM_SPEC, VMEM_SPEC, VMEM_SPEC, HBM_SPEC, HBM_SPEC],
+        out_specs=(VMEM_SPEC,) * 3,
         scratch_shapes=[
             pltpu.VMEM((inner // size, width, size), BF16),
-            pltpu.SemaphoreType.DMA((inner // size,)),
+            pltpu.SemaphoreType.DMA((inner // size + 2,)),
         ],
-        compiler_params=limit(52),
+        compiler_params=limit(50),
         cost_estimate=pl.CostEstimate(
-            flops=1 << 30, bytes_accessed=2 * width * inner, transcendentals=0
+            flops=1 << 30, bytes_accessed=4 * width * inner, transcendentals=0
         ),
         name="ask",
-    )(half, states, gain.reshape(1, width), w_query)
+    )(half, states, gain.reshape(1, width), w_query, value)
 
 
 def prepare_kernel(half, w_keyval, first_key, last_key, w_value, scr, sems):
@@ -232,87 +270,90 @@
     )(index, mine, theirs, gain.reshape(1, width), *weights)
 
 
-def settle_kernel(parts, tokens, gain, encoded, spread):
+def settle_kernel(parts, tokens, gain, after, encoded, memory):
+    del after
     total = tokens[...].astype(F32)
     for k in range(parts.shape[0]):
         total = total + parts[k].astype(F32)
     rounded = total.astype(BF16)
     encoded[...] = rounded
-    memory = norm_rows(rounded, gain[...]).astype(BF16)
-    for k in range(spread.shape[0]):
-        spread[k] = memory
-
-
-def settle(parts, tokens, gain):
-    count, rows, width = parts.shape
+    memory[...] = norm_rows(rounded, gain[...]).astype(BF16)
+
+
+def settle(parts, tokens, gain, after):
+    _, rows, width = parts.shape
     return pl.pallas_call(
         settle_kernel,
         out_shape=(
             jax.ShapeDtypeStruct((rows, width), BF16),
-            jax.ShapeDtypeStruct((count, rows, width), BF16),
-        ),
-        in_specs=[VMEM_SPEC] * 3,
+            jax.ShapeDtypeStruct((rows, width), BF16),
+        ),
+        in_specs=[VMEM_SPEC] * 3 + [HBM_SPEC],
         out_specs=(VMEM_SPEC, VMEM_SPEC),
         compiler_params=limit(8),
         name="settle",
-    )(parts, tokens, gain.reshape(1, width))
-
-
-def project_kernel(half, mine, first_key, last_key, value, w_out, keys, values, first_value, last_value, w_last, sems):
+    )(parts, tokens, gain.reshape(1, width), after)
+
+
+def project_kernel(half, mine, theirs, first_key, last_key, first_value, last_value, w_out, keys, values, w_last, sems):
     inner = keys.shape[1]
     part = inner // 2
     start = pl.multiple_of(half[0] * inner, 128)
+    number = sems.shape[0]
+    step = inner // number
     copies = [
-        pltpu.make_async_copy(value.at[:, pl.ds(0, part)], first_value, sems.at[0]),
-        pltpu.make_async_copy(value.at[:, pl.ds(part, part)], last_value, sems.at[1]),
+        pltpu.make_async_copy(
+            w_out.at[pl.ds(pl.multiple_of(start + k * step, 64), step)],
+            w_last.at[pl.ds(k * step, step)],
+            sems.at[k],
+        )
+        for k in range(number)
     ]
-    last = pltpu.make_async_copy(w_out.at[pl.ds(start, inner)], w_last, sems.at[2])
     for copy in copies:
         copy.start()
-    last.start()
+    rows = jnp.concatenate([mine[...], theirs[...]], axis=0)
     size = min(256, part)
     for k, w_key in enumerate((first_key, last_key)):
         for c in range(part // size):
             keys[:, pl.ds(k * part + c * size, size)] = jnp.dot(
-                mine[...], w_key[:, pl.ds(c * size, size)], preferred_element_type=F32
+                rows, w_key[:, pl.ds(c * size, size)], preferred_element_type=F32
             ).astype(BF16)
     for k, w_value in enumerate((first_value, last_value)):
-        copies[k].wait()
         for c in range(part // size):
             values[:, pl.ds(k * part + c * size, size)] = jnp.dot(
-                mine[...], w_value[:, pl.ds(c * size, size)], preferred_element_type=F32
+                rows, w_value[:, pl.ds(c * size, size)], preferred_element_type=F32
             ).astype(BF16)
-    last.wait()
-
-
-def project(half, mine, first_key, last_key, value, w_attn_out):
+    for copy in copies:
+        copy.wait()
+
+
+def project(half, mine, theirs, weights, w_attn_out):
     rows, width = mine.shape
-    inner = value.shape[1]
+    inner = 2 * weights[0].shape[1]
     return pl.pallas_call(
         project_kernel,
         out_shape=(
-            jax.ShapeDtypeStruct((rows, inner), BF16),
-            jax.ShapeDtypeStruct((rows, inner), BF16),
-            jax.ShapeDtypeStruct((width, inner // 2), BF16),
-            jax.ShapeDtypeStruct((width, inner // 2), BF16),
+            jax.ShapeDtypeStruct((2 * rows, inner), BF16),
+            jax.ShapeDtypeStruct((2 * rows, inner), BF16),
             jax.ShapeDtypeStruct((inner, width), BF16),
         ),
-        in_specs=[SMEM_SPEC] + [VMEM_SPEC] * 3 + [HBM_SPEC, HBM_SPEC],
-        out_specs=(VMEM_SPEC,) * 5,
-        scratch_shapes=[pltpu.SemaphoreType.DMA((3,))],
+        in_specs=[SMEM_SPEC] + [VMEM_SPEC] * 6 + [HBM_SPEC],
+        out_specs=(VMEM_SPEC,) * 3,
+        scratch_shapes=[pltpu.SemaphoreType.DMA((4,))],
         compiler_params=limit(46),
         cost_estimate=pl.CostEstimate(
-            flops=4 * rows * width * inner, bytes_accessed=6 * width * inner, transcendentals=0
+            flops=8 * rows * width * inner, bytes_accessed=6 * width * inner, transcendentals=0
         ),
         name="project",
-    )(half, mine, first_key, last_key, value, w_attn_out)
-
-
-def attend_kernel(near_keys, near_values, theirs, query, allowed, first_key, last_key, first_value, last_value, w_last, out, context):
+    )(half, mine, theirs, *weights, w_attn_out)
+
+
+def attend_kernel(near_keys, near_values, mine, theirs, query, allowed, first_key, last_key, first_value, last_value, w_last, keep, give, context):
     rows, inner = near_keys.shape
-    width = out.shape[1]
+    width = keep.shape[1]
     part = inner // 2
     size = min(256, part)
+    late = jnp.concatenate([mine[...], theirs[...]], axis=0)
     near = allowed[:, :rows] > 0
     far = allowed[:, rows:] > 0
     for c in range(inner // size):
@@ -320,10 +361,8 @@
         w_key = first_key if c * size < part else last_key
         w_value = first_value if c * size < part else last_value
         local = pl.ds(c * size % part, size)
-        far_keys = jnp.dot(theirs[...], w_key[:, local], preferred_element_type=F32).astype(BF16)
-        far_values = jnp.dot(
-            theirs[...], w_value[:, local], preferred_element_type=F32
-        ).astype(BF16)
+        far_keys = jnp.dot(late, w_key[:, local], preferred_element_type=F32).astype(BF16)
+        far_values = jnp.dot(late, w_value[:, local], preferred_element_type=F32).astype(BF16)
         keys = jnp.concatenate([near_keys[:, columns], far_keys], axis=0)
         values = jnp.concatenate([near_values[:, columns], far_values], axis=0)
         for h in range(size // DH):
@@ -346,17 +385,20 @@
             context[:, place] = (summed * (1.0 / total)).astype(BF16)
     for c in range(width // 256):
         columns = pl.ds(c * 256, 256)
-        out[:, columns] = jnp.dot(context[...], w_last[:, columns], preferred_element_type=F32)
-
-
-def attend(near_keys, near_values, theirs, query, allowed, weights, w_last):
-    rows, width = theirs.shape
+        result = jnp.dot(context[...], w_last[:, columns], preferred_element_type=F32)
+        keep[:, columns] = result[: keep.shape[0]]
+        give[:, columns] = result[keep.shape[0] :]
+
+
+def attend(near_keys, near_values, mine, theirs, query, allowed, weights, w_last):
+    rows = near_keys.shape[0]
+    width = mine.shape[1]
     count, inner = query.shape
     return pl.pallas_call(
         attend_kernel,
-        out_shape=jax.ShapeDtypeStruct((count, width), F32),
-        in_specs=[VMEM_SPEC] * 10,
-        out_specs=VMEM_SPEC,
+        out_shape=(jax.ShapeDtypeStruct((count // 2, width), F32),) * 2,
+        in_specs=[VMEM_SPEC] * 11,
+        out_specs=(VMEM_SPEC, VMEM_SPEC),
         scratch_shapes=[pltpu.VMEM((count, inner), BF16)],
         compiler_params=limit(24),
         cost_estimate=pl.CostEstimate(
@@ -365,7 +407,48 @@
             transcendentals=2 * count * rows * inner // DH,
         ),
         name="attend",
-    )(near_keys, near_values, theirs, query, allowed, *weights, w_last)
+    )(near_keys, near_values, mine, theirs, query, allowed, *weights, w_last)
+
+
+def finish_kernel(index, half, parts, states, piece):
+    mp, small, _ = parts.shape
+    start = index[0] * (2 * small) + half[0] * small
+    row = lax.broadcasted_iota(jnp.int32, (small, states.shape[0]), 0)
+    column = lax.broadcasted_iota(jnp.int32, (small, states.shape[0]), 1)
+    pick = jnp.where(column == row + start, 1.0, 0.0).astype(BF16)
+    total = jnp.dot(pick, states[...], preferred_element_type=F32)
+    for k in range(mp):
+        total = total + parts[k].astype(F32)
+    piece[...] = total.astype(BF16)
+
+
+def finish(index, half, parts, states):
+    return pl.pallas_call(
+        finish_kernel,
+        out_shape=jax.ShapeDtypeStruct(parts.shape[1:], BF16),
+        in_specs=[SMEM_SPEC, SMEM_SPEC, VMEM_SPEC, VMEM_SPEC],
+        out_specs=VMEM_SPEC,
+        compiler_params=limit(8),
+        name="finish",
+    )(index, half, parts, states)
+
+
+def join_kernel(half, piece, other, out):
+    first = jnp.where(half[0] == 0, piece[...].astype(F32), other[...].astype(F32))
+    second = jnp.where(half[0] == 0, other[...].astype(F32), piece[...].astype(F32))
+    out[...] = jnp.concatenate([first, second], axis=0).astype(BF16)
+
+
+def join(half, piece, other):
+    small, width = piece.shape
+    return pl.pallas_call(
+        join_kernel,
+        out_shape=jax.ShapeDtypeStruct((2 * small, width), BF16),
+        in_specs=[SMEM_SPEC, VMEM_SPEC, VMEM_SPEC],
+        out_specs=VMEM_SPEC,
+        compiler_params=limit(8),
+        name="join",
+    )(half, piece, other)
 
 
 def per_device(
@@ -395,67 +478,48 @@
 
     half = jnp.reshape(psg_index, (1,)).astype(jnp.int32)
     index = jnp.reshape(mp_index, (1,)).astype(jnp.int32)
-    quarter = mp // 4
-    patterns = [0]
-    blocks = [tokens[None]]
-    for k in (3, 2, 1):
-        blocks.append(lax.ppermute(tokens[None], "mp", [(j, j ^ (k * quarter)) for j in range(mp)]))
-        patterns.append(k * quarter)
-    held = jnp.concatenate(blocks, axis=0)
-    step = quarter // 2
-    while step > 0:
-        got = lax.ppermute(held, "mp", [(j, j ^ step) for j in range(mp)])
-        patterns = patterns + [p ^ step for p in patterns]
-        if step > 1:
-            held = jnp.concatenate([held, got], axis=0)
-        step //= 2
+    held, got, patterns = spread_out(tokens, mp)
     first_in, last_in = stage(index, w_in, 1)
     first_out, last_out = stage(index, w_out, 0)
-    query = ask(half, answer_states, dec_gain, w_query, inner)
-    first_key, last_key, value = prepare(half, w_keyval, inner)
     partial_sums = feed(
         index, held, got, enc_gain, [first_in, last_in, first_out, last_out], patterns
     )
     parts = lax.all_to_all(partial_sums.reshape(mp, row_count, width), "mp", 0, 0)
-    encoded, spread = settle(parts, tokens, final_gain)
-    mine = lax.all_to_all(spread, "mp", 0, 0)
-    mine = mine.reshape(mp * row_count, width)
-    theirs = swap_psg(mine)
-    key_rows = 2 * mp * row_count
-
-    local = jnp.arange(key_rows, dtype=jnp.int32)
-    far = local // (mp * row_count)
-    block = (local % (mp * row_count)) // row_count
-    core = jnp.where(far == 0, psg_index, 1 - psg_index)
-    token_index = (block * psg + core) * row_count + local % row_count
-    allowed = key_mask(token_index, passage_lengths, passage_owner, answer_lengths, answer_count)
-    near_keys, near_values, first_value, last_value, w_last = project(
-        half, mine, first_key, last_key, value, w_attn_out
-    )
-    partial_answer = attend(
-        near_keys,
-        near_values,
-        theirs,
-        query,
-        allowed.astype(jnp.int32),
-        (first_key, last_key, first_value, last_value),
-        w_last,
-    )
-
+    first_key, last_key, value = prepare(half, w_keyval, inner)
+
+    runs = mp * row_count // 2
+    slots = jnp.arange(4 * runs, dtype=jnp.int32)
+    run = slots // runs
+    order = jnp.array(patterns, jnp.int32).reshape(2, 1, mp // 2, 1)
+    order = jnp.broadcast_to(order, (2, 2, mp // 2, row_count)).reshape(-1)
+    block = jnp.bitwise_xor(mp_index, order)
+    core = jnp.bitwise_xor(psg_index, run % 2)
+    token_index = (block * psg + core) * row_count + slots % row_count
     out_count = answer_count // mp
     small = out_count // psg
-    halves = partial_answer.reshape(mp, psg, small, width)
-    keep = lax.dynamic_index_in_dim(halves, psg_index, 1, False)
-    give = lax.dynamic_index_in_dim(halves, 1 - psg_index, 1, False)
-    chip_sum = (keep + swap_psg(give)).astype(jnp.bfloat16)
+    rows = jnp.arange(answer_count, dtype=jnp.int32)
+    side = jnp.bitwise_xor(psg_index, rows // (mp * small))
+    answer_index = rows // small % mp * out_count + side * small + rows % small
+    allowed = key_mask(
+        token_index, answer_index, passage_lengths, passage_owner, answer_lengths
+    ).astype(jnp.int32)
+
+    encoded, memory = settle(parts, tokens, final_gain, allowed)
+    held, got, _ = spread_out(memory, mp)
+    query, first_value, last_value = ask(half, answer_states, dec_gain, w_query, value, mp)
+    held = held.reshape(runs, width)
+    got = got.reshape(runs, width)
+    held_theirs = swap_psg(held)
+    weights = (first_key, last_key, first_value, last_value)
+    near_keys, near_values, w_last = project(half, held, held_theirs, weights, w_attn_out)
+    got_theirs = swap_psg(got)
+    keep, give = attend(
+        near_keys, near_values, got, got_theirs, query, allowed, weights, w_last
+    )
+    chip_sum = (keep + swap_psg(give)).astype(BF16).reshape(mp, small, width)
     answer_parts = lax.all_to_all(chip_sum, "mp", 0, 0)
-    own_start = mp_index * out_count + psg_index * small
-    own_answer = lax.dynamic_slice_in_dim(answer_states, own_start, small, 0).astype(jnp.float32)
-    piece = (own_answer + jnp.sum(answer_parts.astype(jnp.float32), axis=0)).astype(jnp.bfloat16)
-    other = swap_psg(piece)
-    first = jnp.where(psg_index == 0, piece, other)
-    second = jnp.where(psg_index == 0, other, piece)
-    return (encoded, jnp.concatenate([first, second], axis=0))
+    piece = finish(index, half, answer_parts, answer_states)
+    return (encoded, join(half, piece, swap_psg(piece)))
 
 
 def solution(mesh):

time: 69.1 us -> 71.1 us (1.029)
  blocking collectives: 0 us -> 11.2 us
  waiting for transfers between devices: 21.6 us -> 12.6 us
  other arithmetic: 2.5 us -> 1.76 us
    all_to_all x2 -> x0, waiting for transfers between devices: 13.5 us -> none  [the longest x1 7.73 us: per_device(): answer_parts = lax.all_to_all(chip_sum, 'mp', 0, 0)]
    all_to_all x0 -> x1, blocking collectives: none -> 11.2 us  [per_device(): answer_parts = lax.all_to_all(chip_sum, 'mp', 0, 0)]
    all_to_all x2 -> x0, starting transfers between devices: 7.92 us -> none  [the longest x1 4.55 us: per_device(): mine = lax.all_to_all(spread, 'mp', 0, 0)]
    all_to_all x1, waiting for transfers between devices: 1.37 us -> 8.03 us  [per_device(): lax.all_to_all(partial_sums.reshape(mp, row_count, width), 'mp', 0, 0)]
    ppermute x4 -> x8, starting transfers between devices: 7.37 us -> 13 us  [the longest x6 10.2 us: spread_out(): lax.ppermute(x[None], 'mp', [(j, j ^ k * quarter) for j in range(mp)])]
    ppermute x4 -> x8, waiting for transfers between devices: 4.38 us -> 1.9 us  [the longest x6 1.9 us: spread_out(): lax.ppermute(x[None], 'mp', [(j, j ^ k * quarter) for j in range(mp)])]
    all_to_all x1, starting transfers between devices: 3.41 us -> 5.68 us  [per_device(): lax.all_to_all(partial_sums.reshape(mp, row_count, width), 'mp', 0, 0)]
    concatenate x2, other arithmetic: 1.4 us -> 0.04 us  [spread_out(): held = jnp.concatenate(blocks, axis=0)]
  transfers between devices with their start and end apart: 10 -> 13, of which waited for: 7 -> 5; matrix products, arithmetic and copies ran while one was open for 1% -> 3% of each run, Pallas kernels for 26% -> 25%
where the time goes in v7:
time: 71.1 us; the launch traced here: 70.8 us
  Pallas kernels  24.7 us (35%)
  starting transfers between devices  19.4 us (27%)
  waiting for transfers between devices  12.6 us (18%)
  blocking collectives  11.2 us (16%)
  other arithmetic  1.76 us (2%)
  between operations  0.84 us (1%)
    all_to_all x1, blocking collectives, per_device(): answer_parts = lax.all_to_all(chip_sum, 'mp', 0, 0)  11.2 us
    ppermute x6, starting transfers between devices, spread_out(): lax.ppermute(x[None], 'mp', [(j, j ^ k * quarter) for j in range(mp)])  10.2 us
    all_to_all x1, waiting for transfers between devices, per_device(): lax.all_to_all(partial_sums.reshape(mp, row_count, width), 'mp', 0, 0)  8.03 us
    pallas_call x2, Pallas kernels, stage(): pl.pallas_call(functools.partial(stage_kernel, axis=axis), out_shape=(par...  7 us
    pallas_call x1, Pallas kernels, prepare(): pl.pallas_call(prepare_kernel, out_shape=(jax.ShapeDtypeStruct((width, in...  6.58 us
    all_to_all x1, starting transfers between devices, per_device(): lax.all_to_all(partial_sums.reshape(mp, row_count, width), 'mp', 0, 0)  5.68 us
    pallas_call x1, Pallas kernels, feed(): pl.pallas_call(functools.partial(feed_kernel, patterns=patterns), out_sha...  3.24 us
    ppermute x2, starting transfers between devices, spread_out(): got = lax.ppermute(held, 'mp', [(j, j ^ step) for j in range(mp)])  2.84 us
  transfers between devices with their start and end apart: 13, of which 5 were waited for; matrix products, arithmetic and copies ran while one was open for 3% of the time, Pallas kernels for 25%

profile of v7, /device:TPU:0, one launch (start us, length us, event | category | flops | bytes accessed | tf_op | source)
XLA Modules:
  0.0 70.8 jit_solution(16684128542434957154)
XLA Ops:
  0.6 5.1 %collective-permute-start = (bf16[1,16,1024]{2,1,0:T(8,128)(2,1)}, bf16[1,16,1024]{2,1,0:T(8,128)(2,1)S(1)}, u32[]{:S(2)}, u32[]{:S(2)}) collective-permute-start(bf16[1,16,1024]{2,1,0:T(8,128)(2,1)} %bitcast.16), channel_id=1, source_target_pairs={{0,12},{2,14},{4,8},{6,10},{8,4},{10,6},{12,0},{14,2},{1,13},{3,15... | collective-permute-start | bytes 98312 | tf_op jit(solution)/shard_map/ppermute | solution.py:43
  5.8 0.0 collective-permute-start.1
  5.8 0.6 collective-permute-start.2
  6.4 0.7 xor_multiply_fusion
  7.1 0.1 mul.57
  7.2 0.1 broadcast_in_dim.37
  7.2 0.1 mul.58
  7.3 0.7 %select_reduce_fusion.2 = s32[4]{0:T(128)S(1)} fusion(s32[4]{0:T(128)} %param.26), kind=kLoop, calls=%fused_computation.13 | loop fusion | flops 44 | bytes 32 | tf_op jit(solution)/shard_map/reduce_sum | solution.py:33
  8.1 0.0 copy-start.1
  8.1 3.5 %stage.2 = (bf16[1024,2048]{1,0:T(8,128)(2,1)S(1)}, bf16[1024,2048]{1,0:T(8,128)(2,1)S(1)}) custom-call(s32[1]{0:T(128)} %bitcast.after.index, bf16[1024,4096]{1,0:T(8,128)(2,1)} %whole.2), custom_call_target="tpu_custom_call" | custom-call | flops 1073741824 | bytes 16777216 | tf_op jit(solution)/shard_map/stage/pallas_call | solution.py:211
  11.6 0.0 collective-permute-done
  11.6 0.0 collective-permute-done.1
  11.7 0.0 collective-permute-done.2
  11.7 0.0 copy-done.1
  11.7 0.0 copy-start.5
  11.7 0.0 copy-start.6
  11.7 0.0 copy-start.4
  11.7 1.7 %collective-permute-start.3 = (bf16[4,16,1024]{2,1,0:T(8,128)(2,1)S(1)}, bf16[4,16,1024]{2,1,0:T(8,128)(2,1)S(1)}, u32[]{:S(2)}, u32[]{:S(2)}) collective-permute-start(bf16[4,16,1024]{2,1,0:T(8,128)(2,1)S(1)} %pad_maximum_fusion.mine), channel_id=1, source_target_pairs={{0,2},{2,0},{4,6},{6,4},{8,10},{10,8},{12,14},{14,12},{1,3},{3,1},... | collective-permute-start | bytes 393224 | tf_op jit(solution)/shard_map/ppermute | solution.py:48
  13.5 3.5 %stage.3 = (bf16[2048,1024]{1,0:T(8,128)(2,1)S(1)}, bf16[2048,1024]{1,0:T(8,128)(2,1)S(1)}) custom-call(s32[1]{0:T(128)} %bitcast.after.index, bf16[4096,1024]{1,0:T(8,128)(2,1)} %whole.3), custom_call_target="tpu_custom_call" | custom-call | flops 1073741824 | bytes 16777216 | tf_op jit(solution)/shard_map/stage/pallas_call | solution.py:211
  16.9 0.0 copy-done.5
  17.0 0.0 copy-done.6
  17.0 0.1 select_reduce_fusion.1
  17.1 0.0 collective-permute-done.3.theirs
  17.1 0.0 copy-done.4
  17.1 0.0 copy-start.2
  17.1 3.2 %feed.1 = bf16[128,1024]{1,0:T(8,128)(2,1)} custom-call(s32[1]{0:T(128)} %bitcast.after.index, bf16[4,16,1024]{2,1,0:T(8,128)(2,1)S(1)} %pad_maximum_fusion.mine, bf16[4,16,1024]{2,1,0:T(8,128)(2,1)S(1)} %collective-permute-done.3.theirs, f32[1,1024]{1,0:T(1,128)S(1)} %bitcast.26, bf16[1024,2048]{1,0:T(8,128)(2,1)S(1)} %get-tuple-element.19.refs_0_, ...), custom_call_target="tpu_custom_call" | custom-call | flops 2147483648 | bytes 16777216 | tf_op jit(solution)/shard_map/feed/pallas_call | solution.py:256
  20.3 5.7 %all-to-all-start = ((bf16[8,16,1024]{2,1,0:T(8,128)(2,1)}), bf16[8,16,1024]{2,1,0:T(8,128)(2,1)S(1)}, u32[]{:S(2)}, u32[]{:S(2)}) async-start(bf16[8,16,1024]{2,1,0:T(8,128)(2,1)} %bitcast.3), calls=%async_computation | async-start | bytes 524288 | tf_op jit(solution)/shard_map/all_to_all | solution.py:487
  26.0 0.1 convert_reduce_fusion
  26.1 0.1 and_convert_fusion.after.allowed
  26.2 8.0 %all-to-all-done.parts = bf16[8,16,1024]{2,1,0:T(8,128)(2,1)S(1)} async-done(((bf16[8,16,1024]{2,1,0:T(8,128)(2,1)}), bf16[8,16,1024]{2,1,0:T(8,128)(2,1)S(1)}, u32[]{:S(2)}, u32[]{:S(2)}) %all-to-all-start) | async-done | bytes 262176 | tf_op jit(solution)/shard_map/all_to_all | solution.py:487
  34.2 0.0 copy-done.2
  34.2 0.7 settle.1
  34.9 0.6 collective-permute-start.4
  35.4 0.9 %collective-permute-start.5 = (bf16[1,16,1024]{2,1,0:T(8,128)(2,1)S(1)}, bf16[1,16,1024]{2,1,0:T(8,128)(2,1)S(1)}, u32[]{:S(2)}, u32[]{:S(2)}) collective-permute-start(bf16[1,16,1024]{2,1,0:T(8,128)(2,1)S(1)} %bitcast.21), channel_id=1, source_target_pairs={{0,8},{2,10},{4,12},{6,14},{8,0},{10,2},{12,4},{14,6},{1,9},{3,11}... | collective-permute-start | bytes 98312 | tf_op jit(solution)/shard_map/ppermute | solution.py:43
  36.4 2.9 %collective-permute-start.6 = (bf16[1,16,1024]{2,1,0:T(8,128)(2,1)S(1)}, bf16[1,16,1024]{2,1,0:T(8,128)(2,1)S(1)}, u32[]{:S(2)}, u32[]{:S(2)}) collective-permute-start(bf16[1,16,1024]{2,1,0:T(8,128)(2,1)S(1)} %bitcast.22), channel_id=1, source_target_pairs={{0,4},{2,6},{4,0},{6,2},{8,12},{10,14},{12,8},{14,10},{1,5},{3,7},... | collective-permute-start | bytes 98312 | tf_op jit(solution)/shard_map/ppermute | solution.py:43
  39.3 1.3 %collective-permute-done.4 = bf16[1,16,1024]{2,1,0:T(8,128)(2,1)S(1)} collective-permute-done((bf16[1,16,1024]{2,1,0:T(8,128)(2,1)S(1)}, bf16[1,16,1024]{2,1,0:T(8,128)(2,1)S(1)}, u32[]{:S(2)}, u32[]{:S(2)}) %collective-permute-start.4) | collective-permute-done | bytes 32800 | tf_op jit(solution)/shard_map/ppermute | solution.py:43
  40.6 0.0 collective-permute-done.5
  40.6 0.5 collective-permute-done.6
  41.2 1.1 %collective-permute-start.8 = (bf16[4,16,1024]{2,1,0:T(8,128)(2,1)S(1)}, bf16[4,16,1024]{2,1,0:T(8,128)(2,1)S(1)}, u32[]{:S(2)}, u32[]{:S(2)}) collective-permute-start(bf16[4,16,1024]{2,1,0:T(8,128)(2,1)S(1)} %pad_maximum_fusion.1), channel_id=1, source_target_pairs={{0,2},{2,0},{4,6},{6,4},{8,10},{10,8},{12,14},{14,12},{1,3},{3,1},... | collective-permute-start | bytes 393224 | tf_op jit(solution)/shard_map/ppermute | solution.py:48
  42.3 0.0 collective-permute-start.7
  42.3 0.0 copy-start
  42.3 0.0 copy-start.3
  42.3 6.6 %prepare.1 = (bf16[1024,512]{1,0:T(8,128)(2,1)S(1)}, bf16[1024,512]{1,0:T(8,128)(2,1)S(1)}, bf16[1024,1024]{1,0:T(8,128)(2,1)}) custom-call(s32[1]{0:T(128)} %bitcast.5.half, bf16[1024,2,2048]{2,1,0:T(2,128)(2,1)} %w_keyval.1), custom_call_target="tpu_custom_call" | custom-call | flops 1073741824 | bytes 8388608 | tf_op jit(solution)/shard_map/prepare/pallas_call | solution.py:165
  48.9 0.0 collective-permute-done.8
  48.9 0.6 collective-permute-start.9
  49.5 0.0 copy-done
  49.5 0.0 copy-done.3
  49.5 2.3 %ask.1 = (bf16[128,1024]{1,0:T(8,128)(2,1)S(1)}, bf16[1024,512]{1,0:T(8,128)(2,1)S(1)}, bf16[1024,512]{1,0:T(8,128)(2,1)S(1)}) custom-call(s32[1]{0:T(128)} %bitcast.5.half, bf16[128,1024]{1,0:T(8,128)(2,1)S(1)} %copy-done, f32[1,1024]{1,0:T(1,128)S(1)} %bitcast.25, bf16[1024,2048]{1,0:T(8,128)(2,1)} %w_query.1, bf16[1024,1024]{1,0:T(8,128)(2,1)} %get-tuple-element.27.value), custom_call_target="tpu_custom_call" | custom-call | flops 1073741824 | bytes 4194304 | tf_op jit(solution)/shard_map/ask/pallas_call | solution.py:113
  51.8 0.0 collective-permute-done.7.theirs
  51.8 2.1 %project.1 = (bf16[128,1024]{1,0:T(8,128)(2,1)S(1)}, bf16[128,1024]{1,0:T(8,128)(2,1)S(1)}, bf16[1024,1024]{1,0:T(8,128)(2,1)S(1)}) custom-call(s32[1]{0:T(128)} %bitcast.5.half, bf16[64,1024]{1,0:T(8,128)(2,1)S(1)} %bitcast.13, bf16[64,1024]{1,0:T(8,128)(2,1)S(1)} %collective-permute-done.7.theirs, bf16[1024,512]{1,0:T(8,128)(2,1)S(1)} %get-tuple-element.25.first_key, ...), custom_call_target="tpu_custom_call" | custom-call | flops 536870912 | bytes 6291456 | tf_op jit(solution)/shard_map/project/pallas_call | solution.py:333
  53.9 0.0 collective-permute-done.9.theirs
  53.9 2.1 %attend.1 = (f32[64,1024]{1,0:T(8,128)S(1)}, f32[64,1024]{1,0:T(8,128)S(1)}) custom-call(bf16[128,1024]{1,0:T(8,128)(2,1)S(1)} %get-tuple-element.30.near_keys, bf16[128,1024]{1,0:T(8,128)(2,1)S(1)} %get-tuple-element.31.near_values, bf16[64,1024]{1,0:T(8,128)(2,1)S(1)} %bitcast.15, bf16[64,1024]{1,0:T(8,128)(2,1)S(1)} %collective-permute-done.9.theirs, ...), custom_call_target="tpu_custom_call" | custom-call | flops 939524096 | bytes 6291456 | tf_op jit(solution)/shard_map/attend/pallas_call | solution.py:397
  56.0 0.1 collective-permute-start.10
  56.1 1.5 %collective-permute-done.10 = f32[64,1024]{1,0:T(8,128)S(1)} collective-permute-done((f32[64,1024]{1,0:T(8,128)S(1)}, f32[64,1024]{1,0:T(8,128)S(1)}, u32[]{:S(2)}, u32[]{:S(2)}) %collective-permute-start.10) | collective-permute-done | bytes 262176 | tf_op jit(solution)/shard_map/ppermute | solution.py:57
  57.6 11.2 %all_to_all.10.parts = bf16[8,8,1024]{2,1,0:T(8,128)(2,1)S(1)} all-to-all(bf16[8,8,1024]{2,1,0:T(8,128)(2,1)S(1)} %fusion), channel_id=1, replica_groups=mesh['groups'=2,'mp'=8,'psg'=2] {'mp'}, dimensions={0} | all-to-all | bytes 262144 | tf_op jit(solution)/shard_map/all_to_all | solution.py:520
  68.8 0.2 finish.1.piece
  69.0 0.1 collective-permute-start.11
  69.0 1.2 %collective-permute-done.11.other = bf16[8,1024]{1,0:T(8,128)(2,1)S(1)} collective-permute-done((bf16[8,1024]{1,0:T(8,128)(2,1)S(1)}, bf16[8,1024]{1,0:T(8,128)(2,1)S(1)}, u32[]{:S(2)}, u32[]{:S(2)}) %collective-permute-start.11) | collective-permute-done | bytes 16416 | tf_op jit(solution)/shard_map/ppermute | solution.py:57
  70.2 0.6 join.1
  (6 shorter events, 0.1 us)
Async XLA Ops:
  0.6 11.0 %collective-permute-start = (bf16[1,16,1024]{2,1,0:T(8,128)(2,1)}, bf16[1,16,1024]{2,1,0:T(8,128)(2,1)S(1)}, u32[]{:S(2)}, u32[]{:S(2)}) collective-permute-start(bf16[1,16,1024]{2,1,0:T(8,128)(2,1)} %bitcast.16), channel_id=1, source_target_pairs={{0,12},{2,14},{4,8},{6,10},{8,4},{10,6},{12,0},{14,2},{1,13},{3,15... | collective-permute-start | bytes 98312 | tf_op jit(solution)/shard_map/ppermute | solution.py:43
  5.8 5.9 %collective-permute-start.1 = (bf16[1,16,1024]{2,1,0:T(8,128)(2,1)}, bf16[1,16,1024]{2,1,0:T(8,128)(2,1)S(1)}, u32[]{:S(2)}, u32[]{:S(2)}) collective-permute-start(bf16[1,16,1024]{2,1,0:T(8,128)(2,1)} %bitcast.17), channel_id=1, source_target_pairs={{0,8},{2,10},{4,12},{6,14},{8,0},{10,2},{12,4},{14,6},{1,9},{3,11}... | collective-permute-start | bytes 98312 | tf_op jit(solution)/shard_map/ppermute | solution.py:43
  5.8 5.9 %collective-permute-start.2 = (bf16[1,16,1024]{2,1,0:T(8,128)(2,1)}, bf16[1,16,1024]{2,1,0:T(8,128)(2,1)S(1)}, u32[]{:S(2)}, u32[]{:S(2)}) collective-permute-start(bf16[1,16,1024]{2,1,0:T(8,128)(2,1)} %bitcast.18), channel_id=1, source_target_pairs={{0,4},{2,6},{4,0},{6,2},{8,12},{10,14},{12,8},{14,10},{1,5},{3,7},... | collective-permute-start | bytes 98312 | tf_op jit(solution)/shard_map/ppermute | solution.py:43
  8.1 3.6 %copy-start.1 = (bf16[16,1024]{1,0:T(8,128)(2,1)S(1)}, bf16[16,1024]{1,0:T(8,128)(2,1)}, u32[]{:S(2)}) copy-start(bf16[16,1024]{1,0:T(8,128)(2,1)} %tokens.1) | copy-start | bytes 98308
  11.7 5.2 %copy-start.5 = (s32[16]{0:T(128)S(1)}, s32[16]{0:T(128)}, u32[]{:S(2)}) copy-start(s32[16]{0:T(128)} %param.24) | copy-start | bytes 196
  11.7 5.2 %copy-start.6 = (s32[16]{0:T(128)S(1)}, s32[16]{0:T(128)}, u32[]{:S(2)}) copy-start(s32[16]{0:T(128)} %param.25) | copy-start | bytes 196
  11.7 5.3 %copy-start.4 = (f32[1024]{0:T(1024)S(1)}, f32[1024]{0:T(1024)}, u32[]{:S(2)}) copy-start(f32[1024]{0:T(1024)} %param.15) | copy-start | bytes 12292
  11.7 5.3 %collective-permute-start.3 = (bf16[4,16,1024]{2,1,0:T(8,128)(2,1)S(1)}, bf16[4,16,1024]{2,1,0:T(8,128)(2,1)S(1)}, u32[]{:S(2)}, u32[]{:S(2)}) collective-permute-start(bf16[4,16,1024]{2,1,0:T(8,128)(2,1)S(1)} %pad_maximum_fusion.mine), channel_id=1, source_target_pairs={{0,2},{2,0},{4,6},{6,4},{8,10},{10,8},{12,14},{14,12},{1,3},{3,1},... | collective-permute-start | bytes 393224 | tf_op jit(solution)/shard_map/ppermute | solution.py:48
  17.1 17.2 %copy-start.2 = (f32[1024]{0:T(1024)S(1)}, f32[1024]{0:T(1024)}, u32[]{:S(2)}) copy-start(f32[1024]{0:T(1024)} %param.18) | copy-start | bytes 12292
  20.3 13.9 %all-to-all-start = ((bf16[8,16,1024]{2,1,0:T(8,128)(2,1)}), bf16[8,16,1024]{2,1,0:T(8,128)(2,1)S(1)}, u32[]{:S(2)}, u32[]{:S(2)}) async-start(bf16[8,16,1024]{2,1,0:T(8,128)(2,1)} %bitcast.3), calls=%async_computation | async-start | bytes 524288 | tf_op jit(solution)/shard_map/all_to_all | solution.py:487
  34.9 5.7 %collective-permute-start.4 = (bf16[1,16,1024]{2,1,0:T(8,128)(2,1)S(1)}, bf16[1,16,1024]{2,1,0:T(8,128)(2,1)S(1)}, u32[]{:S(2)}, u32[]{:S(2)}) collective-permute-start(bf16[1,16,1024]{2,1,0:T(8,128)(2,1)S(1)} %bitcast.20), channel_id=1, source_target_pairs={{0,12},{2,14},{4,8},{6,10},{8,4},{10,6},{12,0},{14,2},{1,13},{3,15... | collective-permute-start | bytes 98312 | tf_op jit(solution)/shard_map/ppermute | solution.py:43
  35.4 5.2 %collective-permute-start.5 = (bf16[1,16,1024]{2,1,0:T(8,128)(2,1)S(1)}, bf16[1,16,1024]{2,1,0:T(8,128)(2,1)S(1)}, u32[]{:S(2)}, u32[]{:S(2)}) collective-permute-start(bf16[1,16,1024]{2,1,0:T(8,128)(2,1)S(1)} %bitcast.21), channel_id=1, source_target_pairs={{0,8},{2,10},{4,12},{6,14},{8,0},{10,2},{12,4},{14,6},{1,9},{3,11}... | collective-permute-start | bytes 98312 | tf_op jit(solution)/shard_map/ppermute | solution.py:43
  36.4 4.8 %collective-permute-start.6 = (bf16[1,16,1024]{2,1,0:T(8,128)(2,1)S(1)}, bf16[1,16,1024]{2,1,0:T(8,128)(2,1)S(1)}, u32[]{:S(2)}, u32[]{:S(2)}) collective-permute-start(bf16[1,16,1024]{2,1,0:T(8,128)(2,1)S(1)} %bitcast.22), channel_id=1, source_target_pairs={{0,4},{2,6},{4,0},{6,2},{8,12},{10,14},{12,8},{14,10},{1,5},{3,7},... | collective-permute-start | bytes 98312 | tf_op jit(solution)/shard_map/ppermute | solution.py:43
  41.2 7.7 %collective-permute-start.8 = (bf16[4,16,1024]{2,1,0:T(8,128)(2,1)S(1)}, bf16[4,16,1024]{2,1,0:T(8,128)(2,1)S(1)}, u32[]{:S(2)}, u32[]{:S(2)}) collective-permute-start(bf16[4,16,1024]{2,1,0:T(8,128)(2,1)S(1)} %pad_maximum_fusion.1), channel_id=1, source_target_pairs={{0,2},{2,0},{4,6},{6,4},{8,10},{10,8},{12,14},{14,12},{1,3},{3,1},... | collective-permute-start | bytes 393224 | tf_op jit(solution)/shard_map/ppermute | solution.py:48
  42.3 9.5 %collective-permute-start.7 = (bf16[64,1024]{1,0:T(8,128)(2,1)S(1)}, bf16[64,1024]{1,0:T(8,128)(2,1)S(1)}, u32[]{:S(2)}, u32[]{:S(2)}) collective-permute-start(bf16[64,1024]{1,0:T(8,128)(2,1)S(1)} %bitcast.12), channel_id=1, source_target_pairs={{0,1},{1,0},{2,3},{3,2},{4,5},{5,4},{6,7},{7,6},{8,9},{9,8},{10,11... | collective-permute-start | bytes 393224 | tf_op jit(solution)/shard_map/ppermute | solution.py:57
  42.3 7.2 %copy-start = (bf16[128,1024]{1,0:T(8,128)(2,1)S(1)}, bf16[128,1024]{1,0:T(8,128)(2,1)}, u32[]{:S(2)}) copy-start(bf16[128,1024]{1,0:T(8,128)(2,1)} %states.3) | copy-start | bytes 786436
  42.3 7.2 %copy-start.3 = (f32[1024]{0:T(1024)S(1)}, f32[1024]{0:T(1024)}, u32[]{:S(2)}) copy-start(f32[1024]{0:T(1024)} %param.21) | copy-start | bytes 12292
  48.9 5.0 %collective-permute-start.9 = (bf16[64,1024]{1,0:T(8,128)(2,1)S(1)}, bf16[64,1024]{1,0:T(8,128)(2,1)S(1)}, u32[]{:S(2)}, u32[]{:S(2)}) collective-permute-start(bf16[64,1024]{1,0:T(8,128)(2,1)S(1)} %bitcast.14), channel_id=1, source_target_pairs={{0,1},{1,0},{2,3},{3,2},{4,5},{5,4},{6,7},{7,6},{8,9},{9,8},{10,11... | collective-permute-start | bytes 393224 | tf_op jit(solution)/shard_map/ppermute | solution.py:57
  56.0 1.6 %collective-permute-start.10 = (f32[64,1024]{1,0:T(8,128)S(1)}, f32[64,1024]{1,0:T(8,128)S(1)}, u32[]{:S(2)}, u32[]{:S(2)}) collective-permute-start(f32[64,1024]{1,0:T(8,128)S(1)} %get-tuple-element.35), channel_id=1, source_target_pairs={{0,1},{1,0},{2,3},{3,2},{4,5},{5,4},{6,7},{7,6},{8,9},{9,8},{10,11... | collective-permute-start | bytes 786440 | tf_op jit(solution)/shard_map/ppermute | solution.py:57
  69.0 1.2 %collective-permute-start.11 = (bf16[8,1024]{1,0:T(8,128)(2,1)S(1)}, bf16[8,1024]{1,0:T(8,128)(2,1)S(1)}, u32[]{:S(2)}, u32[]{:S(2)}) collective-permute-start(bf16[8,1024]{1,0:T(8,128)(2,1)S(1)} %finish.1.piece), channel_id=1, source_target_pairs={{0,1},{1,0},{2,3},{3,2},{4,5},{5,4},{6,7},{7,6},{8,9},{9,8},{10,11... | collective-permute-start | bytes 49160 | tf_op jit(solution)/shard_map/ppermute | solution.py:57

commit v8 on v7

--- a/solution.py
+++ b/solution.py
@@ -21,18 +21,36 @@
     return wide * factor * gain
 
 
-def key_mask(token_index, answer_index, passage_lengths, passage_owner, answer_lengths):
-    passage = token_index // P_SLOT
-    place = token_index % P_SLOT
-    count = passage_lengths.shape[0]
-    match = passage[:, None] == jnp.arange(count, dtype=jnp.int32)[None, :]
-    token_length = jnp.sum(jnp.where(match, passage_lengths[None, :], 0), axis=1)
-    token_owner = jnp.sum(jnp.where(match, passage_owner[None, :], 0), axis=1)
-    number = answer_lengths.shape[0]
-    order = jnp.arange(number, dtype=jnp.int32)
-    ends = jnp.sum(jnp.where(order[:, None] <= order[None, :], answer_lengths[:, None], 0), axis=0)
-    question = jnp.sum((answer_index[:, None] >= ends[None, :]).astype(jnp.int32), axis=1)
-    return (place < token_length)[None, :] & (token_owner[None, :] == question[:, None])
+def mask_rows(index, half, lengths, owners, answers, shape, patterns, mp, row_count):
+    count, keys = shape
+    psg = 2
+    slot = lax.broadcasted_iota(jnp.int32, (1, keys), 1)
+    run = lax.div(slot, keys // 4)
+    hop = lax.div(lax.rem(slot, keys // 4), row_count) + lax.div(run, 2) * (mp // 2)
+    pattern = jnp.zeros((1, keys), jnp.int32)
+    for k, value in enumerate(patterns):
+        pattern = jnp.where(hop == k, value, pattern)
+    block = index[0] ^ pattern
+    core = half[0] ^ lax.rem(run, 2)
+    token = (block * psg + core) * row_count + lax.rem(slot, row_count)
+    passage = lax.div(token, P_SLOT)
+    place = lax.rem(token, P_SLOT)
+    length = jnp.zeros((1, keys), jnp.int32)
+    owner = jnp.zeros((1, keys), jnp.int32)
+    for k in range(lengths.shape[0]):
+        length = jnp.where(passage == k, lengths[k], length)
+        owner = jnp.where(passage == k, owners[k], owner)
+    owner = jnp.where(place < length, owner, -1)
+    small = count // mp // psg
+    row = lax.broadcasted_iota(jnp.int32, (count, 1), 0)
+    side = half[0] ^ lax.div(row, mp * small)
+    answer = lax.rem(lax.div(row, small), mp) * (psg * small) + side * small + lax.rem(row, small)
+    question = jnp.zeros((count, 1), jnp.int32)
+    end = 0
+    for k in range(answers.shape[0]):
+        end = end + answers[k]
+        question = question + jnp.where(answer >= end, 1, 0)
+    return jnp.where(owner == question, 1, 0)
 
 
 def spread_out(x, mp):
@@ -131,13 +149,14 @@
     )(half, states, gain.reshape(1, width), w_query, value)
 
 
-def prepare_kernel(half, w_keyval, first_key, last_key, w_value, scr, sems):
-    inner = w_value.shape[1]
+def prepare_kernel(half, w_keyval, first_key, last_key, w_value, scr, made, sems):
+    inner = made.shape[1]
+    part = inner // 2
     blocks = scr.shape[0]
     start = pl.multiple_of(half[0] * inner, 128)
     copies = [
         pltpu.make_async_copy(
-            w_keyval.at[pl.ds(b * 128, 128), :, pl.ds(start, inner)], scr.at[b], sems.at[b]
+            w_keyval.at[pl.ds(b * 128, 128), :, pl.ds(start, inner)], scr.at[b], sems.at[0, b]
         )
         for b in range(blocks)
     ]
@@ -147,17 +166,23 @@
     column = lax.broadcasted_iota(jnp.int32, (256, 256), 1)
     source = jnp.where(row < 128, 2 * row, 2 * (row - 128) + 1)
     pick = jnp.where(column == source, 1.0, 0.0).astype(BF16)
+    size = min(256, part)
+    sent = []
     for b in range(blocks):
         rows = pl.ds(b * 128, 128)
         copies[b].wait()
-        for s in range(0, inner, 128):
-            mixed = scr[b, :, :, pl.ds(s, 128)].reshape(256, 128)
+        for s in range(0, inner, size):
+            mixed = scr[b, :, :, pl.ds(s, size)].reshape(256, size)
             apart = jnp.dot(pick, mixed, preferred_element_type=F32).astype(BF16)
-            if s < inner // 2:
-                first_key[rows, pl.ds(s, 128)] = apart[:128]
+            if s < part:
+                first_key[rows, pl.ds(s, size)] = apart[:128]
             else:
-                last_key[rows, pl.ds(s - inner // 2, 128)] = apart[:128]
-            w_value[rows, pl.ds(s, 128)] = apart[128:]
+                last_key[rows, pl.ds(s - part, size)] = apart[:128]
+            made[rows, pl.ds(s, size)] = apart[128:]
+        sent.append(pltpu.make_async_copy(made.at[rows], w_value.at[rows], sems.at[1, b]))
+        sent[-1].start()
+    for copy in sent:
+        copy.wait()
 
 
 def prepare(half, w_keyval, inner):
@@ -170,10 +195,11 @@
             jax.ShapeDtypeStruct((width, inner), BF16),
         ),
         in_specs=[SMEM_SPEC, HBM_SPEC],
-        out_specs=(VMEM_SPEC,) * 3,
+        out_specs=(VMEM_SPEC, VMEM_SPEC, HBM_SPEC),
         scratch_shapes=[
             pltpu.VMEM((width // 128, 128, 2, inner), BF16),
-            pltpu.SemaphoreType.DMA((width // 128,)),
+            pltpu.VMEM((width, inner), BF16),
+            pltpu.SemaphoreType.DMA((2, width // 128)),
         ],
         compiler_params=limit(51),
         cost_estimate=pl.CostEstimate(
@@ -270,8 +296,7 @@
     )(index, mine, theirs, gain.reshape(1, width), *weights)
 
 
-def settle_kernel(parts, tokens, gain, after, encoded, memory):
-    del after
+def settle_kernel(parts, tokens, gain, encoded, memory):
     total = tokens[...].astype(F32)
     for k in range(parts.shape[0]):
         total = total + parts[k].astype(F32)
@@ -280,7 +305,7 @@
     memory[...] = norm_rows(rounded, gain[...]).astype(BF16)
 
 
-def settle(parts, tokens, gain, after):
+def settle(parts, tokens, gain):
     _, rows, width = parts.shape
     return pl.pallas_call(
         settle_kernel,
@@ -288,14 +313,14 @@
             jax.ShapeDtypeStruct((rows, width), BF16),
             jax.ShapeDtypeStruct((rows, width), BF16),
         ),
-        in_specs=[VMEM_SPEC] * 3 + [HBM_SPEC],
+        in_specs=[VMEM_SPEC] * 3,
         out_specs=(VMEM_SPEC, VMEM_SPEC),
         compiler_params=limit(8),
         name="settle",
-    )(parts, tokens, gain.reshape(1, width), after)
-
-
-def project_kernel(half, mine, theirs, first_key, last_key, first_value, last_value, w_out, keys, values, w_last, sems):
+    )(parts, tokens, gain.reshape(1, width))
+
+
+def project_kernel(index, half, lengths, owners, answers, mine, theirs, first_key, last_key, first_value, last_value, w_out, keys, values, w_last, allowed, sems, *, patterns, mp):
     inner = keys.shape[1]
     part = inner // 2
     start = pl.multiple_of(half[0] * inner, 128)
@@ -311,6 +336,10 @@
     ]
     for copy in copies:
         copy.start()
+    row_count = 2 * mine.shape[0] // mp
+    allowed[...] = mask_rows(
+        index, half, lengths, owners, answers, allowed.shape, patterns, mp, row_count
+    )
     rows = jnp.concatenate([mine[...], theirs[...]], axis=0)
     size = min(256, part)
     for k, w_key in enumerate((first_key, last_key)):
@@ -327,25 +356,26 @@
         copy.wait()
 
 
-def project(half, mine, theirs, weights, w_attn_out):
+def project(places, tables, mine, theirs, weights, w_attn_out, patterns, count, mp):
     rows, width = mine.shape
     inner = 2 * weights[0].shape[1]
     return pl.pallas_call(
-        project_kernel,
+        functools.partial(project_kernel, patterns=patterns, mp=mp),
         out_shape=(
             jax.ShapeDtypeStruct((2 * rows, inner), BF16),
             jax.ShapeDtypeStruct((2 * rows, inner), BF16),
             jax.ShapeDtypeStruct((inner, width), BF16),
-        ),
-        in_specs=[SMEM_SPEC] + [VMEM_SPEC] * 6 + [HBM_SPEC],
-        out_specs=(VMEM_SPEC,) * 3,
+            jax.ShapeDtypeStruct((count, 4 * rows), jnp.int32),
+        ),
+        in_specs=[SMEM_SPEC] * 5 + [VMEM_SPEC] * 6 + [HBM_SPEC],
+        out_specs=(VMEM_SPEC,) * 4,
         scratch_shapes=[pltpu.SemaphoreType.DMA((4,))],
         compiler_params=limit(46),
         cost_estimate=pl.CostEstimate(
             flops=8 * rows * width * inner, bytes_accessed=6 * width * inner, transcendentals=0
         ),
         name="project",
-    )(half, mine, theirs, *weights, w_attn_out)
+    )(*places, *tables, mine, theirs, *weights, w_attn_out)
 
 
 def attend_kernel(near_keys, near_values, mine, theirs, query, allowed, first_key, last_key, first_value, last_value, w_last, keep, give, context):
@@ -488,30 +518,25 @@
     first_key, last_key, value = prepare(half, w_keyval, inner)
 
     runs = mp * row_count // 2
-    slots = jnp.arange(4 * runs, dtype=jnp.int32)
-    run = slots // runs
-    order = jnp.array(patterns, jnp.int32).reshape(2, 1, mp // 2, 1)
-    order = jnp.broadcast_to(order, (2, 2, mp // 2, row_count)).reshape(-1)
-    block = jnp.bitwise_xor(mp_index, order)
-    core = jnp.bitwise_xor(psg_index, run % 2)
-    token_index = (block * psg + core) * row_count + slots % row_count
-    out_count = answer_count // mp
-    small = out_count // psg
-    rows = jnp.arange(answer_count, dtype=jnp.int32)
-    side = jnp.bitwise_xor(psg_index, rows // (mp * small))
-    answer_index = rows // small % mp * out_count + side * small + rows % small
-    allowed = key_mask(
-        token_index, answer_index, passage_lengths, passage_owner, answer_lengths
-    ).astype(jnp.int32)
-
-    encoded, memory = settle(parts, tokens, final_gain, allowed)
+    small = answer_count // mp // psg
+    encoded, memory = settle(parts, tokens, final_gain)
     held, got, _ = spread_out(memory, mp)
     query, first_value, last_value = ask(half, answer_states, dec_gain, w_query, value, mp)
     held = held.reshape(runs, width)
     got = got.reshape(runs, width)
     held_theirs = swap_psg(held)
     weights = (first_key, last_key, first_value, last_value)
-    near_keys, near_values, w_last = project(half, held, held_theirs, weights, w_attn_out)
+    near_keys, near_values, w_last, allowed = project(
+        (index, half),
+        (passage_lengths, passage_owner, answer_lengths),
+        held,
+        held_theirs,
+        weights,
+        w_attn_out,
+        patterns,
+        answer_count,
+        mp,
+    )
     got_theirs = swap_psg(got)
     keep, give = attend(
         near_keys, near_values, got, got_theirs, query, allowed, weights, w_last

time: 71.1 us -> 69.6 us (0.979)
  blocking collectives: 11.2 us -> 22.6 us
  starting transfers between devices: 19.4 us -> 13.5 us
  waiting for transfers between devices: 12.6 us -> 8.95 us
  Pallas kernels: 24.7 us -> 22.5 us
  other arithmetic: 1.76 us -> 0.83 us
    all_to_all x0 -> x1, blocking collectives: none -> 11.3 us  [per_device(): lax.all_to_all(partial_sums.reshape(mp, row_count, width), 'mp', 0, 0)]
    all_to_all x1 -> x0, waiting for transfers between devices: 8.03 us -> none  [per_device(): lax.all_to_all(partial_sums.reshape(mp, row_count, width), 'mp', 0, 0)]
    all_to_all x1 -> x0, starting transfers between devices: 5.68 us -> none  [per_device(): lax.all_to_all(partial_sums.reshape(mp, row_count, width), 'mp', 0, 0)]
    ppermute x6, waiting for transfers between devices: 1.9 us -> 6.27 us  [spread_out(): lax.ppermute(x[None], 'mp', [(j, j ^ k * quarter) for j in range(mp)])]
    pallas_call x1, Pallas kernels: 6.58 us -> 4.7 us  [prepare(): pl.pallas_call(prepare_kernel, out_shape=(jax.ShapeDtypeStruct((width, in...]
    reduce_sum x3 -> x0, other arithmetic: 0.91 us -> none  [the longest x1 0.74 us: key_mask(): jnp.sum(jnp.where(order[:, None] <= order[None, :], answer_lengths[:, Non...]
    concatenate x2, other arithmetic: 0.04 us -> 0.8 us  [spread_out(): held = jnp.concatenate(blocks, axis=0)]
  transfers between devices with their start and end apart: 13 -> 12, of which waited for: 5 -> 6; matrix products, arithmetic and copies ran while one was open for 3% -> 0% of each run, Pallas kernels for 25% -> 24%
where the time goes in v8:
time: 69.6 us; the launch traced here: 69.3 us
  blocking collectives  22.6 us (32%)
  Pallas kernels  22.5 us (32%)
  starting transfers between devices  13.5 us (19%)
  waiting for transfers between devices  8.95 us (13%)
  other arithmetic  0.83 us (1%)
  between operations  0.83 us (1%)
    all_to_all x1, blocking collectives, per_device(): lax.all_to_all(partial_sums.reshape(mp, row_count, width), 'mp', 0, 0)  11.3 us
    all_to_all x1, blocking collectives, per_device(): answer_parts = lax.all_to_all(chip_sum, 'mp', 0, 0)  11.3 us
    ppermute x6, starting transfers between devices, spread_out(): lax.ppermute(x[None], 'mp', [(j, j ^ k * quarter) for j in range(mp)])  10.2 us
    pallas_call x2, Pallas kernels, stage(): pl.pallas_call(functools.partial(stage_kernel, axis=axis), out_shape=(par...  7.01 us
    ppermute x6, waiting for transfers between devices, spread_out(): lax.ppermute(x[None], 'mp', [(j, j ^ k * quarter) for j in range(mp)])  6.27 us
    pallas_call x1, Pallas kernels, prepare(): pl.pallas_call(prepare_kernel, out_shape=(jax.ShapeDtypeStruct((width, in...  4.7 us
    ppermute x4, waiting for transfers between devices, swap_psg(): return lax.ppermute(x, 'psg', [(0, 1), (1, 0)])  2.68 us
    ppermute x2, starting transfers between devices, spread_out(): got = lax.ppermute(held, 'mp', [(j, j ^ step) for j in range(mp)])  2.58 us
  transfers between devices with their start and end apart: 12, of which 6 were waited for; matrix products, arithmetic and copies ran while one was open for 0% of the time, Pallas kernels for 24%

profile of v8, /device:TPU:0, one launch (start us, length us, event | category | flops | bytes accessed | tf_op | source)
XLA Modules:
  0.0 69.3 jit_solution(10589791394698273917)
XLA Ops:
  0.6 5.1 %collective-permute-start = (bf16[1,16,1024]{2,1,0:T(8,128)(2,1)}, bf16[1,16,1024]{2,1,0:T(8,128)(2,1)S(1)}, u32[]{:S(2)}, u32[]{:S(2)}) collective-permute-start(bf16[1,16,1024]{2,1,0:T(8,128)(2,1)} %bitcast.17), channel_id=1, source_target_pairs={{0,12},{2,14},{4,8},{6,10},{8,4},{10,6},{12,0},{14,2},{1,13},{3,15... | collective-permute-start | bytes 98312 | tf_op jit(solution)/shard_map/ppermute | solution.py:61
  5.8 0.0 collective-permute-start.1
  5.8 0.6 collective-permute-start.2
  6.4 1.5 %collective-permute-done = bf16[1,16,1024]{2,1,0:T(8,128)(2,1)S(1)} collective-permute-done((bf16[1,16,1024]{2,1,0:T(8,128)(2,1)}, bf16[1,16,1024]{2,1,0:T(8,128)(2,1)S(1)}, u32[]{:S(2)}, u32[]{:S(2)}) %collective-permute-start) | collective-permute-done | bytes 32800 | tf_op jit(solution)/shard_map/ppermute | solution.py:61
  7.9 2.9 %collective-permute-done.1 = bf16[1,16,1024]{2,1,0:T(8,128)(2,1)S(1)} collective-permute-done((bf16[1,16,1024]{2,1,0:T(8,128)(2,1)}, bf16[1,16,1024]{2,1,0:T(8,128)(2,1)S(1)}, u32[]{:S(2)}, u32[]{:S(2)}) %collective-permute-start.1) | collective-permute-done | bytes 32800 | tf_op jit(solution)/shard_map/ppermute | solution.py:61
  10.8 0.0 collective-permute-done.2
  10.8 0.8 %pad_maximum_fusion.mine = bf16[4,16,1024]{2,1,0:T(8,128)(2,1)S(1)} fusion(bf16[1,16,1024]{2,1,0:T(8,128)(2,1)S(1)} %collective-permute-done.2, bf16[1,16,1024]{2,1,0:T(8,128)(2,1)S(1)} %collective-permute-done.1, bf16[1,16,1024]{2,1,0:T(8,128)(2,1)S(1)} %collective-permute-done, bf16[1,16,1024]{2,1,0:T(8,128)(2,1)} %bitcast.20), kind=kLoop, calls=%fused_computation.2 | loop fusion | flops 196608 | bytes 262144 | tf_op jit(solution)/shard_map/concatenate | solution.py:63
  11.6 1.6 %collective-permute-start.3 = (bf16[4,16,1024]{2,1,0:T(8,128)(2,1)S(1)}, bf16[4,16,1024]{2,1,0:T(8,128)(2,1)S(1)}, u32[]{:S(2)}, u32[]{:S(2)}) collective-permute-start(bf16[4,16,1024]{2,1,0:T(8,128)(2,1)S(1)} %pad_maximum_fusion.mine), channel_id=1, source_target_pairs={{0,2},{2,0},{4,6},{6,4},{8,10},{10,8},{12,14},{14,12},{1,3},{3,1},... | collective-permute-start | bytes 393224 | tf_op jit(solution)/shard_map/ppermute | solution.py:66
  13.2 3.5 %stage.2 = (bf16[1024,2048]{1,0:T(8,128)(2,1)S(1)}, bf16[1024,2048]{1,0:T(8,128)(2,1)S(1)}) custom-call(s32[1]{0:T(128)} %bitcast.after.index, bf16[1024,4096]{1,0:T(8,128)(2,1)} %whole.2), custom_call_target="tpu_custom_call" | custom-call | flops 1073741824 | bytes 16777216 | tf_op jit(solution)/shard_map/stage/pallas_call | solution.py:237
  16.7 0.0 copy-start.4
  16.7 3.5 %stage.3 = (bf16[2048,1024]{1,0:T(8,128)(2,1)S(1)}, bf16[2048,1024]{1,0:T(8,128)(2,1)S(1)}) custom-call(s32[1]{0:T(128)} %bitcast.after.index, bf16[4096,1024]{1,0:T(8,128)(2,1)} %whole.3), custom_call_target="tpu_custom_call" | custom-call | flops 1073741824 | bytes 16777216 | tf_op jit(solution)/shard_map/stage/pallas_call | solution.py:237
  20.2 0.0 collective-permute-done.3.theirs
  20.2 0.0 copy-done.4
  20.2 0.0 copy-start.1
  20.2 0.0 copy-start.2
  20.2 2.5 %feed.1 = bf16[128,1024]{1,0:T(8,128)(2,1)S(1)} custom-call(s32[1]{0:T(128)} %bitcast.after.index, bf16[4,16,1024]{2,1,0:T(8,128)(2,1)S(1)} %pad_maximum_fusion.mine, bf16[4,16,1024]{2,1,0:T(8,128)(2,1)S(1)} %collective-permute-done.3.theirs, f32[1,1024]{1,0:T(1,128)S(1)} %bitcast.27, bf16[1024,2048]{1,0:T(8,128)(2,1)S(1)} %get-tuple-element.20.refs_0_, ...), custom_call_target="tpu_custom_call" | custom-call | flops 2147483648 | bytes 16777216 | tf_op jit(solution)/shard_map/feed/pallas_call | solution.py:282
  22.8 11.3 %all_to_all.10.parts = bf16[8,16,1024]{2,1,0:T(8,128)(2,1)S(1)} all-to-all(bf16[8,16,1024]{2,1,0:T(8,128)(2,1)S(1)} %bitcast.12), channel_id=1, replica_groups=mesh['groups'=2,'mp'=8,'psg'=2] {'mp'}, dimensions={0} | all-to-all | bytes 524288 | tf_op jit(solution)/shard_map/all_to_all | solution.py:517
  34.1 0.0 copy-done.1
  34.1 0.0 copy-done.2
  34.1 0.7 settle.1
  34.8 0.6 collective-permute-start.4
  35.3 0.9 %collective-permute-start.5 = (bf16[1,16,1024]{2,1,0:T(8,128)(2,1)S(1)}, bf16[1,16,1024]{2,1,0:T(8,128)(2,1)S(1)}, u32[]{:S(2)}, u32[]{:S(2)}) collective-permute-start(bf16[1,16,1024]{2,1,0:T(8,128)(2,1)S(1)} %bitcast.22), channel_id=1, source_target_pairs={{0,8},{2,10},{4,12},{6,14},{8,0},{10,2},{12,4},{14,6},{1,9},{3,11}... | collective-permute-start | bytes 98312 | tf_op jit(solution)/shard_map/ppermute | solution.py:61
  36.2 2.9 %collective-permute-start.6 = (bf16[1,16,1024]{2,1,0:T(8,128)(2,1)S(1)}, bf16[1,16,1024]{2,1,0:T(8,128)(2,1)S(1)}, u32[]{:S(2)}, u32[]{:S(2)}) collective-permute-start(bf16[1,16,1024]{2,1,0:T(8,128)(2,1)S(1)} %bitcast.23), channel_id=1, source_target_pairs={{0,4},{2,6},{4,0},{6,2},{8,12},{10,14},{12,8},{14,10},{1,5},{3,7},... | collective-permute-start | bytes 98312 | tf_op jit(solution)/shard_map/ppermute | solution.py:61
  39.2 1.3 %collective-permute-done.4 = bf16[1,16,1024]{2,1,0:T(8,128)(2,1)S(1)} collective-permute-done((bf16[1,16,1024]{2,1,0:T(8,128)(2,1)S(1)}, bf16[1,16,1024]{2,1,0:T(8,128)(2,1)S(1)}, u32[]{:S(2)}, u32[]{:S(2)}) %collective-permute-start.4) | collective-permute-done | bytes 32800 | tf_op jit(solution)/shard_map/ppermute | solution.py:61
  40.5 0.0 collective-permute-done.5
  40.5 0.5 collective-permute-done.6
  41.1 1.0 %collective-permute-start.8 = (bf16[4,16,1024]{2,1,0:T(8,128)(2,1)S(1)}, bf16[4,16,1024]{2,1,0:T(8,128)(2,1)S(1)}, u32[]{:S(2)}, u32[]{:S(2)}) collective-permute-start(bf16[4,16,1024]{2,1,0:T(8,128)(2,1)S(1)} %pad_maximum_fusion.1), channel_id=1, source_target_pairs={{0,2},{2,0},{4,6},{6,4},{8,10},{10,8},{12,14},{14,12},{1,3},{3,1},... | collective-permute-start | bytes 393224 | tf_op jit(solution)/shard_map/ppermute | solution.py:66
  42.1 0.0 collective-permute-start.7
  42.1 0.0 copy-start
  42.1 0.0 copy-start.3
  42.1 4.7 %prepare.1 = (bf16[1024,512]{1,0:T(8,128)(2,1)S(1)}, bf16[1024,512]{1,0:T(8,128)(2,1)S(1)}, bf16[1024,1024]{1,0:T(8,128)(2,1)}) custom-call(s32[1]{0:T(128)} %bitcast.5.half, bf16[1024,2,2048]{2,1,0:T(2,128)(2,1)} %w_keyval.1), custom_call_target="tpu_custom_call" | custom-call | flops 1073741824 | bytes 8388608 | tf_op jit(solution)/shard_map/prepare/pallas_call | solution.py:190
  46.8 0.0 copy-start.5
  46.8 0.0 copy-start.6
  46.8 0.0 copy-start.7
  46.8 0.0 collective-permute-done.8
  46.8 0.6 collective-permute-start.9
  47.4 0.0 copy-done
  47.4 0.0 copy-done.3
  47.4 2.3 %ask.1 = (bf16[128,1024]{1,0:T(8,128)(2,1)S(1)}, bf16[1024,512]{1,0:T(8,128)(2,1)S(1)}, bf16[1024,512]{1,0:T(8,128)(2,1)S(1)}) custom-call(s32[1]{0:T(128)} %bitcast.5.half, bf16[128,1024]{1,0:T(8,128)(2,1)S(1)} %copy-done, f32[1,1024]{1,0:T(1,128)S(1)} %bitcast.26, bf16[1024,2048]{1,0:T(8,128)(2,1)} %w_query.1, bf16[1024,1024]{1,0:T(8,128)(2,1)} %get-tuple-element.28.value), custom_call_target="tpu_custom_call" | custom-call | flops 1073741824 | bytes 4194304 | tf_op jit(solution)/shard_map/ask/pallas_call | solution.py:131
  49.7 0.0 collective-permute-done.7.theirs
  49.7 0.0 copy-done.5
  49.7 0.0 copy-done.6
  49.7 0.0 copy-done.7
  49.7 2.5 %project.1 = (bf16[128,1024]{1,0:T(8,128)(2,1)S(1)}, bf16[128,1024]{1,0:T(8,128)(2,1)S(1)}, bf16[1024,1024]{1,0:T(8,128)(2,1)S(1)}, s32[128,256]{1,0:T(8,128)S(1)}) custom-call(s32[1]{0:T(128)} %bitcast.after.index, s32[1]{0:T(128)} %bitcast.5.half, s32[16]{0:T(128)S(1)} %copy-done.5, s32[16]{0:T(128)S(1)} %copy-done.6, s32[4]{0:T(128)S(1)} %copy-done.7, ...), custom_call_target="tpu_custom_call" | custom-call | flops 536870912 | bytes 6291456 | tf_op jit(solution)/shard_map/project/pallas_call | solution.py:362
  52.3 0.0 collective-permute-done.9.theirs
  52.3 2.1 %attend.1 = (f32[64,1024]{1,0:T(8,128)S(1)}, f32[64,1024]{1,0:T(8,128)S(1)}) custom-call(bf16[128,1024]{1,0:T(8,128)(2,1)S(1)} %get-tuple-element.31.near_keys, bf16[128,1024]{1,0:T(8,128)(2,1)S(1)} %get-tuple-element.32.near_values, bf16[64,1024]{1,0:T(8,128)(2,1)S(1)} %bitcast.16, bf16[64,1024]{1,0:T(8,128)(2,1)S(1)} %collective-permute-done.9.theirs, ...), custom_call_target="tpu_custom_call" | custom-call | flops 939524096 | bytes 6291456 | tf_op jit(solution)/shard_map/attend/pallas_call | solution.py:427
  54.3 0.1 collective-permute-start.10
  54.4 1.5 %collective-permute-done.10 = f32[64,1024]{1,0:T(8,128)S(1)} collective-permute-done((f32[64,1024]{1,0:T(8,128)S(1)}, f32[64,1024]{1,0:T(8,128)S(1)}, u32[]{:S(2)}, u32[]{:S(2)}) %collective-permute-start.10) | collective-permute-done | bytes 262176 | tf_op jit(solution)/shard_map/ppermute | solution.py:75
  56.0 11.3 %all_to_all.11.parts = bf16[8,8,1024]{2,1,0:T(8,128)(2,1)S(1)} all-to-all(bf16[8,8,1024]{2,1,0:T(8,128)(2,1)S(1)} %fusion), channel_id=1, replica_groups=mesh['groups'=2,'mp'=8,'psg'=2] {'mp'}, dimensions={0} | all-to-all | bytes 262144 | tf_op jit(solution)/shard_map/all_to_all | solution.py:545
  67.3 0.2 finish.1.piece
  67.5 0.1 collective-permute-start.11
  67.5 1.2 %collective-permute-done.11.other = bf16[8,1024]{1,0:T(8,128)(2,1)S(1)} collective-permute-done((bf16[8,1024]{1,0:T(8,128)(2,1)S(1)}, bf16[8,1024]{1,0:T(8,128)(2,1)S(1)}, u32[]{:S(2)}, u32[]{:S(2)}) %collective-permute-start.11) | collective-permute-done | bytes 16416 | tf_op jit(solution)/shard_map/ppermute | solution.py:75
  68.7 0.6 join.1
  (2 shorter events, 0.1 us)
Async XLA Ops:
  0.6 7.2 %collective-permute-start = (bf16[1,16,1024]{2,1,0:T(8,128)(2,1)}, bf16[1,16,1024]{2,1,0:T(8,128)(2,1)S(1)}, u32[]{:S(2)}, u32[]{:S(2)}) collective-permute-start(bf16[1,16,1024]{2,1,0:T(8,128)(2,1)} %bitcast.17), channel_id=1, source_target_pairs={{0,12},{2,14},{4,8},{6,10},{8,4},{10,6},{12,0},{14,2},{1,13},{3,15... | collective-permute-start | bytes 98312 | tf_op jit(solution)/shard_map/ppermute | solution.py:61
  5.8 5.0 %collective-permute-start.1 = (bf16[1,16,1024]{2,1,0:T(8,128)(2,1)}, bf16[1,16,1024]{2,1,0:T(8,128)(2,1)S(1)}, u32[]{:S(2)}, u32[]{:S(2)}) collective-permute-start(bf16[1,16,1024]{2,1,0:T(8,128)(2,1)} %bitcast.18), channel_id=1, source_target_pairs={{0,8},{2,10},{4,12},{6,14},{8,0},{10,2},{12,4},{14,6},{1,9},{3,11}... | collective-permute-start | bytes 98312 | tf_op jit(solution)/shard_map/ppermute | solution.py:61
  5.8 5.0 %collective-permute-start.2 = (bf16[1,16,1024]{2,1,0:T(8,128)(2,1)}, bf16[1,16,1024]{2,1,0:T(8,128)(2,1)S(1)}, u32[]{:S(2)}, u32[]{:S(2)}) collective-permute-start(bf16[1,16,1024]{2,1,0:T(8,128)(2,1)} %bitcast.19), channel_id=1, source_target_pairs={{0,4},{2,6},{4,0},{6,2},{8,12},{10,14},{12,8},{14,10},{1,5},{3,7},... | collective-permute-start | bytes 98312 | tf_op jit(solution)/shard_map/ppermute | solution.py:61
  11.6 8.6 %collective-permute-start.3 = (bf16[4,16,1024]{2,1,0:T(8,128)(2,1)S(1)}, bf16[4,16,1024]{2,1,0:T(8,128)(2,1)S(1)}, u32[]{:S(2)}, u32[]{:S(2)}) collective-permute-start(bf16[4,16,1024]{2,1,0:T(8,128)(2,1)S(1)} %pad_maximum_fusion.mine), channel_id=1, source_target_pairs={{0,2},{2,0},{4,6},{6,4},{8,10},{10,8},{12,14},{14,12},{1,3},{3,1},... | collective-permute-start | bytes 393224 | tf_op jit(solution)/shard_map/ppermute | solution.py:66
  16.7 3.5 %copy-start.4 = (f32[1024]{0:T(1024)S(1)}, f32[1024]{0:T(1024)}, u32[]{:S(2)}) copy-start(f32[1024]{0:T(1024)} %param.14) | copy-start | bytes 12292
  20.2 13.9 %copy-start.1 = (bf16[16,1024]{1,0:T(8,128)(2,1)S(1)}, bf16[16,1024]{1,0:T(8,128)(2,1)}, u32[]{:S(2)}) copy-start(bf16[16,1024]{1,0:T(8,128)(2,1)} %tokens.1) | copy-start | bytes 98308
  20.2 13.9 %copy-start.2 = (f32[1024]{0:T(1024)S(1)}, f32[1024]{0:T(1024)}, u32[]{:S(2)}) copy-start(f32[1024]{0:T(1024)} %param.17) | copy-start | bytes 12292
  34.8 5.7 %collective-permute-start.4 = (bf16[1,16,1024]{2,1,0:T(8,128)(2,1)S(1)}, bf16[1,16,1024]{2,1,0:T(8,128)(2,1)S(1)}, u32[]{:S(2)}, u32[]{:S(2)}) collective-permute-start(bf16[1,16,1024]{2,1,0:T(8,128)(2,1)S(1)} %bitcast.21), channel_id=1, source_target_pairs={{0,12},{2,14},{4,8},{6,10},{8,4},{10,6},{12,0},{14,2},{1,13},{3,15... | collective-permute-start | bytes 98312 | tf_op jit(solution)/shard_map/ppermute | solution.py:61
  35.3 5.2 %collective-permute-start.5 = (bf16[1,16,1024]{2,1,0:T(8,128)(2,1)S(1)}, bf16[1,16,1024]{2,1,0:T(8,128)(2,1)S(1)}, u32[]{:S(2)}, u32[]{:S(2)}) collective-permute-start(bf16[1,16,1024]{2,1,0:T(8,128)(2,1)S(1)} %bitcast.22), channel_id=1, source_target_pairs={{0,8},{2,10},{4,12},{6,14},{8,0},{10,2},{12,4},{14,6},{1,9},{3,11}... | collective-permute-start | bytes 98312 | tf_op jit(solution)/shard_map/ppermute | solution.py:61
  36.2 4.8 %collective-permute-start.6 = (bf16[1,16,1024]{2,1,0:T(8,128)(2,1)S(1)}, bf16[1,16,1024]{2,1,0:T(8,128)(2,1)S(1)}, u32[]{:S(2)}, u32[]{:S(2)}) collective-permute-start(bf16[1,16,1024]{2,1,0:T(8,128)(2,1)S(1)} %bitcast.23), channel_id=1, source_target_pairs={{0,4},{2,6},{4,0},{6,2},{8,12},{10,14},{12,8},{14,10},{1,5},{3,7},... | collective-permute-start | bytes 98312 | tf_op jit(solution)/shard_map/ppermute | solution.py:61
  41.1 5.7 %collective-permute-start.8 = (bf16[4,16,1024]{2,1,0:T(8,128)(2,1)S(1)}, bf16[4,16,1024]{2,1,0:T(8,128)(2,1)S(1)}, u32[]{:S(2)}, u32[]{:S(2)}) collective-permute-start(bf16[4,16,1024]{2,1,0:T(8,128)(2,1)S(1)} %pad_maximum_fusion.1), channel_id=1, source_target_pairs={{0,2},{2,0},{4,6},{6,4},{8,10},{10,8},{12,14},{14,12},{1,3},{3,1},... | collective-permute-start | bytes 393224 | tf_op jit(solution)/shard_map/ppermute | solution.py:66
  42.1 7.6 %collective-permute-start.7 = (bf16[64,1024]{1,0:T(8,128)(2,1)S(1)}, bf16[64,1024]{1,0:T(8,128)(2,1)S(1)}, u32[]{:S(2)}, u32[]{:S(2)}) collective-permute-start(bf16[64,1024]{1,0:T(8,128)(2,1)S(1)} %bitcast.13), channel_id=1, source_target_pairs={{0,1},{1,0},{2,3},{3,2},{4,5},{5,4},{6,7},{7,6},{8,9},{9,8},{10,11... | collective-permute-start | bytes 393224 | tf_op jit(solution)/shard_map/ppermute | solution.py:75
  42.1 5.3 %copy-start = (bf16[128,1024]{1,0:T(8,128)(2,1)S(1)}, bf16[128,1024]{1,0:T(8,128)(2,1)}, u32[]{:S(2)}) copy-start(bf16[128,1024]{1,0:T(8,128)(2,1)} %states.3) | copy-start | bytes 786436
  42.1 5.3 %copy-start.3 = (f32[1024]{0:T(1024)S(1)}, f32[1024]{0:T(1024)}, u32[]{:S(2)}) copy-start(f32[1024]{0:T(1024)} %param.20) | copy-start | bytes 12292
  46.8 2.9 %copy-start.5 = (s32[16]{0:T(128)S(1)}, s32[16]{0:T(128)}, u32[]{:S(2)}) copy-start(s32[16]{0:T(128)} %lengths.1) | copy-start | bytes 196
  46.8 2.9 %copy-start.6 = (s32[16]{0:T(128)S(1)}, s32[16]{0:T(128)}, u32[]{:S(2)}) copy-start(s32[16]{0:T(128)} %owners.1) | copy-start | bytes 196
  46.8 2.9 %copy-start.7 = (s32[4]{0:T(128)S(1)}, s32[4]{0:T(128)}, u32[]{:S(2)}) copy-start(s32[4]{0:T(128)} %answers.1) | copy-start | bytes 52
  46.8 5.4 %collective-permute-start.9 = (bf16[64,1024]{1,0:T(8,128)(2,1)S(1)}, bf16[64,1024]{1,0:T(8,128)(2,1)S(1)}, u32[]{:S(2)}, u32[]{:S(2)}) collective-permute-start(bf16[64,1024]{1,0:T(8,128)(2,1)S(1)} %bitcast.15), channel_id=1, source_target_pairs={{0,1},{1,0},{2,3},{3,2},{4,5},{5,4},{6,7},{7,6},{8,9},{9,8},{10,11... | collective-permute-start | bytes 393224 | tf_op jit(solution)/shard_map/ppermute | solution.py:75
  54.3 1.6 %collective-permute-start.10 = (f32[64,1024]{1,0:T(8,128)S(1)}, f32[64,1024]{1,0:T(8,128)S(1)}, u32[]{:S(2)}, u32[]{:S(2)}) collective-permute-start(f32[64,1024]{1,0:T(8,128)S(1)} %get-tuple-element.37), channel_id=1, source_target_pairs={{0,1},{1,0},{2,3},{3,2},{4,5},{5,4},{6,7},{7,6},{8,9},{9,8},{10,11... | collective-permute-start | bytes 786440 | tf_op jit(solution)/shard_map/ppermute | solution.py:75
  67.5 1.2 %collective-permute-start.11 = (bf16[8,1024]{1,0:T(8,128)(2,1)S(1)}, bf16[8,1024]{1,0:T(8,128)(2,1)S(1)}, u32[]{:S(2)}, u32[]{:S(2)}) collective-permute-start(bf16[8,1024]{1,0:T(8,128)(2,1)S(1)} %finish.1.piece), channel_id=1, source_target_pairs={{0,1},{1,0},{2,3},{3,2},{4,5},{5,4},{6,7},{7,6},{8,9},{9,8},{10,11... | collective-permute-start | bytes 49160 | tf_op jit(solution)/shard_map/ppermute | solution.py:75

commit v9 on v8

--- a/solution.py
+++ b/solution.py
@@ -86,7 +86,7 @@
     return pltpu.CompilerParams(vmem_limit_bytes=mib << 20)
 
 
-def ask_kernel(half, states, gain, w_query, value, query, first_value, last_value, scr, sems, *, mp):
+def ask_kernel(half, states, gain, settled, w_query, value, query, first_value, last_value, encoded, scr, sems, *, mp):
     inner = query.shape[1]
     part = first_value.shape[1]
     size = scr.shape[2]
@@ -107,6 +107,7 @@
     for copy in copies + others:
         copy.start()
     normed = norm_rows(states[...], gain[...]).astype(BF16)
+    encoded[...] = settled[...]
     count = states.shape[0]
     small = count // mp // 2
     row = lax.broadcasted_iota(jnp.int32, (count, count), 0)
@@ -124,7 +125,7 @@
         copy.wait()
 
 
-def ask(half, states, gain, w_query, value, mp):
+def ask(half, states, gain, settled, w_query, value, mp):
     count, width = states.shape
     inner = value.shape[1]
     size = min(256, inner)
@@ -134,9 +135,10 @@
             jax.ShapeDtypeStruct((count, inner), BF16),
             jax.ShapeDtypeStruct((width, inner // 2), BF16),
             jax.ShapeDtypeStruct((width, inner // 2), BF16),
-        ),
-        in_specs=[SMEM_SPEC, VMEM_SPEC, VMEM_SPEC, HBM_SPEC, HBM_SPEC],
-        out_specs=(VMEM_SPEC,) * 3,
+            jax.ShapeDtypeStruct(settled.shape, BF16),
+        ),
+        in_specs=[SMEM_SPEC] + [VMEM_SPEC] * 3 + [HBM_SPEC, HBM_SPEC],
+        out_specs=(VMEM_SPEC,) * 4,
         scratch_shapes=[
             pltpu.VMEM((inner // size, width, size), BF16),
             pltpu.SemaphoreType.DMA((inner // size + 2,)),
@@ -146,7 +148,7 @@
             flops=1 << 30, bytes_accessed=4 * width * inner, transcendentals=0
         ),
         name="ask",
-    )(half, states, gain.reshape(1, width), w_query, value)
+    )(half, states, gain.reshape(1, width), settled, w_query, value)
 
 
 def prepare_kernel(half, w_keyval, first_key, last_key, w_value, scr, made, sems):
@@ -248,6 +250,46 @@
     )(after, whole)
 
 
+def stage_rows_kernel(after, whole, rows, gain, first, last, normed, sems):
+    del after
+    size = first.shape[0]
+    number = sems.shape[0] // 2
+    step = size // number
+    copies = []
+    for half, out in enumerate((first, last)):
+        for k in range(number):
+            copies.append(
+                pltpu.make_async_copy(
+                    whole.at[pl.ds(half * size + k * step, step)],
+                    out.at[pl.ds(k * step, step)],
+                    sems.at[half * number + k],
+                )
+            )
+    for copy in copies:
+        copy.start()
+    for k in range(rows.shape[0]):
+        normed[k] = norm_rows(rows[k], gain[...]).astype(BF16)
+    for copy in copies:
+        copy.wait()
+
+
+def stage_rows(after, whole, rows, gain):
+    units, width = whole.shape
+    part = jax.ShapeDtypeStruct((units // 2, width), BF16)
+    return pl.pallas_call(
+        stage_rows_kernel,
+        out_shape=(part, part, jax.ShapeDtypeStruct(rows.shape, BF16)),
+        in_specs=[SMEM_SPEC, HBM_SPEC, VMEM_SPEC, VMEM_SPEC],
+        out_specs=(VMEM_SPEC,) * 3,
+        scratch_shapes=[pltpu.SemaphoreType.DMA((8,))],
+        compiler_params=limit(42),
+        cost_estimate=pl.CostEstimate(
+            flops=1 << 30, bytes_accessed=4 * units * width, transcendentals=0
+        ),
+        name="stage_rows",
+    )(after, whole, rows, gain.reshape(1, width))
+
+
 def feed_kernel(index, mine, theirs, gain, *refs, patterns):
     *weights, out, normed, hidden = refs
     half = len(weights) // 2
@@ -257,8 +299,10 @@
     weight = gain[...]
     for k in range(2 * pairs):
         place = pl.multiple_of((index[0] ^ patterns[k]) * rows, rows)
-        states = mine[k] if k < pairs else theirs[k - pairs]
-        normed[pl.ds(place, rows)] = norm_rows(states, weight).astype(BF16)
+        if k < pairs:
+            normed[pl.ds(place, rows)] = mine[k]
+        else:
+            normed[pl.ds(place, rows)] = norm_rows(theirs[k - pairs], weight).astype(BF16)
     for part in range(half):
         for c in range(units // size):
             columns = pl.ds(c * size, size)
@@ -510,7 +554,7 @@
     index = jnp.reshape(mp_index, (1,)).astype(jnp.int32)
     held, got, patterns = spread_out(tokens, mp)
     first_in, last_in = stage(index, w_in, 1)
-    first_out, last_out = stage(index, w_out, 0)
+    first_out, last_out, held = stage_rows(index, w_out, held, enc_gain)
     partial_sums = feed(
         index, held, got, enc_gain, [first_in, last_in, first_out, last_out], patterns
     )
@@ -519,9 +563,11 @@
 
     runs = mp * row_count // 2
     small = answer_count // mp // psg
-    encoded, memory = settle(parts, tokens, final_gain)
+    settled, memory = settle(parts, tokens, final_gain)
     held, got, _ = spread_out(memory, mp)
-    query, first_value, last_value = ask(half, answer_states, dec_gain, w_query, value, mp)
+    query, first_value, last_value, encoded = ask(
+        half, answer_states, dec_gain, settled, w_query, value, mp
+    )
     held = held.reshape(runs, width)
     got = got.reshape(runs, width)
     held_theirs = swap_psg(held)

time: 69.6 us -> 69.8 us (level)
    pallas_call x0 -> x1, Pallas kernels: none -> 3.48 us  [stage_rows(): pl.pallas_call(stage_rows_kernel, out_shape=(part, part, jax.ShapeDtypeSt...]
    pallas_call x2 -> x1, Pallas kernels: 7.01 us -> 3.54 us  [stage(): pl.pallas_call(functools.partial(stage_kernel, axis=axis), out_shape=(par...]
  transfers between devices with their start and end apart: 12 -> 12, of which waited for: 6 -> 6; matrix products, arithmetic and copies ran while one was open for 0% -> 0% of each run, Pallas kernels for 24% -> 25%
where the time goes in v9:
time: 69.8 us; the launch traced here: 69.5 us
  Pallas kernels  22.7 us (33%)
  blocking collectives  22.5 us (32%)
  starting transfers between devices  13.7 us (20%)
  waiting for transfers between devices  8.96 us (13%)
  other arithmetic  0.83 us (1%)
  between operations  0.83 us (1%)
    all_to_all x1, blocking collectives, per_device(): lax.all_to_all(partial_sums.reshape(mp, row_count, width), 'mp', 0, 0)  11.3 us
    all_to_all x1, blocking collectives, per_device(): answer_parts = lax.all_to_all(chip_sum, 'mp', 0, 0)  11.2 us
    ppermute x6, starting transfers between devices, spread_out(): lax.ppermute(x[None], 'mp', [(j, j ^ k * quarter) for j in range(mp)])  10.2 us
    ppermute x6, waiting for transfers between devices, spread_out(): lax.ppermute(x[None], 'mp', [(j, j ^ k * quarter) for j in range(mp)])  6.27 us
    pallas_call x1, Pallas kernels, prepare(): pl.pallas_call(prepare_kernel, out_shape=(jax.ShapeDtypeStruct((width, in...  4.7 us
    pallas_call x1, Pallas kernels, stage(): pl.pallas_call(functools.partial(stage_kernel, axis=axis), out_shape=(par...  3.54 us
    pallas_call x1, Pallas kernels, stage_rows(): pl.pallas_call(stage_rows_kernel, out_shape=(part, part, jax.ShapeDtypeSt...  3.48 us
    pallas_call x1, Pallas kernels, ask(): pl.pallas_call(functools.partial(ask_kernel, mp=mp), out_shape=(jax.Shape...  2.95 us
  transfers between devices with their start and end apart: 12, of which 6 were waited for; matrix products, arithmetic and copies ran while one was open for 0% of the time, Pallas kernels for 25%

profile of v9, /device:TPU:0, one launch (start us, length us, event | category | flops | bytes accessed | tf_op | source)
XLA Modules:
  0.0 69.5 jit_solution(3733199507684477184)
XLA Ops:
  0.6 5.1 %collective-permute-start = (bf16[1,16,1024]{2,1,0:T(8,128)(2,1)}, bf16[1,16,1024]{2,1,0:T(8,128)(2,1)S(1)}, u32[]{:S(2)}, u32[]{:S(2)}) collective-permute-start(bf16[1,16,1024]{2,1,0:T(8,128)(2,1)} %bitcast.17), channel_id=1, source_target_pairs={{0,12},{2,14},{4,8},{6,10},{8,4},{10,6},{12,0},{14,2},{1,13},{3,15... | collective-permute-start | bytes 98312 | tf_op jit(solution)/shard_map/ppermute | solution.py:61
  5.8 0.0 collective-permute-start.1
  5.8 0.6 collective-permute-start.2
  6.4 1.5 %collective-permute-done = bf16[1,16,1024]{2,1,0:T(8,128)(2,1)S(1)} collective-permute-done((bf16[1,16,1024]{2,1,0:T(8,128)(2,1)}, bf16[1,16,1024]{2,1,0:T(8,128)(2,1)S(1)}, u32[]{:S(2)}, u32[]{:S(2)}) %collective-permute-start) | collective-permute-done | bytes 32800 | tf_op jit(solution)/shard_map/ppermute | solution.py:61
  7.9 2.9 %collective-permute-done.1 = bf16[1,16,1024]{2,1,0:T(8,128)(2,1)S(1)} collective-permute-done((bf16[1,16,1024]{2,1,0:T(8,128)(2,1)}, bf16[1,16,1024]{2,1,0:T(8,128)(2,1)S(1)}, u32[]{:S(2)}, u32[]{:S(2)}) %collective-permute-start.1) | collective-permute-done | bytes 32800 | tf_op jit(solution)/shard_map/ppermute | solution.py:61
  10.8 0.0 collective-permute-done.2
  10.8 0.8 %pad_maximum_fusion.rows = bf16[4,16,1024]{2,1,0:T(8,128)(2,1)S(1)} fusion(bf16[1,16,1024]{2,1,0:T(8,128)(2,1)S(1)} %collective-permute-done.2, bf16[1,16,1024]{2,1,0:T(8,128)(2,1)S(1)} %collective-permute-done.1, bf16[1,16,1024]{2,1,0:T(8,128)(2,1)S(1)} %collective-permute-done, bf16[1,16,1024]{2,1,0:T(8,128)(2,1)} %bitcast.20), kind=kLoop, calls=%fused_computation.2 | loop fusion | flops 196608 | bytes 262144 | tf_op jit(solution)/shard_map/concatenate | solution.py:63
  11.6 1.6 %collective-permute-start.3 = (bf16[4,16,1024]{2,1,0:T(8,128)(2,1)S(1)}, bf16[4,16,1024]{2,1,0:T(8,128)(2,1)S(1)}, u32[]{:S(2)}, u32[]{:S(2)}) collective-permute-start(bf16[4,16,1024]{2,1,0:T(8,128)(2,1)S(1)} %pad_maximum_fusion.rows), channel_id=1, source_target_pairs={{0,2},{2,0},{4,6},{6,4},{8,10},{10,8},{12,14},{14,12},{1,3},{3,1},... | collective-permute-start | bytes 393224 | tf_op jit(solution)/shard_map/ppermute | solution.py:66
  13.2 0.0 copy-start.2
  13.2 3.5 %stage.1 = (bf16[1024,2048]{1,0:T(8,128)(2,1)S(1)}, bf16[1024,2048]{1,0:T(8,128)(2,1)S(1)}) custom-call(s32[1]{0:T(128)} %bitcast.2.after.index, bf16[1024,4096]{1,0:T(8,128)(2,1)} %whole.3), custom_call_target="tpu_custom_call" | custom-call | flops 1073741824 | bytes 16777216 | tf_op jit(solution)/shard_map/stage/pallas_call | solution.py:239
  16.7 0.0 copy-done.2
  16.7 3.5 %stage_rows.1 = (bf16[2048,1024]{1,0:T(8,128)(2,1)S(1)}, bf16[2048,1024]{1,0:T(8,128)(2,1)S(1)}, bf16[4,16,1024]{2,1,0:T(8,128)(2,1)S(1)}) custom-call(s32[1]{0:T(128)} %bitcast.2.after.index, bf16[4096,1024]{1,0:T(8,128)(2,1)} %whole.2, bf16[4,16,1024]{2,1,0:T(8,128)(2,1)S(1)} %pad_maximum_fusion.rows, f32[1,1024]{1,0:T(1,128)S(1)} %bitcast.25), custom_call_target="tpu_custom_call" | custom-call | flops 1073741824 | bytes 16777216 | tf_op jit(solution)/shard_map/stage_rows/pallas_call | solution.py:279
  20.2 0.0 collective-permute-done.3.theirs
  20.2 0.0 copy-start.1
  20.2 0.0 copy-start.3
  20.2 2.5 %feed.1 = bf16[128,1024]{1,0:T(8,128)(2,1)S(1)} custom-call(s32[1]{0:T(128)} %bitcast.2.after.index, bf16[4,16,1024]{2,1,0:T(8,128)(2,1)S(1)} %get-tuple-element.22.mine, bf16[4,16,1024]{2,1,0:T(8,128)(2,1)S(1)} %collective-permute-done.3.theirs, f32[1,1024]{1,0:T(1,128)S(1)} %bitcast.26, bf16[1024,2048]{1,0:T(8,128)(2,1)S(1)} %get-tuple-element.23.refs_0_, ...), custom_call_target="tpu_custom_call" | custom-call | flops 2147483648 | bytes 16777216 | tf_op jit(solution)/shard_map/feed/pallas_call | solution.py:326
  22.8 11.3 %all_to_all.10.parts = bf16[8,16,1024]{2,1,0:T(8,128)(2,1)S(1)} all-to-all(bf16[8,16,1024]{2,1,0:T(8,128)(2,1)S(1)} %bitcast.12), channel_id=1, replica_groups=mesh['groups'=2,'mp'=8,'psg'=2] {'mp'}, dimensions={0} | all-to-all | bytes 524288 | tf_op jit(solution)/shard_map/all_to_all | solution.py:561
  34.1 0.0 copy-done.1
  34.1 0.0 copy-done.3
  34.1 0.1 settle.1
  34.2 0.6 collective-permute-start.4
  34.9 0.9 %collective-permute-start.5 = (bf16[1,16,1024]{2,1,0:T(8,128)(2,1)S(1)}, bf16[1,16,1024]{2,1,0:T(8,128)(2,1)S(1)}, u32[]{:S(2)}, u32[]{:S(2)}) collective-permute-start(bf16[1,16,1024]{2,1,0:T(8,128)(2,1)S(1)} %bitcast.22), channel_id=1, source_target_pairs={{0,8},{2,10},{4,12},{6,14},{8,0},{10,2},{12,4},{14,6},{1,9},{3,11}... | collective-permute-start | bytes 98312 | tf_op jit(solution)/shard_map/ppermute | solution.py:61
  35.8 2.9 %collective-permute-start.6 = (bf16[1,16,1024]{2,1,0:T(8,128)(2,1)S(1)}, bf16[1,16,1024]{2,1,0:T(8,128)(2,1)S(1)}, u32[]{:S(2)}, u32[]{:S(2)}) collective-permute-start(bf16[1,16,1024]{2,1,0:T(8,128)(2,1)S(1)} %bitcast.23), channel_id=1, source_target_pairs={{0,4},{2,6},{4,0},{6,2},{8,12},{10,14},{12,8},{14,10},{1,5},{3,7},... | collective-permute-start | bytes 98312 | tf_op jit(solution)/shard_map/ppermute | solution.py:61
  38.7 1.3 %collective-permute-done.4 = bf16[1,16,1024]{2,1,0:T(8,128)(2,1)S(1)} collective-permute-done((bf16[1,16,1024]{2,1,0:T(8,128)(2,1)S(1)}, bf16[1,16,1024]{2,1,0:T(8,128)(2,1)S(1)}, u32[]{:S(2)}, u32[]{:S(2)}) %collective-permute-start.4) | collective-permute-done | bytes 32800 | tf_op jit(solution)/shard_map/ppermute | solution.py:61
  40.0 0.0 collective-permute-done.5
  40.0 0.5 collective-permute-done.6
  40.6 1.1 %collective-permute-start.8 = (bf16[4,16,1024]{2,1,0:T(8,128)(2,1)S(1)}, bf16[4,16,1024]{2,1,0:T(8,128)(2,1)S(1)}, u32[]{:S(2)}, u32[]{:S(2)}) collective-permute-start(bf16[4,16,1024]{2,1,0:T(8,128)(2,1)S(1)} %pad_maximum_fusion.1), channel_id=1, source_target_pairs={{0,2},{2,0},{4,6},{6,4},{8,10},{10,8},{12,14},{14,12},{1,3},{3,1},... | collective-permute-start | bytes 393224 | tf_op jit(solution)/shard_map/ppermute | solution.py:66
  41.7 0.0 collective-permute-start.7
  41.7 0.0 copy-start
  41.7 0.0 copy-start.4
  41.7 4.7 %prepare.1 = (bf16[1024,512]{1,0:T(8,128)(2,1)S(1)}, bf16[1024,512]{1,0:T(8,128)(2,1)S(1)}, bf16[1024,1024]{1,0:T(8,128)(2,1)}) custom-call(s32[1]{0:T(128)} %bitcast.half, bf16[1024,2,2048]{2,1,0:T(2,128)(2,1)} %w_keyval.1), custom_call_target="tpu_custom_call" | custom-call | flops 1073741824 | bytes 8388608 | tf_op jit(solution)/shard_map/prepare/pallas_call | solution.py:192
  46.4 0.0 copy-start.5
  46.5 0.0 copy-start.6
  46.5 0.0 copy-start.7
  46.5 0.0 collective-permute-done.8
  46.5 0.6 collective-permute-start.9
  47.1 0.0 copy-done
  47.1 0.0 copy-done.4
  47.1 3.0 %ask.1 = (bf16[128,1024]{1,0:T(8,128)(2,1)S(1)}, bf16[1024,512]{1,0:T(8,128)(2,1)S(1)}, bf16[1024,512]{1,0:T(8,128)(2,1)S(1)}, bf16[16,1024]{1,0:T(8,128)(2,1)}) custom-call(s32[1]{0:T(128)} %bitcast.half, bf16[128,1024]{1,0:T(8,128)(2,1)S(1)} %copy-done, f32[1,1024]{1,0:T(1,128)S(1)} %bitcast.28, bf16[16,1024]{1,0:T(8,128)(2,1)S(1)} %get-tuple-element.27.settled, ...), custom_call_target="tpu_custom_call" | custom-call | flops 1073741824 | bytes 4194304 | tf_op jit(solution)/shard_map/ask/pallas_call | solution.py:132
  50.0 0.0 collective-permute-done.7.theirs
  50.0 0.0 copy-done.5
  50.1 0.0 copy-done.6
  50.1 0.0 copy-done.7
  50.1 2.5 %project.1 = (bf16[128,1024]{1,0:T(8,128)(2,1)S(1)}, bf16[128,1024]{1,0:T(8,128)(2,1)S(1)}, bf16[1024,1024]{1,0:T(8,128)(2,1)S(1)}, s32[128,256]{1,0:T(8,128)S(1)}) custom-call(s32[1]{0:T(128)} %bitcast.2.after.index, s32[1]{0:T(128)} %bitcast.half, s32[16]{0:T(128)S(1)} %copy-done.5, s32[16]{0:T(128)S(1)} %copy-done.6, s32[4]{0:T(128)S(1)} %copy-done.7, ...), custom_call_target="tpu_custom_call" | custom-call | flops 536870912 | bytes 6291456 | tf_op jit(solution)/shard_map/project/pallas_call | solution.py:406
  52.6 0.0 collective-permute-done.9.theirs
  52.6 2.1 %attend.1 = (f32[64,1024]{1,0:T(8,128)S(1)}, f32[64,1024]{1,0:T(8,128)S(1)}) custom-call(bf16[128,1024]{1,0:T(8,128)(2,1)S(1)} %get-tuple-element.35.near_keys, bf16[128,1024]{1,0:T(8,128)(2,1)S(1)} %get-tuple-element.36.near_values, bf16[64,1024]{1,0:T(8,128)(2,1)S(1)} %bitcast.16, bf16[64,1024]{1,0:T(8,128)(2,1)S(1)} %collective-permute-done.9.theirs, ...), custom_call_target="tpu_custom_call" | custom-call | flops 939524096 | bytes 6291456 | tf_op jit(solution)/shard_map/attend/pallas_call | solution.py:471
  54.7 0.1 collective-permute-start.10
  54.8 1.5 %collective-permute-done.10 = f32[64,1024]{1,0:T(8,128)S(1)} collective-permute-done((f32[64,1024]{1,0:T(8,128)S(1)}, f32[64,1024]{1,0:T(8,128)S(1)}, u32[]{:S(2)}, u32[]{:S(2)}) %collective-permute-start.10) | collective-permute-done | bytes 262176 | tf_op jit(solution)/shard_map/ppermute | solution.py:75
  56.3 11.2 %all_to_all.11.parts = bf16[8,8,1024]{2,1,0:T(8,128)(2,1)S(1)} all-to-all(bf16[8,8,1024]{2,1,0:T(8,128)(2,1)S(1)} %fusion), channel_id=1, replica_groups=mesh['groups'=2,'mp'=8,'psg'=2] {'mp'}, dimensions={0} | all-to-all | bytes 262144 | tf_op jit(solution)/shard_map/all_to_all | solution.py:591
  67.5 0.2 finish.1.piece
  67.7 0.1 collective-permute-start.11
  67.7 1.2 %collective-permute-done.11.other = bf16[8,1024]{1,0:T(8,128)(2,1)S(1)} collective-permute-done((bf16[8,1024]{1,0:T(8,128)(2,1)S(1)}, bf16[8,1024]{1,0:T(8,128)(2,1)S(1)}, u32[]{:S(2)}, u32[]{:S(2)}) %collective-permute-start.11) | collective-permute-done | bytes 16416 | tf_op jit(solution)/shard_map/ppermute | solution.py:75
  68.9 0.6 join.1
  (2 shorter events, 0.1 us)
Async XLA Ops:
  0.6 7.2 %collective-permute-start = (bf16[1,16,1024]{2,1,0:T(8,128)(2,1)}, bf16[1,16,1024]{2,1,0:T(8,128)(2,1)S(1)}, u32[]{:S(2)}, u32[]{:S(2)}) collective-permute-start(bf16[1,16,1024]{2,1,0:T(8,128)(2,1)} %bitcast.17), channel_id=1, source_target_pairs={{0,12},{2,14},{4,8},{6,10},{8,4},{10,6},{12,0},{14,2},{1,13},{3,15... | collective-permute-start | bytes 98312 | tf_op jit(solution)/shard_map/ppermute | solution.py:61
  5.8 5.0 %collective-permute-start.1 = (bf16[1,16,1024]{2,1,0:T(8,128)(2,1)}, bf16[1,16,1024]{2,1,0:T(8,128)(2,1)S(1)}, u32[]{:S(2)}, u32[]{:S(2)}) collective-permute-start(bf16[1,16,1024]{2,1,0:T(8,128)(2,1)} %bitcast.18), channel_id=1, source_target_pairs={{0,8},{2,10},{4,12},{6,14},{8,0},{10,2},{12,4},{14,6},{1,9},{3,11}... | collective-permute-start | bytes 98312 | tf_op jit(solution)/shard_map/ppermute | solution.py:61
  5.8 5.0 %collective-permute-start.2 = (bf16[1,16,1024]{2,1,0:T(8,128)(2,1)}, bf16[1,16,1024]{2,1,0:T(8,128)(2,1)S(1)}, u32[]{:S(2)}, u32[]{:S(2)}) collective-permute-start(bf16[1,16,1024]{2,1,0:T(8,128)(2,1)} %bitcast.19), channel_id=1, source_target_pairs={{0,4},{2,6},{4,0},{6,2},{8,12},{10,14},{12,8},{14,10},{1,5},{3,7},... | collective-permute-start | bytes 98312 | tf_op jit(solution)/shard_map/ppermute | solution.py:61
  11.6 8.6 %collective-permute-start.3 = (bf16[4,16,1024]{2,1,0:T(8,128)(2,1)S(1)}, bf16[4,16,1024]{2,1,0:T(8,128)(2,1)S(1)}, u32[]{:S(2)}, u32[]{:S(2)}) collective-permute-start(bf16[4,16,1024]{2,1,0:T(8,128)(2,1)S(1)} %pad_maximum_fusion.rows), channel_id=1, source_target_pairs={{0,2},{2,0},{4,6},{6,4},{8,10},{10,8},{12,14},{14,12},{1,3},{3,1},... | collective-permute-start | bytes 393224 | tf_op jit(solution)/shard_map/ppermute | solution.py:66
  13.2 3.6 %copy-start.2 = (f32[1024]{0:T(1024)S(1)}, f32[1024]{0:T(1024)}, u32[]{:S(2)}) copy-start(f32[1024]{0:T(1024)} %param.14) | copy-start | bytes 12292
  20.2 13.9 %copy-start.1 = (bf16[16,1024]{1,0:T(8,128)(2,1)S(1)}, bf16[16,1024]{1,0:T(8,128)(2,1)}, u32[]{:S(2)}) copy-start(bf16[16,1024]{1,0:T(8,128)(2,1)} %tokens.1) | copy-start | bytes 98308
  20.2 13.9 %copy-start.3 = (f32[1024]{0:T(1024)S(1)}, f32[1024]{0:T(1024)}, u32[]{:S(2)}) copy-start(f32[1024]{0:T(1024)} %param.17) | copy-start | bytes 12292
  34.2 5.8 %collective-permute-start.4 = (bf16[1,16,1024]{2,1,0:T(8,128)(2,1)S(1)}, bf16[1,16,1024]{2,1,0:T(8,128)(2,1)S(1)}, u32[]{:S(2)}, u32[]{:S(2)}) collective-permute-start(bf16[1,16,1024]{2,1,0:T(8,128)(2,1)S(1)} %bitcast.21), channel_id=1, source_target_pairs={{0,12},{2,14},{4,8},{6,10},{8,4},{10,6},{12,0},{14,2},{1,13},{3,15... | collective-permute-start | bytes 98312 | tf_op jit(solution)/shard_map/ppermute | solution.py:61
  34.9 5.2 %collective-permute-start.5 = (bf16[1,16,1024]{2,1,0:T(8,128)(2,1)S(1)}, bf16[1,16,1024]{2,1,0:T(8,128)(2,1)S(1)}, u32[]{:S(2)}, u32[]{:S(2)}) collective-permute-start(bf16[1,16,1024]{2,1,0:T(8,128)(2,1)S(1)} %bitcast.22), channel_id=1, source_target_pairs={{0,8},{2,10},{4,12},{6,14},{8,0},{10,2},{12,4},{14,6},{1,9},{3,11}... | collective-permute-start | bytes 98312 | tf_op jit(solution)/shard_map/ppermute | solution.py:61
  35.8 4.8 %collective-permute-start.6 = (bf16[1,16,1024]{2,1,0:T(8,128)(2,1)S(1)}, bf16[1,16,1024]{2,1,0:T(8,128)(2,1)S(1)}, u32[]{:S(2)}, u32[]{:S(2)}) collective-permute-start(bf16[1,16,1024]{2,1,0:T(8,128)(2,1)S(1)} %bitcast.23), channel_id=1, source_target_pairs={{0,4},{2,6},{4,0},{6,2},{8,12},{10,14},{12,8},{14,10},{1,5},{3,7},... | collective-permute-start | bytes 98312 | tf_op jit(solution)/shard_map/ppermute | solution.py:61
  40.6 5.9 %collective-permute-start.8 = (bf16[4,16,1024]{2,1,0:T(8,128)(2,1)S(1)}, bf16[4,16,1024]{2,1,0:T(8,128)(2,1)S(1)}, u32[]{:S(2)}, u32[]{:S(2)}) collective-permute-start(bf16[4,16,1024]{2,1,0:T(8,128)(2,1)S(1)} %pad_maximum_fusion.1), channel_id=1, source_target_pairs={{0,2},{2,0},{4,6},{6,4},{8,10},{10,8},{12,14},{14,12},{1,3},{3,1},... | collective-permute-start | bytes 393224 | tf_op jit(solution)/shard_map/ppermute | solution.py:66
  41.7 8.3 %collective-permute-start.7 = (bf16[64,1024]{1,0:T(8,128)(2,1)S(1)}, bf16[64,1024]{1,0:T(8,128)(2,1)S(1)}, u32[]{:S(2)}, u32[]{:S(2)}) collective-permute-start(bf16[64,1024]{1,0:T(8,128)(2,1)S(1)} %bitcast.13), channel_id=1, source_target_pairs={{0,1},{1,0},{2,3},{3,2},{4,5},{5,4},{6,7},{7,6},{8,9},{9,8},{10,11... | collective-permute-start | bytes 393224 | tf_op jit(solution)/shard_map/ppermute | solution.py:75
  41.7 5.3 %copy-start = (bf16[128,1024]{1,0:T(8,128)(2,1)S(1)}, bf16[128,1024]{1,0:T(8,128)(2,1)}, u32[]{:S(2)}) copy-start(bf16[128,1024]{1,0:T(8,128)(2,1)} %states.3) | copy-start | bytes 786436
  41.7 5.3 %copy-start.4 = (f32[1024]{0:T(1024)S(1)}, f32[1024]{0:T(1024)}, u32[]{:S(2)}) copy-start(f32[1024]{0:T(1024)} %param.20) | copy-start | bytes 12292
  46.4 3.6 %copy-start.5 = (s32[16]{0:T(128)S(1)}, s32[16]{0:T(128)}, u32[]{:S(2)}) copy-start(s32[16]{0:T(128)} %lengths.1) | copy-start | bytes 196
  46.5 3.6 %copy-start.6 = (s32[16]{0:T(128)S(1)}, s32[16]{0:T(128)}, u32[]{:S(2)}) copy-start(s32[16]{0:T(128)} %owners.1) | copy-start | bytes 196
  46.5 3.6 %copy-start.7 = (s32[4]{0:T(128)S(1)}, s32[4]{0:T(128)}, u32[]{:S(2)}) copy-start(s32[4]{0:T(128)} %answers.1) | copy-start | bytes 52
  46.5 6.1 %collective-permute-start.9 = (bf16[64,1024]{1,0:T(8,128)(2,1)S(1)}, bf16[64,1024]{1,0:T(8,128)(2,1)S(1)}, u32[]{:S(2)}, u32[]{:S(2)}) collective-permute-start(bf16[64,1024]{1,0:T(8,128)(2,1)S(1)} %bitcast.15), channel_id=1, source_target_pairs={{0,1},{1,0},{2,3},{3,2},{4,5},{5,4},{6,7},{7,6},{8,9},{9,8},{10,11... | collective-permute-start | bytes 393224 | tf_op jit(solution)/shard_map/ppermute | solution.py:75
  54.7 1.6 %collective-permute-start.10 = (f32[64,1024]{1,0:T(8,128)S(1)}, f32[64,1024]{1,0:T(8,128)S(1)}, u32[]{:S(2)}, u32[]{:S(2)}) collective-permute-start(f32[64,1024]{1,0:T(8,128)S(1)} %get-tuple-element.41), channel_id=1, source_target_pairs={{0,1},{1,0},{2,3},{3,2},{4,5},{5,4},{6,7},{7,6},{8,9},{9,8},{10,11... | collective-permute-start | bytes 786440 | tf_op jit(solution)/shard_map/ppermute | solution.py:75
  67.7 1.2 %collective-permute-start.11 = (bf16[8,1024]{1,0:T(8,128)(2,1)S(1)}, bf16[8,1024]{1,0:T(8,128)(2,1)S(1)}, u32[]{:S(2)}, u32[]{:S(2)}) collective-permute-start(bf16[8,1024]{1,0:T(8,128)(2,1)S(1)} %finish.1.piece), channel_id=1, source_target_pairs={{0,1},{1,0},{2,3},{3,2},{4,5},{5,4},{6,7},{7,6},{8,9},{9,8},{10,11... | collective-permute-start | bytes 49160 | tf_op jit(solution)/shard_map/ppermute | solution.py:75

commit v10 on v9

--- a/solution.py
+++ b/solution.py
@@ -86,7 +86,7 @@
     return pltpu.CompilerParams(vmem_limit_bytes=mib << 20)
 
 
-def ask_kernel(half, states, gain, settled, w_query, value, query, first_value, last_value, encoded, scr, sems, *, mp):
+def ask_kernel(half, states, gain, w_query, value, query, first_value, last_value, scr, sems, *, mp):
     inner = query.shape[1]
     part = first_value.shape[1]
     size = scr.shape[2]
@@ -107,7 +107,6 @@
     for copy in copies + others:
         copy.start()
     normed = norm_rows(states[...], gain[...]).astype(BF16)
-    encoded[...] = settled[...]
     count = states.shape[0]
     small = count // mp // 2
     row = lax.broadcasted_iota(jnp.int32, (count, count), 0)
@@ -125,7 +124,7 @@
         copy.wait()
 
 
-def ask(half, states, gain, settled, w_query, value, mp):
+def ask(half, states, gain, w_query, value, mp):
     count, width = states.shape
     inner = value.shape[1]
     size = min(256, inner)
@@ -135,10 +134,9 @@
             jax.ShapeDtypeStruct((count, inner), BF16),
             jax.ShapeDtypeStruct((width, inner // 2), BF16),
             jax.ShapeDtypeStruct((width, inner // 2), BF16),
-            jax.ShapeDtypeStruct(settled.shape, BF16),
-        ),
-        in_specs=[SMEM_SPEC] + [VMEM_SPEC] * 3 + [HBM_SPEC, HBM_SPEC],
-        out_specs=(VMEM_SPEC,) * 4,
+        ),
+        in_specs=[SMEM_SPEC, VMEM_SPEC, VMEM_SPEC, HBM_SPEC, HBM_SPEC],
+        out_specs=(VMEM_SPEC,) * 3,
         scratch_shapes=[
             pltpu.VMEM((inner // size, width, size), BF16),
             pltpu.SemaphoreType.DMA((inner // size + 2,)),
@@ -148,7 +146,7 @@
             flops=1 << 30, bytes_accessed=4 * width * inner, transcendentals=0
         ),
         name="ask",
-    )(half, states, gain.reshape(1, width), settled, w_query, value)
+    )(half, states, gain.reshape(1, width), w_query, value)
 
 
 def prepare_kernel(half, w_keyval, first_key, last_key, w_value, scr, made, sems):
@@ -364,8 +362,15 @@
     )(parts, tokens, gain.reshape(1, width))
 
 
-def project_kernel(index, half, lengths, owners, answers, mine, theirs, first_key, last_key, first_value, last_value, w_out, keys, values, w_last, allowed, sems, *, patterns, mp):
-    inner = keys.shape[1]
+def masked_scores(query, keys, live):
+    scores = lax.dot_general(
+        query, keys, (((1,), (1,)), ((), ())), preferred_element_type=F32
+    ) * DH ** (-0.5)
+    return jnp.where(live, scores, -1e30)
+
+
+def project_kernel(index, half, lengths, owners, answers, settled, query, mine, theirs, first_key, last_key, first_value, last_value, w_out, tops, totals, sums, w_last, allowed, encoded, sems, *, patterns, mp):
+    inner = query.shape[1]
     part = inner // 2
     start = pl.multiple_of(half[0] * inner, 128)
     number = sems.shape[0]
@@ -380,82 +385,95 @@
     ]
     for copy in copies:
         copy.start()
-    row_count = 2 * mine.shape[0] // mp
-    allowed[...] = mask_rows(
-        index, half, lengths, owners, answers, allowed.shape, patterns, mp, row_count
+    encoded[...] = settled[...]
+    count = query.shape[0]
+    keys_here = 2 * mine.shape[0]
+    mask = mask_rows(
+        index,
+        half,
+        lengths,
+        owners,
+        answers,
+        (count, 2 * keys_here),
+        patterns,
+        mp,
+        keys_here // mp,
     )
+    allowed[...] = mask[:, keys_here:]
+    live = mask[:, :keys_here] > 0
     rows = jnp.concatenate([mine[...], theirs[...]], axis=0)
     size = min(256, part)
-    for k, w_key in enumerate((first_key, last_key)):
-        for c in range(part // size):
-            keys[:, pl.ds(k * part + c * size, size)] = jnp.dot(
-                rows, w_key[:, pl.ds(c * size, size)], preferred_element_type=F32
-            ).astype(BF16)
-    for k, w_value in enumerate((first_value, last_value)):
-        for c in range(part // size):
-            values[:, pl.ds(k * part + c * size, size)] = jnp.dot(
-                rows, w_value[:, pl.ds(c * size, size)], preferred_element_type=F32
-            ).astype(BF16)
+    for c in range(inner // size):
+        w_key = first_key if c * size < part else last_key
+        w_value = first_value if c * size < part else last_value
+        local = pl.ds(c * size % part, size)
+        keys = jnp.dot(rows, w_key[:, local], preferred_element_type=F32).astype(BF16)
+        values = jnp.dot(rows, w_value[:, local], preferred_element_type=F32).astype(BF16)
+        for h in range(size // DH):
+            lanes = slice(h * DH, (h + 1) * DH)
+            place = pl.ds(c * size + h * DH, DH)
+            scores = masked_scores(query[:, place], keys[:, lanes], live)
+            top = jnp.max(scores, axis=1, keepdims=True)
+            weights = jnp.where(live, jnp.exp(scores - top), 0.0)
+            total = jnp.sum(weights, axis=1, keepdims=True)
+            tops[:, place] = jnp.broadcast_to(top, (count, DH))
+            totals[:, place] = jnp.broadcast_to(total, (count, DH))
+            sums[:, place] = jnp.dot(
+                weights.astype(BF16), values[:, lanes], preferred_element_type=F32
+            )
     for copy in copies:
         copy.wait()
 
 
-def project(places, tables, mine, theirs, weights, w_attn_out, patterns, count, mp):
+def project(places, tables, settled, query, mine, theirs, weights, w_attn_out, patterns, mp):
     rows, width = mine.shape
-    inner = 2 * weights[0].shape[1]
+    count, inner = query.shape
     return pl.pallas_call(
         functools.partial(project_kernel, patterns=patterns, mp=mp),
         out_shape=(
-            jax.ShapeDtypeStruct((2 * rows, inner), BF16),
-            jax.ShapeDtypeStruct((2 * rows, inner), BF16),
+            jax.ShapeDtypeStruct((count, inner), F32),
+            jax.ShapeDtypeStruct((count, inner), F32),
+            jax.ShapeDtypeStruct((count, inner), F32),
             jax.ShapeDtypeStruct((inner, width), BF16),
-            jax.ShapeDtypeStruct((count, 4 * rows), jnp.int32),
-        ),
-        in_specs=[SMEM_SPEC] * 5 + [VMEM_SPEC] * 6 + [HBM_SPEC],
-        out_specs=(VMEM_SPEC,) * 4,
+            jax.ShapeDtypeStruct((count, 2 * rows), jnp.int32),
+            jax.ShapeDtypeStruct(settled.shape, BF16),
+        ),
+        in_specs=[SMEM_SPEC] * 5 + [VMEM_SPEC] * 8 + [HBM_SPEC],
+        out_specs=(VMEM_SPEC,) * 6,
         scratch_shapes=[pltpu.SemaphoreType.DMA((4,))],
-        compiler_params=limit(46),
+        compiler_params=limit(45),
         cost_estimate=pl.CostEstimate(
             flops=8 * rows * width * inner, bytes_accessed=6 * width * inner, transcendentals=0
         ),
         name="project",
-    )(*places, *tables, mine, theirs, *weights, w_attn_out)
-
-
-def attend_kernel(near_keys, near_values, mine, theirs, query, allowed, first_key, last_key, first_value, last_value, w_last, keep, give, context):
-    rows, inner = near_keys.shape
+    )(*places, *tables, settled, query, mine, theirs, *weights, w_attn_out)
+
+
+def attend_kernel(tops, totals, sums, mine, theirs, query, allowed, first_key, last_key, first_value, last_value, w_last, keep, give, context):
+    inner = query.shape[1]
     width = keep.shape[1]
     part = inner // 2
     size = min(256, part)
     late = jnp.concatenate([mine[...], theirs[...]], axis=0)
-    near = allowed[:, :rows] > 0
-    far = allowed[:, rows:] > 0
+    live = allowed[...] > 0
     for c in range(inner // size):
-        columns = pl.ds(c * size, size)
         w_key = first_key if c * size < part else last_key
         w_value = first_value if c * size < part else last_value
         local = pl.ds(c * size % part, size)
-        far_keys = jnp.dot(late, w_key[:, local], preferred_element_type=F32).astype(BF16)
-        far_values = jnp.dot(late, w_value[:, local], preferred_element_type=F32).astype(BF16)
-        keys = jnp.concatenate([near_keys[:, columns], far_keys], axis=0)
-        values = jnp.concatenate([near_values[:, columns], far_values], axis=0)
+        keys = jnp.dot(late, w_key[:, local], preferred_element_type=F32).astype(BF16)
+        values = jnp.dot(late, w_value[:, local], preferred_element_type=F32).astype(BF16)
         for h in range(size // DH):
             lanes = slice(h * DH, (h + 1) * DH)
             place = pl.ds(c * size + h * DH, DH)
-            scores = lax.dot_general(
-                query[:, place],
-                keys[:, lanes],
-                (((1,), (1,)), ((), ())),
-                preferred_element_type=F32,
-            ) * DH ** (-0.5)
-            near_scores = jnp.where(near, scores[:, :rows], -1e30)
-            far_scores = jnp.where(far, scores[:, rows:], -1e30)
-            top = jnp.max(jnp.maximum(near_scores, far_scores), axis=1, keepdims=True)
-            near_weights = jnp.where(near, jnp.exp(near_scores - top), 0.0)
-            far_weights = jnp.where(far, jnp.exp(far_scores - top), 0.0)
-            total = jnp.sum(near_weights + far_weights, axis=1, keepdims=True)
-            weights = jnp.concatenate([near_weights, far_weights], axis=1).astype(BF16)
-            summed = jnp.dot(weights, values[:, lanes], preferred_element_type=F32)
+            scores = masked_scores(query[:, place], keys[:, lanes], live)
+            near_top = tops[:, place]
+            top = jnp.maximum(near_top, jnp.max(scores, axis=1, keepdims=True))
+            weights = jnp.where(live, jnp.exp(scores - top[:, :1]), 0.0)
+            factor = jnp.exp(near_top - top)
+            total = totals[:, place] * factor + jnp.sum(weights, axis=1, keepdims=True)
+            summed = sums[:, place] * factor + jnp.dot(
+                weights.astype(BF16), values[:, lanes], preferred_element_type=F32
+            )
             context[:, place] = (summed * (1.0 / total)).astype(BF16)
     for c in range(width // 256):
         columns = pl.ds(c * 256, 256)
@@ -464,24 +482,23 @@
         give[:, columns] = result[keep.shape[0] :]
 
 
-def attend(near_keys, near_values, mine, theirs, query, allowed, weights, w_last):
-    rows = near_keys.shape[0]
-    width = mine.shape[1]
+def attend(near, mine, theirs, query, allowed, weights, w_last):
+    rows, width = mine.shape
     count, inner = query.shape
     return pl.pallas_call(
         attend_kernel,
         out_shape=(jax.ShapeDtypeStruct((count // 2, width), F32),) * 2,
-        in_specs=[VMEM_SPEC] * 11,
+        in_specs=[VMEM_SPEC] * 12,
         out_specs=(VMEM_SPEC, VMEM_SPEC),
         scratch_shapes=[pltpu.VMEM((count, inner), BF16)],
         compiler_params=limit(24),
         cost_estimate=pl.CostEstimate(
-            flops=4 * rows * width * inner + 8 * count * rows * inner + 2 * count * inner * width,
+            flops=8 * rows * width * inner + 8 * count * rows * inner + 2 * count * inner * width,
             bytes_accessed=6 * width * inner,
             transcendentals=2 * count * rows * inner // DH,
         ),
         name="attend",
-    )(near_keys, near_values, mine, theirs, query, allowed, *weights, w_last)
+    )(*near, mine, theirs, query, allowed, *weights, w_last)
 
 
 def finish_kernel(index, half, parts, states, piece):
@@ -565,28 +582,25 @@
     small = answer_count // mp // psg
     settled, memory = settle(parts, tokens, final_gain)
     held, got, _ = spread_out(memory, mp)
-    query, first_value, last_value, encoded = ask(
-        half, answer_states, dec_gain, settled, w_query, value, mp
-    )
+    query, first_value, last_value = ask(half, answer_states, dec_gain, w_query, value, mp)
     held = held.reshape(runs, width)
     got = got.reshape(runs, width)
     held_theirs = swap_psg(held)
     weights = (first_key, last_key, first_value, last_value)
-    near_keys, near_values, w_last, allowed = project(
+    *near, w_last, allowed, encoded = project(
         (index, half),
         (passage_lengths, passage_owner, answer_lengths),
+        settled,
+        query,
         held,
         held_theirs,
         weights,
         w_attn_out,
         patterns,
-        answer_count,
         mp,
     )
     got_theirs = swap_psg(got)
-    keep, give = attend(
-        near_keys, near_values, got, got_theirs, query, allowed, weights, w_last
-    )
+    keep, give = attend(near, got, got_theirs, query, allowed, weights, w_last)
     chip_sum = (keep + swap_psg(give)).astype(BF16).reshape(mp, small, width)
     answer_parts = lax.all_to_all(chip_sum, "mp", 0, 0)
     piece = finish(index, half, answer_parts, answer_states)

time: 69.8 us -> 72.5 us (1.039)
  Pallas kernels: 22.7 us -> 25.4 us
    pallas_call x1, Pallas kernels: 2.53 us -> 4.92 us  [project(): pl.pallas_call(functools.partial(project_kernel, patterns=patterns, mp=mp...]
    pallas_call x1, Pallas kernels: 2.05 us -> 3.05 us  [attend(): pl.pallas_call(attend_kernel, out_shape=(jax.ShapeDtypeStruct((count // 2...]
  transfers between devices with their start and end apart: 12 -> 12, of which waited for: 6 -> 6; matrix products, arithmetic and copies ran while one was open for 0% -> 0% of each run, Pallas kernels for 25% -> 26%
where the time goes in v10:
time: 72.5 us; the launch traced here: 72.2 us
  Pallas kernels  25.4 us (35%)
  blocking collectives  22.5 us (31%)
  starting transfers between devices  13.7 us (19%)
  waiting for transfers between devices  8.96 us (12%)
  other arithmetic  0.83 us (1%)
  between operations  0.83 us (1%)
    all_to_all x1, blocking collectives, per_device(): lax.all_to_all(partial_sums.reshape(mp, row_count, width), 'mp', 0, 0)  11.3 us
    all_to_all x1, blocking collectives, per_device(): answer_parts = lax.all_to_all(chip_sum, 'mp', 0, 0)  11.2 us
    ppermute x6, starting transfers between devices, spread_out(): lax.ppermute(x[None], 'mp', [(j, j ^ k * quarter) for j in range(mp)])  10.2 us
    ppermute x6, waiting for transfers between devices, spread_out(): lax.ppermute(x[None], 'mp', [(j, j ^ k * quarter) for j in range(mp)])  6.27 us
    pallas_call x1, Pallas kernels, project(): pl.pallas_call(functools.partial(project_kernel, patterns=patterns, mp=mp...  4.92 us
    pallas_call x1, Pallas kernels, prepare(): pl.pallas_call(prepare_kernel, out_shape=(jax.ShapeDtypeStruct((width, in...  4.7 us
    pallas_call x1, Pallas kernels, stage(): pl.pallas_call(functools.partial(stage_kernel, axis=axis), out_shape=(par...  3.54 us
    pallas_call x1, Pallas kernels, stage_rows(): pl.pallas_call(stage_rows_kernel, out_shape=(part, part, jax.ShapeDtypeSt...  3.48 us
  transfers between devices with their start and end apart: 12, of which 6 were waited for; matrix products, arithmetic and copies ran while one was open for 0% of the time, Pallas kernels for 26%

profile of v10, /device:TPU:0, one launch (start us, length us, event | category | flops | bytes accessed | tf_op | source)
XLA Modules:
  0.0 72.2 jit_solution(10808903787850085617)
XLA Ops:
  0.6 5.1 %collective-permute-start = (bf16[1,16,1024]{2,1,0:T(8,128)(2,1)}, bf16[1,16,1024]{2,1,0:T(8,128)(2,1)S(1)}, u32[]{:S(2)}, u32[]{:S(2)}) collective-permute-start(bf16[1,16,1024]{2,1,0:T(8,128)(2,1)} %bitcast.17), channel_id=1, source_target_pairs={{0,12},{2,14},{4,8},{6,10},{8,4},{10,6},{12,0},{14,2},{1,13},{3,15... | collective-permute-start | bytes 98312 | tf_op jit(solution)/shard_map/ppermute | solution.py:61
  5.8 0.0 collective-permute-start.1
  5.8 0.6 collective-permute-start.2
  6.4 1.5 %collective-permute-done = bf16[1,16,1024]{2,1,0:T(8,128)(2,1)S(1)} collective-permute-done((bf16[1,16,1024]{2,1,0:T(8,128)(2,1)}, bf16[1,16,1024]{2,1,0:T(8,128)(2,1)S(1)}, u32[]{:S(2)}, u32[]{:S(2)}) %collective-permute-start) | collective-permute-done | bytes 32800 | tf_op jit(solution)/shard_map/ppermute | solution.py:61
  7.9 2.9 %collective-permute-done.1 = bf16[1,16,1024]{2,1,0:T(8,128)(2,1)S(1)} collective-permute-done((bf16[1,16,1024]{2,1,0:T(8,128)(2,1)}, bf16[1,16,1024]{2,1,0:T(8,128)(2,1)S(1)}, u32[]{:S(2)}, u32[]{:S(2)}) %collective-permute-start.1) | collective-permute-done | bytes 32800 | tf_op jit(solution)/shard_map/ppermute | solution.py:61
  10.8 0.0 collective-permute-done.2
  10.8 0.8 %pad_maximum_fusion.rows = bf16[4,16,1024]{2,1,0:T(8,128)(2,1)S(1)} fusion(bf16[1,16,1024]{2,1,0:T(8,128)(2,1)S(1)} %collective-permute-done.2, bf16[1,16,1024]{2,1,0:T(8,128)(2,1)S(1)} %collective-permute-done.1, bf16[1,16,1024]{2,1,0:T(8,128)(2,1)S(1)} %collective-permute-done, bf16[1,16,1024]{2,1,0:T(8,128)(2,1)} %bitcast.20), kind=kLoop, calls=%fused_computation.2 | loop fusion | flops 196608 | bytes 262144 | tf_op jit(solution)/shard_map/concatenate | solution.py:63
  11.6 1.6 %collective-permute-start.3 = (bf16[4,16,1024]{2,1,0:T(8,128)(2,1)S(1)}, bf16[4,16,1024]{2,1,0:T(8,128)(2,1)S(1)}, u32[]{:S(2)}, u32[]{:S(2)}) collective-permute-start(bf16[4,16,1024]{2,1,0:T(8,128)(2,1)S(1)} %pad_maximum_fusion.rows), channel_id=1, source_target_pairs={{0,2},{2,0},{4,6},{6,4},{8,10},{10,8},{12,14},{14,12},{1,3},{3,1},... | collective-permute-start | bytes 393224 | tf_op jit(solution)/shard_map/ppermute | solution.py:66
  13.2 0.0 copy-start.2
  13.2 3.5 %stage.1 = (bf16[1024,2048]{1,0:T(8,128)(2,1)S(1)}, bf16[1024,2048]{1,0:T(8,128)(2,1)S(1)}) custom-call(s32[1]{0:T(128)} %bitcast.after.index, bf16[1024,4096]{1,0:T(8,128)(2,1)} %whole.3), custom_call_target="tpu_custom_call" | custom-call | flops 1073741824 | bytes 16777216 | tf_op jit(solution)/shard_map/stage/pallas_call | solution.py:237
  16.7 0.0 copy-done.2
  16.7 3.5 %stage_rows.1 = (bf16[2048,1024]{1,0:T(8,128)(2,1)S(1)}, bf16[2048,1024]{1,0:T(8,128)(2,1)S(1)}, bf16[4,16,1024]{2,1,0:T(8,128)(2,1)S(1)}) custom-call(s32[1]{0:T(128)} %bitcast.after.index, bf16[4096,1024]{1,0:T(8,128)(2,1)} %whole.2, bf16[4,16,1024]{2,1,0:T(8,128)(2,1)S(1)} %pad_maximum_fusion.rows, f32[1,1024]{1,0:T(1,128)S(1)} %bitcast.25), custom_call_target="tpu_custom_call" | custom-call | flops 1073741824 | bytes 16777216 | tf_op jit(solution)/shard_map/stage_rows/pallas_call | solution.py:277
  20.2 0.0 collective-permute-done.3.theirs
  20.2 0.0 copy-start.1
  20.2 0.0 copy-start.3
  20.2 2.5 %feed.1 = bf16[128,1024]{1,0:T(8,128)(2,1)S(1)} custom-call(s32[1]{0:T(128)} %bitcast.after.index, bf16[4,16,1024]{2,1,0:T(8,128)(2,1)S(1)} %get-tuple-element.23.mine, bf16[4,16,1024]{2,1,0:T(8,128)(2,1)S(1)} %collective-permute-done.3.theirs, f32[1,1024]{1,0:T(1,128)S(1)} %bitcast.26, bf16[1024,2048]{1,0:T(8,128)(2,1)S(1)} %get-tuple-element.24.refs_0_, ...), custom_call_target="tpu_custom_call" | custom-call | flops 2147483648 | bytes 16777216 | tf_op jit(solution)/shard_map/feed/pallas_call | solution.py:324
  22.8 11.3 %all_to_all.10.parts = bf16[8,16,1024]{2,1,0:T(8,128)(2,1)S(1)} all-to-all(bf16[8,16,1024]{2,1,0:T(8,128)(2,1)S(1)} %bitcast.12), channel_id=1, replica_groups=mesh['groups'=2,'mp'=8,'psg'=2] {'mp'}, dimensions={0} | all-to-all | bytes 524288 | tf_op jit(solution)/shard_map/all_to_all | solution.py:578
  34.1 0.0 copy-done.1
  34.1 0.0 copy-done.3
  34.1 0.1 settle.1
  34.2 0.6 collective-permute-start.4
  34.9 0.9 %collective-permute-start.5 = (bf16[1,16,1024]{2,1,0:T(8,128)(2,1)S(1)}, bf16[1,16,1024]{2,1,0:T(8,128)(2,1)S(1)}, u32[]{:S(2)}, u32[]{:S(2)}) collective-permute-start(bf16[1,16,1024]{2,1,0:T(8,128)(2,1)S(1)} %bitcast.22), channel_id=1, source_target_pairs={{0,8},{2,10},{4,12},{6,14},{8,0},{10,2},{12,4},{14,6},{1,9},{3,11}... | collective-permute-start | bytes 98312 | tf_op jit(solution)/shard_map/ppermute | solution.py:61
  35.8 2.9 %collective-permute-start.6 = (bf16[1,16,1024]{2,1,0:T(8,128)(2,1)S(1)}, bf16[1,16,1024]{2,1,0:T(8,128)(2,1)S(1)}, u32[]{:S(2)}, u32[]{:S(2)}) collective-permute-start(bf16[1,16,1024]{2,1,0:T(8,128)(2,1)S(1)} %bitcast.23), channel_id=1, source_target_pairs={{0,4},{2,6},{4,0},{6,2},{8,12},{10,14},{12,8},{14,10},{1,5},{3,7},... | collective-permute-start | bytes 98312 | tf_op jit(solution)/shard_map/ppermute | solution.py:61
  38.7 1.3 %collective-permute-done.4 = bf16[1,16,1024]{2,1,0:T(8,128)(2,1)S(1)} collective-permute-done((bf16[1,16,1024]{2,1,0:T(8,128)(2,1)S(1)}, bf16[1,16,1024]{2,1,0:T(8,128)(2,1)S(1)}, u32[]{:S(2)}, u32[]{:S(2)}) %collective-permute-start.4) | collective-permute-done | bytes 32800 | tf_op jit(solution)/shard_map/ppermute | solution.py:61
  40.0 0.0 collective-permute-done.5
  40.0 0.5 collective-permute-done.6
  40.6 1.1 %collective-permute-start.8 = (bf16[4,16,1024]{2,1,0:T(8,128)(2,1)S(1)}, bf16[4,16,1024]{2,1,0:T(8,128)(2,1)S(1)}, u32[]{:S(2)}, u32[]{:S(2)}) collective-permute-start(bf16[4,16,1024]{2,1,0:T(8,128)(2,1)S(1)} %pad_maximum_fusion.1), channel_id=1, source_target_pairs={{0,2},{2,0},{4,6},{6,4},{8,10},{10,8},{12,14},{14,12},{1,3},{3,1},... | collective-permute-start | bytes 393224 | tf_op jit(solution)/shard_map/ppermute | solution.py:66
  41.7 0.0 collective-permute-start.7
  41.7 0.0 copy-start
  41.7 0.0 copy-start.4
  41.7 4.7 %prepare.1 = (bf16[1024,512]{1,0:T(8,128)(2,1)S(1)}, bf16[1024,512]{1,0:T(8,128)(2,1)S(1)}, bf16[1024,1024]{1,0:T(8,128)(2,1)}) custom-call(s32[1]{0:T(128)} %bitcast.1.half, bf16[1024,2,2048]{2,1,0:T(2,128)(2,1)} %w_keyval.1), custom_call_target="tpu_custom_call" | custom-call | flops 1073741824 | bytes 8388608 | tf_op jit(solution)/shard_map/prepare/pallas_call | solution.py:190
  46.4 0.0 copy-start.5
  46.5 0.0 copy-start.6
  46.5 0.0 copy-start.7
  46.5 0.0 collective-permute-done.8
  46.5 0.6 collective-permute-start.9
  47.1 0.0 copy-done
  47.1 0.0 copy-done.4
  47.1 2.3 %ask.1 = (bf16[128,1024]{1,0:T(8,128)(2,1)S(1)}, bf16[1024,512]{1,0:T(8,128)(2,1)S(1)}, bf16[1024,512]{1,0:T(8,128)(2,1)S(1)}) custom-call(s32[1]{0:T(128)} %bitcast.1.half, bf16[128,1024]{1,0:T(8,128)(2,1)S(1)} %copy-done, f32[1,1024]{1,0:T(1,128)S(1)} %bitcast.28, bf16[1024,2048]{1,0:T(8,128)(2,1)} %w_query.1, bf16[1024,1024]{1,0:T(8,128)(2,1)} %get-tuple-element.29.value), custom_call_target="tpu_custom_call" | custom-call | flops 1073741824 | bytes 4194304 | tf_op jit(solution)/shard_map/ask/pallas_call | solution.py:131
  49.4 0.0 collective-permute-done.7.theirs
  49.4 0.0 copy-done.5
  49.4 0.0 copy-done.6
  49.4 0.0 copy-done.7
  49.4 4.9 %project.1 = (f32[128,1024]{1,0:T(8,128)S(1)}, f32[128,1024]{1,0:T(8,128)S(1)}, f32[128,1024]{1,0:T(8,128)S(1)}, bf16[1024,1024]{1,0:T(8,128)(2,1)S(1)}, s32[128...) custom-call(s32[1]{0:T(128)} %bitcast.after.index, s32[1]{0:T(128)} %bitcast.1.half, s32[16]{0:T(128)S(1)} %copy-done.5, ...), custom_call_target="tpu_custom_call" | custom-call | flops 536870912 | bytes 6291456 | tf_op jit(solution)/shard_map/project/pallas_call | solution.py:431
  54.3 0.0 collective-permute-done.9.theirs
  54.3 3.0 %attend.1 = (f32[64,1024]{1,0:T(8,128)S(1)}, f32[64,1024]{1,0:T(8,128)S(1)}) custom-call(f32[128,1024]{1,0:T(8,128)S(1)} %get-tuple-element.37.tops, f32[128,1024]{1,0:T(8,128)S(1)} %get-tuple-element.38.totals, f32[128,1024]{1,0:T(8,128)S(1)} %get-tuple-element.39.sums, bf16[64,1024]{1,0:T(8,128)(2,1)S(1)} %bitcast.16, ...), custom_call_target="tpu_custom_call" | custom-call | flops 872415232 | bytes 6291456 | tf_op jit(solution)/shard_map/attend/pallas_call | solution.py:488
  57.4 0.1 collective-permute-start.10
  57.5 1.5 %collective-permute-done.10 = f32[64,1024]{1,0:T(8,128)S(1)} collective-permute-done((f32[64,1024]{1,0:T(8,128)S(1)}, f32[64,1024]{1,0:T(8,128)S(1)}, u32[]{:S(2)}, u32[]{:S(2)}) %collective-permute-start.10) | collective-permute-done | bytes 262176 | tf_op jit(solution)/shard_map/ppermute | solution.py:75
  59.0 11.2 %all_to_all.11.parts = bf16[8,8,1024]{2,1,0:T(8,128)(2,1)S(1)} all-to-all(bf16[8,8,1024]{2,1,0:T(8,128)(2,1)S(1)} %fusion), channel_id=1, replica_groups=mesh['groups'=2,'mp'=8,'psg'=2] {'mp'}, dimensions={0} | all-to-all | bytes 262144 | tf_op jit(solution)/shard_map/all_to_all | solution.py:605
  70.2 0.2 finish.1.piece
  70.4 0.1 collective-permute-start.11
  70.4 1.2 %collective-permute-done.11.other = bf16[8,1024]{1,0:T(8,128)(2,1)S(1)} collective-permute-done((bf16[8,1024]{1,0:T(8,128)(2,1)S(1)}, bf16[8,1024]{1,0:T(8,128)(2,1)S(1)}, u32[]{:S(2)}, u32[]{:S(2)}) %collective-permute-start.11) | collective-permute-done | bytes 16416 | tf_op jit(solution)/shard_map/ppermute | solution.py:75
  71.6 0.6 join.1
  (2 shorter events, 0.1 us)
Async XLA Ops:
  0.6 7.2 %collective-permute-start = (bf16[1,16,1024]{2,1,0:T(8,128)(2,1)}, bf16[1,16,1024]{2,1,0:T(8,128)(2,1)S(1)}, u32[]{:S(2)}, u32[]{:S(2)}) collective-permute-start(bf16[1,16,1024]{2,1,0:T(8,128)(2,1)} %bitcast.17), channel_id=1, source_target_pairs={{0,12},{2,14},{4,8},{6,10},{8,4},{10,6},{12,0},{14,2},{1,13},{3,15... | collective-permute-start | bytes 98312 | tf_op jit(solution)/shard_map/ppermute | solution.py:61
  5.8 5.0 %collective-permute-start.1 = (bf16[1,16,1024]{2,1,0:T(8,128)(2,1)}, bf16[1,16,1024]{2,1,0:T(8,128)(2,1)S(1)}, u32[]{:S(2)}, u32[]{:S(2)}) collective-permute-start(bf16[1,16,1024]{2,1,0:T(8,128)(2,1)} %bitcast.18), channel_id=1, source_target_pairs={{0,8},{2,10},{4,12},{6,14},{8,0},{10,2},{12,4},{14,6},{1,9},{3,11}... | collective-permute-start | bytes 98312 | tf_op jit(solution)/shard_map/ppermute | solution.py:61
  5.8 5.0 %collective-permute-start.2 = (bf16[1,16,1024]{2,1,0:T(8,128)(2,1)}, bf16[1,16,1024]{2,1,0:T(8,128)(2,1)S(1)}, u32[]{:S(2)}, u32[]{:S(2)}) collective-permute-start(bf16[1,16,1024]{2,1,0:T(8,128)(2,1)} %bitcast.19), channel_id=1, source_target_pairs={{0,4},{2,6},{4,0},{6,2},{8,12},{10,14},{12,8},{14,10},{1,5},{3,7},... | collective-permute-start | bytes 98312 | tf_op jit(solution)/shard_map/ppermute | solution.py:61
  11.6 8.6 %collective-permute-start.3 = (bf16[4,16,1024]{2,1,0:T(8,128)(2,1)S(1)}, bf16[4,16,1024]{2,1,0:T(8,128)(2,1)S(1)}, u32[]{:S(2)}, u32[]{:S(2)}) collective-permute-start(bf16[4,16,1024]{2,1,0:T(8,128)(2,1)S(1)} %pad_maximum_fusion.rows), channel_id=1, source_target_pairs={{0,2},{2,0},{4,6},{6,4},{8,10},{10,8},{12,14},{14,12},{1,3},{3,1},... | collective-permute-start | bytes 393224 | tf_op jit(solution)/shard_map/ppermute | solution.py:66
  13.2 3.6 %copy-start.2 = (f32[1024]{0:T(1024)S(1)}, f32[1024]{0:T(1024)}, u32[]{:S(2)}) copy-start(f32[1024]{0:T(1024)} %param.14) | copy-start | bytes 12292
  20.2 13.9 %copy-start.1 = (bf16[16,1024]{1,0:T(8,128)(2,1)S(1)}, bf16[16,1024]{1,0:T(8,128)(2,1)}, u32[]{:S(2)}) copy-start(bf16[16,1024]{1,0:T(8,128)(2,1)} %tokens.1) | copy-start | bytes 98308
  20.2 13.9 %copy-start.3 = (f32[1024]{0:T(1024)S(1)}, f32[1024]{0:T(1024)}, u32[]{:S(2)}) copy-start(f32[1024]{0:T(1024)} %param.17) | copy-start | bytes 12292
  34.2 5.8 %collective-permute-start.4 = (bf16[1,16,1024]{2,1,0:T(8,128)(2,1)S(1)}, bf16[1,16,1024]{2,1,0:T(8,128)(2,1)S(1)}, u32[]{:S(2)}, u32[]{:S(2)}) collective-permute-start(bf16[1,16,1024]{2,1,0:T(8,128)(2,1)S(1)} %bitcast.21), channel_id=1, source_target_pairs={{0,12},{2,14},{4,8},{6,10},{8,4},{10,6},{12,0},{14,2},{1,13},{3,15... | collective-permute-start | bytes 98312 | tf_op jit(solution)/shard_map/ppermute | solution.py:61
  34.9 5.2 %collective-permute-start.5 = (bf16[1,16,1024]{2,1,0:T(8,128)(2,1)S(1)}, bf16[1,16,1024]{2,1,0:T(8,128)(2,1)S(1)}, u32[]{:S(2)}, u32[]{:S(2)}) collective-permute-start(bf16[1,16,1024]{2,1,0:T(8,128)(2,1)S(1)} %bitcast.22), channel_id=1, source_target_pairs={{0,8},{2,10},{4,12},{6,14},{8,0},{10,2},{12,4},{14,6},{1,9},{3,11}... | collective-permute-start | bytes 98312 | tf_op jit(solution)/shard_map/ppermute | solution.py:61
  35.8 4.8 %collective-permute-start.6 = (bf16[1,16,1024]{2,1,0:T(8,128)(2,1)S(1)}, bf16[1,16,1024]{2,1,0:T(8,128)(2,1)S(1)}, u32[]{:S(2)}, u32[]{:S(2)}) collective-permute-start(bf16[1,16,1024]{2,1,0:T(8,128)(2,1)S(1)} %bitcast.23), channel_id=1, source_target_pairs={{0,4},{2,6},{4,0},{6,2},{8,12},{10,14},{12,8},{14,10},{1,5},{3,7},... | collective-permute-start | bytes 98312 | tf_op jit(solution)/shard_map/ppermute | solution.py:61
  40.6 5.9 %collective-permute-start.8 = (bf16[4,16,1024]{2,1,0:T(8,128)(2,1)S(1)}, bf16[4,16,1024]{2,1,0:T(8,128)(2,1)S(1)}, u32[]{:S(2)}, u32[]{:S(2)}) collective-permute-start(bf16[4,16,1024]{2,1,0:T(8,128)(2,1)S(1)} %pad_maximum_fusion.1), channel_id=1, source_target_pairs={{0,2},{2,0},{4,6},{6,4},{8,10},{10,8},{12,14},{14,12},{1,3},{3,1},... | collective-permute-start | bytes 393224 | tf_op jit(solution)/shard_map/ppermute | solution.py:66
  41.7 7.6 %collective-permute-start.7 = (bf16[64,1024]{1,0:T(8,128)(2,1)S(1)}, bf16[64,1024]{1,0:T(8,128)(2,1)S(1)}, u32[]{:S(2)}, u32[]{:S(2)}) collective-permute-start(bf16[64,1024]{1,0:T(8,128)(2,1)S(1)} %bitcast.13), channel_id=1, source_target_pairs={{0,1},{1,0},{2,3},{3,2},{4,5},{5,4},{6,7},{7,6},{8,9},{9,8},{10,11... | collective-permute-start | bytes 393224 | tf_op jit(solution)/shard_map/ppermute | solution.py:75
  41.7 5.3 %copy-start = (bf16[128,1024]{1,0:T(8,128)(2,1)S(1)}, bf16[128,1024]{1,0:T(8,128)(2,1)}, u32[]{:S(2)}) copy-start(bf16[128,1024]{1,0:T(8,128)(2,1)} %states.3) | copy-start | bytes 786436
  41.7 5.3 %copy-start.4 = (f32[1024]{0:T(1024)S(1)}, f32[1024]{0:T(1024)}, u32[]{:S(2)}) copy-start(f32[1024]{0:T(1024)} %param.20) | copy-start | bytes 12292
  46.4 2.9 %copy-start.5 = (s32[16]{0:T(128)S(1)}, s32[16]{0:T(128)}, u32[]{:S(2)}) copy-start(s32[16]{0:T(128)} %lengths.1) | copy-start | bytes 196
  46.5 2.9 %copy-start.6 = (s32[16]{0:T(128)S(1)}, s32[16]{0:T(128)}, u32[]{:S(2)}) copy-start(s32[16]{0:T(128)} %owners.1) | copy-start | bytes 196
  46.5 2.9 %copy-start.7 = (s32[4]{0:T(128)S(1)}, s32[4]{0:T(128)}, u32[]{:S(2)}) copy-start(s32[4]{0:T(128)} %answers.1) | copy-start | bytes 52
  46.5 7.8 %collective-permute-start.9 = (bf16[64,1024]{1,0:T(8,128)(2,1)S(1)}, bf16[64,1024]{1,0:T(8,128)(2,1)S(1)}, u32[]{:S(2)}, u32[]{:S(2)}) collective-permute-start(bf16[64,1024]{1,0:T(8,128)(2,1)S(1)} %bitcast.15), channel_id=1, source_target_pairs={{0,1},{1,0},{2,3},{3,2},{4,5},{5,4},{6,7},{7,6},{8,9},{9,8},{10,11... | collective-permute-start | bytes 393224 | tf_op jit(solution)/shard_map/ppermute | solution.py:75
  57.4 1.6 %collective-permute-start.10 = (f32[64,1024]{1,0:T(8,128)S(1)}, f32[64,1024]{1,0:T(8,128)S(1)}, u32[]{:S(2)}, u32[]{:S(2)}) collective-permute-start(f32[64,1024]{1,0:T(8,128)S(1)} %get-tuple-element.43), channel_id=1, source_target_pairs={{0,1},{1,0},{2,3},{3,2},{4,5},{5,4},{6,7},{7,6},{8,9},{9,8},{10,11... | collective-permute-start | bytes 786440 | tf_op jit(solution)/shard_map/ppermute | solution.py:75
  70.4 1.2 %collective-permute-start.11 = (bf16[8,1024]{1,0:T(8,128)(2,1)S(1)}, bf16[8,1024]{1,0:T(8,128)(2,1)S(1)}, u32[]{:S(2)}, u32[]{:S(2)}) collective-permute-start(bf16[8,1024]{1,0:T(8,128)(2,1)S(1)} %finish.1.piece), channel_id=1, source_target_pairs={{0,1},{1,0},{2,3},{3,2},{4,5},{5,4},{6,7},{7,6},{8,9},{9,8},{10,11... | collective-permute-start | bytes 49160 | tf_op jit(solution)/shard_map/ppermute | solution.py:75

commit v11 on v9

--- a/solution.py
+++ b/solution.py
@@ -86,7 +86,7 @@
     return pltpu.CompilerParams(vmem_limit_bytes=mib << 20)
 
 
-def ask_kernel(half, states, gain, settled, w_query, value, query, first_value, last_value, encoded, scr, sems, *, mp):
+def ask_kernel(half, states, gain, w_query, value, query, first_value, last_value, scr, sems, *, mp):
     inner = query.shape[1]
     part = first_value.shape[1]
     size = scr.shape[2]
@@ -107,7 +107,6 @@
     for copy in copies + others:
         copy.start()
     normed = norm_rows(states[...], gain[...]).astype(BF16)
-    encoded[...] = settled[...]
     count = states.shape[0]
     small = count // mp // 2
     row = lax.broadcasted_iota(jnp.int32, (count, count), 0)
@@ -125,7 +124,7 @@
         copy.wait()
 
 
-def ask(half, states, gain, settled, w_query, value, mp):
+def ask(half, states, gain, w_query, value, mp):
     count, width = states.shape
     inner = value.shape[1]
     size = min(256, inner)
@@ -135,10 +134,9 @@
             jax.ShapeDtypeStruct((count, inner), BF16),
             jax.ShapeDtypeStruct((width, inner // 2), BF16),
             jax.ShapeDtypeStruct((width, inner // 2), BF16),
-            jax.ShapeDtypeStruct(settled.shape, BF16),
-        ),
-        in_specs=[SMEM_SPEC] + [VMEM_SPEC] * 3 + [HBM_SPEC, HBM_SPEC],
-        out_specs=(VMEM_SPEC,) * 4,
+        ),
+        in_specs=[SMEM_SPEC, VMEM_SPEC, VMEM_SPEC, HBM_SPEC, HBM_SPEC],
+        out_specs=(VMEM_SPEC,) * 3,
         scratch_shapes=[
             pltpu.VMEM((inner // size, width, size), BF16),
             pltpu.SemaphoreType.DMA((inner // size + 2,)),
@@ -148,7 +146,7 @@
             flops=1 << 30, bytes_accessed=4 * width * inner, transcendentals=0
         ),
         name="ask",
-    )(half, states, gain.reshape(1, width), settled, w_query, value)
+    )(half, states, gain.reshape(1, width), w_query, value)
 
 
 def prepare_kernel(half, w_keyval, first_key, last_key, w_value, scr, made, sems):
@@ -364,7 +362,7 @@
     )(parts, tokens, gain.reshape(1, width))
 
 
-def project_kernel(index, half, lengths, owners, answers, mine, theirs, first_key, last_key, first_value, last_value, w_out, keys, values, w_last, allowed, sems, *, patterns, mp):
+def project_kernel(index, half, lengths, owners, answers, settled, mine, theirs, first_key, last_key, first_value, last_value, w_out, keys, values, w_last, allowed, encoded, sems, *, patterns, mp):
     inner = keys.shape[1]
     part = inner // 2
     start = pl.multiple_of(half[0] * inner, 128)
@@ -380,6 +378,7 @@
     ]
     for copy in copies:
         copy.start()
+    encoded[...] = settled[...]
     row_count = 2 * mine.shape[0] // mp
     allowed[...] = mask_rows(
         index, half, lengths, owners, answers, allowed.shape, patterns, mp, row_count
@@ -400,7 +399,7 @@
         copy.wait()
 
 
-def project(places, tables, mine, theirs, weights, w_attn_out, patterns, count, mp):
+def project(places, tables, settled, mine, theirs, weights, w_attn_out, patterns, count, mp):
     rows, width = mine.shape
     inner = 2 * weights[0].shape[1]
     return pl.pallas_call(
@@ -410,16 +409,17 @@
             jax.ShapeDtypeStruct((2 * rows, inner), BF16),
             jax.ShapeDtypeStruct((inner, width), BF16),
             jax.ShapeDtypeStruct((count, 4 * rows), jnp.int32),
-        ),
-        in_specs=[SMEM_SPEC] * 5 + [VMEM_SPEC] * 6 + [HBM_SPEC],
-        out_specs=(VMEM_SPEC,) * 4,
+            jax.ShapeDtypeStruct(settled.shape, BF16),
+        ),
+        in_specs=[SMEM_SPEC] * 5 + [VMEM_SPEC] * 7 + [HBM_SPEC],
+        out_specs=(VMEM_SPEC,) * 5,
         scratch_shapes=[pltpu.SemaphoreType.DMA((4,))],
         compiler_params=limit(46),
         cost_estimate=pl.CostEstimate(
             flops=8 * rows * width * inner, bytes_accessed=6 * width * inner, transcendentals=0
         ),
         name="project",
-    )(*places, *tables, mine, theirs, *weights, w_attn_out)
+    )(*places, *tables, settled, mine, theirs, *weights, w_attn_out)
 
 
 def attend_kernel(near_keys, near_values, mine, theirs, query, allowed, first_key, last_key, first_value, last_value, w_last, keep, give, context):
@@ -565,16 +565,15 @@
     small = answer_count // mp // psg
     settled, memory = settle(parts, tokens, final_gain)
     held, got, _ = spread_out(memory, mp)
-    query, first_value, last_value, encoded = ask(
-        half, answer_states, dec_gain, settled, w_query, value, mp
-    )
+    query, first_value, last_value = ask(half, answer_states, dec_gain, w_query, value, mp)
     held = held.reshape(runs, width)
     got = got.reshape(runs, width)
     held_theirs = swap_psg(held)
     weights = (first_key, last_key, first_value, last_value)
-    near_keys, near_values, w_last, allowed = project(
+    near_keys, near_values, w_last, allowed, encoded = project(
         (index, half),
         (passage_lengths, passage_owner, answer_lengths),
+        settled,
         held,
         held_theirs,
         weights,

time: 69.8 us -> 69.8 us (level)
  no operation moved by 1% of the time
where the time goes in v11:
time: 69.8 us; the launch traced here: 69.5 us
  Pallas kernels  22.6 us (32%)
  blocking collectives  22.5 us (32%)
  starting transfers between devices  13.7 us (20%)
  waiting for transfers between devices  8.95 us (13%)
  other arithmetic  0.83 us (1%)
  between operations  0.83 us (1%)
    all_to_all x1, blocking collectives, per_device(): lax.all_to_all(partial_sums.reshape(mp, row_count, width), 'mp', 0, 0)  11.3 us
    all_to_all x1, blocking collectives, per_device(): answer_parts = lax.all_to_all(chip_sum, 'mp', 0, 0)  11.2 us
    ppermute x6, starting transfers between devices, spread_out(): lax.ppermute(x[None], 'mp', [(j, j ^ k * quarter) for j in range(mp)])  10.2 us
    ppermute x6, waiting for transfers between devices, spread_out(): lax.ppermute(x[None], 'mp', [(j, j ^ k * quarter) for j in range(mp)])  6.27 us
    pallas_call x1, Pallas kernels, prepare(): pl.pallas_call(prepare_kernel, out_shape=(jax.ShapeDtypeStruct((width, in...  4.7 us
    pallas_call x1, Pallas kernels, stage(): pl.pallas_call(functools.partial(stage_kernel, axis=axis), out_shape=(par...  3.54 us
    pallas_call x1, Pallas kernels, stage_rows(): pl.pallas_call(stage_rows_kernel, out_shape=(part, part, jax.ShapeDtypeSt...  3.48 us
    pallas_call x1, Pallas kernels, project(): pl.pallas_call(functools.partial(project_kernel, patterns=patterns, mp=mp...  3.15 us
  transfers between devices with their start and end apart: 12, of which 6 were waited for; matrix products, arithmetic and copies ran while one was open for 0% of the time, Pallas kernels for 25%

profile of v11, /device:TPU:0, one launch (start us, length us, event | category | flops | bytes accessed | tf_op | source)
XLA Modules:
  0.0 69.5 jit_solution(8338882187743311281)
XLA Ops:
  0.6 5.1 %collective-permute-start = (bf16[1,16,1024]{2,1,0:T(8,128)(2,1)}, bf16[1,16,1024]{2,1,0:T(8,128)(2,1)S(1)}, u32[]{:S(2)}, u32[]{:S(2)}) collective-permute-start(bf16[1,16,1024]{2,1,0:T(8,128)(2,1)} %bitcast.17), channel_id=1, source_target_pairs={{0,12},{2,14},{4,8},{6,10},{8,4},{10,6},{12,0},{14,2},{1,13},{3,15... | collective-permute-start | bytes 98312 | tf_op jit(solution)/shard_map/ppermute | solution.py:61
  5.8 0.0 collective-permute-start.1
  5.8 0.6 collective-permute-start.2
  6.4 1.5 %collective-permute-done = bf16[1,16,1024]{2,1,0:T(8,128)(2,1)S(1)} collective-permute-done((bf16[1,16,1024]{2,1,0:T(8,128)(2,1)}, bf16[1,16,1024]{2,1,0:T(8,128)(2,1)S(1)}, u32[]{:S(2)}, u32[]{:S(2)}) %collective-permute-start) | collective-permute-done | bytes 32800 | tf_op jit(solution)/shard_map/ppermute | solution.py:61
  7.9 2.9 %collective-permute-done.1 = bf16[1,16,1024]{2,1,0:T(8,128)(2,1)S(1)} collective-permute-done((bf16[1,16,1024]{2,1,0:T(8,128)(2,1)}, bf16[1,16,1024]{2,1,0:T(8,128)(2,1)S(1)}, u32[]{:S(2)}, u32[]{:S(2)}) %collective-permute-start.1) | collective-permute-done | bytes 32800 | tf_op jit(solution)/shard_map/ppermute | solution.py:61
  10.8 0.0 collective-permute-done.2
  10.8 0.8 %pad_maximum_fusion.rows = bf16[4,16,1024]{2,1,0:T(8,128)(2,1)S(1)} fusion(bf16[1,16,1024]{2,1,0:T(8,128)(2,1)S(1)} %collective-permute-done.2, bf16[1,16,1024]{2,1,0:T(8,128)(2,1)S(1)} %collective-permute-done.1, bf16[1,16,1024]{2,1,0:T(8,128)(2,1)S(1)} %collective-permute-done, bf16[1,16,1024]{2,1,0:T(8,128)(2,1)} %bitcast.20), kind=kLoop, calls=%fused_computation.2 | loop fusion | flops 196608 | bytes 262144 | tf_op jit(solution)/shard_map/concatenate | solution.py:63
  11.6 1.6 %collective-permute-start.3 = (bf16[4,16,1024]{2,1,0:T(8,128)(2,1)S(1)}, bf16[4,16,1024]{2,1,0:T(8,128)(2,1)S(1)}, u32[]{:S(2)}, u32[]{:S(2)}) collective-permute-start(bf16[4,16,1024]{2,1,0:T(8,128)(2,1)S(1)} %pad_maximum_fusion.rows), channel_id=1, source_target_pairs={{0,2},{2,0},{4,6},{6,4},{8,10},{10,8},{12,14},{14,12},{1,3},{3,1},... | collective-permute-start | bytes 393224 | tf_op jit(solution)/shard_map/ppermute | solution.py:66
  13.2 0.0 copy-start.2
  13.2 3.5 %stage.1 = (bf16[1024,2048]{1,0:T(8,128)(2,1)S(1)}, bf16[1024,2048]{1,0:T(8,128)(2,1)S(1)}) custom-call(s32[1]{0:T(128)} %bitcast.after.index, bf16[1024,4096]{1,0:T(8,128)(2,1)} %whole.3), custom_call_target="tpu_custom_call" | custom-call | flops 1073741824 | bytes 16777216 | tf_op jit(solution)/shard_map/stage/pallas_call | solution.py:237
  16.7 0.0 copy-done.2
  16.7 3.5 %stage_rows.1 = (bf16[2048,1024]{1,0:T(8,128)(2,1)S(1)}, bf16[2048,1024]{1,0:T(8,128)(2,1)S(1)}, bf16[4,16,1024]{2,1,0:T(8,128)(2,1)S(1)}) custom-call(s32[1]{0:T(128)} %bitcast.after.index, bf16[4096,1024]{1,0:T(8,128)(2,1)} %whole.2, bf16[4,16,1024]{2,1,0:T(8,128)(2,1)S(1)} %pad_maximum_fusion.rows, f32[1,1024]{1,0:T(1,128)S(1)} %bitcast.25), custom_call_target="tpu_custom_call" | custom-call | flops 1073741824 | bytes 16777216 | tf_op jit(solution)/shard_map/stage_rows/pallas_call | solution.py:277
  20.2 0.0 collective-permute-done.3.theirs
  20.2 0.0 copy-start.1
  20.2 0.0 copy-start.3
  20.2 2.5 %feed.1 = bf16[128,1024]{1,0:T(8,128)(2,1)S(1)} custom-call(s32[1]{0:T(128)} %bitcast.after.index, bf16[4,16,1024]{2,1,0:T(8,128)(2,1)S(1)} %get-tuple-element.22.mine, bf16[4,16,1024]{2,1,0:T(8,128)(2,1)S(1)} %collective-permute-done.3.theirs, f32[1,1024]{1,0:T(1,128)S(1)} %bitcast.26, bf16[1024,2048]{1,0:T(8,128)(2,1)S(1)} %get-tuple-element.23.refs_0_, ...), custom_call_target="tpu_custom_call" | custom-call | flops 2147483648 | bytes 16777216 | tf_op jit(solution)/shard_map/feed/pallas_call | solution.py:324
  22.8 11.3 %all_to_all.10.parts = bf16[8,16,1024]{2,1,0:T(8,128)(2,1)S(1)} all-to-all(bf16[8,16,1024]{2,1,0:T(8,128)(2,1)S(1)} %bitcast.12), channel_id=1, replica_groups=mesh['groups'=2,'mp'=8,'psg'=2] {'mp'}, dimensions={0} | all-to-all | bytes 524288 | tf_op jit(solution)/shard_map/all_to_all | solution.py:561
  34.1 0.0 copy-done.1
  34.1 0.0 copy-done.3
  34.1 0.1 settle.1
  34.2 0.6 collective-permute-start.4
  34.9 0.9 %collective-permute-start.5 = (bf16[1,16,1024]{2,1,0:T(8,128)(2,1)S(1)}, bf16[1,16,1024]{2,1,0:T(8,128)(2,1)S(1)}, u32[]{:S(2)}, u32[]{:S(2)}) collective-permute-start(bf16[1,16,1024]{2,1,0:T(8,128)(2,1)S(1)} %bitcast.22), channel_id=1, source_target_pairs={{0,8},{2,10},{4,12},{6,14},{8,0},{10,2},{12,4},{14,6},{1,9},{3,11}... | collective-permute-start | bytes 98312 | tf_op jit(solution)/shard_map/ppermute | solution.py:61
  35.8 2.9 %collective-permute-start.6 = (bf16[1,16,1024]{2,1,0:T(8,128)(2,1)S(1)}, bf16[1,16,1024]{2,1,0:T(8,128)(2,1)S(1)}, u32[]{:S(2)}, u32[]{:S(2)}) collective-permute-start(bf16[1,16,1024]{2,1,0:T(8,128)(2,1)S(1)} %bitcast.23), channel_id=1, source_target_pairs={{0,4},{2,6},{4,0},{6,2},{8,12},{10,14},{12,8},{14,10},{1,5},{3,7},... | collective-permute-start | bytes 98312 | tf_op jit(solution)/shard_map/ppermute | solution.py:61
  38.7 1.3 %collective-permute-done.4 = bf16[1,16,1024]{2,1,0:T(8,128)(2,1)S(1)} collective-permute-done((bf16[1,16,1024]{2,1,0:T(8,128)(2,1)S(1)}, bf16[1,16,1024]{2,1,0:T(8,128)(2,1)S(1)}, u32[]{:S(2)}, u32[]{:S(2)}) %collective-permute-start.4) | collective-permute-done | bytes 32800 | tf_op jit(solution)/shard_map/ppermute | solution.py:61
  40.0 0.0 collective-permute-done.5
  40.0 0.5 collective-permute-done.6
  40.6 1.1 %collective-permute-start.8 = (bf16[4,16,1024]{2,1,0:T(8,128)(2,1)S(1)}, bf16[4,16,1024]{2,1,0:T(8,128)(2,1)S(1)}, u32[]{:S(2)}, u32[]{:S(2)}) collective-permute-start(bf16[4,16,1024]{2,1,0:T(8,128)(2,1)S(1)} %pad_maximum_fusion.1), channel_id=1, source_target_pairs={{0,2},{2,0},{4,6},{6,4},{8,10},{10,8},{12,14},{14,12},{1,3},{3,1},... | collective-permute-start | bytes 393224 | tf_op jit(solution)/shard_map/ppermute | solution.py:66
  41.7 0.0 collective-permute-start.7
  41.7 0.0 copy-start
  41.7 0.0 copy-start.4
  41.7 4.7 %prepare.1 = (bf16[1024,512]{1,0:T(8,128)(2,1)S(1)}, bf16[1024,512]{1,0:T(8,128)(2,1)S(1)}, bf16[1024,1024]{1,0:T(8,128)(2,1)}) custom-call(s32[1]{0:T(128)} %bitcast.1.half, bf16[1024,2,2048]{2,1,0:T(2,128)(2,1)} %w_keyval.1), custom_call_target="tpu_custom_call" | custom-call | flops 1073741824 | bytes 8388608 | tf_op jit(solution)/shard_map/prepare/pallas_call | solution.py:190
  46.4 0.0 copy-start.5
  46.5 0.0 copy-start.6
  46.5 0.0 copy-start.7
  46.5 0.0 collective-permute-done.8
  46.5 0.6 collective-permute-start.9
  47.1 0.0 copy-done
  47.1 0.0 copy-done.4
  47.1 2.3 %ask.1 = (bf16[128,1024]{1,0:T(8,128)(2,1)S(1)}, bf16[1024,512]{1,0:T(8,128)(2,1)S(1)}, bf16[1024,512]{1,0:T(8,128)(2,1)S(1)}) custom-call(s32[1]{0:T(128)} %bitcast.1.half, bf16[128,1024]{1,0:T(8,128)(2,1)S(1)} %copy-done, f32[1,1024]{1,0:T(1,128)S(1)} %bitcast.28, bf16[1024,2048]{1,0:T(8,128)(2,1)} %w_query.1, bf16[1024,1024]{1,0:T(8,128)(2,1)} %get-tuple-element.31.value), custom_call_target="tpu_custom_call" | custom-call | flops 1073741824 | bytes 4194304 | tf_op jit(solution)/shard_map/ask/pallas_call | solution.py:131
  49.4 0.0 collective-permute-done.7.theirs
  49.4 0.0 copy-done.5
  49.4 0.0 copy-done.6
  49.4 0.0 copy-done.7
  49.4 3.1 %project.1 = (bf16[128,1024]{1,0:T(8,128)(2,1)S(1)}, bf16[128,1024]{1,0:T(8,128)(2,1)S(1)}, bf16[1024,1024]{1,0:T(8,128)(2,1)S(1)}, s32[128,256]{1,0:T(8,128)S(1)}, bf16[16,1024]{1,0:T(8,128)(2,1)}) custom-call(s32[1]{0:T(128)} %bitcast.after.index, s32[1]{0:T(128)} %bitcast.1.half, s32[16]{0:T(128)S(1)} %copy-done.5, s32[16]{0:T(128)S(1)} %copy-done.6, ...), custom_call_target="tpu_custom_call" | custom-call | flops 536870912 | bytes 6291456 | tf_op jit(solution)/shard_map/project/pallas_call | solution.py:405
  52.6 0.0 collective-permute-done.9.theirs
  52.6 2.1 %attend.1 = (f32[64,1024]{1,0:T(8,128)S(1)}, f32[64,1024]{1,0:T(8,128)S(1)}) custom-call(bf16[128,1024]{1,0:T(8,128)(2,1)S(1)} %get-tuple-element.35.near_keys, bf16[128,1024]{1,0:T(8,128)(2,1)S(1)} %get-tuple-element.36.near_values, bf16[64,1024]{1,0:T(8,128)(2,1)S(1)} %bitcast.16, bf16[64,1024]{1,0:T(8,128)(2,1)S(1)} %collective-permute-done.9.theirs, ...), custom_call_target="tpu_custom_call" | custom-call | flops 939524096 | bytes 6291456 | tf_op jit(solution)/shard_map/attend/pallas_call | solution.py:471
  54.6 0.1 collective-permute-start.10
  54.7 1.5 %collective-permute-done.10 = f32[64,1024]{1,0:T(8,128)S(1)} collective-permute-done((f32[64,1024]{1,0:T(8,128)S(1)}, f32[64,1024]{1,0:T(8,128)S(1)}, u32[]{:S(2)}, u32[]{:S(2)}) %collective-permute-start.10) | collective-permute-done | bytes 262176 | tf_op jit(solution)/shard_map/ppermute | solution.py:75
  56.3 11.2 %all_to_all.11.parts = bf16[8,8,1024]{2,1,0:T(8,128)(2,1)S(1)} all-to-all(bf16[8,8,1024]{2,1,0:T(8,128)(2,1)S(1)} %fusion), channel_id=1, replica_groups=mesh['groups'=2,'mp'=8,'psg'=2] {'mp'}, dimensions={0} | all-to-all | bytes 262144 | tf_op jit(solution)/shard_map/all_to_all | solution.py:590
  67.4 0.2 finish.1.piece
  67.6 0.1 collective-permute-start.11
  67.7 1.2 %collective-permute-done.11.other = bf16[8,1024]{1,0:T(8,128)(2,1)S(1)} collective-permute-done((bf16[8,1024]{1,0:T(8,128)(2,1)S(1)}, bf16[8,1024]{1,0:T(8,128)(2,1)S(1)}, u32[]{:S(2)}, u32[]{:S(2)}) %collective-permute-start.11) | collective-permute-done | bytes 16416 | tf_op jit(solution)/shard_map/ppermute | solution.py:75
  68.9 0.6 join.1
  (2 shorter events, 0.1 us)
Async XLA Ops:
  0.6 7.2 %collective-permute-start = (bf16[1,16,1024]{2,1,0:T(8,128)(2,1)}, bf16[1,16,1024]{2,1,0:T(8,128)(2,1)S(1)}, u32[]{:S(2)}, u32[]{:S(2)}) collective-permute-start(bf16[1,16,1024]{2,1,0:T(8,128)(2,1)} %bitcast.17), channel_id=1, source_target_pairs={{0,12},{2,14},{4,8},{6,10},{8,4},{10,6},{12,0},{14,2},{1,13},{3,15... | collective-permute-start | bytes 98312 | tf_op jit(solution)/shard_map/ppermute | solution.py:61
  5.8 5.0 %collective-permute-start.1 = (bf16[1,16,1024]{2,1,0:T(8,128)(2,1)}, bf16[1,16,1024]{2,1,0:T(8,128)(2,1)S(1)}, u32[]{:S(2)}, u32[]{:S(2)}) collective-permute-start(bf16[1,16,1024]{2,1,0:T(8,128)(2,1)} %bitcast.18), channel_id=1, source_target_pairs={{0,8},{2,10},{4,12},{6,14},{8,0},{10,2},{12,4},{14,6},{1,9},{3,11}... | collective-permute-start | bytes 98312 | tf_op jit(solution)/shard_map/ppermute | solution.py:61
  5.8 5.0 %collective-permute-start.2 = (bf16[1,16,1024]{2,1,0:T(8,128)(2,1)}, bf16[1,16,1024]{2,1,0:T(8,128)(2,1)S(1)}, u32[]{:S(2)}, u32[]{:S(2)}) collective-permute-start(bf16[1,16,1024]{2,1,0:T(8,128)(2,1)} %bitcast.19), channel_id=1, source_target_pairs={{0,4},{2,6},{4,0},{6,2},{8,12},{10,14},{12,8},{14,10},{1,5},{3,7},... | collective-permute-start | bytes 98312 | tf_op jit(solution)/shard_map/ppermute | solution.py:61
  11.6 8.6 %collective-permute-start.3 = (bf16[4,16,1024]{2,1,0:T(8,128)(2,1)S(1)}, bf16[4,16,1024]{2,1,0:T(8,128)(2,1)S(1)}, u32[]{:S(2)}, u32[]{:S(2)}) collective-permute-start(bf16[4,16,1024]{2,1,0:T(8,128)(2,1)S(1)} %pad_maximum_fusion.rows), channel_id=1, source_target_pairs={{0,2},{2,0},{4,6},{6,4},{8,10},{10,8},{12,14},{14,12},{1,3},{3,1},... | collective-permute-start | bytes 393224 | tf_op jit(solution)/shard_map/ppermute | solution.py:66
  13.2 3.6 %copy-start.2 = (f32[1024]{0:T(1024)S(1)}, f32[1024]{0:T(1024)}, u32[]{:S(2)}) copy-start(f32[1024]{0:T(1024)} %param.14) | copy-start | bytes 12292
  20.2 13.9 %copy-start.1 = (bf16[16,1024]{1,0:T(8,128)(2,1)S(1)}, bf16[16,1024]{1,0:T(8,128)(2,1)}, u32[]{:S(2)}) copy-start(bf16[16,1024]{1,0:T(8,128)(2,1)} %tokens.1) | copy-start | bytes 98308
  20.2 13.9 %copy-start.3 = (f32[1024]{0:T(1024)S(1)}, f32[1024]{0:T(1024)}, u32[]{:S(2)}) copy-start(f32[1024]{0:T(1024)} %param.17) | copy-start | bytes 12292
  34.2 5.8 %collective-permute-start.4 = (bf16[1,16,1024]{2,1,0:T(8,128)(2,1)S(1)}, bf16[1,16,1024]{2,1,0:T(8,128)(2,1)S(1)}, u32[]{:S(2)}, u32[]{:S(2)}) collective-permute-start(bf16[1,16,1024]{2,1,0:T(8,128)(2,1)S(1)} %bitcast.21), channel_id=1, source_target_pairs={{0,12},{2,14},{4,8},{6,10},{8,4},{10,6},{12,0},{14,2},{1,13},{3,15... | collective-permute-start | bytes 98312 | tf_op jit(solution)/shard_map/ppermute | solution.py:61
  34.9 5.2 %collective-permute-start.5 = (bf16[1,16,1024]{2,1,0:T(8,128)(2,1)S(1)}, bf16[1,16,1024]{2,1,0:T(8,128)(2,1)S(1)}, u32[]{:S(2)}, u32[]{:S(2)}) collective-permute-start(bf16[1,16,1024]{2,1,0:T(8,128)(2,1)S(1)} %bitcast.22), channel_id=1, source_target_pairs={{0,8},{2,10},{4,12},{6,14},{8,0},{10,2},{12,4},{14,6},{1,9},{3,11}... | collective-permute-start | bytes 98312 | tf_op jit(solution)/shard_map/ppermute | solution.py:61
  35.8 4.8 %collective-permute-start.6 = (bf16[1,16,1024]{2,1,0:T(8,128)(2,1)S(1)}, bf16[1,16,1024]{2,1,0:T(8,128)(2,1)S(1)}, u32[]{:S(2)}, u32[]{:S(2)}) collective-permute-start(bf16[1,16,1024]{2,1,0:T(8,128)(2,1)S(1)} %bitcast.23), channel_id=1, source_target_pairs={{0,4},{2,6},{4,0},{6,2},{8,12},{10,14},{12,8},{14,10},{1,5},{3,7},... | collective-permute-start | bytes 98312 | tf_op jit(solution)/shard_map/ppermute | solution.py:61
  40.6 5.9 %collective-permute-start.8 = (bf16[4,16,1024]{2,1,0:T(8,128)(2,1)S(1)}, bf16[4,16,1024]{2,1,0:T(8,128)(2,1)S(1)}, u32[]{:S(2)}, u32[]{:S(2)}) collective-permute-start(bf16[4,16,1024]{2,1,0:T(8,128)(2,1)S(1)} %pad_maximum_fusion.1), channel_id=1, source_target_pairs={{0,2},{2,0},{4,6},{6,4},{8,10},{10,8},{12,14},{14,12},{1,3},{3,1},... | collective-permute-start | bytes 393224 | tf_op jit(solution)/shard_map/ppermute | solution.py:66
  41.7 7.6 %collective-permute-start.7 = (bf16[64,1024]{1,0:T(8,128)(2,1)S(1)}, bf16[64,1024]{1,0:T(8,128)(2,1)S(1)}, u32[]{:S(2)}, u32[]{:S(2)}) collective-permute-start(bf16[64,1024]{1,0:T(8,128)(2,1)S(1)} %bitcast.13), channel_id=1, source_target_pairs={{0,1},{1,0},{2,3},{3,2},{4,5},{5,4},{6,7},{7,6},{8,9},{9,8},{10,11... | collective-permute-start | bytes 393224 | tf_op jit(solution)/shard_map/ppermute | solution.py:75
  41.7 5.3 %copy-start = (bf16[128,1024]{1,0:T(8,128)(2,1)S(1)}, bf16[128,1024]{1,0:T(8,128)(2,1)}, u32[]{:S(2)}) copy-start(bf16[128,1024]{1,0:T(8,128)(2,1)} %states.3) | copy-start | bytes 786436
  41.7 5.3 %copy-start.4 = (f32[1024]{0:T(1024)S(1)}, f32[1024]{0:T(1024)}, u32[]{:S(2)}) copy-start(f32[1024]{0:T(1024)} %param.20) | copy-start | bytes 12292
  46.4 2.9 %copy-start.5 = (s32[16]{0:T(128)S(1)}, s32[16]{0:T(128)}, u32[]{:S(2)}) copy-start(s32[16]{0:T(128)} %lengths.1) | copy-start | bytes 196
  46.5 2.9 %copy-start.6 = (s32[16]{0:T(128)S(1)}, s32[16]{0:T(128)}, u32[]{:S(2)}) copy-start(s32[16]{0:T(128)} %owners.1) | copy-start | bytes 196
  46.5 2.9 %copy-start.7 = (s32[4]{0:T(128)S(1)}, s32[4]{0:T(128)}, u32[]{:S(2)}) copy-start(s32[4]{0:T(128)} %answers.1) | copy-start | bytes 52
  46.5 6.1 %collective-permute-start.9 = (bf16[64,1024]{1,0:T(8,128)(2,1)S(1)}, bf16[64,1024]{1,0:T(8,128)(2,1)S(1)}, u32[]{:S(2)}, u32[]{:S(2)}) collective-permute-start(bf16[64,1024]{1,0:T(8,128)(2,1)S(1)} %bitcast.15), channel_id=1, source_target_pairs={{0,1},{1,0},{2,3},{3,2},{4,5},{5,4},{6,7},{7,6},{8,9},{9,8},{10,11... | collective-permute-start | bytes 393224 | tf_op jit(solution)/shard_map/ppermute | solution.py:75
  54.6 1.6 %collective-permute-start.10 = (f32[64,1024]{1,0:T(8,128)S(1)}, f32[64,1024]{1,0:T(8,128)S(1)}, u32[]{:S(2)}, u32[]{:S(2)}) collective-permute-start(f32[64,1024]{1,0:T(8,128)S(1)} %get-tuple-element.41), channel_id=1, source_target_pairs={{0,1},{1,0},{2,3},{3,2},{4,5},{5,4},{6,7},{7,6},{8,9},{9,8},{10,11... | collective-permute-start | bytes 786440 | tf_op jit(solution)/shard_map/ppermute | solution.py:75
  67.6 1.2 %collective-permute-start.11 = (bf16[8,1024]{1,0:T(8,128)(2,1)S(1)}, bf16[8,1024]{1,0:T(8,128)(2,1)S(1)}, u32[]{:S(2)}, u32[]{:S(2)}) collective-permute-start(bf16[8,1024]{1,0:T(8,128)(2,1)S(1)} %finish.1.piece), channel_id=1, source_target_pairs={{0,1},{1,0},{2,3},{3,2},{4,5},{5,4},{6,7},{7,6},{8,9},{9,8},{10,11... | collective-permute-start | bytes 49160 | tf_op jit(solution)/shard_map/ppermute | solution.py:75

commit v12 on v11

--- a/solution.py
+++ b/solution.py
@@ -461,7 +461,7 @@
         columns = pl.ds(c * 256, 256)
         result = jnp.dot(context[...], w_last[:, columns], preferred_element_type=F32)
         keep[:, columns] = result[: keep.shape[0]]
-        give[:, columns] = result[keep.shape[0] :]
+        give[:, columns] = result[keep.shape[0] :].astype(BF16)
 
 
 def attend(near_keys, near_values, mine, theirs, query, allowed, weights, w_last):
@@ -470,7 +470,10 @@
     count, inner = query.shape
     return pl.pallas_call(
         attend_kernel,
-        out_shape=(jax.ShapeDtypeStruct((count // 2, width), F32),) * 2,
+        out_shape=(
+            jax.ShapeDtypeStruct((count // 2, width), F32),
+            jax.ShapeDtypeStruct((count // 2, width), BF16),
+        ),
         in_specs=[VMEM_SPEC] * 11,
         out_specs=(VMEM_SPEC, VMEM_SPEC),
         scratch_shapes=[pltpu.VMEM((count, inner), BF16)],
@@ -586,7 +589,7 @@
     keep, give = attend(
         near_keys, near_values, got, got_theirs, query, allowed, weights, w_last
     )
-    chip_sum = (keep + swap_psg(give)).astype(BF16).reshape(mp, small, width)
+    chip_sum = (keep + swap_psg(give).astype(F32)).astype(BF16).reshape(mp, small, width)
     answer_parts = lax.all_to_all(chip_sum, "mp", 0, 0)
     piece = finish(index, half, answer_parts, answer_states)
     return (encoded, join(half, piece, swap_psg(piece)))

time: 69.8 us -> 69.6 us (level)
  no operation moved by 1% of the time
where the time goes in v12:
time: 69.6 us; the launch traced here: 69.3 us
  Pallas kernels  22.6 us (32%)
  blocking collectives  22.5 us (32%)
  starting transfers between devices  13.7 us (20%)
  waiting for transfers between devices  8.77 us (13%)
  other arithmetic  0.83 us (1%)
  between operations  0.83 us (1%)
    all_to_all x1, blocking collectives, per_device(): lax.all_to_all(partial_sums.reshape(mp, row_count, width), 'mp', 0, 0)  11.3 us
    all_to_all x1, blocking collectives, per_device(): answer_parts = lax.all_to_all(chip_sum, 'mp', 0, 0)  11.2 us
    ppermute x6, starting transfers between devices, spread_out(): lax.ppermute(x[None], 'mp', [(j, j ^ k * quarter) for j in range(mp)])  10.2 us
    ppermute x6, waiting for transfers between devices, spread_out(): lax.ppermute(x[None], 'mp', [(j, j ^ k * quarter) for j in range(mp)])  6.27 us
    pallas_call x1, Pallas kernels, prepare(): pl.pallas_call(prepare_kernel, out_shape=(jax.ShapeDtypeStruct((width, in...  4.7 us
    pallas_call x1, Pallas kernels, stage(): pl.pallas_call(functools.partial(stage_kernel, axis=axis), out_shape=(par...  3.54 us
    pallas_call x1, Pallas kernels, stage_rows(): pl.pallas_call(stage_rows_kernel, out_shape=(part, part, jax.ShapeDtypeSt...  3.48 us
    pallas_call x1, Pallas kernels, project(): pl.pallas_call(functools.partial(project_kernel, patterns=patterns, mp=mp...  3.15 us
  transfers between devices with their start and end apart: 12, of which 6 were waited for; matrix products, arithmetic and copies ran while one was open for 0% of the time, Pallas kernels for 25%

profile of v12, /device:TPU:0, one launch (start us, length us, event | category | flops | bytes accessed | tf_op | source)
XLA Modules:
  0.0 69.3 jit_solution(10730795275561189650)
XLA Ops:
  0.6 5.1 %collective-permute-start = (bf16[1,16,1024]{2,1,0:T(8,128)(2,1)}, bf16[1,16,1024]{2,1,0:T(8,128)(2,1)S(1)}, u32[]{:S(2)}, u32[]{:S(2)}) collective-permute-start(bf16[1,16,1024]{2,1,0:T(8,128)(2,1)} %bitcast.17), channel_id=1, source_target_pairs={{0,12},{2,14},{4,8},{6,10},{8,4},{10,6},{12,0},{14,2},{1,13},{3,15... | collective-permute-start | bytes 98312 | tf_op jit(solution)/shard_map/ppermute | solution.py:61
  5.8 0.0 collective-permute-start.1
  5.8 0.6 collective-permute-start.2
  6.4 1.5 %collective-permute-done = bf16[1,16,1024]{2,1,0:T(8,128)(2,1)S(1)} collective-permute-done((bf16[1,16,1024]{2,1,0:T(8,128)(2,1)}, bf16[1,16,1024]{2,1,0:T(8,128)(2,1)S(1)}, u32[]{:S(2)}, u32[]{:S(2)}) %collective-permute-start) | collective-permute-done | bytes 32800 | tf_op jit(solution)/shard_map/ppermute | solution.py:61
  7.9 2.9 %collective-permute-done.1 = bf16[1,16,1024]{2,1,0:T(8,128)(2,1)S(1)} collective-permute-done((bf16[1,16,1024]{2,1,0:T(8,128)(2,1)}, bf16[1,16,1024]{2,1,0:T(8,128)(2,1)S(1)}, u32[]{:S(2)}, u32[]{:S(2)}) %collective-permute-start.1) | collective-permute-done | bytes 32800 | tf_op jit(solution)/shard_map/ppermute | solution.py:61
  10.8 0.0 collective-permute-done.2
  10.8 0.8 %pad_maximum_fusion.rows = bf16[4,16,1024]{2,1,0:T(8,128)(2,1)S(1)} fusion(bf16[1,16,1024]{2,1,0:T(8,128)(2,1)S(1)} %collective-permute-done.2, bf16[1,16,1024]{2,1,0:T(8,128)(2,1)S(1)} %collective-permute-done.1, bf16[1,16,1024]{2,1,0:T(8,128)(2,1)S(1)} %collective-permute-done, bf16[1,16,1024]{2,1,0:T(8,128)(2,1)} %bitcast.20), kind=kLoop, calls=%fused_computation.2 | loop fusion | flops 196608 | bytes 262144 | tf_op jit(solution)/shard_map/concatenate | solution.py:63
  11.6 1.6 %collective-permute-start.3 = (bf16[4,16,1024]{2,1,0:T(8,128)(2,1)S(1)}, bf16[4,16,1024]{2,1,0:T(8,128)(2,1)S(1)}, u32[]{:S(2)}, u32[]{:S(2)}) collective-permute-start(bf16[4,16,1024]{2,1,0:T(8,128)(2,1)S(1)} %pad_maximum_fusion.rows), channel_id=1, source_target_pairs={{0,2},{2,0},{4,6},{6,4},{8,10},{10,8},{12,14},{14,12},{1,3},{3,1},... | collective-permute-start | bytes 393224 | tf_op jit(solution)/shard_map/ppermute | solution.py:66
  13.2 0.0 copy-start.2
  13.2 3.5 %stage.1 = (bf16[1024,2048]{1,0:T(8,128)(2,1)S(1)}, bf16[1024,2048]{1,0:T(8,128)(2,1)S(1)}) custom-call(s32[1]{0:T(128)} %bitcast.after.index, bf16[1024,4096]{1,0:T(8,128)(2,1)} %whole.3), custom_call_target="tpu_custom_call" | custom-call | flops 1073741824 | bytes 16777216 | tf_op jit(solution)/shard_map/stage/pallas_call | solution.py:237
  16.7 0.0 copy-done.2
  16.7 3.5 %stage_rows.1 = (bf16[2048,1024]{1,0:T(8,128)(2,1)S(1)}, bf16[2048,1024]{1,0:T(8,128)(2,1)S(1)}, bf16[4,16,1024]{2,1,0:T(8,128)(2,1)S(1)}) custom-call(s32[1]{0:T(128)} %bitcast.after.index, bf16[4096,1024]{1,0:T(8,128)(2,1)} %whole.2, bf16[4,16,1024]{2,1,0:T(8,128)(2,1)S(1)} %pad_maximum_fusion.rows, f32[1,1024]{1,0:T(1,128)S(1)} %bitcast.25), custom_call_target="tpu_custom_call" | custom-call | flops 1073741824 | bytes 16777216 | tf_op jit(solution)/shard_map/stage_rows/pallas_call | solution.py:277
  20.2 0.0 collective-permute-done.3.theirs
  20.2 0.0 copy-start.1
  20.2 0.0 copy-start.3
  20.2 2.5 %feed.1 = bf16[128,1024]{1,0:T(8,128)(2,1)S(1)} custom-call(s32[1]{0:T(128)} %bitcast.after.index, bf16[4,16,1024]{2,1,0:T(8,128)(2,1)S(1)} %get-tuple-element.22.mine, bf16[4,16,1024]{2,1,0:T(8,128)(2,1)S(1)} %collective-permute-done.3.theirs, f32[1,1024]{1,0:T(1,128)S(1)} %bitcast.26, bf16[1024,2048]{1,0:T(8,128)(2,1)S(1)} %get-tuple-element.23.refs_0_, ...), custom_call_target="tpu_custom_call" | custom-call | flops 2147483648 | bytes 16777216 | tf_op jit(solution)/shard_map/feed/pallas_call | solution.py:324
  22.8 11.3 %all_to_all.10.parts = bf16[8,16,1024]{2,1,0:T(8,128)(2,1)S(1)} all-to-all(bf16[8,16,1024]{2,1,0:T(8,128)(2,1)S(1)} %bitcast.12), channel_id=1, replica_groups=mesh['groups'=2,'mp'=8,'psg'=2] {'mp'}, dimensions={0} | all-to-all | bytes 524288 | tf_op jit(solution)/shard_map/all_to_all | solution.py:564
  34.1 0.0 copy-done.1
  34.1 0.0 copy-done.3
  34.1 0.1 settle.1
  34.2 0.6 collective-permute-start.4
  34.9 0.9 %collective-permute-start.5 = (bf16[1,16,1024]{2,1,0:T(8,128)(2,1)S(1)}, bf16[1,16,1024]{2,1,0:T(8,128)(2,1)S(1)}, u32[]{:S(2)}, u32[]{:S(2)}) collective-permute-start(bf16[1,16,1024]{2,1,0:T(8,128)(2,1)S(1)} %bitcast.22), channel_id=1, source_target_pairs={{0,8},{2,10},{4,12},{6,14},{8,0},{10,2},{12,4},{14,6},{1,9},{3,11}... | collective-permute-start | bytes 98312 | tf_op jit(solution)/shard_map/ppermute | solution.py:61
  35.8 2.9 %collective-permute-start.6 = (bf16[1,16,1024]{2,1,0:T(8,128)(2,1)S(1)}, bf16[1,16,1024]{2,1,0:T(8,128)(2,1)S(1)}, u32[]{:S(2)}, u32[]{:S(2)}) collective-permute-start(bf16[1,16,1024]{2,1,0:T(8,128)(2,1)S(1)} %bitcast.23), channel_id=1, source_target_pairs={{0,4},{2,6},{4,0},{6,2},{8,12},{10,14},{12,8},{14,10},{1,5},{3,7},... | collective-permute-start | bytes 98312 | tf_op jit(solution)/shard_map/ppermute | solution.py:61
  38.7 1.3 %collective-permute-done.4 = bf16[1,16,1024]{2,1,0:T(8,128)(2,1)S(1)} collective-permute-done((bf16[1,16,1024]{2,1,0:T(8,128)(2,1)S(1)}, bf16[1,16,1024]{2,1,0:T(8,128)(2,1)S(1)}, u32[]{:S(2)}, u32[]{:S(2)}) %collective-permute-start.4) | collective-permute-done | bytes 32800 | tf_op jit(solution)/shard_map/ppermute | solution.py:61
  40.0 0.0 collective-permute-done.5
  40.0 0.5 collective-permute-done.6
  40.6 1.1 %collective-permute-start.8 = (bf16[4,16,1024]{2,1,0:T(8,128)(2,1)S(1)}, bf16[4,16,1024]{2,1,0:T(8,128)(2,1)S(1)}, u32[]{:S(2)}, u32[]{:S(2)}) collective-permute-start(bf16[4,16,1024]{2,1,0:T(8,128)(2,1)S(1)} %pad_maximum_fusion.1), channel_id=1, source_target_pairs={{0,2},{2,0},{4,6},{6,4},{8,10},{10,8},{12,14},{14,12},{1,3},{3,1},... | collective-permute-start | bytes 393224 | tf_op jit(solution)/shard_map/ppermute | solution.py:66
  41.7 0.0 collective-permute-start.7
  41.7 0.0 copy-start
  41.7 0.0 copy-start.4
  41.7 4.7 %prepare.1 = (bf16[1024,512]{1,0:T(8,128)(2,1)S(1)}, bf16[1024,512]{1,0:T(8,128)(2,1)S(1)}, bf16[1024,1024]{1,0:T(8,128)(2,1)}) custom-call(s32[1]{0:T(128)} %bitcast.1.half, bf16[1024,2,2048]{2,1,0:T(2,128)(2,1)} %w_keyval.1), custom_call_target="tpu_custom_call" | custom-call | flops 1073741824 | bytes 8388608 | tf_op jit(solution)/shard_map/prepare/pallas_call | solution.py:190
  46.4 0.0 copy-start.5
  46.5 0.0 copy-start.6
  46.5 0.0 copy-start.7
  46.5 0.0 collective-permute-done.8
  46.5 0.6 collective-permute-start.9
  47.1 0.0 copy-done
  47.1 0.0 copy-done.4
  47.1 2.3 %ask.1 = (bf16[128,1024]{1,0:T(8,128)(2,1)S(1)}, bf16[1024,512]{1,0:T(8,128)(2,1)S(1)}, bf16[1024,512]{1,0:T(8,128)(2,1)S(1)}) custom-call(s32[1]{0:T(128)} %bitcast.1.half, bf16[128,1024]{1,0:T(8,128)(2,1)S(1)} %copy-done, f32[1,1024]{1,0:T(1,128)S(1)} %bitcast.28, bf16[1024,2048]{1,0:T(8,128)(2,1)} %w_query.1, bf16[1024,1024]{1,0:T(8,128)(2,1)} %get-tuple-element.31.value), custom_call_target="tpu_custom_call" | custom-call | flops 1073741824 | bytes 4194304 | tf_op jit(solution)/shard_map/ask/pallas_call | solution.py:131
  49.4 0.0 collective-permute-done.7.theirs
  49.4 0.0 copy-done.5
  49.4 0.0 copy-done.6
  49.4 0.0 copy-done.7
  49.4 3.1 %project.1 = (bf16[128,1024]{1,0:T(8,128)(2,1)S(1)}, bf16[128,1024]{1,0:T(8,128)(2,1)S(1)}, bf16[1024,1024]{1,0:T(8,128)(2,1)S(1)}, s32[128,256]{1,0:T(8,128)S(1)}, bf16[16,1024]{1,0:T(8,128)(2,1)}) custom-call(s32[1]{0:T(128)} %bitcast.after.index, s32[1]{0:T(128)} %bitcast.1.half, s32[16]{0:T(128)S(1)} %copy-done.5, s32[16]{0:T(128)S(1)} %copy-done.6, ...), custom_call_target="tpu_custom_call" | custom-call | flops 536870912 | bytes 6291456 | tf_op jit(solution)/shard_map/project/pallas_call | solution.py:405
  52.6 0.0 collective-permute-done.9.theirs
  52.6 2.1 %attend.1 = (f32[64,1024]{1,0:T(8,128)S(1)}, bf16[64,1024]{1,0:T(8,128)(2,1)S(1)}) custom-call(bf16[128,1024]{1,0:T(8,128)(2,1)S(1)} %get-tuple-element.35.near_keys, bf16[128,1024]{1,0:T(8,128)(2,1)S(1)} %get-tuple-element.36.near_values, bf16[64,1024]{1,0:T(8,128)(2,1)S(1)} %bitcast.16, bf16[64,1024]{1,0:T(8,128)(2,1)S(1)} %collective-permute-done.9.theirs, ...), custom_call_target="tpu_custom_call" | custom-call | flops 939524096 | bytes 6291456 | tf_op jit(solution)/shard_map/attend/pallas_call | solution.py:471
  54.6 0.1 collective-permute-start.10
  54.7 1.3 %collective-permute-done.10 = bf16[64,1024]{1,0:T(8,128)(2,1)S(1)} collective-permute-done((bf16[64,1024]{1,0:T(8,128)(2,1)S(1)}, bf16[64,1024]{1,0:T(8,128)(2,1)S(1)}, u32[]{:S(2)}, u32[]{:S(2)}) %collective-permute-start.10) | collective-permute-done | bytes 131104 | tf_op jit(solution)/shard_map/ppermute | solution.py:75
  56.1 11.2 %all_to_all.11.parts = bf16[8,8,1024]{2,1,0:T(8,128)(2,1)S(1)} all-to-all(bf16[8,8,1024]{2,1,0:T(8,128)(2,1)S(1)} %fusion), channel_id=1, replica_groups=mesh['groups'=2,'mp'=8,'psg'=2] {'mp'}, dimensions={0} | all-to-all | bytes 262144 | tf_op jit(solution)/shard_map/all_to_all | solution.py:593
  67.3 0.2 finish.1.piece
  67.4 0.1 collective-permute-start.11
  67.5 1.2 %collective-permute-done.11.other = bf16[8,1024]{1,0:T(8,128)(2,1)S(1)} collective-permute-done((bf16[8,1024]{1,0:T(8,128)(2,1)S(1)}, bf16[8,1024]{1,0:T(8,128)(2,1)S(1)}, u32[]{:S(2)}, u32[]{:S(2)}) %collective-permute-start.11) | collective-permute-done | bytes 16416 | tf_op jit(solution)/shard_map/ppermute | solution.py:75
  68.7 0.6 join.1
  (2 shorter events, 0.1 us)
Async XLA Ops:
  0.6 7.2 %collective-permute-start = (bf16[1,16,1024]{2,1,0:T(8,128)(2,1)}, bf16[1,16,1024]{2,1,0:T(8,128)(2,1)S(1)}, u32[]{:S(2)}, u32[]{:S(2)}) collective-permute-start(bf16[1,16,1024]{2,1,0:T(8,128)(2,1)} %bitcast.17), channel_id=1, source_target_pairs={{0,12},{2,14},{4,8},{6,10},{8,4},{10,6},{12,0},{14,2},{1,13},{3,15... | collective-permute-start | bytes 98312 | tf_op jit(solution)/shard_map/ppermute | solution.py:61
  5.8 5.0 %collective-permute-start.1 = (bf16[1,16,1024]{2,1,0:T(8,128)(2,1)}, bf16[1,16,1024]{2,1,0:T(8,128)(2,1)S(1)}, u32[]{:S(2)}, u32[]{:S(2)}) collective-permute-start(bf16[1,16,1024]{2,1,0:T(8,128)(2,1)} %bitcast.18), channel_id=1, source_target_pairs={{0,8},{2,10},{4,12},{6,14},{8,0},{10,2},{12,4},{14,6},{1,9},{3,11}... | collective-permute-start | bytes 98312 | tf_op jit(solution)/shard_map/ppermute | solution.py:61
  5.8 5.0 %collective-permute-start.2 = (bf16[1,16,1024]{2,1,0:T(8,128)(2,1)}, bf16[1,16,1024]{2,1,0:T(8,128)(2,1)S(1)}, u32[]{:S(2)}, u32[]{:S(2)}) collective-permute-start(bf16[1,16,1024]{2,1,0:T(8,128)(2,1)} %bitcast.19), channel_id=1, source_target_pairs={{0,4},{2,6},{4,0},{6,2},{8,12},{10,14},{12,8},{14,10},{1,5},{3,7},... | collective-permute-start | bytes 98312 | tf_op jit(solution)/shard_map/ppermute | solution.py:61
  11.6 8.6 %collective-permute-start.3 = (bf16[4,16,1024]{2,1,0:T(8,128)(2,1)S(1)}, bf16[4,16,1024]{2,1,0:T(8,128)(2,1)S(1)}, u32[]{:S(2)}, u32[]{:S(2)}) collective-permute-start(bf16[4,16,1024]{2,1,0:T(8,128)(2,1)S(1)} %pad_maximum_fusion.rows), channel_id=1, source_target_pairs={{0,2},{2,0},{4,6},{6,4},{8,10},{10,8},{12,14},{14,12},{1,3},{3,1},... | collective-permute-start | bytes 393224 | tf_op jit(solution)/shard_map/ppermute | solution.py:66
  13.2 3.6 %copy-start.2 = (f32[1024]{0:T(1024)S(1)}, f32[1024]{0:T(1024)}, u32[]{:S(2)}) copy-start(f32[1024]{0:T(1024)} %param.14) | copy-start | bytes 12292
  20.2 13.9 %copy-start.1 = (bf16[16,1024]{1,0:T(8,128)(2,1)S(1)}, bf16[16,1024]{1,0:T(8,128)(2,1)}, u32[]{:S(2)}) copy-start(bf16[16,1024]{1,0:T(8,128)(2,1)} %tokens.1) | copy-start | bytes 98308
  20.2 13.9 %copy-start.3 = (f32[1024]{0:T(1024)S(1)}, f32[1024]{0:T(1024)}, u32[]{:S(2)}) copy-start(f32[1024]{0:T(1024)} %param.17) | copy-start | bytes 12292
  34.2 5.8 %collective-permute-start.4 = (bf16[1,16,1024]{2,1,0:T(8,128)(2,1)S(1)}, bf16[1,16,1024]{2,1,0:T(8,128)(2,1)S(1)}, u32[]{:S(2)}, u32[]{:S(2)}) collective-permute-start(bf16[1,16,1024]{2,1,0:T(8,128)(2,1)S(1)} %bitcast.21), channel_id=1, source_target_pairs={{0,12},{2,14},{4,8},{6,10},{8,4},{10,6},{12,0},{14,2},{1,13},{3,15... | collective-permute-start | bytes 98312 | tf_op jit(solution)/shard_map/ppermute | solution.py:61
  34.9 5.2 %collective-permute-start.5 = (bf16[1,16,1024]{2,1,0:T(8,128)(2,1)S(1)}, bf16[1,16,1024]{2,1,0:T(8,128)(2,1)S(1)}, u32[]{:S(2)}, u32[]{:S(2)}) collective-permute-start(bf16[1,16,1024]{2,1,0:T(8,128)(2,1)S(1)} %bitcast.22), channel_id=1, source_target_pairs={{0,8},{2,10},{4,12},{6,14},{8,0},{10,2},{12,4},{14,6},{1,9},{3,11}... | collective-permute-start | bytes 98312 | tf_op jit(solution)/shard_map/ppermute | solution.py:61
  35.8 4.8 %collective-permute-start.6 = (bf16[1,16,1024]{2,1,0:T(8,128)(2,1)S(1)}, bf16[1,16,1024]{2,1,0:T(8,128)(2,1)S(1)}, u32[]{:S(2)}, u32[]{:S(2)}) collective-permute-start(bf16[1,16,1024]{2,1,0:T(8,128)(2,1)S(1)} %bitcast.23), channel_id=1, source_target_pairs={{0,4},{2,6},{4,0},{6,2},{8,12},{10,14},{12,8},{14,10},{1,5},{3,7},... | collective-permute-start | bytes 98312 | tf_op jit(solution)/shard_map/ppermute | solution.py:61
  40.6 5.9 %collective-permute-start.8 = (bf16[4,16,1024]{2,1,0:T(8,128)(2,1)S(1)}, bf16[4,16,1024]{2,1,0:T(8,128)(2,1)S(1)}, u32[]{:S(2)}, u32[]{:S(2)}) collective-permute-start(bf16[4,16,1024]{2,1,0:T(8,128)(2,1)S(1)} %pad_maximum_fusion.1), channel_id=1, source_target_pairs={{0,2},{2,0},{4,6},{6,4},{8,10},{10,8},{12,14},{14,12},{1,3},{3,1},... | collective-permute-start | bytes 393224 | tf_op jit(solution)/shard_map/ppermute | solution.py:66
  41.7 7.6 %collective-permute-start.7 = (bf16[64,1024]{1,0:T(8,128)(2,1)S(1)}, bf16[64,1024]{1,0:T(8,128)(2,1)S(1)}, u32[]{:S(2)}, u32[]{:S(2)}) collective-permute-start(bf16[64,1024]{1,0:T(8,128)(2,1)S(1)} %bitcast.13), channel_id=1, source_target_pairs={{0,1},{1,0},{2,3},{3,2},{4,5},{5,4},{6,7},{7,6},{8,9},{9,8},{10,11... | collective-permute-start | bytes 393224 | tf_op jit(solution)/shard_map/ppermute | solution.py:75
  41.7 5.3 %copy-start = (bf16[128,1024]{1,0:T(8,128)(2,1)S(1)}, bf16[128,1024]{1,0:T(8,128)(2,1)}, u32[]{:S(2)}) copy-start(bf16[128,1024]{1,0:T(8,128)(2,1)} %states.3) | copy-start | bytes 786436
  41.7 5.3 %copy-start.4 = (f32[1024]{0:T(1024)S(1)}, f32[1024]{0:T(1024)}, u32[]{:S(2)}) copy-start(f32[1024]{0:T(1024)} %param.20) | copy-start | bytes 12292
  46.4 2.9 %copy-start.5 = (s32[16]{0:T(128)S(1)}, s32[16]{0:T(128)}, u32[]{:S(2)}) copy-start(s32[16]{0:T(128)} %lengths.1) | copy-start | bytes 196
  46.5 2.9 %copy-start.6 = (s32[16]{0:T(128)S(1)}, s32[16]{0:T(128)}, u32[]{:S(2)}) copy-start(s32[16]{0:T(128)} %owners.1) | copy-start | bytes 196
  46.5 2.9 %copy-start.7 = (s32[4]{0:T(128)S(1)}, s32[4]{0:T(128)}, u32[]{:S(2)}) copy-start(s32[4]{0:T(128)} %answers.1) | copy-start | bytes 52
  46.5 6.1 %collective-permute-start.9 = (bf16[64,1024]{1,0:T(8,128)(2,1)S(1)}, bf16[64,1024]{1,0:T(8,128)(2,1)S(1)}, u32[]{:S(2)}, u32[]{:S(2)}) collective-permute-start(bf16[64,1024]{1,0:T(8,128)(2,1)S(1)} %bitcast.15), channel_id=1, source_target_pairs={{0,1},{1,0},{2,3},{3,2},{4,5},{5,4},{6,7},{7,6},{8,9},{9,8},{10,11... | collective-permute-start | bytes 393224 | tf_op jit(solution)/shard_map/ppermute | solution.py:75
  54.6 1.4 %collective-permute-start.10 = (bf16[64,1024]{1,0:T(8,128)(2,1)S(1)}, bf16[64,1024]{1,0:T(8,128)(2,1)S(1)}, u32[]{:S(2)}, u32[]{:S(2)}) collective-permute-start(bf16[64,1024]{1,0:T(8,128)(2,1)S(1)} %get-tuple-element.41), channel_id=1, source_target_pairs={{0,1},{1,0},{2,3},{3,2},{4,5},{5,4},{6,7},{7,6},{8,9},{9,8},{10,11... | collective-permute-start | bytes 393224 | tf_op jit(solution)/shard_map/ppermute | solution.py:75
  67.4 1.2 %collective-permute-start.11 = (bf16[8,1024]{1,0:T(8,128)(2,1)S(1)}, bf16[8,1024]{1,0:T(8,128)(2,1)S(1)}, u32[]{:S(2)}, u32[]{:S(2)}) collective-permute-start(bf16[8,1024]{1,0:T(8,128)(2,1)S(1)} %finish.1.piece), channel_id=1, source_target_pairs={{0,1},{1,0},{2,3},{3,2},{4,5},{5,4},{6,7},{7,6},{8,9},{9,8},{10,11... | collective-permute-start | bytes 49160 | tf_op jit(solution)/shard_map/ppermute | solution.py:75
